TPU v7x, 512 devices: a whole 4x4x16 slice. The times are simulated.
512 devices in a mesh: seq: 128 (over y, z, core), head: 4 (over x).
Axes of the slice: x: 4, y: 4, z: 16, core: 2. Of those that a mesh axis runs over, the one named last changes fastest.
Arguments:
- queries: float32 [768, 16384], P('head', 'seq'), may hold values from -6 to 6
- keys: float32 [768, 16384], P('head', 'seq'), may hold values from -6 to 6
- values: float32 [768, 16384], P('head', 'seq'), may hold values from -6 to 6
- counts: int32 [128], P('seq'), may hold values from 32 to 128
- out_weight: float32 [768, 768], P('head'), may hold values from -0.3125 to 0.3125
- cotangent: float32 [768, 16384], P('head', 'seq'), may hold values from -6 to 6
Outputs:
- output: float32 [768, 16384], P('head', 'seq')
- query_grad: float32 [768, 16384], P('head', 'seq')
- key_grad: float32 [768, 16384], P('head', 'seq')
- value_grad: float32 [768, 16384], P('head', 'seq')
- weight_grad: float32 [768, 768], P('head')
All inputs are finite; a program needn't handle non-finite values.
Results may differ from a plain program's by a relative error of at most 0.0014.
Values sent between devices are 32-bit elements; how exact they have to be, the bound alone decides.
No kernel may reach another device: no remote copies, remote signals or barrier semaphores. Data moves between devices by JAX's collectives and lax.ppermute only.
A program may use at most 64 MiB of HBM per device.

v0:
```python
import jax
import jax.numpy as jnp
from jax import lax
from jax.sharding import Mesh
from jax.sharding import PartitionSpec as P

HEAD = 64
SPACING_LOCAL = 1
SPACING_CENTRAL = 4
SPACING_WIDE = 16
LOG2_LOCAL = 1
LOG2_CENTRAL = 4
SEQ = ("seq_0", "seq_1", "seq_2")


PRECISE = lax.Precision.HIGHEST
MASKED_SCORE = -1e30


def from_partner(shard, axis, apart):
    return lax.ppermute(shard, axis, [(i, i ^ 1 << apart) for i in range(lax.axis_size(axis))])


def rows_first(arrays, axis, dims):
    turned = [jnp.moveaxis(a, dim, 0) for a, dim in zip(arrays, dims)]
    widths = [t[0].size for t in turned]
    both = jnp.concatenate([t.reshape(-1, w) for t, w in zip(turned, widths)], axis=1)
    filled = lax.all_gather(both, axis, axis=0, tiled=True)
    pieces = jnp.split(filled, [sum(widths[:k]) for k in range(1, len(widths))], axis=1)
    return tuple(
        (
            jnp.moveaxis(b.reshape(-1, *t.shape[1:]), 0, dim)
            for b, t, dim in zip(pieces, turned, dims)
        )
    )


def cut_along(shard, dim, devices):
    dims = shard.shape
    pieces = shard.reshape(*dims[:dim], devices, dims[dim] // devices, *dims[dim + 1 :])
    return jnp.moveaxis(pieces, dim, 0)


def sum_at_owner(shard, axis, dim):
    devices = lax.axis_size(axis)
    pieces = lax.all_to_all(cut_along(shard, dim, devices), axis, 0, 0, tiled=True)
    return jnp.sum(pieces, axis=0)


def sent_to_all(shard, axis):
    copies = jnp.broadcast_to(shard, (lax.axis_size(axis), *shard.shape))
    return lax.all_to_all(copies, axis, split_axis=0, concat_axis=0, tiled=True)


def joined_along(pieces, dim):
    pieces = jnp.moveaxis(pieces, 0, dim)
    dims = pieces.shape
    return pieces.reshape(*dims[:dim], dims[dim] * dims[dim + 1], *dims[dim + 2 :])


def gather_directly(shard, axis, dim):
    pieces = sent_to_all(shard, axis)
    return joined_along(pieces, dim)


def rows_for(lines, devices):
    spare = -len(lines) % devices
    return jnp.pad(lines, [(0, spare)] + [(0, 0)] * (lines.ndim - 1))


def gather_axes(shard, axes, dim):
    far, near = axes
    pieces = sent_to_all(sent_to_all(shard, far), near)
    return joined_along(pieces.swapaxes(0, 1).reshape(-1, *shard.shape), dim)


def sum_in_two_steps(shard, axes, dim):
    far, near = axes
    own = sum_at_owner(cut_along(shard, dim, lax.axis_size(far)), near, dim + 1)
    return jnp.sum(lax.all_to_all(own, far, 0, 0, tiled=True), axis=0)


def sum_by_parts(shard, axes):
    lines = shard.reshape(-1)
    padded = rows_for(lines, lax.axis_size(axes[0]) * lax.axis_size(axes[1]))
    whole = gather_axes(sum_in_two_steps(padded, axes, 0), axes, 0)
    return lax.slice_in_dim(whole, 0, len(lines)).reshape(shard.shape)


def pick_rows(block, chooser):
    spacing = chooser.shape[1]
    if spacing == 1:
        return block
    shaped = block.reshape(block.shape[:-1] + (block.shape[-1] // spacing, spacing))
    factor = chooser.reshape((chooser.shape[0],) + (1,) * (block.ndim - 1) + (spacing,))
    return jnp.sum(shaped * factor, axis=-1)


def place_rows(piece, chooser, filler):
    spacing = chooser.shape[1]
    if spacing == 1:
        return piece
    chosen = (chooser > 0.5).reshape((chooser.shape[0],) + (1,) * (piece.ndim - 1) + (spacing,))
    spread = jnp.where(chosen, piece[..., None], filler)
    return spread.reshape(piece.shape[:-1] + (piece.shape[-1] * spacing,))


def scores_of(query_rows, key_rows, key_live, score_scale):
    raw = jnp.einsum("heq,hek->hqk", query_rows, key_rows, precision=PRECISE) * score_scale
    return jnp.where(key_live[:, None, :] > 0.5, raw, MASKED_SCORE)


def segment_rows(bundle, extras, levels):
    for bit_index in range(levels):
        other_bundle, other_extras = from_partner((bundle, extras), SEQ, bit_index)
        bundle = jnp.concatenate([bundle, other_bundle], axis=3)
        extras = jnp.concatenate([extras, other_extras], axis=3)
    return (bundle, extras)


def key_side(key_own, value_own, own_live, far_query, far_grad, far_lse, far_delta, score_scale):
    scores = scores_of(far_query, key_own, own_live, score_scale)
    probabilities = jnp.exp(scores - far_lse[:, :, None])
    value_part = jnp.einsum("hqk,heq->hek", probabilities, far_grad, precision=PRECISE)
    prob_grads = jnp.einsum("heq,hek->hqk", far_grad, value_own, precision=PRECISE)
    score_grads = probabilities * (prob_grads - far_delta[:, :, None])
    key_part = score_scale * jnp.einsum("hqk,heq->hek", score_grads, far_query, precision=PRECISE)
    return (key_part, value_part)


def segment_grads_of(
    key_own, value_own, own_live, query_rows, grad_rows, lse_rows, delta_rows, levels, score_scale
):
    bundle = jnp.stack([query_rows, grad_rows])
    extras = jnp.stack([lse_rows, delta_rows])[:, :, None, :]
    bundle, extras = segment_rows(bundle, extras, levels)
    return key_side(
        key_own,
        value_own,
        own_live,
        bundle[0],
        bundle[1],
        extras[0, :, 0, :],
        extras[1, :, 0, :],
        score_scale,
    )


def on_device(queries, keys, values, counts, out_weight, cotangent):
    columns, row_count = queries.shape
    local_heads = columns // HEAD
    score_scale = HEAD ** (-0.5)
    shard_levels = lax.axis_size(SEQ).bit_length() - 1
    branches = (
        (SPACING_LOCAL, min(LOG2_LOCAL, shard_levels)),
        (SPACING_CENTRAL, min(LOG2_CENTRAL, shard_levels)),
    )
    global_heads = lax.axis_index("head") * local_heads + jnp.arange(local_heads, dtype=jnp.int32)
    active_rows = (jnp.arange(row_count, dtype=jnp.int32) < counts[0]).astype(jnp.float32)
    live_heads = jnp.broadcast_to(active_rows[None, :], (local_heads, row_count))
    q_all = queries.reshape(local_heads, HEAD, row_count)
    k_all = keys.reshape(local_heads, HEAD, row_count)
    v_all = values.reshape(local_heads, HEAD, row_count)

    def chooser_for(spacing):
        offsets = global_heads % spacing
        return (jnp.arange(spacing, dtype=jnp.int32)[None, :] == offsets[:, None]).astype(
            jnp.float32
        )

    remembered = []
    out_list = []
    lse_list = []
    for spacing_factor, levels in branches:
        chooser = chooser_for(spacing_factor)
        query_rows = pick_rows(q_all, chooser)
        key_own = pick_rows(k_all, chooser)
        value_own = pick_rows(v_all, chooser)
        own_live = pick_rows(live_heads, chooser)
        pairs, extras = segment_rows(
            jnp.stack([key_own, value_own]), own_live[None, :, None, :], levels
        )
        key_rows = pairs[0]
        value_rows = pairs[1]
        key_live = extras[0, :, 0, :]
        scores = scores_of(query_rows, key_rows, key_live, score_scale)
        row_max = jnp.max(scores, axis=-1)
        weights = jnp.exp(scores - row_max[..., None])
        denominator = jnp.sum(weights, axis=-1)
        branch_out = (
            jnp.einsum("hqk,hek->heq", weights, value_rows, precision=PRECISE)
            / denominator[:, None, :]
        )
        log_total = row_max + jnp.log(denominator)
        out_list.append(place_rows(branch_out, chooser, 0.0))
        lse_list.append(place_rows(log_total, chooser, MASKED_SCORE))
        remembered.append(
            (
                chooser,
                levels,
                query_rows,
                key_own,
                value_own,
                own_live,
                key_rows,
                value_rows,
                key_live,
            )
        )
    far_chooser = chooser_for(SPACING_WIDE)
    far_query = pick_rows(q_all, far_chooser)
    far_key = pick_rows(k_all, far_chooser)
    far_value = pick_rows(v_all, far_chooser)
    far_live = pick_rows(live_heads, far_chooser)
    far_pairs = jnp.stack([far_key, far_value])
    far_extras = far_live[None, :, None, :]
    far_rows = far_query.shape[2]
    running_max = jnp.full((local_heads, far_rows), MASKED_SCORE, jnp.float32)
    pairs_piece, extras_piece = rows_first((far_pairs, far_extras), SEQ, (3, 3))
    absorb_scores = scores_of(far_query, pairs_piece[0], extras_piece[0, :, 0, :], score_scale)
    newest = jnp.maximum(running_max, jnp.max(absorb_scores, axis=-1))
    weights = jnp.exp(absorb_scores - newest[..., None])
    summed = jnp.sum(weights, axis=-1)
    gathered = jnp.einsum("hqk,hek->heq", weights, pairs_piece[1], precision=PRECISE)
    out_list.append(place_rows(gathered / summed[:, None, :], far_chooser, 0.0))
    lse_list.append(place_rows(newest + jnp.log(summed), far_chooser, MASKED_SCORE))
    stacked = jnp.stack(lse_list)
    row_peak = jnp.max(stacked, axis=0)
    combined_lse = row_peak + jnp.log(jnp.sum(jnp.exp(stacked - row_peak[None]), axis=0))
    combined = jnp.zeros((local_heads, HEAD, row_count), jnp.float32)
    for spread_lse, spread_out in zip(lse_list, out_list):
        combined = combined + jnp.exp(spread_lse - combined_lse)[:, None, :] * spread_out
    attended = (combined * active_rows[None, None, :]).reshape(columns, row_count)
    terms = lax.dot_general(
        out_weight,
        attended,
        (((0,), (0,)), ((), ())),
        precision=PRECISE,
        preferred_element_type=jnp.float32,
    )
    output = sum_at_owner(terms, "head", 0)
    full_grad = gather_directly(cotangent, "head", 0)
    grad_attended = jnp.dot(
        out_weight, full_grad, precision=PRECISE, preferred_element_type=jnp.float32
    )
    weight_local = lax.dot_general(
        attended,
        full_grad,
        (((1,), (1,)), ((), ())),
        precision=PRECISE,
        preferred_element_type=jnp.float32,
    )
    weight_grad = sum_by_parts(weight_local, (("seq_0", "seq_1"), "seq_2"))
    grad_all = grad_attended.reshape(local_heads, HEAD, row_count) * active_rows[None, None, :]
    delta_all = jnp.sum(grad_all * combined, axis=1)
    query_grad = jnp.zeros((local_heads, HEAD, row_count), jnp.float32)
    key_grad = jnp.zeros((local_heads, HEAD, row_count), jnp.float32)
    value_grad = jnp.zeros((local_heads, HEAD, row_count), jnp.float32)
    for (
        chooser,
        levels,
        query_rows,
        key_own,
        value_own,
        own_live,
        key_rows,
        value_rows,
        key_live,
    ) in remembered:
        grad_rows = pick_rows(grad_all, chooser)
        lse_rows = pick_rows(combined_lse, chooser)
        delta_rows = pick_rows(delta_all, chooser)
        scores = scores_of(query_rows, key_rows, key_live, score_scale)
        probabilities = jnp.exp(scores - lse_rows[:, :, None])
        prob_grads = jnp.einsum("heq,hek->hqk", grad_rows, value_rows, precision=PRECISE)
        score_grads = probabilities * (prob_grads - delta_rows[:, :, None])
        query_part = score_scale * jnp.einsum(
            "hqk,hek->heq", score_grads, key_rows, precision=PRECISE
        )
        key_part, value_part = segment_grads_of(
            key_own,
            value_own,
            own_live,
            query_rows,
            grad_rows,
            lse_rows,
            delta_rows,
            levels,
            score_scale,
        )
        query_grad = query_grad + place_rows(query_part, chooser, 0.0)
        key_grad = key_grad + place_rows(key_part, chooser, 0.0)
        value_grad = value_grad + place_rows(value_part, chooser, 0.0)
    far_grad = pick_rows(grad_all, far_chooser)
    far_lse = pick_rows(combined_lse, far_chooser)
    far_delta = pick_rows(delta_all, far_chooser)
    pairs_piece, extras_piece = rows_first((far_pairs, far_extras), SEQ, (3, 3))
    scores = scores_of(far_query, pairs_piece[0], extras_piece[0, :, 0, :], score_scale)
    probabilities = jnp.exp(scores - far_lse[:, :, None])
    prob_grads = jnp.einsum("heq,hek->hqk", far_grad, pairs_piece[1], precision=PRECISE)
    score_grads = probabilities * (prob_grads - far_delta[:, :, None])
    far_query_part = score_scale * jnp.einsum(
        "hqk,hek->heq", score_grads, pairs_piece[0], precision=PRECISE
    )
    far_bundle = jnp.stack([far_query, far_grad])
    far_stats = jnp.stack([far_lse, far_delta])[:, :, None, :]
    bundle_piece, stats_piece = rows_first((far_bundle, far_stats), SEQ, (3, 3))
    key_part, value_part = key_side(
        far_key,
        far_value,
        far_live,
        bundle_piece[0],
        bundle_piece[1],
        stats_piece[0, :, 0, :],
        stats_piece[1, :, 0, :],
        score_scale,
    )
    query_grad = query_grad + place_rows(far_query_part, far_chooser, 0.0)
    key_grad = key_grad + place_rows(key_part, far_chooser, 0.0)
    value_grad = value_grad + place_rows(value_part, far_chooser, 0.0)
    return (
        output,
        query_grad.reshape(columns, row_count),
        key_grad.reshape(columns, row_count),
        value_grad.reshape(columns, row_count),
        weight_grad,
    )


def solution(mesh):
    split = Mesh(
        mesh.devices.reshape(4, 16, 2, mesh.shape["head"]), ("seq_0", "seq_1", "seq_2", "head")
    )
    in_specs = (
        P("head", SEQ),
        P("head", SEQ),
        P("head", SEQ),
        P(SEQ),
        P("head", None),
        P("head", SEQ),
    )
    out_specs = (P("head", SEQ), P("head", SEQ), P("head", SEQ), P("head", SEQ), P("head", None))
    return jax.shard_map(
        on_device, mesh=split, in_specs=in_specs, out_specs=out_specs, check_vma=False
    )
```

profile of v0, /device:TPU:1, one launch (start us, length us, event | category | flops | bytes accessed | tf_op | source)
XLA Modules:
  0.0 441.4 jit_solution(12118240763969096378)
XLA Ops:
  8.0 8.7 %collective-permute-start = (f32[1,3,1,128]{3,1,2,0:T(4,128)S(1)}, f32[1,3,1,128]{3,1,2,0:T(4,128)S(1)}, u32[]{:S(2)}, u32[]{:S(2)}) collective-permute-start(f32[1,3,1,128]{3,1,2,0:T(4,128)S(1)} %broadcast_in_dim_broadcast_in_dim.2), channel_id=1, source_target_pairs={{0,4},{4,0},{8,12},{12,8},{16,20},{20,16},{24,28},{28,24},{32,36},... | collective-permute-start | bytes 4616 | tf_op jit(solution)/shard_map/ppermute | solution.py:21
  20.5 2.5 collective-permute-start.1
  24.7 3.5 all-to-all-start.1
  39.7 7.1 %collective-permute-start.5 = (f32[1,3,1,256]{3,1,2,0:T(4,128)S(1)}, f32[1,3,1,256]{3,1,2,0:T(4,128)S(1)}, u32[]{:S(2)}, u32[]{:S(2)}) collective-permute-start(f32[1,3,1,256]{3,1,2,0:T(4,128)S(1)} %pad_maximum_fusion.16), channel_id=1, source_target_pairs={{0,32},{4,36},{8,40},{12,44},{16,48},{20,52},{24,56},{28,60},{32,0... | collective-permute-start | bytes 9224 | tf_op jit(solution)/shard_map/ppermute | solution.py:21
  54.5 4.3 collective-permute-start.6
  60.0 3.1 collective-permute-start.7
  63.2 2.6 collective-permute-start.12
  65.8 2.2 collective-permute-done.7
  68.2 4.2 collective-permute-start.8
  72.4 3.4 collective-permute-start.10
  77.9 3.6 collective-permute-done.8
  81.7 7.4 %collective-permute-start.9 = (f32[2,3,64,256]{3,2,1,0:T(8,128)S(1)}, f32[2,3,64,256]{3,2,1,0:T(8,128)}, u32[]{:S(2)}, u32[]{:S(2)}) collective-permute-start(f32[2,3,64,256]{3,2,1,0:T(8,128)S(1)} %pad_maximum_fusion.1), channel_id=1, source_target_pairs={{0,32},{4,36},{8,40},{12,44},{16,48},{20,52},{24,56},{28,60},{32,0... | collective-permute-start | bytes 1179656 | tf_op jit(solution)/shard_map/ppermute | solution.py:21
  93.4 10.5 %collective-permute-done.14 = f32[2,3,64,128]{3,2,1,0:T(8,128)S(1)} collective-permute-done((f32[2,3,64,128]{3,2,1,0:T(8,128)}, f32[2,3,64,128]{3,2,1,0:T(8,128)S(1)}, u32[]{:S(2)}, u32[]{:S(2)}) %collective-permute-start.14) | collective-permute-done | bytes 196640 | tf_op jit(solution)/shard_map/ppermute | solution.py:21
  104.9 45.4 %collective-permute-start.15 = (f32[2,3,64,256]{3,2,1,0:T(8,128)}, f32[2,3,64,256]{3,2,1,0:T(8,128)}, u32[]{:S(2)}, u32[]{:S(2)}) collective-permute-start(f32[2,3,64,256]{3,2,1,0:T(8,128)} %pad_maximum_fusion.3), channel_id=1, source_target_pairs={{0,32},{4,36},{8,40},{12,44},{16,48},{20,52},{24,56},{28,60},{32,0... | collective-permute-start | bytes 1179656 | tf_op jit(solution)/shard_map/ppermute | solution.py:21
  155.9 12.3 %collective-permute-done.15 = f32[2,3,64,256]{3,2,1,0:T(8,128)} collective-permute-done((f32[2,3,64,256]{3,2,1,0:T(8,128)}, f32[2,3,64,256]{3,2,1,0:T(8,128)}, u32[]{:S(2)}, u32[]{:S(2)}) %collective-permute-start.15) | collective-permute-done | bytes 393248 | tf_op jit(solution)/shard_map/ppermute | solution.py:21
  169.6 73.2 %all-gather.3.cloned.1.call-done = f32[1024,387]{1,0:T(8,128)} async-done(((f32[8,387]{1,0:T(8,128)}), f32[1024,387]{1,0:T(8,128)}) %all-gather.3.cloned.1.call-update) | async-done | bytes 1585168 | tf_op jit(solution)/shard_map/all_gather | solution.py:28
  244.7 2.7 split.19
  269.9 2.9 multiply_reduce_fusion.6
  286.9 2.2 convolution_bitcast_fusion
  291.2 4.9 %all_to_all.38 = f32[2,64,1152]{2,1,0:T(8,128)} all-to-all(f32[2,64,1152]{2,1,0:T(8,128)S(1)} %bitcast.244), channel_id=1, replica_groups=mesh['seq_0'=4,'seq_1'=16,'seq_2'=2,'head'=4] {'seq_2'}, dimensions={0} | all-to-all | bytes 1179648 | tf_op jit(solution)/shard_map/all_to_all | solution.py:46
  299.9 10.6 %all-to-all-start.3 = ((f32[64,1,1152]{2,1,0:T(1,128)}), f32[64,1,1152]{2,1,0:T(1,128)}, u32[]{:S(2)}, u32[]{:S(2)}) async-start(f32[64,1,1152]{2,1,0:T(1,128)} %all_to_all.27), calls=%async_computation.3 | async-start | bytes 589824 | tf_op jit(solution)/shard_map/all_to_all | solution.py:80
  312.6 2.3 fusion
  314.9 2.7 collective-permute-start.16
  319.2 3.3 collective-permute-start.17
  326.5 4.1 collective-permute-start.18
  332.9 4.0 all-to-all-start
  337.6 7.0 %collective-permute-start.19 = (f32[2,3,1,256]{3,1,0,2:T(4,128)S(1)}, f32[2,3,1,256]{3,1,0,2:T(4,128)S(1)}, u32[]{:S(2)}, u32[]{:S(2)}) collective-permute-start(f32[2,3,1,256]{3,1,0,2:T(4,128)S(1)} %pad_maximum_fusion.14), channel_id=1, source_target_pairs={{0,32},{4,36},{8,40},{12,44},{16,48},{20,52},{24,56},{28,60},{32,0... | collective-permute-start | bytes 18440 | tf_op jit(solution)/shard_map/ppermute | solution.py:21
  348.2 12.1 %all-to-all-start.4 = ((f32[64,1,1152]{2,1,0:T(1,128)}), f32[64,1,1152]{2,1,0:T(1,128)}, u32[]{:S(2)}, u32[]{:S(2)}) async-start(f32[64,1,1152]{2,1,0:T(1,128)} %broadcast_in_dim.367), calls=%async_computation.4 | async-start | bytes 589824 | tf_op jit(solution)/shard_map/all_to_all | solution.py:52
  364.3 15.6 %all-to-all-done.4 = f32[64,1,1152]{2,1,0:T(1,128)} async-done(((f32[64,1,1152]{2,1,0:T(1,128)}), f32[64,1,1152]{2,1,0:T(1,128)}, u32[]{:S(2)}, u32[]{:S(2)}) %all-to-all-start.4) | async-done | bytes 294944 | tf_op jit(solution)/shard_map/all_to_all | solution.py:52
  380.9 8.7 %all_to_all.39 = f32[2,64,1152]{2,1,0:T(8,128)S(1)} all-to-all(f32[2,64,1152]{2,1,0:T(8,128)S(1)} %broadcast_in_dim.368), channel_id=1, replica_groups=mesh['seq_0'=4,'seq_1'=16,'seq_2'=2,'head'=4] {'seq_2'}, dimensions={0} | all-to-all | bytes 1179648 | tf_op jit(solution)/shard_map/all_to_all | solution.py:52
  391.4 30.2 %all-gather.5.cloned.1.call-done = f32[1024,390]{1,0:T(8,128)} async-done(((f32[8,390]{1,0:T(8,128)}), f32[1024,390]{1,0:T(8,128)}) %all-gather.5.cloned.1.call-update) | async-done | bytes 1597456 | tf_op jit(solution)/shard_map/all_gather | solution.py:28
  422.9 2.7 split.20
  (287 shorter events, 115.7 us)
Async XLA Ops:
  7.2 40.9 %copy-start = (f32[192,768]{1,0:T(8,128)S(1)}, f32[192,768]{1,0:T(8,128)}, u32[]{:S(2)}) copy-start(f32[192,768]{1,0:T(8,128)} %param.10) | copy-start | bytes 1769476
  7.2 30.4 %copy-start.10 = (f32[192,128]{1,0:T(8,128)S(1)}, f32[192,128]{1,0:T(8,128)}, u32[]{:S(2)}) copy-start(f32[192,128]{1,0:T(8,128)} %param.7) | copy-start | bytes 294916
  7.2 30.5 %copy-start.12 = (f32[192,128]{1,0:T(8,128)S(1)}, f32[192,128]{1,0:T(8,128)}, u32[]{:S(2)}) copy-start(f32[192,128]{1,0:T(8,128)} %param.8) | copy-start | bytes 294916
  7.9 40.2 %copy-start.45 = (f32[128]{0:T(128)}, f32[128]{0:T(128)S(1)}, u32[]{:S(2)}) copy-start(f32[128]{0:T(128)S(1)} %compare_convert_fusion) | copy-start | bytes 1540
  8.0 38.9 %collective-permute-start = (f32[1,3,1,128]{3,1,2,0:T(4,128)S(1)}, f32[1,3,1,128]{3,1,2,0:T(4,128)S(1)}, u32[]{:S(2)}, u32[]{:S(2)}) collective-permute-start(f32[1,3,1,128]{3,1,2,0:T(4,128)S(1)} %broadcast_in_dim_broadcast_in_dim.2), channel_id=1, source_target_pairs={{0,4},{4,0},{8,12},{12,8},{16,20},{20,16},{24,28},{28,24},{32,36},... | collective-permute-start | bytes 4616 | tf_op jit(solution)/shard_map/ppermute | solution.py:21
  16.9 12.0 %collective-permute-start.2 = (f32[1,3,1,32]{3,1,2,0:T(4,128)S(1)}, f32[1,3,1,32]{3,1,2,0:T(4,128)S(1)}, u32[]{:S(2)}, u32[]{:S(2)}) collective-permute-start(f32[1,3,1,32]{3,1,2,0:T(4,128)S(1)} %bitcast.276), channel_id=1, source_target_pairs={{0,4},{4,0},{8,12},{12,8},{16,20},{20,16},{24,28},{28,24},{32,36},... | collective-permute-start | bytes 1160 | tf_op jit(solution)/shard_map/ppermute | solution.py:21
  20.5 30.7 %collective-permute-start.1 = (f32[2,3,64,128]{3,2,1,0:T(8,128)}, f32[2,3,64,128]{3,2,1,0:T(8,128)}, u32[]{:S(2)}, u32[]{:S(2)}) collective-permute-start(f32[2,3,64,128]{3,2,1,0:T(8,128)} %pad_maximum_fusion.4), channel_id=1, source_target_pairs={{0,4},{4,0},{8,12},{12,8},{16,20},{20,16},{24,28},{28,24},{32,36},... | collective-permute-start | bytes 589832 | tf_op jit(solution)/shard_map/ppermute | solution.py:21
  24.7 23.4 %all-to-all-start.1 = ((f32[4,192,128]{2,1,0:T(8,128)}), f32[4,192,128]{2,1,0:T(8,128)S(1)}, u32[]{:S(2)}, u32[]{:S(2)}) async-start(f32[4,192,128]{2,1,0:T(8,128)} %broadcast_in_dim.342), calls=%async_computation.1 | async-start | bytes 786432 | tf_op jit(solution)/shard_map/all_to_all | solution.py:52
  28.2 214.6 %all-gather.3.cloned.1.call-start = ((), (), s32[]{:S(2)}) async-start(), calls=%async_computation.6 | async-start | bytes 2113536 | tf_op jit(solution)/shard_map/all_gather | solution.py:28
  29.0 4.6 %collective-permute-start.3 = (f32[1,3,1,64]{3,1,2,0:T(4,128)S(1)}, f32[1,3,1,64]{3,1,2,0:T(4,128)S(1)}, u32[]{:S(2)}, u32[]{:S(2)}) collective-permute-start(f32[1,3,1,64]{3,1,2,0:T(4,128)S(1)} %pad_maximum_fusion.20), channel_id=1, source_target_pairs={{0,8},{4,12},{8,0},{12,4},{16,24},{20,28},{24,16},{28,20},{32,40},... | collective-permute-start | bytes 2312 | tf_op jit(solution)/shard_map/ppermute | solution.py:21
  33.7 6.0 %collective-permute-start.4 = (f32[1,3,1,128]{3,1,2,0:T(4,128)S(1)}, f32[1,3,1,128]{3,1,2,0:T(4,128)S(1)}, u32[]{:S(2)}, u32[]{:S(2)}) collective-permute-start(f32[1,3,1,128]{3,1,2,0:T(4,128)S(1)} %pad_maximum_fusion.21), channel_id=1, source_target_pairs={{0,16},{4,20},{8,24},{12,28},{16,0},{20,4},{24,8},{28,12},{32,48},... | collective-permute-start | bytes 4616 | tf_op jit(solution)/shard_map/ppermute | solution.py:21
  39.7 8.2 %collective-permute-start.5 = (f32[1,3,1,256]{3,1,2,0:T(4,128)S(1)}, f32[1,3,1,256]{3,1,2,0:T(4,128)S(1)}, u32[]{:S(2)}, u32[]{:S(2)}) collective-permute-start(f32[1,3,1,256]{3,1,2,0:T(4,128)S(1)} %pad_maximum_fusion.16), channel_id=1, source_target_pairs={{0,32},{4,36},{8,40},{12,44},{16,48},{20,52},{24,56},{28,60},{32,0... | collective-permute-start | bytes 9224 | tf_op jit(solution)/shard_map/ppermute | solution.py:21
  50.6 371.0 %all-gather.5.cloned.1.call-start = ((), (), s32[]{:S(2)}) async-start(), calls=%async_computation.7 | async-start | bytes 2113536 | tf_op jit(solution)/shard_map/all_gather | solution.py:28
  54.5 5.4 %collective-permute-start.6 = (f32[2,3,64,32]{3,2,1,0:T(8,128)S(1)}, f32[2,3,64,32]{3,2,1,0:T(8,128)S(1)}, u32[]{:S(2)}, u32[]{:S(2)}) collective-permute-start(f32[2,3,64,32]{3,2,1,0:T(8,128)S(1)} %pad_maximum_fusion.5), channel_id=1, source_target_pairs={{0,4},{4,0},{8,12},{12,8},{16,20},{20,16},{24,28},{28,24},{32,36},... | collective-permute-start | bytes 147464 | tf_op jit(solution)/shard_map/ppermute | solution.py:21
  60.0 8.0 %collective-permute-start.7 = (f32[2,3,64,64]{3,2,1,0:T(8,128)S(1)}, f32[2,3,64,64]{3,2,1,0:T(8,128)S(1)}, u32[]{:S(2)}, u32[]{:S(2)}) collective-permute-start(f32[2,3,64,64]{3,2,1,0:T(8,128)S(1)} %pad_maximum_fusion.6), channel_id=1, source_target_pairs={{0,8},{4,12},{8,0},{12,4},{16,24},{20,28},{24,16},{28,20},{32,40},... | collective-permute-start | bytes 294920 | tf_op jit(solution)/shard_map/ppermute | solution.py:21
  63.2 12.6 %collective-permute-start.12 = (f32[2,3,64,32]{3,2,1,0:T(8,128)S(1)}, f32[2,3,64,32]{3,2,1,0:T(8,128)S(1)}, u32[]{:S(2)}, u32[]{:S(2)}) collective-permute-start(f32[2,3,64,32]{3,2,1,0:T(8,128)S(1)} %pad_maximum_fusion.9), channel_id=1, source_target_pairs={{0,4},{4,0},{8,12},{12,8},{16,20},{20,16},{24,28},{28,24},{32,36},... | collective-permute-start | bytes 147464 | tf_op jit(solution)/shard_map/ppermute | solution.py:21
  68.2 13.3 %collective-permute-start.8 = (f32[2,3,64,128]{3,2,1,0:T(8,128)S(1)}, f32[2,3,64,128]{3,2,1,0:T(8,128)S(1)}, u32[]{:S(2)}, u32[]{:S(2)}) collective-permute-start(f32[2,3,64,128]{3,2,1,0:T(8,128)S(1)} %pad_maximum_fusion.7), channel_id=1, source_target_pairs={{0,16},{4,20},{8,24},{12,28},{16,0},{20,4},{24,8},{28,12},{32,48},... | collective-permute-start | bytes 589832 | tf_op jit(solution)/shard_map/ppermute | solution.py:21
  72.4 20.2 %collective-permute-start.10 = (f32[2,3,64,128]{3,2,1,0:T(8,128)S(1)}, f32[2,3,64,128]{3,2,1,0:T(8,128)S(1)}, u32[]{:S(2)}, u32[]{:S(2)}) collective-permute-start(f32[2,3,64,128]{3,2,1,0:T(8,128)S(1)} %pad_maximum_fusion.8), channel_id=1, source_target_pairs={{0,4},{4,0},{8,12},{12,8},{16,20},{20,16},{24,28},{28,24},{32,36},... | collective-permute-start | bytes 589832 | tf_op jit(solution)/shard_map/ppermute | solution.py:21
  76.0 13.2 %collective-permute-start.13 = (f32[2,3,64,64]{3,2,1,0:T(8,128)S(1)}, f32[2,3,64,64]{3,2,1,0:T(8,128)S(1)}, u32[]{:S(2)}, u32[]{:S(2)}) collective-permute-start(f32[2,3,64,64]{3,2,1,0:T(8,128)S(1)} %pad_maximum_fusion.10), channel_id=1, source_target_pairs={{0,8},{4,12},{8,0},{12,4},{16,24},{20,28},{24,16},{28,20},{32,40},... | collective-permute-start | bytes 294920 | tf_op jit(solution)/shard_map/ppermute | solution.py:21
  81.7 68.6 %collective-permute-start.9 = (f32[2,3,64,256]{3,2,1,0:T(8,128)S(1)}, f32[2,3,64,256]{3,2,1,0:T(8,128)}, u32[]{:S(2)}, u32[]{:S(2)}) collective-permute-start(f32[2,3,64,256]{3,2,1,0:T(8,128)S(1)} %pad_maximum_fusion.1), channel_id=1, source_target_pairs={{0,32},{4,36},{8,40},{12,44},{16,48},{20,52},{24,56},{28,60},{32,0... | collective-permute-start | bytes 1179656 | tf_op jit(solution)/shard_map/ppermute | solution.py:21
  90.0 13.9 %collective-permute-start.14 = (f32[2,3,64,128]{3,2,1,0:T(8,128)}, f32[2,3,64,128]{3,2,1,0:T(8,128)S(1)}, u32[]{:S(2)}, u32[]{:S(2)}) collective-permute-start(f32[2,3,64,128]{3,2,1,0:T(8,128)} %pad_maximum_fusion.11), channel_id=1, source_target_pairs={{0,16},{4,20},{8,24},{12,28},{16,0},{20,4},{24,8},{28,12},{32,48},... | collective-permute-start | bytes 589832 | tf_op jit(solution)/shard_map/ppermute | solution.py:21
  93.4 58.3 %copy-start.27 = (pred[3,512]{1,0:T(4,128)(4,1)S(1)}, pred[3,512]{1,0:T(4,128)(4,1)}, u32[]{:S(2)}) copy-start(pred[3,512]{1,0:T(4,128)(4,1)} %compare_bitcast_fusion) | copy-start | bytes 4612
  104.9 47.4 %copy-start.42 = (pred[3,4]{1,0:T(4,128)(4,1)S(1)}, pred[3,4]{1,0:T(4,128)(4,1)}, u32[]{:S(2)}) copy-start(pred[3,4]{1,0:T(4,128)(4,1)} %copy-done.41) | copy-start | bytes 40
  104.9 63.3 %collective-permute-start.15 = (f32[2,3,64,256]{3,2,1,0:T(8,128)}, f32[2,3,64,256]{3,2,1,0:T(8,128)}, u32[]{:S(2)}, u32[]{:S(2)}) collective-permute-start(f32[2,3,64,256]{3,2,1,0:T(8,128)} %pad_maximum_fusion.3), channel_id=1, source_target_pairs={{0,32},{4,36},{8,40},{12,44},{16,48},{20,52},{24,56},{28,60},{32,0... | collective-permute-start | bytes 1179656 | tf_op jit(solution)/shard_map/ppermute | solution.py:21
  284.7 45.9 %collective-permute-start.11 = (f32[2,3,1,128]{3,1,0,2:T(4,128)}, f32[2,3,1,128]{3,1,0,2:T(4,128)}, u32[]{:S(2)}, u32[]{:S(2)}) collective-permute-start(f32[2,3,1,128]{3,1,0,2:T(4,128)} %maximum_bitcast_fusion.2), channel_id=1, source_target_pairs={{0,4},{4,0},{8,12},{12,8},{16,20},{20,16},{24,28},{28,24},{32,36},... | collective-permute-start | bytes 9224 | tf_op jit(solution)/shard_map/ppermute | solution.py:21
  299.9 32.9 %all-to-all-start.3 = ((f32[64,1,1152]{2,1,0:T(1,128)}), f32[64,1,1152]{2,1,0:T(1,128)}, u32[]{:S(2)}, u32[]{:S(2)}) async-start(f32[64,1,1152]{2,1,0:T(1,128)} %all_to_all.27), calls=%async_computation.3 | async-start | bytes 589824 | tf_op jit(solution)/shard_map/all_to_all | solution.py:80
  314.9 4.2 collective-permute-start.16
  319.2 7.2 %collective-permute-start.17 = (f32[2,3,1,64]{3,1,0,2:T(4,128)S(1)}, f32[2,3,1,64]{3,1,0,2:T(4,128)S(1)}, u32[]{:S(2)}, u32[]{:S(2)}) collective-permute-start(f32[2,3,1,64]{3,1,0,2:T(4,128)S(1)} %pad_maximum_fusion.17), channel_id=1, source_target_pairs={{0,8},{4,12},{8,0},{12,4},{16,24},{20,28},{24,16},{28,20},{32,40},... | collective-permute-start | bytes 4616 | tf_op jit(solution)/shard_map/ppermute | solution.py:21
  326.5 10.3 %collective-permute-start.18 = (f32[2,3,1,128]{3,1,0,2:T(4,128)S(1)}, f32[2,3,1,128]{3,1,0,2:T(4,128)S(1)}, u32[]{:S(2)}, u32[]{:S(2)}) collective-permute-start(f32[2,3,1,128]{3,1,0,2:T(4,128)S(1)} %pad_maximum_fusion.18), channel_id=1, source_target_pairs={{0,16},{4,20},{8,24},{12,28},{16,0},{20,4},{24,8},{28,12},{32,48},... | collective-permute-start | bytes 9224 | tf_op jit(solution)/shard_map/ppermute | solution.py:21
  332.9 14.5 %all-to-all-start = ((f32[4,192,128]{2,1,0:T(8,128)}), f32[4,192,128]{2,1,0:T(8,128)S(1)}, u32[]{:S(2)}, u32[]{:S(2)}) async-start(f32[4,192,128]{2,1,0:T(8,128)} %bitcast.33), calls=%async_computation | async-start | bytes 786432 | tf_op jit(solution)/shard_map/all_to_all | solution.py:46
  337.6 8.5 %collective-permute-start.19 = (f32[2,3,1,256]{3,1,0,2:T(4,128)S(1)}, f32[2,3,1,256]{3,1,0,2:T(4,128)S(1)}, u32[]{:S(2)}, u32[]{:S(2)}) collective-permute-start(f32[2,3,1,256]{3,1,0,2:T(4,128)S(1)} %pad_maximum_fusion.14), channel_id=1, source_target_pairs={{0,32},{4,36},{8,40},{12,44},{16,48},{20,52},{24,56},{28,60},{32,0... | collective-permute-start | bytes 18440 | tf_op jit(solution)/shard_map/ppermute | solution.py:21
  348.2 31.7 %all-to-all-start.4 = ((f32[64,1,1152]{2,1,0:T(1,128)}), f32[64,1,1152]{2,1,0:T(1,128)}, u32[]{:S(2)}, u32[]{:S(2)}) async-start(f32[64,1,1152]{2,1,0:T(1,128)} %broadcast_in_dim.367), calls=%async_computation.4 | async-start | bytes 589824 | tf_op jit(solution)/shard_map/all_to_all | solution.py:52
  (40 other events, 436.4 us)
Sparse Core Ops, SparseCore 0:
  50.7 192.0 all-gather.2
  283.5 137.9 all-gather.4
where the time goes:
time: 444 us; the launch traced here: 441 us
  waiting for transfers between devices  151 us (34%)
  starting transfers between devices  148 us (33%)
  local copies, waits for them, and re-layouts  54.4 us (12%)
  matrix products  30.4 us (7%)
  other arithmetic  27.7 us (6%)
  between operations  16 us (4%)
  blocking collectives  13.7 us (3%)
    ppermute x20, starting transfers between devices, from_partner(): lax.ppermute(shard, axis, [(i, i ^ 1 << apart) for i in range(lax.axis_si...  118 us
    all_gather x2, waiting for transfers between devices, rows_first(): filled = lax.all_gather(both, axis, axis=0, tiled=True)  103 us
    ppermute x20, waiting for transfers between devices, from_partner(): lax.ppermute(shard, axis, [(i, i ^ 1 << apart) for i in range(lax.axis_si...  32.5 us
    broadcast_in_dim x27, local copies, waits for them, and re-layouts, place_rows(): spread = jnp.where(chosen, piece[..., None], filler)  15.7 us
    all_to_all x2, starting transfers between devices, sent_to_all(): return lax.all_to_all(copies, axis, split_axis=0, concat_axis=0, tiled=True)  15.6 us
    all_to_all x2, waiting for transfers between devices, sent_to_all(): return lax.all_to_all(copies, axis, split_axis=0, concat_axis=0, tiled=True)  15.6 us
    all_to_all x1, starting transfers between devices, sum_in_two_steps(): return jnp.sum(lax.all_to_all(own, far, 0, 0, tiled=True), axis=0)  10.6 us
    split x6, local copies, waits for them, and re-layouts, rows_first(): jnp.split(filled, [sum(widths[:k]) for k in range(1, len(widths))], axis=1)  10.3 us
  transfers between devices with their start and end apart: 26, of which 10 were waited for; matrix products, arithmetic and copies ran while one was open for 13% of the time, Pallas kernels for 0%

commit v1 on v0

v1 whole, which is shorter than its diff:
```python
import jax
import jax.numpy as jnp
from jax import lax
from jax.experimental import pallas as pl
from jax.experimental.pallas import tpu as pltpu
from jax.sharding import Mesh
from jax.sharding import PartitionSpec as P

HEAD = 64
LOCAL_HEADS = 3
TOKENS = 128
SPACING_CENTRAL = 4
SPACING_WIDE = 16
MID_ROWS = TOKENS // SPACING_CENTRAL
FAR_ROWS = TOKENS // SPACING_WIDE
FAR_BLOCK = LOCAL_HEADS * FAR_ROWS
MID_BLOCK = LOCAL_HEADS * MID_ROWS
NEAR_BLOCK = LOCAL_HEADS * TOKENS
SCALE = HEAD ** (-0.5)
MASKED_SCORE = -1e30
DEAD_MARK = 1e6
DEAD_LEVEL = 1e5
INTERPRET = False
SEQ = ("y", "zh", "zl", "c")
Z = ("zh", "zl")


def dot(a, b, ca, cb):
    return lax.dot_general(
        a,
        b,
        (((ca,), (cb,)), ((), ())),
        precision=lax.Precision.HIGHEST,
        preferred_element_type=jnp.float32,
    )


def iota(shape, dim):
    return lax.broadcasted_iota(jnp.int32, shape, dim)


def chooser(rows, spacing, offset):
    shape = (rows, TOKENS)
    return (iota(shape, 1) == iota(shape, 0) * spacing + offset).astype(jnp.float32)


def placer(rows, spacing, offset):
    shape = (TOKENS, rows)
    return (iota(shape, 0) == iota(shape, 1) * spacing + offset).astype(jnp.float32)


def kernel_call(body, out_shape, operands, scalars):
    in_specs = [pl.BlockSpec(memory_space=pltpu.SMEM)] * scalars + [
        pl.BlockSpec(memory_space=pltpu.VMEM)
    ] * (len(operands) - scalars)
    return pl.pallas_call(
        body,
        out_shape=out_shape,
        in_specs=in_specs,
        out_specs=jax.tree.map(lambda _: pl.BlockSpec(memory_space=pltpu.VMEM), out_shape),
        interpret=INTERPRET,
    )(*operands)


def shaped(*dims):
    return jax.ShapeDtypeStruct(dims, jnp.float32)


def pack_body(count, base, k_ref, v_ref, far_ref, mid_ref, near_ref):
    feature = iota((2 * HEAD, TOKENS), 0)
    live = iota((2 * HEAD, TOKENS), 1) < count[0]
    for j in range(LOCAL_HEADS):
        rows = slice(HEAD * j, HEAD * (j + 1))
        both = jnp.concatenate([k_ref[rows, :], v_ref[rows, :]], axis=0)
        both = jnp.where(live, both, jnp.where(feature == 0, DEAD_MARK, 0.0))
        turned = both.T
        near_ref[TOKENS * j : TOKENS * (j + 1), :] = turned
        head = base[0] + j
        far = dot(chooser(FAR_ROWS, SPACING_WIDE, head % SPACING_WIDE), turned, 1, 0)
        mid = dot(chooser(MID_ROWS, SPACING_CENTRAL, head % SPACING_CENTRAL), turned, 1, 0)
        for i in range(far_ref.shape[0]):
            far_ref[i, FAR_ROWS * j : FAR_ROWS * (j + 1), :] = far
        for i in range(mid_ref.shape[0]):
            mid_ref[i, MID_ROWS * j : MID_ROWS * (j + 1), :] = mid


def query_body(count, base, q_ref, w_ref, cot_ref, far_ref, mid_ref, near_ref):
    live = iota((HEAD, TOKENS), 1) < count[0]
    grads = dot(w_ref[...], cot_ref[...], 1, 0)
    for j in range(LOCAL_HEADS):
        rows = slice(HEAD * j, HEAD * (j + 1))
        both = jnp.concatenate(
            [q_ref[rows, :] * SCALE, jnp.where(live, grads[rows, :], 0.0)], axis=0
        )
        turned = both.T
        head = base[0] + j
        near_ref[j] = turned
        far_ref[j] = dot(chooser(FAR_ROWS, SPACING_WIDE, head % SPACING_WIDE), turned, 1, 0)
        mid_ref[j] = dot(
            chooser(MID_ROWS, SPACING_CENTRAL, head % SPACING_CENTRAL), turned, 1, 0
        )


def branch_scores(turned, pairs):
    rows = turned.shape[0]
    left = iota((rows, 2 * HEAD), 1) < HEAD
    mark = ((iota((8, 2 * HEAD), 0) == 0) & (iota((8, 2 * HEAD), 1) == 0)).astype(jnp.float32)
    queries = jnp.concatenate(
        [jnp.where(left, turned, 0.0), jnp.where(left, 0.0, turned)], axis=0
    )
    products = dot(jnp.concatenate([queries, mark], axis=0), pairs, 1, 1)
    dead = products[2 * rows : 2 * rows + 1, :] > DEAD_LEVEL
    scores = jnp.where(dead, MASKED_SCORE, products[:rows])
    prob_grads = products[rows : 2 * rows]
    top = jnp.max(scores, axis=1, keepdims=True)
    weights = jnp.exp(scores - top)
    total = jnp.sum(weights, axis=1, keepdims=True)
    pulled = jnp.sum(weights * prob_grads, axis=1, keepdims=True)
    return queries, weights, prob_grads, top, total, pulled


def branch_grads(queries, weights, prob_grads, factor, delta, pairs):
    rows = weights.shape[0]
    probs = weights * factor
    score_grads = probs * (prob_grads - delta)
    both = jnp.concatenate([score_grads, probs], axis=0)
    sums = dot(both, pairs, 1, 0)
    left = iota((rows, 2 * HEAD), 1) < HEAD
    query_side = jnp.where(left, sums[:rows], sums[rows:])
    key_side = dot(both, queries, 0, 0)
    return query_side, key_side


def attention_body(
    count,
    base,
    core,
    qf_ref,
    qm_ref,
    qn_ref,
    near_own,
    near_other,
    mid_own,
    mid_other,
    far_own,
    far_other,
    w_ref,
    cot_ref,
    dq_ref,
    terms_ref,
    keep_ref,
    send_ref,
    *,
    unit_rows,
):
    units = far_own.shape[0]
    mid_units = mid_own.shape[0]
    mid_at = units * unit_rows
    near_at = mid_at + mid_units * MID_BLOCK
    lanes = iota((TOKENS, 128), 1)
    position = iota((TOKENS, 1), 0)
    attended = []
    for j in range(LOCAL_HEADS):
        head = base[0] + j
        fs = slice(FAR_ROWS * j, FAR_ROWS * (j + 1))
        ms = slice(MID_ROWS * j, MID_ROWS * (j + 1))
        ns = slice(TOKENS * j, TOKENS * (j + 1))
        far_pairs = jnp.concatenate(
            [
                far_own[:, fs, :].reshape(units * FAR_ROWS, 128),
                far_other[:, fs, :].reshape(units * FAR_ROWS, 128),
            ],
            axis=0,
        )
        mid_pairs = jnp.concatenate(
            [
                mid_own[:, ms, :].reshape(mid_units * MID_ROWS, 128),
                mid_other[:, ms, :].reshape(mid_units * MID_ROWS, 128),
            ],
            axis=0,
        )
        near_pairs = jnp.concatenate([near_own[ns, :], near_other[ns, :]], axis=0)
        far_off = head % SPACING_WIDE
        mid_off = head % SPACING_CENTRAL
        far = branch_scores(qf_ref[j], far_pairs)
        mid = branch_scores(qm_ref[j], mid_pairs)
        near = branch_scores(qn_ref[j], near_pairs)

        def columns(branch, rows):
            at = iota((rows, 128), 1)
            return jnp.where(at == 0, branch[3], jnp.where(at == 1, branch[4], branch[5]))

        far_put = placer(FAR_ROWS, SPACING_WIDE, far_off)
        mid_put = placer(MID_ROWS, SPACING_CENTRAL, mid_off)
        far_stats = dot(far_put, columns(far, FAR_ROWS), 1, 0)
        mid_stats = dot(mid_put, columns(mid, MID_ROWS), 1, 0)
        in_far = position % SPACING_WIDE == far_off
        in_mid = position % SPACING_CENTRAL == mid_off
        far_top = jnp.where(in_far, far_stats[:, 0:1], MASKED_SCORE)
        mid_top = jnp.where(in_mid, mid_stats[:, 0:1], MASKED_SCORE)
        near_top = near[3]
        top = jnp.maximum(near_top, jnp.maximum(mid_top, far_top))
        far_factor = jnp.exp(far_top - top)
        mid_factor = jnp.exp(mid_top - top)
        near_factor = jnp.exp(near_top - top)
        total = (
            near_factor * near[4]
            + mid_factor * mid_stats[:, 1:2]
            + far_factor * far_stats[:, 1:2]
        )
        far_factor = far_factor / total
        mid_factor = mid_factor / total
        near_factor = near_factor / total
        delta = (
            near_factor * near[5]
            + mid_factor * mid_stats[:, 2:3]
            + far_factor * far_stats[:, 2:3]
        )
        back = jnp.where(
            lanes == 0, far_factor, jnp.where(lanes == 1, mid_factor, delta)
        )
        far_back = dot(chooser(FAR_ROWS, SPACING_WIDE, far_off), back, 1, 0)
        mid_back = dot(chooser(MID_ROWS, SPACING_CENTRAL, mid_off), back, 1, 0)
        near_q, near_k = branch_grads(*near[:3], near_factor, delta, near_pairs)
        mid_q, mid_k = branch_grads(*mid[:3], mid_back[:, 1:2], mid_back[:, 2:3], mid_pairs)
        far_q, far_k = branch_grads(*far[:3], far_back[:, 0:1], far_back[:, 2:3], far_pairs)
        query_side = near_q + dot(mid_put, mid_q, 1, 0) + dot(far_put, far_q, 1, 0)
        turned = query_side.T
        dq_ref[HEAD * j : HEAD * (j + 1), :] = turned[:HEAD] * SCALE
        attended.append(turned[HEAD:])
        for ref, half in ((keep_ref, 0), (send_ref, 1)):
            for i in range(units):
                at = (half * units + i) * FAR_ROWS
                to = i * unit_rows + FAR_ROWS * j
                ref[to : to + FAR_ROWS, :] = far_k[at : at + FAR_ROWS]
            for i in range(mid_units):
                at = (half * mid_units + i) * MID_ROWS
                to = mid_at + i * MID_BLOCK + MID_ROWS * j
                ref[to : to + MID_ROWS, :] = mid_k[at : at + MID_ROWS]
            to = near_at + TOKENS * j
            ref[to : to + TOKENS, :] = near_k[half * TOKENS : (half + 1) * TOKENS]
    live = iota((HEAD * LOCAL_HEADS, TOKENS), 1) < count[0]
    rows = jnp.where(live, jnp.concatenate(attended, axis=0), 0.0)
    terms_ref[...] = dot(w_ref[...], rows, 0, 0)
    weight = dot(rows, cot_ref[...], 1, 1)
    wide = weight.shape[1] // 128
    tiles = [
        weight[8 * (t // wide) : 8 * (t // wide) + 8, 128 * (t % wide) : 128 * (t % wide) + 128]
        for t in range(wide * weight.shape[0] // 8)
    ]
    empty = jnp.zeros((8, 128), jnp.float32)
    first = core[0] == 0

    def tile(half, i, slot):
        t = slot * 2 * units + half * units + i
        return tiles[t] if t < len(tiles) else empty

    for i in range(units):
        for slot in range((unit_rows - FAR_BLOCK) // 8):
            low, high = tile(0, i, slot), tile(1, i, slot)
            to = i * unit_rows + FAR_BLOCK + 8 * slot
            keep_ref[to : to + 8, :] = jnp.where(first, low, high)
            send_ref[to : to + 8, :] = jnp.where(first, high, low)


def finish_body(base, far_ref, mid_ref, near_ref, other_ref, dk_ref, dv_ref):
    far_sum = far_ref[0, :FAR_BLOCK, :]
    for i in range(1, far_ref.shape[0]):
        far_sum = far_sum + far_ref[i, :FAR_BLOCK, :]
    mid_sum = mid_ref[0]
    for i in range(1, mid_ref.shape[0]):
        mid_sum = mid_sum + mid_ref[i]
    for j in range(LOCAL_HEADS):
        head = base[0] + j
        ns = slice(TOKENS * j, TOKENS * (j + 1))
        far_put = placer(FAR_ROWS, SPACING_WIDE, head % SPACING_WIDE)
        mid_put = placer(MID_ROWS, SPACING_CENTRAL, head % SPACING_CENTRAL)
        both = (
            near_ref[ns, :]
            + other_ref[ns, :]
            + dot(mid_put, mid_sum[MID_ROWS * j : MID_ROWS * (j + 1)], 1, 0)
            + dot(far_put, far_sum[FAR_ROWS * j : FAR_ROWS * (j + 1)], 1, 0)
        )
        turned = both.T
        dk_ref[HEAD * j : HEAD * (j + 1), :] = turned[:HEAD]
        dv_ref[HEAD * j : HEAD * (j + 1), :] = turned[HEAD:]


def exchange(pieces, axis):
    dims = pieces.shape
    flat = pieces.reshape(dims[0] * dims[1], dims[2])
    return lax.all_to_all(flat, axis, 0, 0, tiled=True).reshape(dims)


def from_partner(x):
    return lax.ppermute(x, "c", [(0, 1), (1, 0)])


def on_device(queries, keys, values, counts, out_weight, cotangent):
    ny, nz, nzl = lax.axis_size("y"), lax.axis_size(Z), lax.axis_size("zl")
    heads = lax.axis_size("h")
    columns, tokens = queries.shape
    base = (lax.axis_index("h") * LOCAL_HEADS).astype(jnp.int32).reshape(1)
    core = lax.axis_index("c").astype(jnp.int32).reshape(1)

    cot = exchange(jnp.broadcast_to(cotangent, (heads, columns, tokens)), "h")
    full_cot = cot.reshape(heads * columns, tokens)

    far_out, mid_out, near_own = kernel_call(
        pack_body,
        (shaped(nz, FAR_BLOCK, 128), shaped(nzl, MID_BLOCK, 128), shaped(NEAR_BLOCK, 128)),
        (counts, base, keys, values),
        2,
    )
    near_other = from_partner(near_own)
    far_line = exchange(far_out, Z)
    mid_own = exchange(mid_out, "zl")
    mid_other = from_partner(mid_own)
    far_plane = exchange(
        jnp.broadcast_to(far_line.reshape(1, nz * FAR_BLOCK, 128), (ny, nz * FAR_BLOCK, 128)), "y"
    )
    far_own = far_plane.reshape(ny * nz, FAR_BLOCK, 128)
    far_other = from_partner(far_own)

    query_far, query_mid, query_near = kernel_call(
        query_body,
        (
            shaped(LOCAL_HEADS, FAR_ROWS, 128),
            shaped(LOCAL_HEADS, MID_ROWS, 128),
            shaped(LOCAL_HEADS, TOKENS, 128),
        ),
        (counts, base, queries, out_weight, full_cot),
        2,
    )
    units = ny * nz
    tiles = out_weight.size // 1024
    slots = -(-tiles // (2 * units))
    unit_rows = FAR_BLOCK + 8 * slots
    rows = units * unit_rows + nzl * MID_BLOCK + NEAR_BLOCK
    query_grad, terms, keep, send = kernel_call(
        lambda *refs: attention_body(*refs, unit_rows=unit_rows),
        (shaped(columns, tokens), shaped(heads * columns, tokens), shaped(rows, 128), shaped(rows, 128)),
        (
            counts,
            base,
            core,
            query_far,
            query_mid,
            query_near,
            near_own,
            near_other,
            mid_own,
            mid_other,
            far_own,
            far_other,
            out_weight,
            full_cot,
        ),
        3,
    )
    received = from_partner(send)
    output = jnp.sum(exchange(terms.reshape(heads, columns, tokens), "h"), axis=0)

    mid_at = units * unit_rows
    near_at = mid_at + nzl * MID_BLOCK
    plane = (keep[:mid_at] + received[:mid_at]).reshape(ny, nz * unit_rows, 128)
    line = jnp.sum(exchange(plane, "y"), axis=0).reshape(nz, unit_rows, 128)
    parts = exchange(line, Z)
    mid_sums = exchange(
        (keep[mid_at:near_at] + received[mid_at:near_at]).reshape(nzl, MID_BLOCK, 128), "zl"
    )
    key_grad, value_grad = kernel_call(
        finish_body,
        (shaped(columns, tokens), shaped(columns, tokens)),
        (base, parts, mid_sums, keep[near_at:], received[near_at:]),
        1,
    )

    own_tiles = jnp.sum(parts[:, FAR_BLOCK:], axis=0)
    depth = 8 * slots
    in_line = exchange(jnp.broadcast_to(own_tiles, (nz, depth, 128)), Z)
    in_plane = exchange(
        jnp.broadcast_to(in_line.reshape(1, nz * depth, 128), (ny, nz * depth, 128)), "y"
    )
    own_half = in_plane.reshape(units, depth, 128)
    other_half = from_partner(own_half)
    first = core[0] == 0
    everything = jnp.stack(
        [jnp.where(first, own_half, other_half), jnp.where(first, other_half, own_half)]
    ).reshape(2 * units, slots, 8, 128)
    ordered = everything.swapaxes(0, 1).reshape(2 * units * slots, 8, 128)[:tiles]
    wide = out_weight.shape[1] // 128
    weight_grad = (
        ordered.reshape(tiles // wide, wide, 8, 128).swapaxes(1, 2).reshape(out_weight.shape)
    )
    return output, query_grad, key_grad, value_grad, weight_grad


def solution(mesh):
    split = Mesh(
        mesh.devices.reshape(4, 2, 8, 2, mesh.shape["head"]), ("y", "zh", "zl", "c", "h")
    )
    return on_mesh(split)


def on_mesh(split):
    in_specs = (
        P("h", SEQ),
        P("h", SEQ),
        P("h", SEQ),
        P(SEQ),
        P("h", None),
        P("h", SEQ),
    )
    out_specs = (P("h", SEQ), P("h", SEQ), P("h", SEQ), P("h", SEQ), P("h", None))
    return jax.shard_map(
        on_device, mesh=split, in_specs=in_specs, out_specs=out_specs, check_vma=False
    )
```

time: 444 us -> 241 us (0.54)
  the two profiles are of different devices: /device:TPU:1 before, /device:TPU:2 now
where the time goes in v1:
time: 241 us; the launch traced here: 240 us
  blocking collectives  113 us (47%)
  waiting for transfers between devices  56.7 us (24%)
  starting transfers between devices  34.5 us (14%)
  Pallas kernels  23.1 us (10%)
  local copies, waits for them, and re-layouts  6.71 us (3%)
  other arithmetic  4.14 us (2%)
    all_to_all x5, blocking collectives, exchange(): return lax.all_to_all(flat, axis, 0, 0, tiled=True).reshape(dims)  113 us
    all_to_all x5, waiting for transfers between devices, exchange(): return lax.all_to_all(flat, axis, 0, 0, tiled=True).reshape(dims)  52.6 us
    all_to_all x5, starting transfers between devices, exchange(): return lax.all_to_all(flat, axis, 0, 0, tiled=True).reshape(dims)  25 us
    pallas_call x4, Pallas kernels, kernel_call(): pl.pallas_call(body, out_shape=out_shape, in_specs=in_specs, out_specs=ja...  23.1 us
    ppermute x5, starting transfers between devices, from_partner(): return lax.ppermute(x, 'c', [(0, 1), (1, 0)])  9.56 us
  transfers between devices with their start and end apart: 10, of which 6 were waited for; matrix products, arithmetic and copies ran while one was open for 2% of the time, Pallas kernels for 3%

profile of v1, /device:TPU:2, one launch (start us, length us, event | category | flops | bytes accessed | tf_op | source)
XLA Modules:
  0.0 239.6 jit_solution(9450387775064859786)
XLA Ops:
  1.3 2.4 shard_map.102
  3.6 31.7 %all_to_all.74 = f32[16,24,128]{2,1,0:T(8,128)S(1)} all-to-all(f32[16,24,128]{2,1,0:T(8,128)} %get-tuple-element.22), channel_id=1, replica_groups=mesh['y'=4,'zh'=2,'zl'=8,'c'=2,'h'=4] {'zh','zl'}, dimensions={0} | all-to-all | bytes 393216 | tf_op jit(solution)/shard_map/all_to_all | solution.py:292
  35.4 13.9 %all_to_all.75 = f32[4,384,128]{2,1,0:T(8,128)S(1)} all-to-all(f32[4,384,128]{2,1,0:T(8,128)S(1)} %broadcast_in_dim.22), channel_id=1, replica_groups=mesh['y'=4,'zh'=2,'zl'=8,'c'=2,'h'=4] {'y'}, dimensions={0} | all-to-all | bytes 1572864 | tf_op jit(solution)/shard_map/all_to_all | solution.py:292
  49.3 7.7 %all-to-all-start.1 = ((f32[8,96,128]{2,1,0:T(8,128)}), f32[8,96,128]{2,1,0:T(8,128)S(1)}, u32[]{:S(2)}, u32[]{:S(2)}) async-start(f32[8,96,128]{2,1,0:T(8,128)} %get-tuple-element.21), calls=%async_computation.1 | async-start | bytes 786432 | tf_op jit(solution)/shard_map/all_to_all | solution.py:292
  57.0 1.9 collective-permute-start.2
  58.9 20.1 %all-to-all-done.1.refs_8_ = f32[8,96,128]{2,1,0:T(8,128)S(1)} async-done(((f32[8,96,128]{2,1,0:T(8,128)}), f32[8,96,128]{2,1,0:T(8,128)S(1)}, u32[]{:S(2)}, u32[]{:S(2)}) %all-to-all-start.1) | async-done | bytes 393248 | tf_op jit(solution)/shard_map/all_to_all | solution.py:292
  78.9 1.9 collective-permute-start.1
  80.9 0.8 broadcast_in_dim.20
  81.6 4.8 %all-to-all-start = ((f32[4,192,128]{2,1,0:T(8,128)}), f32[4,192,128]{2,1,0:T(8,128)S(1)}, u32[]{:S(2)}, u32[]{:S(2)}) async-start(f32[4,192,128]{2,1,0:T(8,128)} %broadcast_in_dim.20), calls=%async_computation | async-start | bytes 786432 | tf_op jit(solution)/shard_map/all_to_all | solution.py:292
  86.5 1.9 collective-permute-start
  88.4 5.4 %all-to-all-done = f32[4,192,128]{2,1,0:T(8,128)S(1)} async-done(((f32[4,192,128]{2,1,0:T(8,128)}), f32[4,192,128]{2,1,0:T(8,128)S(1)}, u32[]{:S(2)}, u32[]{:S(2)}) %all-to-all-start) | async-done | bytes 393248 | tf_op jit(solution)/shard_map/all_to_all | solution.py:292
  93.8 0.7 copy-done
  94.5 3.6 %shard_map.101 = (f32[3,8,128]{2,1,0:T(8,128)}, f32[3,32,128]{2,1,0:T(8,128)}, f32[3,128,128]{2,1,0:T(8,128)}) custom-call(s32[1]{0:T(128)S(6)} %copy.12.count.refs_0_, s32[1]{0:T(128)} %bitcast.base.refs_1_, f32[192,128]{1,0:T(8,128)} %q_ref.1, f32[192,768]{1,0:T(8,128)} %refs_12_.1, f32[768,128]{1,0:T(8,128)} %bitcast.26), custom_call_target="tpu_custom_call" | custom-call | tf_op jit(solution)/shard_map/pallas_call | solution.py:56
  99.2 14.8 %shard_map.103 = (f32[192,128]{1,0:T(8,128)}, f32[768,128]{1,0:T(8,128)}, f32[3712,128]{1,0:T(8,128)}, f32[3712,128]{1,0:T(8,128)}) custom-call(s32[1]{0:T(128)S(6)} %copy.12.count.refs_0_, s32[1]{0:T(128)} %bitcast.base.refs_1_, s32[1]{0:T(128)} %bitcast.1.refs_2_, f32[3,8,128]{2,1,0:T(8,128)} %get-tuple-element.17.refs_3_, ...), custom_call_target="tpu_custom_call" | custom-call | tf_op jit(solution)/shard_map/pallas_call | solution.py:56
  114.0 1.9 collective-permute-start.3
  115.9 4.1 %collective-permute-done.3 = f32[3712,128]{1,0:T(8,128)S(1)} collective-permute-done((f32[3712,128]{1,0:T(8,128)}, f32[3712,128]{1,0:T(8,128)S(1)}, u32[]{:S(2)}, u32[]{:S(2)}) %collective-permute-start.3) | collective-permute-done | bytes 1900576 | tf_op jit(solution)/shard_map/ppermute | solution.py:296
  119.9 1.4 slice_add_fusion
  121.4 20.9 %all_to_all.76 = f32[4,640,128]{2,1,0:T(8,128)S(1)} all-to-all(f32[4,640,128]{2,1,0:T(8,128)S(1)} %bitcast.24), channel_id=1, replica_groups=mesh['y'=4,'zh'=2,'zl'=8,'c'=2,'h'=4] {'y'}, dimensions={0} | all-to-all | bytes 2621440 | tf_op jit(solution)/shard_map/all_to_all | solution.py:292
  142.4 25.9 %all_to_all.77.far_ref = f32[16,40,128]{2,1,0:T(8,128)S(1)} all-to-all(f32[16,40,128]{2,1,0:T(8,128)S(1)} %bitcast.33), channel_id=1, replica_groups=mesh['y'=4,'zh'=2,'zl'=8,'c'=2,'h'=4] {'zh','zl'}, dimensions={0} | all-to-all | bytes 655360 | tf_op jit(solution)/shard_map/all_to_all | solution.py:292
  168.3 4.9 %all-to-all-start.4 = ((f32[4,192,128]{2,1,0:T(8,128)}), f32[4,192,128]{2,1,0:T(8,128)S(1)}, u32[]{:S(2)}, u32[]{:S(2)}) async-start(f32[4,192,128]{2,1,0:T(8,128)} %bitcast.37), calls=%async_computation.4 | async-start | bytes 786432 | tf_op jit(solution)/shard_map/all_to_all | solution.py:292
  173.2 5.9 %all-to-all-done.4 = f32[4,192,128]{2,1,0:T(8,128)S(1)} async-done(((f32[4,192,128]{2,1,0:T(8,128)}), f32[4,192,128]{2,1,0:T(8,128)S(1)}, u32[]{:S(2)}, u32[]{:S(2)}) %all-to-all-start.4) | async-done | bytes 393248 | tf_op jit(solution)/shard_map/all_to_all | solution.py:292
  179.1 20.6 %all_to_all.78 = f32[16,16,128]{2,1,0:T(8,128)S(1)} all-to-all(f32[16,16,128]{2,1,0:T(8,128)S(1)} %broadcast_in_dim.23), channel_id=1, replica_groups=mesh['y'=4,'zh'=2,'zl'=8,'c'=2,'h'=4] {'zh','zl'}, dimensions={0} | all-to-all | bytes 262144 | tf_op jit(solution)/shard_map/all_to_all | solution.py:292
  199.7 0.8 broadcast_in_dim.25
  200.5 3.5 %all-to-all-start.9 = ((f32[4,256,128]{2,1,0:T(8,128)}), f32[4,256,128]{2,1,0:T(8,128)S(1)}, u32[]{:S(2)}, u32[]{:S(2)}) async-start(f32[4,256,128]{2,1,0:T(8,128)} %broadcast_in_dim.25), calls=%async_computation.9 | async-start | bytes 1048576 | tf_op jit(solution)/shard_map/all_to_all | solution.py:292
  204.0 1.8 slice_add_fusion.1
  205.8 6.3 %all-to-all-done.9 = f32[4,256,128]{2,1,0:T(8,128)S(1)} async-done(((f32[4,256,128]{2,1,0:T(8,128)}), f32[4,256,128]{2,1,0:T(8,128)S(1)}, u32[]{:S(2)}, u32[]{:S(2)}) %all-to-all-start.9) | async-done | bytes 524320 | tf_op jit(solution)/shard_map/all_to_all | solution.py:292
  212.0 4.1 %all-to-all-start.7 = ((f32[8,96,128]{2,1,0:T(8,128)}), f32[8,96,128]{2,1,0:T(8,128)}, u32[]{:S(2)}, u32[]{:S(2)}) async-start(f32[8,96,128]{2,1,0:T(8,128)} %bitcast.8), calls=%async_computation.7 | async-start | bytes 786432 | tf_op jit(solution)/shard_map/all_to_all | solution.py:292
  216.1 1.9 collective-permute-start.4
  218.1 1.6 slice.28.near_ref
  221.0 15.0 %all-to-all-done.7.mid_ref = f32[8,96,128]{2,1,0:T(8,128)} async-done(((f32[8,96,128]{2,1,0:T(8,128)}), f32[8,96,128]{2,1,0:T(8,128)}, u32[]{:S(2)}, u32[]{:S(2)}) %all-to-all-start.7) | async-done | bytes 393248 | tf_op jit(solution)/shard_map/all_to_all | solution.py:292
  236.1 2.4 %shard_map.104 = (f32[192,128]{1,0:T(8,128)}, f32[192,128]{1,0:T(8,128)}) custom-call(s32[1]{0:T(128)} %bitcast.base.refs_1_, f32[16,40,128]{2,1,0:T(8,128)} %copy-done.2, f32[8,96,128]{2,1,0:T(8,128)} %all-to-all-done.7.mid_ref, f32[384,128]{1,0:T(8,128)} %slice.28.near_ref, f32[384,128]{1,0:T(8,128)} %slice.34.other_ref), custom_call_target="tpu_custom_call" | custom-call | tf_op jit(solution)/shard_map/pallas_call | solution.py:56
  238.7 0.9 slice.36
  (30 shorter events, 2.8 us)
Async XLA Ops:
  3.6 77.2 %copy-start.8 = (f32[192,128]{1,0:T(8,128)S(1)}, f32[192,128]{1,0:T(8,128)}, u32[]{:S(2)}) copy-start(f32[192,128]{1,0:T(8,128)} %param.11) | copy-start | bytes 294916
  35.4 51.1 %copy-start.6 = (f32[384,128]{1,0:T(8,128)S(1)}, f32[384,128]{1,0:T(8,128)}, u32[]{:S(2)}) copy-start(f32[384,128]{1,0:T(8,128)} %get-tuple-element.20.refs_6_) | copy-start | bytes 589828
  49.3 48.8 %copy-start.1 = (f32[4,384,128]{2,1,0:T(8,128)}, f32[4,384,128]{2,1,0:T(8,128)S(1)}, u32[]{:S(2)}) copy-start(f32[4,384,128]{2,1,0:T(8,128)S(1)} %all_to_all.75) | copy-start | bytes 2359300
  49.3 29.7 %all-to-all-start.1 = ((f32[8,96,128]{2,1,0:T(8,128)}), f32[8,96,128]{2,1,0:T(8,128)S(1)}, u32[]{:S(2)}, u32[]{:S(2)}) async-start(f32[8,96,128]{2,1,0:T(8,128)} %get-tuple-element.21), calls=%async_computation.1 | async-start | bytes 786432 | tf_op jit(solution)/shard_map/all_to_all | solution.py:292
  57.0 41.1 %collective-permute-start.2 = (f32[64,24,128]{2,1,0:T(8,128)S(1)}, f32[64,24,128]{2,1,0:T(8,128)S(1)}, u32[]{:S(2)}, u32[]{:S(2)}) collective-permute-start(f32[64,24,128]{2,1,0:T(8,128)S(1)} %bitcast.28), channel_id=1, source_target_pairs={{0,4},{4,0},{1,5},{5,1},{2,6},{6,2},{3,7},{7,3},{8,12},{12,8},{9,1... | collective-permute-start | bytes 2359304 | tf_op jit(solution)/shard_map/ppermute | solution.py:296
  78.9 19.2 %copy-start.3 = (f32[8,96,128]{2,1,0:T(8,128)}, f32[8,96,128]{2,1,0:T(8,128)S(1)}, u32[]{:S(2)}) copy-start(f32[8,96,128]{2,1,0:T(8,128)S(1)} %all-to-all-done.1.refs_8_) | copy-start | bytes 1179652
  78.9 19.1 %collective-permute-start.1 = (f32[8,96,128]{2,1,0:T(8,128)S(1)}, f32[8,96,128]{2,1,0:T(8,128)S(1)}, u32[]{:S(2)}, u32[]{:S(2)}) collective-permute-start(f32[8,96,128]{2,1,0:T(8,128)S(1)} %all-to-all-done.1.refs_8_), channel_id=1, source_target_pairs={{0,4},{4,0},{1,5},{5,1},{2,6},{6,2},{3,7},{7,3},{8,12},{12,8},{9,1... | collective-permute-start | bytes 1179656 | tf_op jit(solution)/shard_map/ppermute | solution.py:296
  81.6 12.1 %all-to-all-start = ((f32[4,192,128]{2,1,0:T(8,128)}), f32[4,192,128]{2,1,0:T(8,128)S(1)}, u32[]{:S(2)}, u32[]{:S(2)}) async-start(f32[4,192,128]{2,1,0:T(8,128)} %broadcast_in_dim.20), calls=%async_computation | async-start | bytes 786432 | tf_op jit(solution)/shard_map/all_to_all | solution.py:292
  86.5 11.6 %collective-permute-start = (f32[384,128]{1,0:T(8,128)S(1)}, f32[384,128]{1,0:T(8,128)S(1)}, u32[]{:S(2)}, u32[]{:S(2)}) collective-permute-start(f32[384,128]{1,0:T(8,128)S(1)} %copy-done.6), channel_id=1, source_target_pairs={{0,4},{4,0},{1,5},{5,1},{2,6},{6,2},{3,7},{7,3},{8,12},{12,8},{9,1... | collective-permute-start | bytes 589832 | tf_op jit(solution)/shard_map/ppermute | solution.py:296
  93.8 0.7 copy-start
  98.1 0.7 copy-start.7
  98.1 0.8 copy-start.5
  98.1 1.1 copy-start.4
  114.0 6.0 %collective-permute-start.3 = (f32[3712,128]{1,0:T(8,128)}, f32[3712,128]{1,0:T(8,128)S(1)}, u32[]{:S(2)}, u32[]{:S(2)}) collective-permute-start(f32[3712,128]{1,0:T(8,128)} %get-tuple-element.26), channel_id=1, source_target_pairs={{0,4},{4,0},{1,5},{5,1},{2,6},{6,2},{3,7},{7,3},{8,12},{12,8},{9,1... | collective-permute-start | bytes 5701640 | tf_op jit(solution)/shard_map/ppermute | solution.py:296
  168.3 37.5 %copy-start.2 = (f32[16,40,128]{2,1,0:T(8,128)}, f32[16,40,128]{2,1,0:T(8,128)S(1)}, u32[]{:S(2)}) copy-start(f32[16,40,128]{2,1,0:T(8,128)S(1)} %all_to_all.77.far_ref) | copy-start | bytes 983044
  168.3 10.8 %all-to-all-start.4 = ((f32[4,192,128]{2,1,0:T(8,128)}), f32[4,192,128]{2,1,0:T(8,128)S(1)}, u32[]{:S(2)}, u32[]{:S(2)}) async-start(f32[4,192,128]{2,1,0:T(8,128)} %bitcast.37), calls=%async_computation.4 | async-start | bytes 786432 | tf_op jit(solution)/shard_map/all_to_all | solution.py:292
  200.5 11.5 %all-to-all-start.9 = ((f32[4,256,128]{2,1,0:T(8,128)}), f32[4,256,128]{2,1,0:T(8,128)S(1)}, u32[]{:S(2)}, u32[]{:S(2)}) async-start(f32[4,256,128]{2,1,0:T(8,128)} %broadcast_in_dim.25), calls=%async_computation.9 | async-start | bytes 1048576 | tf_op jit(solution)/shard_map/all_to_all | solution.py:292
  212.0 24.0 %all-to-all-start.7 = ((f32[8,96,128]{2,1,0:T(8,128)}), f32[8,96,128]{2,1,0:T(8,128)}, u32[]{:S(2)}, u32[]{:S(2)}) async-start(f32[8,96,128]{2,1,0:T(8,128)} %bitcast.8), calls=%async_computation.7 | async-start | bytes 786432 | tf_op jit(solution)/shard_map/all_to_all | solution.py:292
  216.1 22.3 %collective-permute-start.4 = (f32[64,16,128]{2,1,0:T(8,128)S(1)}, f32[64,16,128]{2,1,0:T(8,128)S(1)}, u32[]{:S(2)}, u32[]{:S(2)}) collective-permute-start(f32[64,16,128]{2,1,0:T(8,128)S(1)} %bitcast.31), channel_id=1, source_target_pairs={{0,4},{4,0},{1,5},{5,1},{2,6},{6,2},{3,7},{7,3},{8,12},{12,8},{9,1... | collective-permute-start | bytes 1572872 | tf_op jit(solution)/shard_map/ppermute | solution.py:296

commit v2 on v1

v2 whole, which is shorter than its diff:
```python
import jax
import jax.numpy as jnp
from jax import lax
from jax.experimental import pallas as pl
from jax.experimental.pallas import tpu as pltpu
from jax.sharding import Mesh
from jax.sharding import PartitionSpec as P

HEAD = 64
LOCAL_HEADS = 3
TOKENS = 128
SPACING_CENTRAL = 4
SPACING_WIDE = 16
MID_ROWS = TOKENS // SPACING_CENTRAL
FAR_ROWS = TOKENS // SPACING_WIDE
FAR_BLOCK = LOCAL_HEADS * FAR_ROWS
MID_BLOCK = LOCAL_HEADS * MID_ROWS
NEAR_BLOCK = LOCAL_HEADS * TOKENS
SCALE = HEAD ** (-0.5)
MASKED_SCORE = -1e30
DEAD_MARK = 1e6
DEAD_LEVEL = 1e5
INTERPRET = False
SEQ = ("y", "zh", "zl", "c")
Z = ("zh", "zl")


def dot(a, b, ca, cb):
    return lax.dot_general(
        a,
        b,
        (((ca,), (cb,)), ((), ())),
        precision=lax.Precision.HIGHEST,
        preferred_element_type=jnp.float32,
    )


def halves(x):
    high = x.astype(jnp.bfloat16)
    return high, (x - high.astype(jnp.float32)).astype(jnp.bfloat16)


def dot3(a, b, ca, cb):
    a_high, a_low = halves(a)
    b_high, b_low = halves(b)

    def one(x, y):
        return lax.dot_general(
            x, y, (((ca,), (cb,)), ((), ())), preferred_element_type=jnp.float32
        )

    return one(a_low, b_high) + one(a_high, b_low) + one(a_high, b_high)


def iota(shape, dim):
    return lax.broadcasted_iota(jnp.int32, shape, dim)


def chooser(rows, spacing, offset):
    shape = (rows, TOKENS)
    return (iota(shape, 1) == iota(shape, 0) * spacing + offset).astype(jnp.float32)


def placer(rows, spacing, offset):
    shape = (TOKENS, rows)
    return (iota(shape, 0) == iota(shape, 1) * spacing + offset).astype(jnp.float32)


def kernel_call(body, out_shape, operands, scalars):
    in_specs = [pl.BlockSpec(memory_space=pltpu.SMEM)] * scalars + [
        pl.BlockSpec(memory_space=pltpu.VMEM)
    ] * (len(operands) - scalars)
    return pl.pallas_call(
        body,
        out_shape=out_shape,
        in_specs=in_specs,
        out_specs=jax.tree.map(lambda _: pl.BlockSpec(memory_space=pltpu.VMEM), out_shape),
        interpret=INTERPRET,
    )(*operands)


def shaped(*dims):
    return jax.ShapeDtypeStruct(dims, jnp.float32)


def pack_body(count, base, k_ref, v_ref, far_ref, mid_ref, near_ref):
    feature = iota((2 * HEAD, TOKENS), 0)
    live = iota((2 * HEAD, TOKENS), 1) < count[0]
    for j in range(LOCAL_HEADS):
        rows = slice(HEAD * j, HEAD * (j + 1))
        both = jnp.concatenate([k_ref[rows, :], v_ref[rows, :]], axis=0)
        both = jnp.where(live, both, jnp.where(feature == 0, DEAD_MARK, 0.0))
        turned = both.T
        near_ref[TOKENS * j : TOKENS * (j + 1), :] = turned
        head = base[0] + j
        far = dot(chooser(FAR_ROWS, SPACING_WIDE, head % SPACING_WIDE), turned, 1, 0)
        mid = dot(chooser(MID_ROWS, SPACING_CENTRAL, head % SPACING_CENTRAL), turned, 1, 0)
        for i in range(far_ref.shape[0]):
            far_ref[i, FAR_ROWS * j : FAR_ROWS * (j + 1), :] = far
        for i in range(mid_ref.shape[0]):
            mid_ref[i, MID_ROWS * j : MID_ROWS * (j + 1), :] = mid


def query_body(count, base, q_ref, w_ref, own_ref, one_ref, two_ref, three_ref, *outs):
    far_ref, mid_ref, near_ref, cot_ref = outs
    columns = own_ref.shape[0]
    heads = cot_ref.shape[0] // columns
    group = base[0] // LOCAL_HEADS
    for k, ref in enumerate((own_ref, one_ref, two_ref, three_ref)):
        at = pl.multiple_of(columns * ((group + heads - k) % heads), columns)
        cot_ref[pl.ds(at, columns), :] = ref[...]
    live = iota((HEAD, TOKENS), 1) < count[0]
    grads = dot(w_ref[...], cot_ref[...], 1, 0)
    for j in range(LOCAL_HEADS):
        rows = slice(HEAD * j, HEAD * (j + 1))
        both = jnp.concatenate(
            [q_ref[rows, :] * SCALE, jnp.where(live, grads[rows, :], 0.0)], axis=0
        )
        turned = both.T
        head = base[0] + j
        near_ref[j] = turned
        far_ref[j] = dot(chooser(FAR_ROWS, SPACING_WIDE, head % SPACING_WIDE), turned, 1, 0)
        mid_ref[j] = dot(
            chooser(MID_ROWS, SPACING_CENTRAL, head % SPACING_CENTRAL), turned, 1, 0
        )


def split_queries(turned):
    left = iota(turned.shape, 1) < HEAD
    return jnp.concatenate([jnp.where(left, turned, 0.0), jnp.where(left, 0.0, turned)], axis=0)


def branch_scores(turned, pairs):
    rows = turned.shape[0]
    mark = ((iota((8, 2 * HEAD), 0) == 0) & (iota((8, 2 * HEAD), 1) == 0)).astype(jnp.float32)
    products = dot(jnp.concatenate([split_queries(turned), mark], axis=0), pairs, 1, 1)
    dead = products[2 * rows : 2 * rows + 1, :] > DEAD_LEVEL
    scores = jnp.where(dead, MASKED_SCORE, products[:rows])
    prob_grads = products[rows : 2 * rows]
    top = jnp.max(scores, axis=1, keepdims=True)
    weights = jnp.exp(scores - top)
    total = jnp.sum(weights, axis=1, keepdims=True)
    pulled = jnp.sum(weights * prob_grads, axis=1, keepdims=True)
    at = iota((rows, 128), 1)
    stats = jnp.where(at == 0, top, jnp.where(at == 1, total, pulled))
    return jnp.concatenate([prob_grads, weights], axis=0), stats


def branch_grads(both, factor, delta):
    rows = both.shape[0] // 2
    probs = both[rows:] * factor
    return jnp.concatenate([probs * (both[:rows] - delta), probs], axis=0)


def query_side(both, pairs):
    rows = both.shape[0] // 2
    sums = dot3(both, pairs, 1, 0)
    left = iota((rows, 2 * HEAD), 1) < HEAD
    return jnp.where(left, sums[:rows], sums[rows:])


def gathered(refs, rows):
    parts = []
    for ref in refs:
        part = ref[:, rows, :]
        parts.append(part.reshape(part.shape[0] * part.shape[1], 128))
    return jnp.concatenate(parts, axis=0)


def head_slice(j, rows):
    return slice(rows * j, rows * (j + 1))


def near_pairs_of(own, other, j):
    rows = head_slice(j, TOKENS)
    return jnp.concatenate([own[rows, :], other[rows, :]], axis=0)


def scores_body(*refs):
    qf_ref, qn_ref, near_own, near_other = refs[:4]
    far_refs = refs[4:-4]
    far_both, far_stats, near_both, near_stats = refs[-4:]
    for j in range(LOCAL_HEADS):
        pairs = gathered(far_refs, head_slice(j, FAR_ROWS))
        far_both[j], far_stats[j] = branch_scores(qf_ref[j], pairs)
        near_both[j], near_stats[j] = branch_scores(
            qn_ref[j], near_pairs_of(near_own, near_other, j)
        )


def attention_body(*refs):
    count, base = refs[:2]
    qm_ref, near_own, near_other, mid_own, mid_other, w_ref, cot_ref = refs[2:9]
    far_in, far_stats_ref, near_in, near_stats_ref = refs[9:13]
    outs = refs[-10:]
    far_refs = refs[13:-10]
    dq_ref, weight_ref, far_both, mid_both, near_both = outs[:5]
    term_refs, terms_ref = outs[5:9], outs[9]
    lanes = iota((TOKENS, 128), 1)
    position = iota((TOKENS, 1), 0)
    attended = []
    for j in range(LOCAL_HEADS):
        head = base[0] + j
        far_off = head % SPACING_WIDE
        mid_off = head % SPACING_CENTRAL
        mid_pairs = gathered((mid_own, mid_other), head_slice(j, MID_ROWS))
        mid_start, mid_column = branch_scores(qm_ref[j], mid_pairs)
        far_put = placer(FAR_ROWS, SPACING_WIDE, far_off)
        mid_put = placer(MID_ROWS, SPACING_CENTRAL, mid_off)
        far_stats = dot(far_put, far_stats_ref[j], 1, 0)
        mid_stats = dot(mid_put, mid_column, 1, 0)
        near_stats = near_stats_ref[j]
        in_far = position % SPACING_WIDE == far_off
        in_mid = position % SPACING_CENTRAL == mid_off
        far_top = jnp.where(in_far, far_stats[:, 0:1], MASKED_SCORE)
        mid_top = jnp.where(in_mid, mid_stats[:, 0:1], MASKED_SCORE)
        near_top = near_stats[:, 0:1]
        top = jnp.maximum(near_top, jnp.maximum(mid_top, far_top))
        far_factor = jnp.exp(far_top - top)
        mid_factor = jnp.exp(mid_top - top)
        near_factor = jnp.exp(near_top - top)
        total = (
            near_factor * near_stats[:, 1:2]
            + mid_factor * mid_stats[:, 1:2]
            + far_factor * far_stats[:, 1:2]
        )
        far_factor = far_factor / total
        mid_factor = mid_factor / total
        near_factor = near_factor / total
        delta = (
            near_factor * near_stats[:, 2:3]
            + mid_factor * mid_stats[:, 2:3]
            + far_factor * far_stats[:, 2:3]
        )
        back = jnp.where(lanes == 0, far_factor, jnp.where(lanes == 1, mid_factor, delta))
        far_back = dot(chooser(FAR_ROWS, SPACING_WIDE, far_off), back, 1, 0)
        mid_back = dot(chooser(MID_ROWS, SPACING_CENTRAL, mid_off), back, 1, 0)
        near = branch_grads(near_in[j], near_factor, delta)
        mid = branch_grads(mid_start, mid_back[:, 1:2], mid_back[:, 2:3])
        far = branch_grads(far_in[j], far_back[:, 0:1], far_back[:, 2:3])
        far_both[j] = far
        mid_both[j] = mid
        near_both[j] = near
        side = (
            query_side(near, near_pairs_of(near_own, near_other, j))
            + dot(mid_put, query_side(mid, mid_pairs), 1, 0)
            + dot(far_put, query_side(far, gathered(far_refs, head_slice(j, FAR_ROWS))), 1, 0)
        )
        turned = side.T
        dq_ref[HEAD * j : HEAD * (j + 1), :] = turned[:HEAD] * SCALE
        attended.append(turned[HEAD:])
    live = iota((HEAD * LOCAL_HEADS, TOKENS), 1) < count[0]
    rows = jnp.where(live, jnp.concatenate(attended, axis=0), 0.0)
    terms_ref[...] = dot3(w_ref[...], rows, 0, 0)
    columns = term_refs[0].shape[0]
    heads = terms_ref.shape[0] // columns
    group = base[0] // LOCAL_HEADS
    for k, ref in enumerate(term_refs):
        at = pl.multiple_of(columns * ((group + k) % heads), columns)
        ref[...] = terms_ref[pl.ds(at, columns), :]
    weight = dot3(rows, cot_ref[...], 1, 1)
    for b in range(weight.shape[1] // 128):
        weight_ref[columns * b : columns * (b + 1), :] = weight[:, 128 * b : 128 * b + 128]


def keys_body(far_both, mid_both, near_both, qf_ref, qm_ref, qn_ref, *outs):
    far_refs, mid_refs, near_refs = outs[:2], outs[2:4], outs[4:]
    for j in range(LOCAL_HEADS):
        for both, q_ref, refs, rows in (
            (mid_both, qm_ref, mid_refs, MID_ROWS),
            (far_both, qf_ref, far_refs, FAR_ROWS),
        ):
            sums = dot3(both[j], split_queries(q_ref[j]), 0, 0)
            half = sums.shape[0] // 2
            for i, ref in enumerate(refs):
                ref[:, head_slice(j, rows), :] = sums[half * i : half * (i + 1)].reshape(
                    half // rows, rows, 128
                )
        sums = dot3(near_both[j], split_queries(qn_ref[j]), 0, 0)
        for i, ref in enumerate(near_refs):
            ref[head_slice(j, TOKENS), :] = sums[TOKENS * i : TOKENS * (i + 1)]


def finish_body(base, far_ref, mid_ref, near_ref, other_ref, dk_ref, dv_ref):
    far_sum = far_ref[0, :FAR_BLOCK, :]
    for i in range(1, far_ref.shape[0]):
        far_sum = far_sum + far_ref[i, :FAR_BLOCK, :]
    mid_sum = mid_ref[0, :MID_BLOCK, :]
    for i in range(1, mid_ref.shape[0]):
        mid_sum = mid_sum + mid_ref[i, :MID_BLOCK, :]
    for j in range(LOCAL_HEADS):
        head = base[0] + j
        ns = slice(TOKENS * j, TOKENS * (j + 1))
        far_put = placer(FAR_ROWS, SPACING_WIDE, head % SPACING_WIDE)
        mid_put = placer(MID_ROWS, SPACING_CENTRAL, head % SPACING_CENTRAL)
        both = (
            near_ref[ns, :]
            + other_ref[ns, :]
            + dot(mid_put, mid_sum[MID_ROWS * j : MID_ROWS * (j + 1)], 1, 0)
            + dot(far_put, far_sum[FAR_ROWS * j : FAR_ROWS * (j + 1)], 1, 0)
        )
        turned = both.T
        dk_ref[HEAD * j : HEAD * (j + 1), :] = turned[:HEAD]
        dv_ref[HEAD * j : HEAD * (j + 1), :] = turned[HEAD:]


def exchange(pieces, axis):
    return lax.all_to_all(pieces, axis, 0, 0, tiled=True)


def to_all(piece, axis):
    return exchange(jnp.broadcast_to(piece, (lax.axis_size(axis), *piece.shape)), axis)


def shifted(x, axis, apart):
    size = lax.axis_size(axis)
    return lax.ppermute(x, axis, [(i, (i + apart) % size) for i in range(size)])


def on_device(queries, keys, values, counts, out_weight, cotangent):
    ny, nz, nzh, nzl = (lax.axis_size(axis) for axis in ("y", Z, "zh", "zl"))
    heads = lax.axis_size("h")
    columns, tokens = queries.shape
    base = (lax.axis_index("h") * LOCAL_HEADS).astype(jnp.int32).reshape(1)

    cots = [cotangent] + [shifted(cotangent, "h", k % heads) for k in range(1, 4)]
    far_out, mid_out, near_own = kernel_call(
        pack_body,
        (shaped(nz, FAR_BLOCK, 128), shaped(nzl, MID_BLOCK, 128), shaped(NEAR_BLOCK, 128)),
        (counts, base, keys, values),
        2,
    )
    near_other = shifted(near_own, "c", 1)
    far_line = exchange(far_out, Z)
    query_far, query_mid, query_near, full_cot = kernel_call(
        query_body,
        (
            shaped(LOCAL_HEADS, FAR_ROWS, 128),
            shaped(LOCAL_HEADS, MID_ROWS, 128),
            shaped(LOCAL_HEADS, TOKENS, 128),
            shaped(heads * columns, tokens),
        ),
        (counts, base, queries, out_weight, *cots),
        2,
    )
    mid_own = exchange(mid_out, "zl")
    far_plane = [far_line] + [shifted(far_line, "y", k) for k in range(1, ny)]
    far_blocks = far_plane + [shifted(x, "c", 1) for x in far_plane]
    far_keys = 2 * ny * nz * FAR_ROWS
    far_both, far_stats, near_both, near_stats = kernel_call(
        scores_body,
        (
            shaped(LOCAL_HEADS, 2 * FAR_ROWS, far_keys),
            shaped(LOCAL_HEADS, FAR_ROWS, 128),
            shaped(LOCAL_HEADS, 2 * TOKENS, 2 * TOKENS),
            shaped(LOCAL_HEADS, TOKENS, 128),
        ),
        (query_far, query_near, near_own, near_other, *far_blocks),
        0,
    )
    mid_other = shifted(mid_own, "c", 1)
    mid_keys = 2 * nzl * MID_ROWS
    query_grad, weight, far_both, mid_both, near_both, *terms = kernel_call(
        attention_body,
        (
            shaped(columns, tokens),
            shaped(out_weight.size // 128, 128),
            shaped(LOCAL_HEADS, 2 * FAR_ROWS, far_keys),
            shaped(LOCAL_HEADS, 2 * MID_ROWS, mid_keys),
            shaped(LOCAL_HEADS, 2 * TOKENS, 2 * TOKENS),
        )
        + (shaped(columns, tokens),) * 4
        + (shaped(heads * columns, tokens),),
        (
            counts,
            base,
            query_mid,
            near_own,
            near_other,
            mid_own,
            mid_other,
            out_weight,
            full_cot,
            far_both,
            far_stats,
            near_both,
            near_stats,
            *far_blocks,
        ),
        2,
    )
    planes = 2 * ny
    weight_parts = exchange(weight.reshape(planes, -1, 128), ("y", "c"))
    far_keep, far_send, mid_keep, mid_send, near_keep, near_send = kernel_call(
        keys_body,
        (shaped(ny * nz, FAR_BLOCK, 128),) * 2
        + (shaped(nzl, MID_BLOCK, 128),) * 2
        + (shaped(NEAR_BLOCK, 128),) * 2,
        (far_both, mid_both, near_both, query_far, query_mid, query_near),
        0,
    )
    mid_got = shifted(mid_send, "c", 1)
    weight_line = jnp.sum(weight_parts, axis=0).reshape(nzl, -1, 128)
    mid_sums = exchange(jnp.concatenate([mid_keep + mid_got, weight_line], axis=1), "zl")
    far_got = shifted(far_send, "c", 1)
    near_got = shifted(near_send, "c", 1)
    pieces = [far_keep[nz * k : nz * (k + 1)] + far_got[nz * k : nz * (k + 1)] for k in range(ny)]
    pieces = pieces[:1] + [shifted(pieces[k], "y", -k) for k in range(1, ny)]
    far_total = sum(pieces[1:], pieces[0])
    weight_own = jnp.sum(mid_sums[:, MID_BLOCK:], axis=0)
    depth = weight_own.shape[0]
    parts = exchange(
        jnp.concatenate(
            [far_total, jnp.broadcast_to(weight_own, (nz, depth, 128))], axis=1
        ),
        Z,
    )
    got = [terms[0]] + [shifted(terms[k], "h", k % heads) for k in range(1, 4)]
    output = sum(got[1:], got[0])
    weight_whole = jnp.sum(parts[:, FAR_BLOCK:].reshape(nzh, nzl, depth, 128), axis=0)
    weight_rows = to_all(weight_whole.reshape(nzl * depth, 128), ("y", "c"))
    weight_grad = (
        weight_rows.reshape(out_weight.shape[1] // 128, out_weight.shape[0], 128)
        .swapaxes(0, 1)
        .reshape(out_weight.shape)
    )
    key_grad, value_grad = kernel_call(
        finish_body,
        (shaped(columns, tokens), shaped(columns, tokens)),
        (base, parts, mid_sums, near_keep, near_got),
        1,
    )
    return output, query_grad, key_grad, value_grad, weight_grad


def solution(mesh):
    split = Mesh(
        mesh.devices.reshape(4, 2, 8, 2, mesh.shape["head"]), ("y", "zh", "zl", "c", "h")
    )
    return on_mesh(split)


def on_mesh(split):
    in_specs = (
        P("h", SEQ),
        P("h", SEQ),
        P("h", SEQ),
        P(SEQ),
        P("h", None),
        P("h", SEQ),
    )
    out_specs = (P("h", SEQ), P("h", SEQ), P("h", SEQ), P("h", SEQ), P("h", None))
    return jax.shard_map(
        on_device, mesh=split, in_specs=in_specs, out_specs=out_specs, check_vma=False
    )
```

time: 241 us -> 204 us (0.85)
  the two profiles are of different devices: /device:TPU:2 before, /device:TPU:1 now
where the time goes in v2:
time: 204 us; the launch traced here: 202 us
  starting transfers between devices  96 us (47%)
  blocking collectives  55.8 us (27%)
  Pallas kernels  27.3 us (13%)
  waiting for transfers between devices  13.2 us (6%)
  local copies, waits for them, and re-layouts  5.46 us (3%)
  other arithmetic  2.73 us (1%)
    ppermute x21, starting transfers between devices, shifted(): return lax.ppermute(x, axis, [(i, (i + apart) % size) for i in range(size)])  60.2 us
    all_to_all x2, blocking collectives, exchange(): return lax.all_to_all(pieces, axis, 0, 0, tiled=True)  55.8 us
    all_to_all x4, starting transfers between devices, exchange(): return lax.all_to_all(pieces, axis, 0, 0, tiled=True)  35.8 us
    pallas_call x6, Pallas kernels, kernel_call(): pl.pallas_call(body, out_shape=out_shape, in_specs=in_specs, out_specs=ja...  27.3 us
    ppermute x21, waiting for transfers between devices, shifted(): return lax.ppermute(x, axis, [(i, (i + apart) % size) for i in range(size)])  12.2 us
  transfers between devices with their start and end apart: 25, of which 7 were waited for; matrix products, arithmetic and copies ran while one was open for 1% of the time, Pallas kernels for 7%

profile of v2, /device:TPU:1, one launch (start us, length us, event | category | flops | bytes accessed | tf_op | source)
XLA Modules:
  0.0 202.3 jit_solution(12617931324990276216)
XLA Ops:
  1.3 2.3 %shard_map.102 = (f32[16,24,128]{2,1,0:T(8,128)}, f32[8,96,128]{2,1,0:T(8,128)}, f32[384,128]{1,0:T(8,128)}) custom-call(s32[1]{0:T(128)S(6)} %copy.15.count.refs_0_, s32[1]{0:T(128)} %bitcast.base.refs_1_, f32[192,128]{1,0:T(8,128)} %k_ref.1, f32[192,128]{1,0:T(8,128)} %v_ref.1), custom_call_target="tpu_custom_call" | custom-call | tf_op jit(solution)/shard_map/pallas_call | solution.py:73
  3.6 28.2 %all_to_all.30.refs_4_.refs_13_ = f32[16,24,128]{2,1,0:T(8,128)S(1)} all-to-all(f32[16,24,128]{2,1,0:T(8,128)} %get-tuple-element.39), channel_id=1, replica_groups=mesh['y'=4,'zh'=2,'zl'=8,'c'=2,'h'=4] {'zh','zl'}, dimensions={0} | all-to-all | bytes 393216 | tf_op jit(solution)/shard_map/all_to_all | solution.py:308
  31.8 8.9 %all-to-all-start = ((f32[8,96,128]{2,1,0:T(8,128)}), f32[8,96,128]{2,1,0:T(8,128)S(1)}, u32[]{:S(2)}, u32[]{:S(2)}) async-start(f32[8,96,128]{2,1,0:T(8,128)} %get-tuple-element.35), calls=%async_computation | async-start | bytes 786432 | tf_op jit(solution)/shard_map/all_to_all | solution.py:308
  40.7 4.7 %collective-permute-start.1 = (f32[192,128]{1,0:T(8,128)S(1)}, f32[192,128]{1,0:T(8,128)S(1)}, u32[]{:S(2)}, u32[]{:S(2)}) collective-permute-start(f32[192,128]{1,0:T(8,128)S(1)} %copy-done.16), channel_id=1, source_target_pairs={{0,2},{1,3},{2,0},{3,1},{4,6},{5,7},{6,4},{7,5},{8,10},{9,11},{10,... | collective-permute-start | bytes 294920 | tf_op jit(solution)/shard_map/ppermute | solution.py:317
  45.4 2.2 %collective-permute-start = (f32[192,128]{1,0:T(8,128)S(1)}, f32[192,128]{1,0:T(8,128)S(1)}, u32[]{:S(2)}, u32[]{:S(2)}) collective-permute-start(f32[192,128]{1,0:T(8,128)S(1)} %copy-done.16), channel_id=1, source_target_pairs={{0,1},{1,2},{2,3},{3,0},{4,5},{5,6},{6,7},{7,4},{8,9},{9,10},{10,1... | collective-permute-start | bytes 294920 | tf_op jit(solution)/shard_map/ppermute | solution.py:317
  47.6 4.3 %collective-permute-start.2 = (f32[192,128]{1,0:T(8,128)S(1)}, f32[192,128]{1,0:T(8,128)S(1)}, u32[]{:S(2)}, u32[]{:S(2)}) collective-permute-start(f32[192,128]{1,0:T(8,128)S(1)} %copy-done.16), channel_id=1, source_target_pairs={{0,3},{1,0},{2,1},{3,2},{4,7},{5,4},{6,5},{7,6},{8,11},{9,8},{10,9... | collective-permute-start | bytes 294920 | tf_op jit(solution)/shard_map/ppermute | solution.py:317
  51.9 3.7 %collective-permute-start.3 = (f32[384,128]{1,0:T(8,128)S(1)}, f32[384,128]{1,0:T(8,128)S(1)}, u32[]{:S(2)}, u32[]{:S(2)}) collective-permute-start(f32[384,128]{1,0:T(8,128)S(1)} %copy-done.4), channel_id=1, source_target_pairs={{0,4},{4,0},{1,5},{5,1},{2,6},{6,2},{3,7},{7,3},{8,12},{12,8},{9,1... | collective-permute-start | bytes 589832 | tf_op jit(solution)/shard_map/ppermute | solution.py:317
  55.6 4.6 %collective-permute-start.7 = (f32[16,24,128]{2,1,0:T(8,128)S(1)}, f32[16,24,128]{2,1,0:T(8,128)S(1)}, u32[]{:S(2)}, u32[]{:S(2)}) collective-permute-start(f32[16,24,128]{2,1,0:T(8,128)S(1)} %all_to_all.30.refs_4_.refs_13_), channel_id=1, source_target_pairs={{0,384},{128,0},{256,128},{384,256},{1,385},{129,1},{257,129},{385... | collective-permute-start | bytes 589832 | tf_op jit(solution)/shard_map/ppermute | solution.py:317
  60.3 2.3 %collective-permute-start.6 = (f32[16,24,128]{2,1,0:T(8,128)S(1)}, f32[16,24,128]{2,1,0:T(8,128)S(1)}, u32[]{:S(2)}, u32[]{:S(2)}) collective-permute-start(f32[16,24,128]{2,1,0:T(8,128)S(1)} %all_to_all.30.refs_4_.refs_13_), channel_id=1, source_target_pairs={{0,256},{128,384},{256,0},{384,128},{1,257},{129,385},{257,1},{385... | collective-permute-start | bytes 589832 | tf_op jit(solution)/shard_map/ppermute | solution.py:317
  62.6 2.6 %collective-permute-start.5 = (f32[16,24,128]{2,1,0:T(8,128)S(1)}, f32[16,24,128]{2,1,0:T(8,128)S(1)}, u32[]{:S(2)}, u32[]{:S(2)}) collective-permute-start(f32[16,24,128]{2,1,0:T(8,128)S(1)} %all_to_all.30.refs_4_.refs_13_), channel_id=1, source_target_pairs={{0,128},{128,256},{256,384},{384,0},{1,129},{129,257},{257,385},{3... | collective-permute-start | bytes 589832 | tf_op jit(solution)/shard_map/ppermute | solution.py:317
  65.2 2.8 %collective-permute-start.4 = (f32[8,96,128]{2,1,0:T(8,128)S(1)}, f32[8,96,128]{2,1,0:T(8,128)S(1)}, u32[]{:S(2)}, u32[]{:S(2)}) collective-permute-start(f32[8,96,128]{2,1,0:T(8,128)S(1)} %all-to-all-done.refs_5_), channel_id=1, source_target_pairs={{0,4},{4,0},{1,5},{5,1},{2,6},{6,2},{3,7},{7,3},{8,12},{12,8},{9,1... | collective-permute-start | bytes 1179656 | tf_op jit(solution)/shard_map/ppermute | solution.py:317
  68.0 1.9 collective-permute-start.8
  70.0 2.4 %collective-permute-start.11 = (f32[16,24,128]{2,1,0:T(8,128)S(1)}, f32[16,24,128]{2,1,0:T(8,128)S(1)}, u32[]{:S(2)}, u32[]{:S(2)}) collective-permute-start(f32[16,24,128]{2,1,0:T(8,128)S(1)} %collective-permute-done.7.refs_7_.refs_16_), channel_id=1, source_target_pairs={{0,4},{4,0},{1,5},{5,1},{2,6},{6,2},{3,7},{7,3},{8,12},{12,8},{9,1... | collective-permute-start | bytes 589832 | tf_op jit(solution)/shard_map/ppermute | solution.py:317
  74.7 2.4 %collective-permute-start.9 = (f32[16,24,128]{2,1,0:T(8,128)S(1)}, f32[16,24,128]{2,1,0:T(8,128)S(1)}, u32[]{:S(2)}, u32[]{:S(2)}) collective-permute-start(f32[16,24,128]{2,1,0:T(8,128)S(1)} %collective-permute-done.5.refs_5_.refs_14_), channel_id=1, source_target_pairs={{0,4},{4,0},{1,5},{5,1},{2,6},{6,2},{3,7},{7,3},{8,12},{12,8},{9,1... | collective-permute-start | bytes 589832 | tf_op jit(solution)/shard_map/ppermute | solution.py:317
  77.2 3.6 %shard_map.101 = (f32[3,8,128]{2,1,0:T(8,128)}, f32[3,32,128]{2,1,0:T(8,128)}, f32[3,128,128]{2,1,0:T(8,128)}, f32[768,128]{1,0:T(8,128)}) custom-call(s32[1]{0:T(128)S(6)} %copy.15.count.refs_0_, s32[1]{0:T(128)} %bitcast.base.refs_1_, f32[192,128]{1,0:T(8,128)} %q_ref.1, f32[192,768]{1,0:T(8,128)} %refs_7_.1, f32[192,128]{1,0:T(8,128)} %own_ref.1, ...), custom_call_target="tpu_custom_call" | custom-call | tf_op jit(solution)/shard_map/pallas_call | solution.py:73
  81.7 4.8 %shard_map.103 = (f32[3,16,1024]{2,1,0:T(8,128)}, f32[3,8,128]{2,1,0:T(8,128)}, f32[3,256,256]{2,1,0:T(8,128)}, f32[3,128,128]{2,1,0:T(8,128)}) custom-call(f32[3,8,128]{2,1,0:T(8,128)} %get-tuple-element.37.refs_0_.qf_ref, f32[3,128,128]{2,1,0:T(8,128)} %get-tuple-element.38.refs_1_.qn_ref, f32[384,128]{1,0:T(8,128)} %get-tuple-element.34.refs_2_.refs_3_, ...), custom_call_target="tpu_custom_call" | custom-call | tf_op jit(solution)/shard_map/pallas_call | solution.py:73
  87.3 9.8 %shard_map.104 = (f32[192,128]{1,0:T(8,128)}, f32[1152,128]{1,0:T(8,128)}, f32[3,16,1024]{2,1,0:T(8,128)}, f32[3,64,512]{2,1,0:T(8,128)}, f32[3,256,256]{2,1,0:T...) custom-call(s32[1]{0:T(128)S(6)} %copy.15.count.refs_0_, ...), custom_call_target="tpu_custom_call" | custom-call | tf_op jit(solution)/shard_map/pallas_call | solution.py:73
  97.1 3.8 %all-to-all-start.2 = ((f32[8,144,128]{2,1,0:T(8,128)}), f32[8,144,128]{2,1,0:T(8,128)S(1)}, u32[]{:S(2)}, u32[]{:S(2)}) async-start(f32[8,144,128]{2,1,0:T(8,128)} %bitcast.12), calls=%async_computation.2 | async-start | bytes 1179648 | tf_op jit(solution)/shard_map/all_to_all | solution.py:308
  100.9 4.2 %shard_map.105 = (f32[64,24,128]{2,1,0:T(8,128)}, f32[64,24,128]{2,1,0:T(8,128)}, f32[8,96,128]{2,1,0:T(8,128)}, f32[8,96,128]{2,1,0:T(8,128)}, f32[384,128]{1,0:T(8,128)}, /*index=5*/f32[384,128]{1,0:T(8,128)}) custom-call(f32[3,16,1024]{2,1,0:T(8,128)} %get-tuple-element.49.far_both, f32[3,64,512]{2,1,0:T(8,128)} %get-tuple-element.50.mid_both, ...), custom_call_target="tpu_custom_call" | custom-call | tf_op jit(solution)/shard_map/pallas_call | solution.py:73
  111.9 9.6 %all-to-all-start.3 = ((f32[8,114,128]{2,1,0:T(8,128)}), f32[8,114,128]{2,1,0:T(8,128)S(1)}, u32[]{:S(2)}, u32[]{:S(2)}) async-start(f32[8,114,128]{2,1,0:T(8,128)} %pad_maximum_fusion), calls=%async_computation.3 | async-start | bytes 983040 | tf_op jit(solution)/shard_map/all_to_all | solution.py:308
  121.5 3.2 %collective-permute-start.15 = (f32[64,24,128]{2,1,0:T(8,128)S(1)}, f32[64,24,128]{2,1,0:T(8,128)S(1)}, u32[]{:S(2)}, u32[]{:S(2)}) collective-permute-start(f32[64,24,128]{2,1,0:T(8,128)S(1)} %copy-done.21), channel_id=1, source_target_pairs={{0,4},{4,0},{1,5},{5,1},{2,6},{6,2},{3,7},{7,3},{8,12},{12,8},{9,1... | collective-permute-start | bytes 2359304 | tf_op jit(solution)/shard_map/ppermute | solution.py:317
  126.6 2.9 %collective-permute-start.16 = (f32[16,24,128]{2,1,0:T(8,128)S(1)}, f32[16,24,128]{2,1,0:T(8,128)S(1)}, u32[]{:S(2)}, u32[]{:S(2)}) collective-permute-start(f32[16,24,128]{2,1,0:T(8,128)S(1)} %get-tuple-element.61), channel_id=1, source_target_pairs={{0,384},{128,0},{256,128},{384,256},{1,385},{129,1},{257,129},{385... | collective-permute-start | bytes 589832 | tf_op jit(solution)/shard_map/ppermute | solution.py:317
  129.5 2.4 %collective-permute-start.18 = (f32[16,24,128]{2,1,0:T(8,128)S(1)}, f32[16,24,128]{2,1,0:T(8,128)S(1)}, u32[]{:S(2)}, u32[]{:S(2)}) collective-permute-start(f32[16,24,128]{2,1,0:T(8,128)S(1)} %get-tuple-element.62), channel_id=1, source_target_pairs={{0,128},{128,256},{256,384},{384,0},{1,129},{129,257},{257,385},{3... | collective-permute-start | bytes 589832 | tf_op jit(solution)/shard_map/ppermute | solution.py:317
  131.9 3.2 %collective-permute-start.17 = (f32[16,24,128]{2,1,0:T(8,128)S(1)}, f32[16,24,128]{2,1,0:T(8,128)S(1)}, u32[]{:S(2)}, u32[]{:S(2)}) collective-permute-start(f32[16,24,128]{2,1,0:T(8,128)S(1)} %get-tuple-element.63), channel_id=1, source_target_pairs={{0,256},{128,384},{256,0},{384,128},{1,257},{129,385},{257,1},{385... | collective-permute-start | bytes 589832 | tf_op jit(solution)/shard_map/ppermute | solution.py:317
  135.1 3.7 %collective-permute-done.18 = f32[16,24,128]{2,1,0:T(8,128)S(1)} collective-permute-done((f32[16,24,128]{2,1,0:T(8,128)S(1)}, f32[16,24,128]{2,1,0:T(8,128)S(1)}, u32[]{:S(2)}, u32[]{:S(2)}) %collective-permute-start.18) | collective-permute-done | bytes 196640 | tf_op jit(solution)/shard_map/ppermute | solution.py:317
  138.9 3.3 %collective-permute-done.17 = f32[16,24,128]{2,1,0:T(8,128)S(1)} collective-permute-done((f32[16,24,128]{2,1,0:T(8,128)S(1)}, f32[16,24,128]{2,1,0:T(8,128)S(1)}, u32[]{:S(2)}, u32[]{:S(2)}) %collective-permute-start.17) | collective-permute-done | bytes 196640 | tf_op jit(solution)/shard_map/ppermute | solution.py:317
  143.0 27.5 %all_to_all.31.far_ref = f32[16,42,128]{2,1,0:T(8,128)S(1)} all-to-all(f32[16,42,128]{2,1,0:T(8,128)S(1)} %pad_maximum_fusion.1), channel_id=1, replica_groups=mesh['y'=4,'zh'=2,'zl'=8,'c'=2,'h'=4] {'zh','zl'}, dimensions={0} | all-to-all | bytes 688128 | tf_op jit(solution)/shard_map/all_to_all | solution.py:308
  172.2 13.5 %all-to-all-start.5 = ((f32[8,144,128]{2,1,0:T(8,128)}), f32[8,144,128]{2,1,0:T(8,128)S(1)}, u32[]{:S(2)}, u32[]{:S(2)}) async-start(f32[8,144,128]{2,1,0:T(8,128)} %broadcast_in_dim.7), calls=%async_computation.5 | async-start | bytes 1179648 | tf_op jit(solution)/shard_map/all_to_all | solution.py:308
  187.6 2.8 %collective-permute-start.13 = (f32[192,128]{1,0:T(8,128)S(1)}, f32[192,128]{1,0:T(8,128)S(1)}, u32[]{:S(2)}, u32[]{:S(2)}) collective-permute-start(f32[192,128]{1,0:T(8,128)S(1)} %copy-done.24), channel_id=1, source_target_pairs={{0,2},{1,3},{2,0},{3,1},{4,6},{5,7},{6,4},{7,5},{8,10},{9,11},{10,... | collective-permute-start | bytes 294920 | tf_op jit(solution)/shard_map/ppermute | solution.py:317
  190.4 3.7 %collective-permute-start.14 = (f32[192,128]{1,0:T(8,128)S(1)}, f32[192,128]{1,0:T(8,128)S(1)}, u32[]{:S(2)}, u32[]{:S(2)}) collective-permute-start(f32[192,128]{1,0:T(8,128)S(1)} %copy-done.23), channel_id=1, source_target_pairs={{0,3},{1,0},{2,1},{3,2},{4,7},{5,4},{6,5},{7,6},{8,11},{9,8},{10,9... | collective-permute-start | bytes 294920 | tf_op jit(solution)/shard_map/ppermute | solution.py:317
  194.1 2.5 %collective-permute-start.20 = (f32[384,128]{1,0:T(8,128)S(1)}, f32[384,128]{1,0:T(8,128)S(1)}, u32[]{:S(2)}, u32[]{:S(2)}) collective-permute-start(f32[384,128]{1,0:T(8,128)S(1)} %copy-done.22), channel_id=1, source_target_pairs={{0,4},{4,0},{1,5},{5,1},{2,6},{6,2},{3,7},{7,3},{8,12},{12,8},{9,1... | collective-permute-start | bytes 589832 | tf_op jit(solution)/shard_map/ppermute | solution.py:317
  198.9 2.5 %shard_map.106 = (f32[192,128]{1,0:T(8,128)}, f32[192,128]{1,0:T(8,128)}) custom-call(s32[1]{0:T(128)} %bitcast.base.refs_1_, f32[16,42,128]{2,1,0:T(8,128)} %copy-done, f32[8,114,128]{2,1,0:T(8,128)} %copy-done.1, f32[384,128]{1,0:T(8,128)} %get-tuple-element.57.near_ref, f32[384,128]{1,0:T(8,128)} %copy-done.15), custom_call_target="tpu_custom_call" | custom-call | tf_op jit(solution)/shard_map/pallas_call | solution.py:73
  (93 shorter events, 20.1 us)
Async XLA Ops:
  31.8 36.2 %copy-start.2 = (f32[16,24,128]{2,1,0:T(8,128)}, f32[16,24,128]{2,1,0:T(8,128)S(1)}, u32[]{:S(2)}) copy-start(f32[16,24,128]{2,1,0:T(8,128)S(1)} %all_to_all.30.refs_4_.refs_13_) | copy-start | bytes 589828
  31.8 20.1 %copy-start.4 = (f32[384,128]{1,0:T(8,128)S(1)}, f32[384,128]{1,0:T(8,128)}, u32[]{:S(2)}) copy-start(f32[384,128]{1,0:T(8,128)} %get-tuple-element.34.refs_2_.refs_3_) | copy-start | bytes 589828
  31.8 33.4 %all-to-all-start = ((f32[8,96,128]{2,1,0:T(8,128)}), f32[8,96,128]{2,1,0:T(8,128)S(1)}, u32[]{:S(2)}, u32[]{:S(2)}) async-start(f32[8,96,128]{2,1,0:T(8,128)} %get-tuple-element.35), calls=%async_computation | async-start | bytes 786432 | tf_op jit(solution)/shard_map/all_to_all | solution.py:308
  40.7 19.5 %collective-permute-start.1 = (f32[192,128]{1,0:T(8,128)S(1)}, f32[192,128]{1,0:T(8,128)S(1)}, u32[]{:S(2)}, u32[]{:S(2)}) collective-permute-start(f32[192,128]{1,0:T(8,128)S(1)} %copy-done.16), channel_id=1, source_target_pairs={{0,2},{1,3},{2,0},{3,1},{4,6},{5,7},{6,4},{7,5},{8,10},{9,11},{10,... | collective-permute-start | bytes 294920 | tf_op jit(solution)/shard_map/ppermute | solution.py:317
  45.4 17.1 %collective-permute-start = (f32[192,128]{1,0:T(8,128)S(1)}, f32[192,128]{1,0:T(8,128)S(1)}, u32[]{:S(2)}, u32[]{:S(2)}) collective-permute-start(f32[192,128]{1,0:T(8,128)S(1)} %copy-done.16), channel_id=1, source_target_pairs={{0,1},{1,2},{2,3},{3,0},{4,5},{5,6},{6,7},{7,4},{8,9},{9,10},{10,1... | collective-permute-start | bytes 294920 | tf_op jit(solution)/shard_map/ppermute | solution.py:317
  47.6 17.6 %collective-permute-start.2 = (f32[192,128]{1,0:T(8,128)S(1)}, f32[192,128]{1,0:T(8,128)S(1)}, u32[]{:S(2)}, u32[]{:S(2)}) collective-permute-start(f32[192,128]{1,0:T(8,128)S(1)} %copy-done.16), channel_id=1, source_target_pairs={{0,3},{1,0},{2,1},{3,2},{4,7},{5,4},{6,5},{7,6},{8,11},{9,8},{10,9... | collective-permute-start | bytes 294920 | tf_op jit(solution)/shard_map/ppermute | solution.py:317
  51.9 16.1 %collective-permute-start.3 = (f32[384,128]{1,0:T(8,128)S(1)}, f32[384,128]{1,0:T(8,128)S(1)}, u32[]{:S(2)}, u32[]{:S(2)}) collective-permute-start(f32[384,128]{1,0:T(8,128)S(1)} %copy-done.4), channel_id=1, source_target_pairs={{0,4},{4,0},{1,5},{5,1},{2,6},{6,2},{3,7},{7,3},{8,12},{12,8},{9,1... | collective-permute-start | bytes 589832 | tf_op jit(solution)/shard_map/ppermute | solution.py:317
  55.6 14.3 %collective-permute-start.7 = (f32[16,24,128]{2,1,0:T(8,128)S(1)}, f32[16,24,128]{2,1,0:T(8,128)S(1)}, u32[]{:S(2)}, u32[]{:S(2)}) collective-permute-start(f32[16,24,128]{2,1,0:T(8,128)S(1)} %all_to_all.30.refs_4_.refs_13_), channel_id=1, source_target_pairs={{0,384},{128,0},{256,128},{384,256},{1,385},{129,1},{257,129},{385... | collective-permute-start | bytes 589832 | tf_op jit(solution)/shard_map/ppermute | solution.py:317
  60.3 16.8 %copy-start.17 = (f32[192,128]{1,0:T(8,128)}, f32[192,128]{1,0:T(8,128)S(1)}, u32[]{:S(2)}) copy-start(f32[192,128]{1,0:T(8,128)S(1)} %collective-permute-done.1.two_ref) | copy-start | bytes 294916
  60.3 12.1 %collective-permute-start.6 = (f32[16,24,128]{2,1,0:T(8,128)S(1)}, f32[16,24,128]{2,1,0:T(8,128)S(1)}, u32[]{:S(2)}, u32[]{:S(2)}) collective-permute-start(f32[16,24,128]{2,1,0:T(8,128)S(1)} %all_to_all.30.refs_4_.refs_13_), channel_id=1, source_target_pairs={{0,256},{128,384},{256,0},{384,128},{1,257},{129,385},{257,1},{385... | collective-permute-start | bytes 589832 | tf_op jit(solution)/shard_map/ppermute | solution.py:317
  62.6 12.1 %collective-permute-start.5 = (f32[16,24,128]{2,1,0:T(8,128)S(1)}, f32[16,24,128]{2,1,0:T(8,128)S(1)}, u32[]{:S(2)}, u32[]{:S(2)}) collective-permute-start(f32[16,24,128]{2,1,0:T(8,128)S(1)} %all_to_all.30.refs_4_.refs_13_), channel_id=1, source_target_pairs={{0,128},{128,256},{256,384},{384,0},{1,129},{129,257},{257,385},{3... | collective-permute-start | bytes 589832 | tf_op jit(solution)/shard_map/ppermute | solution.py:317
  65.2 15.6 %copy-start.3 = (f32[8,96,128]{2,1,0:T(8,128)}, f32[8,96,128]{2,1,0:T(8,128)S(1)}, u32[]{:S(2)}) copy-start(f32[8,96,128]{2,1,0:T(8,128)S(1)} %all-to-all-done.refs_5_) | copy-start | bytes 1179652
  65.2 21.3 %collective-permute-start.4 = (f32[8,96,128]{2,1,0:T(8,128)S(1)}, f32[8,96,128]{2,1,0:T(8,128)S(1)}, u32[]{:S(2)}, u32[]{:S(2)}) collective-permute-start(f32[8,96,128]{2,1,0:T(8,128)S(1)} %all-to-all-done.refs_5_), channel_id=1, source_target_pairs={{0,4},{4,0},{1,5},{5,1},{2,6},{6,2},{3,7},{7,3},{8,12},{12,8},{9,1... | collective-permute-start | bytes 1179656 | tf_op jit(solution)/shard_map/ppermute | solution.py:317
  68.0 12.8 %collective-permute-start.8 = (f32[16,24,128]{2,1,0:T(8,128)S(1)}, f32[16,24,128]{2,1,0:T(8,128)S(1)}, u32[]{:S(2)}, u32[]{:S(2)}) collective-permute-start(f32[16,24,128]{2,1,0:T(8,128)S(1)} %all_to_all.30.refs_4_.refs_13_), channel_id=1, source_target_pairs={{0,4},{4,0},{1,5},{5,1},{2,6},{6,2},{3,7},{7,3},{8,12},{12,8},{9,1... | collective-permute-start | bytes 589832 | tf_op jit(solution)/shard_map/ppermute | solution.py:317
  70.0 10.9 %collective-permute-start.11 = (f32[16,24,128]{2,1,0:T(8,128)S(1)}, f32[16,24,128]{2,1,0:T(8,128)S(1)}, u32[]{:S(2)}, u32[]{:S(2)}) collective-permute-start(f32[16,24,128]{2,1,0:T(8,128)S(1)} %collective-permute-done.7.refs_7_.refs_16_), channel_id=1, source_target_pairs={{0,4},{4,0},{1,5},{5,1},{2,6},{6,2},{3,7},{7,3},{8,12},{12,8},{9,1... | collective-permute-start | bytes 589832 | tf_op jit(solution)/shard_map/ppermute | solution.py:317
  72.4 8.4 %collective-permute-start.10 = (f32[16,24,128]{2,1,0:T(8,128)S(1)}, f32[16,24,128]{2,1,0:T(8,128)S(1)}, u32[]{:S(2)}, u32[]{:S(2)}) collective-permute-start(f32[16,24,128]{2,1,0:T(8,128)S(1)} %collective-permute-done.6.refs_6_.refs_15_), channel_id=1, source_target_pairs={{0,4},{4,0},{1,5},{5,1},{2,6},{6,2},{3,7},{7,3},{8,12},{12,8},{9,1... | collective-permute-start | bytes 589832 | tf_op jit(solution)/shard_map/ppermute | solution.py:317
  74.7 6.2 %collective-permute-start.9 = (f32[16,24,128]{2,1,0:T(8,128)S(1)}, f32[16,24,128]{2,1,0:T(8,128)S(1)}, u32[]{:S(2)}, u32[]{:S(2)}) collective-permute-start(f32[16,24,128]{2,1,0:T(8,128)S(1)} %collective-permute-done.5.refs_5_.refs_14_), channel_id=1, source_target_pairs={{0,4},{4,0},{1,5},{5,1},{2,6},{6,2},{3,7},{7,3},{8,12},{12,8},{9,1... | collective-permute-start | bytes 589832 | tf_op jit(solution)/shard_map/ppermute | solution.py:317
  97.1 13.9 %all-to-all-start.2 = ((f32[8,144,128]{2,1,0:T(8,128)}), f32[8,144,128]{2,1,0:T(8,128)S(1)}, u32[]{:S(2)}, u32[]{:S(2)}) async-start(f32[8,144,128]{2,1,0:T(8,128)} %bitcast.12), calls=%async_computation.2 | async-start | bytes 1179648 | tf_op jit(solution)/shard_map/all_to_all | solution.py:308
  105.1 3.8 %collective-permute-start.19 = (f32[8,96,128]{2,1,0:T(8,128)}, f32[8,96,128]{2,1,0:T(8,128)S(1)}, u32[]{:S(2)}, u32[]{:S(2)}) collective-permute-start(f32[8,96,128]{2,1,0:T(8,128)} %get-tuple-element.55), channel_id=1, source_target_pairs={{0,4},{4,0},{1,5},{5,1},{2,6},{6,2},{3,7},{7,3},{8,12},{12,8},{9,1... | collective-permute-start | bytes 1179656 | tf_op jit(solution)/shard_map/ppermute | solution.py:317
  111.9 30.3 %all-to-all-start.3 = ((f32[8,114,128]{2,1,0:T(8,128)}), f32[8,114,128]{2,1,0:T(8,128)S(1)}, u32[]{:S(2)}, u32[]{:S(2)}) async-start(f32[8,114,128]{2,1,0:T(8,128)} %pad_maximum_fusion), calls=%async_computation.3 | async-start | bytes 983040 | tf_op jit(solution)/shard_map/all_to_all | solution.py:308
  121.5 5.1 %collective-permute-start.15 = (f32[64,24,128]{2,1,0:T(8,128)S(1)}, f32[64,24,128]{2,1,0:T(8,128)S(1)}, u32[]{:S(2)}, u32[]{:S(2)}) collective-permute-start(f32[64,24,128]{2,1,0:T(8,128)S(1)} %copy-done.21), channel_id=1, source_target_pairs={{0,4},{4,0},{1,5},{5,1},{2,6},{6,2},{3,7},{7,3},{8,12},{12,8},{9,1... | collective-permute-start | bytes 2359304 | tf_op jit(solution)/shard_map/ppermute | solution.py:317
  126.6 8.5 %collective-permute-start.16 = (f32[16,24,128]{2,1,0:T(8,128)S(1)}, f32[16,24,128]{2,1,0:T(8,128)S(1)}, u32[]{:S(2)}, u32[]{:S(2)}) collective-permute-start(f32[16,24,128]{2,1,0:T(8,128)S(1)} %get-tuple-element.61), channel_id=1, source_target_pairs={{0,384},{128,0},{256,128},{384,256},{1,385},{129,1},{257,129},{385... | collective-permute-start | bytes 589832 | tf_op jit(solution)/shard_map/ppermute | solution.py:317
  129.5 9.3 %collective-permute-start.18 = (f32[16,24,128]{2,1,0:T(8,128)S(1)}, f32[16,24,128]{2,1,0:T(8,128)S(1)}, u32[]{:S(2)}, u32[]{:S(2)}) collective-permute-start(f32[16,24,128]{2,1,0:T(8,128)S(1)} %get-tuple-element.62), channel_id=1, source_target_pairs={{0,128},{128,256},{256,384},{384,0},{1,129},{129,257},{257,385},{3... | collective-permute-start | bytes 589832 | tf_op jit(solution)/shard_map/ppermute | solution.py:317
  131.9 10.2 %collective-permute-start.17 = (f32[16,24,128]{2,1,0:T(8,128)S(1)}, f32[16,24,128]{2,1,0:T(8,128)S(1)}, u32[]{:S(2)}, u32[]{:S(2)}) collective-permute-start(f32[16,24,128]{2,1,0:T(8,128)S(1)} %get-tuple-element.63), channel_id=1, source_target_pairs={{0,256},{128,384},{256,0},{384,128},{1,257},{129,385},{257,1},{385... | collective-permute-start | bytes 589832 | tf_op jit(solution)/shard_map/ppermute | solution.py:317
  172.2 18.3 %copy-start.23 = (f32[192,128]{1,0:T(8,128)S(1)}, f32[192,128]{1,0:T(8,128)}, u32[]{:S(2)}) copy-start(f32[192,128]{1,0:T(8,128)} %get-tuple-element.47) | copy-start | bytes 294916
  172.2 22.0 %copy-start.22 = (f32[384,128]{1,0:T(8,128)S(1)}, f32[384,128]{1,0:T(8,128)}, u32[]{:S(2)}) copy-start(f32[384,128]{1,0:T(8,128)} %get-tuple-element.58) | copy-start | bytes 589828
  172.2 25.4 %copy-start.20 = (f32[192,128]{1,0:T(8,128)S(1)}, f32[192,128]{1,0:T(8,128)}, u32[]{:S(2)}) copy-start(f32[192,128]{1,0:T(8,128)} %get-tuple-element.44) | copy-start | bytes 294916
  172.2 29.2 %all-to-all-start.5 = ((f32[8,144,128]{2,1,0:T(8,128)}), f32[8,144,128]{2,1,0:T(8,128)S(1)}, u32[]{:S(2)}, u32[]{:S(2)}) async-start(f32[8,144,128]{2,1,0:T(8,128)} %broadcast_in_dim.7), calls=%async_computation.5 | async-start | bytes 1179648 | tf_op jit(solution)/shard_map/all_to_all | solution.py:308
  185.7 11.0 %collective-permute-start.12 = (f32[192,128]{1,0:T(8,128)S(1)}, f32[192,128]{1,0:T(8,128)S(1)}, u32[]{:S(2)}, u32[]{:S(2)}) collective-permute-start(f32[192,128]{1,0:T(8,128)S(1)} %copy-done.25), channel_id=1, source_target_pairs={{0,1},{1,2},{2,3},{3,0},{4,5},{5,6},{6,7},{7,4},{8,9},{9,10},{10,1... | collective-permute-start | bytes 294920 | tf_op jit(solution)/shard_map/ppermute | solution.py:317
  187.6 9.0 %collective-permute-start.13 = (f32[192,128]{1,0:T(8,128)S(1)}, f32[192,128]{1,0:T(8,128)S(1)}, u32[]{:S(2)}, u32[]{:S(2)}) collective-permute-start(f32[192,128]{1,0:T(8,128)S(1)} %copy-done.24), channel_id=1, source_target_pairs={{0,2},{1,3},{2,0},{3,1},{4,6},{5,7},{6,4},{7,5},{8,10},{9,11},{10,... | collective-permute-start | bytes 294920 | tf_op jit(solution)/shard_map/ppermute | solution.py:317
  190.4 7.2 %collective-permute-start.14 = (f32[192,128]{1,0:T(8,128)S(1)}, f32[192,128]{1,0:T(8,128)S(1)}, u32[]{:S(2)}, u32[]{:S(2)}) collective-permute-start(f32[192,128]{1,0:T(8,128)S(1)} %copy-done.23), channel_id=1, source_target_pairs={{0,3},{1,0},{2,1},{3,2},{4,7},{5,4},{6,5},{7,6},{8,11},{9,8},{10,9... | collective-permute-start | bytes 294920 | tf_op jit(solution)/shard_map/ppermute | solution.py:317
  194.1 4.1 %collective-permute-start.20 = (f32[384,128]{1,0:T(8,128)S(1)}, f32[384,128]{1,0:T(8,128)S(1)}, u32[]{:S(2)}, u32[]{:S(2)}) collective-permute-start(f32[384,128]{1,0:T(8,128)S(1)} %copy-done.22), channel_id=1, source_target_pairs={{0,4},{4,0},{1,5},{5,1},{2,6},{6,2},{3,7},{7,3},{8,12},{12,8},{9,1... | collective-permute-start | bytes 589832 | tf_op jit(solution)/shard_map/ppermute | solution.py:317
  (19 other events, 134.5 us)

commit v3 on v2

--- a/solution.py
+++ b/solution.py
@@ -101,16 +101,9 @@
             mid_ref[i, MID_ROWS * j : MID_ROWS * (j + 1), :] = mid
 
 
-def query_body(count, base, q_ref, w_ref, own_ref, one_ref, two_ref, three_ref, *outs):
-    far_ref, mid_ref, near_ref, cot_ref = outs
-    columns = own_ref.shape[0]
-    heads = cot_ref.shape[0] // columns
-    group = base[0] // LOCAL_HEADS
-    for k, ref in enumerate((own_ref, one_ref, two_ref, three_ref)):
-        at = pl.multiple_of(columns * ((group + heads - k) % heads), columns)
-        cot_ref[pl.ds(at, columns), :] = ref[...]
+def query_body(count, base, q_ref, w_ref, cot_ref, far_ref, mid_ref, near_ref):
     live = iota((HEAD, TOKENS), 1) < count[0]
-    grads = dot(w_ref[...], cot_ref[...], 1, 0)
+    grads = dot3(w_ref[...], cot_ref[...], 1, 0)
     for j in range(LOCAL_HEADS):
         rows = slice(HEAD * j, HEAD * (j + 1))
         both = jnp.concatenate(
@@ -133,7 +126,7 @@
 def branch_scores(turned, pairs):
     rows = turned.shape[0]
     mark = ((iota((8, 2 * HEAD), 0) == 0) & (iota((8, 2 * HEAD), 1) == 0)).astype(jnp.float32)
-    products = dot(jnp.concatenate([split_queries(turned), mark], axis=0), pairs, 1, 1)
+    products = dot3(jnp.concatenate([split_queries(turned), mark], axis=0), pairs, 1, 1)
     dead = products[2 * rows : 2 * rows + 1, :] > DEAD_LEVEL
     scores = jnp.where(dead, MASKED_SCORE, products[:rows])
     prob_grads = products[rows : 2 * rows]
@@ -176,26 +169,24 @@
     return jnp.concatenate([own[rows, :], other[rows, :]], axis=0)
 
 
-def scores_body(*refs):
-    qf_ref, qn_ref, near_own, near_other = refs[:4]
-    far_refs = refs[4:-4]
-    far_both, far_stats, near_both, near_stats = refs[-4:]
-    for j in range(LOCAL_HEADS):
-        pairs = gathered(far_refs, head_slice(j, FAR_ROWS))
-        far_both[j], far_stats[j] = branch_scores(qf_ref[j], pairs)
-        near_both[j], near_stats[j] = branch_scores(
-            qn_ref[j], near_pairs_of(near_own, near_other, j)
-        )
+def near_scores_body(q_ref, near_own, near_other, both_ref, stats_ref):
+    for j in range(LOCAL_HEADS):
+        pairs = near_pairs_of(near_own, near_other, j)
+        both_ref[j], stats_ref[j] = branch_scores(q_ref[j], pairs)
+
+
+def far_scores_body(q_ref, far_own, far_other, both_ref, stats_ref):
+    for j in range(LOCAL_HEADS):
+        pairs = gathered((far_own, far_other), head_slice(j, FAR_ROWS))
+        both_ref[j], stats_ref[j] = branch_scores(q_ref[j], pairs)
 
 
 def attention_body(*refs):
     count, base = refs[:2]
-    qm_ref, near_own, near_other, mid_own, mid_other, w_ref, cot_ref = refs[2:9]
-    far_in, far_stats_ref, near_in, near_stats_ref = refs[9:13]
-    outs = refs[-10:]
-    far_refs = refs[13:-10]
-    dq_ref, weight_ref, far_both, mid_both, near_both = outs[:5]
-    term_refs, terms_ref = outs[5:9], outs[9]
+    qm_ref, near_own, near_other, mid_own, mid_other, cot_ref = refs[2:8]
+    far_in, far_stats_ref, near_in, near_stats_ref = refs[8:12]
+    far_refs = refs[12:14]
+    dq_ref, attended_ref, weight_ref, far_both, mid_both, near_both = refs[14:]
     lanes = iota((TOKENS, 128), 1)
     position = iota((TOKENS, 1), 0)
     attended = []
@@ -251,34 +242,84 @@
         attended.append(turned[HEAD:])
     live = iota((HEAD * LOCAL_HEADS, TOKENS), 1) < count[0]
     rows = jnp.where(live, jnp.concatenate(attended, axis=0), 0.0)
-    terms_ref[...] = dot3(w_ref[...], rows, 0, 0)
+    attended_ref[...] = rows
+    columns = rows.shape[0]
+    weight = dot3(rows, cot_ref[...], 1, 1)
+    for b in range(weight.shape[1] // 128):
+        weight_ref[columns * b : columns * (b + 1), :] = weight[:, 128 * b : 128 * b + 128]
+
+
+def terms_body(base, attended_ref, w_ref, *refs):
+    term_refs, terms_ref = refs[:4], refs[4]
+    terms_ref[...] = dot3(w_ref[...], attended_ref[...], 0, 0)
     columns = term_refs[0].shape[0]
     heads = terms_ref.shape[0] // columns
     group = base[0] // LOCAL_HEADS
     for k, ref in enumerate(term_refs):
         at = pl.multiple_of(columns * ((group + k) % heads), columns)
         ref[...] = terms_ref[pl.ds(at, columns), :]
-    weight = dot3(rows, cot_ref[...], 1, 1)
-    for b in range(weight.shape[1] // 128):
-        weight_ref[columns * b : columns * (b + 1), :] = weight[:, 128 * b : 128 * b + 128]
-
-
-def keys_body(far_both, mid_both, near_both, qf_ref, qm_ref, qn_ref, *outs):
-    far_refs, mid_refs, near_refs = outs[:2], outs[2:4], outs[4:]
-    for j in range(LOCAL_HEADS):
-        for both, q_ref, refs, rows in (
-            (mid_both, qm_ref, mid_refs, MID_ROWS),
-            (far_both, qf_ref, far_refs, FAR_ROWS),
-        ):
-            sums = dot3(both[j], split_queries(q_ref[j]), 0, 0)
-            half = sums.shape[0] // 2
-            for i, ref in enumerate(refs):
-                ref[:, head_slice(j, rows), :] = sums[half * i : half * (i + 1)].reshape(
-                    half // rows, rows, 128
-                )
+
+
+def wide_keys(both, turned, refs, j):
+    sums = dot3(both, split_queries(turned), 0, 0)
+    rows = turned.shape[0]
+    half = sums.shape[0] // 2
+    for i, ref in enumerate(refs):
+        ref[:, head_slice(j, rows), :] = sums[half * i : half * (i + 1)].reshape(
+            half // rows, rows, 128
+        )
+
+
+def mid_keys_body(both_ref, q_ref, *refs):
+    for j in range(LOCAL_HEADS):
+        wide_keys(both_ref[j], q_ref[j], refs, j)
+
+
+def keys_body(far_both, near_both, qf_ref, qn_ref, *outs):
+    for j in range(LOCAL_HEADS):
+        wide_keys(far_both[j], qf_ref[j], outs[:2], j)
         sums = dot3(near_both[j], split_queries(qn_ref[j]), 0, 0)
-        for i, ref in enumerate(near_refs):
+        for i, ref in enumerate(outs[2:]):
             ref[head_slice(j, TOKENS), :] = sums[TOKENS * i : TOKENS * (i + 1)]
+
+
+def total_of(ref):
+    total = ref[0]
+    for i in range(1, ref.shape[0]):
+        total = total + ref[i]
+    return total
+
+
+def mid_join_body(keep_ref, got_ref, weight_ref, out_ref):
+    weight = total_of(weight_ref)
+    depth = weight.shape[0] // out_ref.shape[0]
+    for i in range(out_ref.shape[0]):
+        out_ref[i, :MID_BLOCK, :] = keep_ref[i] + got_ref[i]
+        out_ref[i, MID_BLOCK:, :] = weight[depth * i : depth * (i + 1)]
+
+
+def far_join_body(mid_ref, *refs):
+    out_ref = refs[-1]
+    weight = mid_ref[0, MID_BLOCK:, :]
+    for i in range(1, mid_ref.shape[0]):
+        weight = weight + mid_ref[i, MID_BLOCK:, :]
+    for i in range(out_ref.shape[0]):
+        total = refs[0][i]
+        for ref in refs[1:-1]:
+            total = total + ref[i]
+        out_ref[i, :FAR_BLOCK, :] = total
+        out_ref[i, FAR_BLOCK:, :] = weight
+
+
+def weight_join_body(far_ref, out_ref):
+    lines = out_ref.shape[1] // (far_ref.shape[1] - FAR_BLOCK)
+    depth = out_ref.shape[1] // lines
+    for i in range(lines):
+        total = far_ref[i, FAR_BLOCK:, :]
+        for at in range(i + lines, far_ref.shape[0], lines):
+            total = total + far_ref[at, FAR_BLOCK:, :]
+        for to in range(out_ref.shape[0]):
+            out_ref[to, depth * i : depth * (i + 1), :] = total
 
 
 def finish_body(base, far_ref, mid_ref, near_ref, other_ref, dk_ref, dv_ref):
@@ -304,6 +345,13 @@
         dv_ref[HEAD * j : HEAD * (j + 1), :] = turned[HEAD:]
 
 
+def weight_order_body(in_ref, out_ref):
+    rows = out_ref.shape[0]
+    every = in_ref[...].reshape(in_ref.shape[0] * in_ref.shape[1], 128)
+    for b in range(out_ref.shape[1] // 128):
+        out_ref[:, 128 * b : 128 * b + 128] = every[rows * b : rows * (b + 1)]
+
+
 def exchange(pieces, axis):
     return lax.all_to_all(pieces, axis, 0, 0, tiled=True)
 
@@ -318,12 +366,12 @@
 
 
 def on_device(queries, keys, values, counts, out_weight, cotangent):
-    ny, nz, nzh, nzl = (lax.axis_size(axis) for axis in ("y", Z, "zh", "zl"))
+    ny, nz, _, nzl = (lax.axis_size(axis) for axis in ("y", Z, "zh", "zl"))
     heads = lax.axis_size("h")
     columns, tokens = queries.shape
     base = (lax.axis_index("h") * LOCAL_HEADS).astype(jnp.int32).reshape(1)
 
-    cots = [cotangent] + [shifted(cotangent, "h", k % heads) for k in range(1, 4)]
+    full_cot = to_all(cotangent, "h").reshape(heads * columns, tokens)
     far_out, mid_out, near_own = kernel_call(
         pack_body,
         (shaped(nz, FAR_BLOCK, 128), shaped(nzl, MID_BLOCK, 128), shaped(NEAR_BLOCK, 128)),
@@ -332,45 +380,46 @@
     )
     near_other = shifted(near_own, "c", 1)
     far_line = exchange(far_out, Z)
-    query_far, query_mid, query_near, full_cot = kernel_call(
+    query_far, query_mid, query_near = kernel_call(
         query_body,
         (
             shaped(LOCAL_HEADS, FAR_ROWS, 128),
             shaped(LOCAL_HEADS, MID_ROWS, 128),
             shaped(LOCAL_HEADS, TOKENS, 128),
-            shaped(heads * columns, tokens),
         ),
-        (counts, base, queries, out_weight, *cots),
+        (counts, base, queries, out_weight, full_cot),
         2,
     )
+    near_both, near_stats = kernel_call(
+        near_scores_body,
+        (shaped(LOCAL_HEADS, 2 * TOKENS, 2 * TOKENS), shaped(LOCAL_HEADS, TOKENS, 128)),
+        (query_near, near_own, near_other),
+        0,
+    )
     mid_own = exchange(mid_out, "zl")
-    far_plane = [far_line] + [shifted(far_line, "y", k) for k in range(1, ny)]
-    far_blocks = far_plane + [shifted(x, "c", 1) for x in far_plane]
+    far_own = jnp.concatenate(
+        [far_line] + [shifted(far_line, "y", k) for k in range(1, ny)], axis=0
+    )
+    far_other = shifted(far_own, "c", 1)
     far_keys = 2 * ny * nz * FAR_ROWS
-    far_both, far_stats, near_both, near_stats = kernel_call(
-        scores_body,
-        (
-            shaped(LOCAL_HEADS, 2 * FAR_ROWS, far_keys),
-            shaped(LOCAL_HEADS, FAR_ROWS, 128),
-            shaped(LOCAL_HEADS, 2 * TOKENS, 2 * TOKENS),
-            shaped(LOCAL_HEADS, TOKENS, 128),
-        ),
-        (query_far, query_near, near_own, near_other, *far_blocks),
+    far_both, far_stats = kernel_call(
+        far_scores_body,
+        (shaped(LOCAL_HEADS, 2 * FAR_ROWS, far_keys), shaped(LOCAL_HEADS, FAR_ROWS, 128)),
+        (query_far, far_own, far_other),
         0,
     )
     mid_other = shifted(mid_own, "c", 1)
     mid_keys = 2 * nzl * MID_ROWS
-    query_grad, weight, far_both, mid_both, near_both, *terms = kernel_call(
+    query_grad, attended, weight, far_both, mid_both, near_both = kernel_call(
         attention_body,
         (
+            shaped(columns, tokens),
             shaped(columns, tokens),
             shaped(out_weight.size // 128, 128),
             shaped(LOCAL_HEADS, 2 * FAR_ROWS, far_keys),
             shaped(LOCAL_HEADS, 2 * MID_ROWS, mid_keys),
             shaped(LOCAL_HEADS, 2 * TOKENS, 2 * TOKENS),
-        )
-        + (shaped(columns, tokens),) * 4
-        + (shaped(heads * columns, tokens),),
+        ),
         (
             counts,
             base,
@@ -379,51 +428,53 @@
             near_other,
             mid_own,
             mid_other,
-            out_weight,
             full_cot,
             far_both,
             far_stats,
             near_both,
             near_stats,
-            *far_blocks,
+            far_own,
+            far_other,
         ),
         2,
     )
     planes = 2 * ny
     weight_parts = exchange(weight.reshape(planes, -1, 128), ("y", "c"))
-    far_keep, far_send, mid_keep, mid_send, near_keep, near_send = kernel_call(
+    mid_keep, mid_send = kernel_call(
+        mid_keys_body, (shaped(nzl, MID_BLOCK, 128),) * 2, (mid_both, query_mid), 0
+    )
+    mid_got = shifted(mid_send, "c", 1)
+    depth = weight.shape[0] // (planes * nzl)
+    mid_join = kernel_call(
+        mid_join_body, shaped(nzl, MID_BLOCK + depth, 128), (mid_keep, mid_got, weight_parts), 0
+    )
+    mid_sums = exchange(mid_join, "zl")
+    far_keep, far_send, near_keep, near_send = kernel_call(
         keys_body,
-        (shaped(ny * nz, FAR_BLOCK, 128),) * 2
-        + (shaped(nzl, MID_BLOCK, 128),) * 2
-        + (shaped(NEAR_BLOCK, 128),) * 2,
-        (far_both, mid_both, near_both, query_far, query_mid, query_near),
+        (shaped(ny * nz, FAR_BLOCK, 128),) * 2 + (shaped(NEAR_BLOCK, 128),) * 2,
+        (far_both, near_both, query_far, query_near),
         0,
     )
-    mid_got = shifted(mid_send, "c", 1)
-    weight_line = jnp.sum(weight_parts, axis=0).reshape(nzl, -1, 128)
-    mid_sums = exchange(jnp.concatenate([mid_keep + mid_got, weight_line], axis=1), "zl")
     far_got = shifted(far_send, "c", 1)
     near_got = shifted(near_send, "c", 1)
     pieces = [far_keep[nz * k : nz * (k + 1)] + far_got[nz * k : nz * (k + 1)] for k in range(ny)]
     pieces = pieces[:1] + [shifted(pieces[k], "y", -k) for k in range(1, ny)]
-    far_total = sum(pieces[1:], pieces[0])
-    weight_own = jnp.sum(mid_sums[:, MID_BLOCK:], axis=0)
-    depth = weight_own.shape[0]
-    parts = exchange(
-        jnp.concatenate(
-            [far_total, jnp.broadcast_to(weight_own, (nz, depth, 128))], axis=1
-        ),
-        Z,
+    far_join = kernel_call(
+        far_join_body, shaped(nz, FAR_BLOCK + depth, 128), (mid_sums, *pieces), 0
+    )
+    parts = exchange(far_join, Z)
+    terms = kernel_call(
+        terms_body,
+        (shaped(columns, tokens),) * 4 + (shaped(heads * columns, tokens),),
+        (base, attended, out_weight),
+        1,
     )
     got = [terms[0]] + [shifted(terms[k], "h", k % heads) for k in range(1, 4)]
     output = sum(got[1:], got[0])
-    weight_whole = jnp.sum(parts[:, FAR_BLOCK:].reshape(nzh, nzl, depth, 128), axis=0)
-    weight_rows = to_all(weight_whole.reshape(nzl * depth, 128), ("y", "c"))
-    weight_grad = (
-        weight_rows.reshape(out_weight.shape[1] // 128, out_weight.shape[0], 128)
-        .swapaxes(0, 1)
-        .reshape(out_weight.shape)
-    )
+    weight_rows = exchange(
+        kernel_call(weight_join_body, shaped(planes, nzl * depth, 128), (parts,), 0), ("y", "c")
+    )
+    weight_grad = kernel_call(weight_order_body, shaped(*out_weight.shape), (weight_rows,), 0)
     key_grad, value_grad = kernel_call(
         finish_body,
         (shaped(columns, tokens), shaped(columns, tokens)),

time: 204 us -> 217 us (1.064)
  waiting for transfers between devices: 13.2 us -> 26.4 us
  starting transfers between devices: 96 us -> 83.1 us
  Pallas kernels: 27.3 us -> 38.1 us
    ppermute x21 -> x15, starting transfers between devices: 60.2 us -> 47.5 us  [shifted(): return lax.ppermute(x, axis, [(i, (i + apart) % size) for i in range(size)])]
    pallas_call x6 -> x13, Pallas kernels: 27.3 us -> 38.1 us  [kernel_call(): pl.pallas_call(body, out_shape=out_shape, in_specs=in_specs, out_specs=ja...]
    all_to_all x4 -> x5, waiting for transfers between devices: 0.99 us -> 9.54 us  [exchange(): return lax.all_to_all(pieces, axis, 0, 0, tiled=True)]
    ppermute x21 -> x15, waiting for transfers between devices: 12.2 us -> 16.9 us  [shifted(): return lax.ppermute(x, axis, [(i, (i + apart) % size) for i in range(size)])]
    unnamed x52 -> x37, local copies, waits for them, and re-layouts: 3.7 us -> 6.28 us
    all_to_all x4 -> x5, starting transfers between devices: 35.8 us -> 35.6 us  [exchange(): return lax.all_to_all(pieces, axis, 0, 0, tiled=True)]
  transfers between devices with their start and end apart: 25 -> 20, of which waited for: 7 -> 9; matrix products, arithmetic and copies ran while one was open for 1% -> 2% of each run, Pallas kernels for 7% -> 9%
where the time goes in v3:
time: 217 us; the launch traced here: 215 us
  starting transfers between devices  83.1 us (38%)
  blocking collectives  54.8 us (25%)
  Pallas kernels  38.1 us (18%)
  waiting for transfers between devices  26.4 us (12%)
  local copies, waits for them, and re-layouts  7.07 us (3%)
  other arithmetic  3.55 us (2%)
    all_to_all x2, blocking collectives, exchange(): return lax.all_to_all(pieces, axis, 0, 0, tiled=True)  54.8 us
    ppermute x15, starting transfers between devices, shifted(): return lax.ppermute(x, axis, [(i, (i + apart) % size) for i in range(size)])  47.5 us
    pallas_call x13, Pallas kernels, kernel_call(): pl.pallas_call(body, out_shape=out_shape, in_specs=in_specs, out_specs=ja...  38.1 us
    all_to_all x5, starting transfers between devices, exchange(): return lax.all_to_all(pieces, axis, 0, 0, tiled=True)  35.6 us
    ppermute x15, waiting for transfers between devices, shifted(): return lax.ppermute(x, axis, [(i, (i + apart) % size) for i in range(size)])  16.9 us
    all_to_all x5, waiting for transfers between devices, exchange(): return lax.all_to_all(pieces, axis, 0, 0, tiled=True)  9.54 us
    unnamed x37, local copies, waits for them, and re-layouts  6.28 us
  transfers between devices with their start and end apart: 20, of which 9 were waited for; matrix products, arithmetic and copies ran while one was open for 2% of the time, Pallas kernels for 9%

profile of v3, /device:TPU:1, one launch (start us, length us, event | category | flops | bytes accessed | tf_op | source)
XLA Modules:
  0.0 214.7 jit_solution(12383890159157859751)
XLA Ops:
  1.3 2.3 %shard_map.102 = (f32[16,24,128]{2,1,0:T(8,128)}, f32[8,96,128]{2,1,0:T(8,128)}, f32[384,128]{1,0:T(8,128)}) custom-call(s32[1]{0:T(128)S(6)} %copy.14.count.refs_0_, s32[1]{0:T(128)} %bitcast.base.refs_1_, f32[192,128]{1,0:T(8,128)} %k_ref.1, f32[192,128]{1,0:T(8,128)} %v_ref.1), custom_call_target="tpu_custom_call" | custom-call | tf_op jit(solution)/shard_map/pallas_call | solution.py:73
  3.6 28.2 %all_to_all.35 = f32[16,24,128]{2,1,0:T(8,128)S(1)} all-to-all(f32[16,24,128]{2,1,0:T(8,128)} %get-tuple-element.37), channel_id=1, replica_groups=mesh['y'=4,'zh'=2,'zl'=8,'c'=2,'h'=4] {'zh','zl'}, dimensions={0} | all-to-all | bytes 393216 | tf_op jit(solution)/shard_map/all_to_all | solution.py:356
  31.8 8.8 %all-to-all-start.1 = ((f32[8,96,128]{2,1,0:T(8,128)}), f32[8,96,128]{2,1,0:T(8,128)S(1)}, u32[]{:S(2)}, u32[]{:S(2)}) async-start(f32[8,96,128]{2,1,0:T(8,128)} %get-tuple-element.35), calls=%async_computation.1 | async-start | bytes 786432 | tf_op jit(solution)/shard_map/all_to_all | solution.py:356
  40.6 3.2 %collective-permute-start.2 = (f32[16,24,128]{2,1,0:T(8,128)S(1)}, f32[16,24,128]{2,1,0:T(8,128)S(1)}, u32[]{:S(2)}, u32[]{:S(2)}) collective-permute-start(f32[16,24,128]{2,1,0:T(8,128)S(1)} %all_to_all.35), channel_id=1, source_target_pairs={{0,128},{128,256},{256,384},{384,0},{1,129},{129,257},{257,385},{3... | collective-permute-start | bytes 589832 | tf_op jit(solution)/shard_map/ppermute | solution.py:365
  43.8 3.4 %collective-permute-start.4 = (f32[16,24,128]{2,1,0:T(8,128)S(1)}, f32[16,24,128]{2,1,0:T(8,128)S(1)}, u32[]{:S(2)}, u32[]{:S(2)}) collective-permute-start(f32[16,24,128]{2,1,0:T(8,128)S(1)} %all_to_all.35), channel_id=1, source_target_pairs={{0,384},{128,0},{256,128},{384,256},{1,385},{129,1},{257,129},{385... | collective-permute-start | bytes 589832 | tf_op jit(solution)/shard_map/ppermute | solution.py:365
  47.2 3.5 %collective-permute-start.3 = (f32[16,24,128]{2,1,0:T(8,128)S(1)}, f32[16,24,128]{2,1,0:T(8,128)S(1)}, u32[]{:S(2)}, u32[]{:S(2)}) collective-permute-start(f32[16,24,128]{2,1,0:T(8,128)S(1)} %all_to_all.35), channel_id=1, source_target_pairs={{0,256},{128,384},{256,0},{384,128},{1,257},{129,385},{257,1},{385... | collective-permute-start | bytes 589832 | tf_op jit(solution)/shard_map/ppermute | solution.py:365
  50.8 4.8 %collective-permute-done.3 = f32[16,24,128]{2,1,0:T(8,128)S(1)} collective-permute-done((f32[16,24,128]{2,1,0:T(8,128)S(1)}, f32[16,24,128]{2,1,0:T(8,128)S(1)}, u32[]{:S(2)}, u32[]{:S(2)}) %collective-permute-start.3) | collective-permute-done | bytes 196640 | tf_op jit(solution)/shard_map/ppermute | solution.py:365
  55.7 4.2 %collective-permute-start.5 = (f32[64,24,128]{2,1,0:T(8,128)S(1)}, f32[64,24,128]{2,1,0:T(8,128)S(1)}, u32[]{:S(2)}, u32[]{:S(2)}) collective-permute-start(f32[64,24,128]{2,1,0:T(8,128)S(1)} %constant_dynamic-update-slice_fusion.far_own.refs_12_), channel_id=1, source_target_pairs={{0,4},{4,0},{1,5},{5,1},{2,6},{6,2},{3,7},{7,3},{8,12},{12,8},{9,1... | collective-permute-start | bytes 2359304 | tf_op jit(solution)/shard_map/ppermute | solution.py:365
  59.9 6.7 %collective-permute-start.1 = (f32[8,96,128]{2,1,0:T(8,128)S(1)}, f32[8,96,128]{2,1,0:T(8,128)S(1)}, u32[]{:S(2)}, u32[]{:S(2)}) collective-permute-start(f32[8,96,128]{2,1,0:T(8,128)S(1)} %all-to-all-done.1.refs_5_), channel_id=1, source_target_pairs={{0,4},{4,0},{1,5},{5,1},{2,6},{6,2},{3,7},{7,3},{8,12},{12,8},{9,1... | collective-permute-start | bytes 1179656 | tf_op jit(solution)/shard_map/ppermute | solution.py:365
  67.4 4.1 %all-to-all-start = ((f32[4,192,128]{2,1,0:T(8,128)}), f32[4,192,128]{2,1,0:T(8,128)S(1)}, u32[]{:S(2)}, u32[]{:S(2)}) async-start(f32[4,192,128]{2,1,0:T(8,128)} %broadcast_in_dim.3), calls=%async_computation | async-start | bytes 786432 | tf_op jit(solution)/shard_map/all_to_all | solution.py:356
  73.7 5.7 %all-to-all-done = f32[4,192,128]{2,1,0:T(8,128)S(1)} async-done(((f32[4,192,128]{2,1,0:T(8,128)}), f32[4,192,128]{2,1,0:T(8,128)S(1)}, u32[]{:S(2)}, u32[]{:S(2)}) %all-to-all-start) | async-done | bytes 393248 | tf_op jit(solution)/shard_map/all_to_all | solution.py:356
  80.1 2.7 %shard_map.101 = (f32[3,8,128]{2,1,0:T(8,128)}, f32[3,32,128]{2,1,0:T(8,128)}, f32[3,128,128]{2,1,0:T(8,128)}) custom-call(s32[1]{0:T(128)S(6)} %copy.14.count.refs_0_, s32[1]{0:T(128)} %bitcast.base.refs_1_, f32[192,128]{1,0:T(8,128)} %q_ref.1, f32[192,768]{1,0:T(8,128)} %w_ref.3, f32[768,128]{1,0:T(8,128)} %bitcast.3), custom_call_target="tpu_custom_call" | custom-call | tf_op jit(solution)/shard_map/pallas_call | solution.py:73
  83.6 2.7 %shard_map.104 = (f32[3,256,256]{2,1,0:T(8,128)}, f32[3,128,128]{2,1,0:T(8,128)}) custom-call(f32[3,128,128]{2,1,0:T(8,128)} %get-tuple-element.40.q_ref.qn_ref, f32[384,128]{1,0:T(8,128)} %get-tuple-element.34.near_own.refs_3_, f32[384,128]{1,0:T(8,128)} %copy-done.8), custom_call_target="tpu_custom_call" | custom-call | tf_op jit(solution)/shard_map/pallas_call | solution.py:73
  87.1 3.1 %shard_map.103 = (f32[3,16,1024]{2,1,0:T(8,128)}, f32[3,8,128]{2,1,0:T(8,128)}) custom-call(f32[3,8,128]{2,1,0:T(8,128)} %get-tuple-element.36.q_ref.qf_ref, f32[64,24,128]{2,1,0:T(8,128)} %copy-done.1, f32[64,24,128]{2,1,0:T(8,128)} %copy-done.3), custom_call_target="tpu_custom_call" | custom-call | tf_op jit(solution)/shard_map/pallas_call | solution.py:73
  91.0 8.3 %shard_map.105 = (f32[192,128]{1,0:T(8,128)}, f32[192,128]{1,0:T(8,128)}, f32[1152,128]{1,0:T(8,128)}, f32[3,16,1024]{2,1,0:T(8,128)}, f32[3,64,512]{2,1,0:T(8,128)}, /*index=5*/f32[3,256,256]{2,1,0:T(8,128)}) custom-call(s32[1]{0:T(128)S(6)} %copy.14.count.refs_0_, s32[1]{0:T(128)} %bitcast.base.refs_1_, f32[3,32,128]{2,1,0:T(8,128)} %get-tuple-element.33.refs_2_.q_ref, ...), custom_call_target="tpu_custom_call" | custom-call | tf_op jit(solution)/shard_map/pallas_call | solution.py:73
  99.2 5.6 %all-to-all-start.3 = ((f32[8,144,128]{2,1,0:T(8,128)}), f32[8,144,128]{2,1,0:T(8,128)S(1)}, u32[]{:S(2)}, u32[]{:S(2)}) async-start(f32[8,144,128]{2,1,0:T(8,128)} %bitcast.5), calls=%async_computation.3 | async-start | bytes 1179648 | tf_op jit(solution)/shard_map/all_to_all | solution.py:356
  104.9 2.4 %shard_map.107 = (f32[8,96,128]{2,1,0:T(8,128)}, f32[8,96,128]{2,1,0:T(8,128)}) custom-call(f32[3,64,512]{2,1,0:T(8,128)} %get-tuple-element.49.both_ref, f32[3,32,128]{2,1,0:T(8,128)} %get-tuple-element.33.refs_2_.q_ref), custom_call_target="tpu_custom_call" | custom-call | tf_op jit(solution)/shard_map/pallas_call | solution.py:73
  111.1 3.9 %all-to-all-done.3.weight_ref = f32[8,144,128]{2,1,0:T(8,128)S(1)} async-done(((f32[8,144,128]{2,1,0:T(8,128)}), f32[8,144,128]{2,1,0:T(8,128)S(1)}, u32[]{:S(2)}, u32[]{:S(2)}) %all-to-all-start.3) | async-done | bytes 589856 | tf_op jit(solution)/shard_map/all_to_all | solution.py:356
  117.9 4.0 %all-to-all-start.4 = ((f32[8,114,128]{2,1,0:T(8,128)}), f32[8,114,128]{2,1,0:T(8,128)S(1)}, u32[]{:S(2)}, u32[]{:S(2)}) async-start(f32[8,114,128]{2,1,0:T(8,128)} %shard_map.108), calls=%async_computation.4 | async-start | bytes 983040 | tf_op jit(solution)/shard_map/all_to_all | solution.py:356
  121.9 3.6 %shard_map.109 = (f32[64,24,128]{2,1,0:T(8,128)}, f32[64,24,128]{2,1,0:T(8,128)}, f32[384,128]{1,0:T(8,128)}, f32[384,128]{1,0:T(8,128)}) custom-call(f32[3,16,1024]{2,1,0:T(8,128)} %get-tuple-element.53.far_both, f32[3,256,256]{2,1,0:T(8,128)} %get-tuple-element.54.near_both, f32[3,8,128]{2,1,0:T(8,128)} %get-tuple-element.36.q_ref.qf_ref, ...), custom_call_target="tpu_custom_call" | custom-call | tf_op jit(solution)/shard_map/pallas_call | solution.py:73
  125.5 3.1 %collective-permute-start.10 = (f32[64,24,128]{2,1,0:T(8,128)}, f32[64,24,128]{2,1,0:T(8,128)S(1)}, u32[]{:S(2)}, u32[]{:S(2)}) collective-permute-start(f32[64,24,128]{2,1,0:T(8,128)} %get-tuple-element.56), channel_id=1, source_target_pairs={{0,4},{4,0},{1,5},{5,1},{2,6},{6,2},{3,7},{7,3},{8,12},{12,8},{9,1... | collective-permute-start | bytes 2359304 | tf_op jit(solution)/shard_map/ppermute | solution.py:365
  134.9 3.7 %collective-permute-start.12 = (f32[16,24,128]{2,1,0:T(8,128)S(1)}, f32[16,24,128]{2,1,0:T(8,128)S(1)}, u32[]{:S(2)}, u32[]{:S(2)}) collective-permute-start(f32[16,24,128]{2,1,0:T(8,128)S(1)} %get-tuple-element.62), channel_id=1, source_target_pairs={{0,256},{128,384},{256,0},{384,128},{1,257},{129,385},{257,1},{385... | collective-permute-start | bytes 589832 | tf_op jit(solution)/shard_map/ppermute | solution.py:365
  138.6 2.5 %collective-permute-start.11 = (f32[16,24,128]{2,1,0:T(8,128)S(1)}, f32[16,24,128]{2,1,0:T(8,128)S(1)}, u32[]{:S(2)}, u32[]{:S(2)}) collective-permute-start(f32[16,24,128]{2,1,0:T(8,128)S(1)} %get-tuple-element.63), channel_id=1, source_target_pairs={{0,384},{128,0},{256,128},{384,256},{1,385},{129,1},{257,129},{385... | collective-permute-start | bytes 589832 | tf_op jit(solution)/shard_map/ppermute | solution.py:365
  142.5 3.1 %collective-permute-done.12.refs_2_ = f32[16,24,128]{2,1,0:T(8,128)S(1)} collective-permute-done((f32[16,24,128]{2,1,0:T(8,128)S(1)}, f32[16,24,128]{2,1,0:T(8,128)S(1)}, u32[]{:S(2)}, u32[]{:S(2)}) %collective-permute-start.12) | collective-permute-done | bytes 196640 | tf_op jit(solution)/shard_map/ppermute | solution.py:365
  145.6 2.8 %collective-permute-done.11.refs_1_ = f32[16,24,128]{2,1,0:T(8,128)S(1)} collective-permute-done((f32[16,24,128]{2,1,0:T(8,128)S(1)}, f32[16,24,128]{2,1,0:T(8,128)S(1)}, u32[]{:S(2)}, u32[]{:S(2)}) %collective-permute-start.11) | collective-permute-done | bytes 196640 | tf_op jit(solution)/shard_map/ppermute | solution.py:365
  151.3 26.6 %all_to_all.36.far_ref = f32[16,42,128]{2,1,0:T(8,128)} all-to-all(f32[16,42,128]{2,1,0:T(8,128)} %shard_map.110), channel_id=1, replica_groups=mesh['y'=4,'zh'=2,'zl'=8,'c'=2,'h'=4] {'zh','zl'}, dimensions={0} | all-to-all | bytes 688128 | tf_op jit(solution)/shard_map/all_to_all | solution.py:356
  179.7 13.1 %all-to-all-start.6 = ((f32[8,144,128]{2,1,0:T(8,128)}), f32[8,144,128]{2,1,0:T(8,128)S(1)}, u32[]{:S(2)}, u32[]{:S(2)}) async-start(f32[8,144,128]{2,1,0:T(8,128)} %shard_map.112), calls=%async_computation.6 | async-start | bytes 1179648 | tf_op jit(solution)/shard_map/all_to_all | solution.py:356
  192.9 2.6 %shard_map.106 = (f32[192,128]{1,0:T(8,128)}, f32[192,128]{1,0:T(8,128)}, f32[192,128]{1,0:T(8,128)}, f32[192,128]{1,0:T(8,128)}, f32[768,128]{1,0:T(8,128)}) custom-call(s32[1]{0:T(128)} %bitcast.base.refs_1_, f32[192,128]{1,0:T(8,128)} %get-tuple-element.43.attended_ref, f32[192,768]{1,0:T(8,128)} %w_ref.3), custom_call_target="tpu_custom_call" | custom-call | tf_op jit(solution)/shard_map/pallas_call | solution.py:73
  197.7 3.7 %collective-permute-start.7 = (f32[192,128]{1,0:T(8,128)}, f32[192,128]{1,0:T(8,128)S(1)}, u32[]{:S(2)}, u32[]{:S(2)}) collective-permute-start(f32[192,128]{1,0:T(8,128)} %get-tuple-element.46), channel_id=1, source_target_pairs={{0,2},{1,3},{2,0},{3,1},{4,6},{5,7},{6,4},{7,5},{8,10},{9,11},{10,... | collective-permute-start | bytes 294920 | tf_op jit(solution)/shard_map/ppermute | solution.py:365
  201.4 2.5 %collective-permute-start.8 = (f32[192,128]{1,0:T(8,128)}, f32[192,128]{1,0:T(8,128)S(1)}, u32[]{:S(2)}, u32[]{:S(2)}) collective-permute-start(f32[192,128]{1,0:T(8,128)} %get-tuple-element.47), channel_id=1, source_target_pairs={{0,3},{1,0},{2,1},{3,2},{4,7},{5,4},{6,5},{7,6},{8,11},{9,8},{10,9... | collective-permute-start | bytes 294920 | tf_op jit(solution)/shard_map/ppermute | solution.py:365
  203.9 2.5 %collective-permute-start.14 = (f32[384,128]{1,0:T(8,128)S(1)}, f32[384,128]{1,0:T(8,128)S(1)}, u32[]{:S(2)}, u32[]{:S(2)}) collective-permute-start(f32[384,128]{1,0:T(8,128)S(1)} %copy-done.16), channel_id=1, source_target_pairs={{0,4},{4,0},{1,5},{5,1},{2,6},{6,2},{3,7},{7,3},{8,12},{12,8},{9,1... | collective-permute-start | bytes 589832 | tf_op jit(solution)/shard_map/ppermute | solution.py:365
  209.5 2.5 %shard_map.111 = (f32[192,128]{1,0:T(8,128)}, f32[192,128]{1,0:T(8,128)}) custom-call(s32[1]{0:T(128)} %bitcast.base.refs_1_, f32[16,42,128]{2,1,0:T(8,128)} %all_to_all.36.far_ref, f32[8,114,128]{2,1,0:T(8,128)} %copy-done, f32[384,128]{1,0:T(8,128)} %get-tuple-element.57.near_ref, f32[384,128]{1,0:T(8,128)} %copy-done.11), custom_call_target="tpu_custom_call" | custom-call | tf_op jit(solution)/shard_map/pallas_call | solution.py:73
  (64 shorter events, 33.4 us)
Async XLA Ops:
  31.8 28.0 %all-to-all-start.1 = ((f32[8,96,128]{2,1,0:T(8,128)}), f32[8,96,128]{2,1,0:T(8,128)S(1)}, u32[]{:S(2)}, u32[]{:S(2)}) async-start(f32[8,96,128]{2,1,0:T(8,128)} %get-tuple-element.35), calls=%async_computation.1 | async-start | bytes 786432 | tf_op jit(solution)/shard_map/all_to_all | solution.py:356
  40.6 10.1 %collective-permute-start.2 = (f32[16,24,128]{2,1,0:T(8,128)S(1)}, f32[16,24,128]{2,1,0:T(8,128)S(1)}, u32[]{:S(2)}, u32[]{:S(2)}) collective-permute-start(f32[16,24,128]{2,1,0:T(8,128)S(1)} %all_to_all.35), channel_id=1, source_target_pairs={{0,128},{128,256},{256,384},{384,0},{1,129},{129,257},{257,385},{3... | collective-permute-start | bytes 589832 | tf_op jit(solution)/shard_map/ppermute | solution.py:365
  43.8 11.8 %collective-permute-start.4 = (f32[16,24,128]{2,1,0:T(8,128)S(1)}, f32[16,24,128]{2,1,0:T(8,128)S(1)}, u32[]{:S(2)}, u32[]{:S(2)}) collective-permute-start(f32[16,24,128]{2,1,0:T(8,128)S(1)} %all_to_all.35), channel_id=1, source_target_pairs={{0,384},{128,0},{256,128},{384,256},{1,385},{129,1},{257,129},{385... | collective-permute-start | bytes 589832 | tf_op jit(solution)/shard_map/ppermute | solution.py:365
  47.2 8.4 %collective-permute-start.3 = (f32[16,24,128]{2,1,0:T(8,128)S(1)}, f32[16,24,128]{2,1,0:T(8,128)S(1)}, u32[]{:S(2)}, u32[]{:S(2)}) collective-permute-start(f32[16,24,128]{2,1,0:T(8,128)S(1)} %all_to_all.35), channel_id=1, source_target_pairs={{0,256},{128,384},{256,0},{384,128},{1,257},{129,385},{257,1},{385... | collective-permute-start | bytes 589832 | tf_op jit(solution)/shard_map/ppermute | solution.py:365
  55.6 11.0 %copy-start.15 = (f32[192,128]{1,0:T(8,128)S(1)}, f32[192,128]{1,0:T(8,128)}, u32[]{:S(2)}) copy-start(f32[192,128]{1,0:T(8,128)} %param.11) | copy-start | bytes 294916
  55.7 27.2 %copy-start.1 = (f32[64,24,128]{2,1,0:T(8,128)}, f32[64,24,128]{2,1,0:T(8,128)S(1)}, u32[]{:S(2)}) copy-start(f32[64,24,128]{2,1,0:T(8,128)S(1)} %constant_dynamic-update-slice_fusion.far_own.refs_12_) | copy-start | bytes 2359300
  55.7 30.6 %collective-permute-start.5 = (f32[64,24,128]{2,1,0:T(8,128)S(1)}, f32[64,24,128]{2,1,0:T(8,128)S(1)}, u32[]{:S(2)}, u32[]{:S(2)}) collective-permute-start(f32[64,24,128]{2,1,0:T(8,128)S(1)} %constant_dynamic-update-slice_fusion.far_own.refs_12_), channel_id=1, source_target_pairs={{0,4},{4,0},{1,5},{5,1},{2,6},{6,2},{3,7},{7,3},{8,12},{12,8},{9,1... | collective-permute-start | bytes 2359304 | tf_op jit(solution)/shard_map/ppermute | solution.py:365
  59.9 7.5 %copy-start.6 = (f32[8,96,128]{2,1,0:T(8,128)}, f32[8,96,128]{2,1,0:T(8,128)S(1)}, u32[]{:S(2)}) copy-start(f32[8,96,128]{2,1,0:T(8,128)S(1)} %all-to-all-done.1.refs_5_) | copy-start | bytes 1179652
  59.9 30.3 %collective-permute-start.1 = (f32[8,96,128]{2,1,0:T(8,128)S(1)}, f32[8,96,128]{2,1,0:T(8,128)S(1)}, u32[]{:S(2)}, u32[]{:S(2)}) collective-permute-start(f32[8,96,128]{2,1,0:T(8,128)S(1)} %all-to-all-done.1.refs_5_), channel_id=1, source_target_pairs={{0,4},{4,0},{1,5},{5,1},{2,6},{6,2},{3,7},{7,3},{8,12},{12,8},{9,1... | collective-permute-start | bytes 1179656 | tf_op jit(solution)/shard_map/ppermute | solution.py:365
  67.4 4.2 %copy-start.7 = (f32[384,128]{1,0:T(8,128)S(1)}, f32[384,128]{1,0:T(8,128)}, u32[]{:S(2)}) copy-start(f32[384,128]{1,0:T(8,128)} %get-tuple-element.34.near_own.refs_3_) | copy-start | bytes 589828
  67.4 12.0 %all-to-all-start = ((f32[4,192,128]{2,1,0:T(8,128)}), f32[4,192,128]{2,1,0:T(8,128)S(1)}, u32[]{:S(2)}, u32[]{:S(2)}) async-start(f32[4,192,128]{2,1,0:T(8,128)} %broadcast_in_dim.3), calls=%async_computation | async-start | bytes 786432 | tf_op jit(solution)/shard_map/all_to_all | solution.py:356
  71.5 11.4 %collective-permute-start = (f32[384,128]{1,0:T(8,128)S(1)}, f32[384,128]{1,0:T(8,128)S(1)}, u32[]{:S(2)}, u32[]{:S(2)}) collective-permute-start(f32[384,128]{1,0:T(8,128)S(1)} %copy-done.7), channel_id=1, source_target_pairs={{0,4},{4,0},{1,5},{5,1},{2,6},{6,2},{3,7},{7,3},{8,12},{12,8},{9,1... | collective-permute-start | bytes 589832 | tf_op jit(solution)/shard_map/ppermute | solution.py:365
  86.2 0.9 copy-start.3
  99.2 15.7 %all-to-all-start.3 = ((f32[8,144,128]{2,1,0:T(8,128)}), f32[8,144,128]{2,1,0:T(8,128)S(1)}, u32[]{:S(2)}, u32[]{:S(2)}) async-start(f32[8,144,128]{2,1,0:T(8,128)} %bitcast.5), calls=%async_computation.3 | async-start | bytes 1179648 | tf_op jit(solution)/shard_map/all_to_all | solution.py:356
  107.2 3.8 %collective-permute-start.9 = (f32[8,96,128]{2,1,0:T(8,128)}, f32[8,96,128]{2,1,0:T(8,128)S(1)}, u32[]{:S(2)}, u32[]{:S(2)}) collective-permute-start(f32[8,96,128]{2,1,0:T(8,128)} %get-tuple-element.51), channel_id=1, source_target_pairs={{0,4},{4,0},{1,5},{5,1},{2,6},{6,2},{3,7},{7,3},{8,12},{12,8},{9,1... | collective-permute-start | bytes 1179656 | tf_op jit(solution)/shard_map/ppermute | solution.py:365
  111.1 3.9 %copy-start.10 = (f32[8,96,128]{2,1,0:T(8,128)}, f32[8,96,128]{2,1,0:T(8,128)S(1)}, u32[]{:S(2)}) copy-start(f32[8,96,128]{2,1,0:T(8,128)S(1)} %collective-permute-done.9.got_ref) | copy-start | bytes 1179652
  114.9 0.8 copy-start.4
  117.9 30.4 %all-to-all-start.4 = ((f32[8,114,128]{2,1,0:T(8,128)}), f32[8,114,128]{2,1,0:T(8,128)S(1)}, u32[]{:S(2)}, u32[]{:S(2)}) async-start(f32[8,114,128]{2,1,0:T(8,128)} %shard_map.108), calls=%async_computation.4 | async-start | bytes 983040 | tf_op jit(solution)/shard_map/all_to_all | solution.py:356
  125.5 5.3 %collective-permute-start.10 = (f32[64,24,128]{2,1,0:T(8,128)}, f32[64,24,128]{2,1,0:T(8,128)S(1)}, u32[]{:S(2)}, u32[]{:S(2)}) collective-permute-start(f32[64,24,128]{2,1,0:T(8,128)} %get-tuple-element.56), channel_id=1, source_target_pairs={{0,4},{4,0},{1,5},{5,1},{2,6},{6,2},{3,7},{7,3},{8,12},{12,8},{9,1... | collective-permute-start | bytes 2359304 | tf_op jit(solution)/shard_map/ppermute | solution.py:365
  132.7 9.8 %collective-permute-start.13 = (f32[16,24,128]{2,1,0:T(8,128)S(1)}, f32[16,24,128]{2,1,0:T(8,128)S(1)}, u32[]{:S(2)}, u32[]{:S(2)}) collective-permute-start(f32[16,24,128]{2,1,0:T(8,128)S(1)} %get-tuple-element.61), channel_id=1, source_target_pairs={{0,128},{128,256},{256,384},{384,0},{1,129},{129,257},{257,385},{3... | collective-permute-start | bytes 589832 | tf_op jit(solution)/shard_map/ppermute | solution.py:365
  134.9 10.7 %collective-permute-start.12 = (f32[16,24,128]{2,1,0:T(8,128)S(1)}, f32[16,24,128]{2,1,0:T(8,128)S(1)}, u32[]{:S(2)}, u32[]{:S(2)}) collective-permute-start(f32[16,24,128]{2,1,0:T(8,128)S(1)} %get-tuple-element.62), channel_id=1, source_target_pairs={{0,256},{128,384},{256,0},{384,128},{1,257},{129,385},{257,1},{385... | collective-permute-start | bytes 589832 | tf_op jit(solution)/shard_map/ppermute | solution.py:365
  138.6 9.7 %collective-permute-start.11 = (f32[16,24,128]{2,1,0:T(8,128)S(1)}, f32[16,24,128]{2,1,0:T(8,128)S(1)}, u32[]{:S(2)}, u32[]{:S(2)}) collective-permute-start(f32[16,24,128]{2,1,0:T(8,128)S(1)} %get-tuple-element.63), channel_id=1, source_target_pairs={{0,384},{128,0},{256,128},{384,256},{1,385},{129,1},{257,129},{385... | collective-permute-start | bytes 589832 | tf_op jit(solution)/shard_map/ppermute | solution.py:365
  142.5 5.8 %copy-start.12 = (f32[16,24,128]{2,1,0:T(8,128)}, f32[16,24,128]{2,1,0:T(8,128)S(1)}, u32[]{:S(2)}) copy-start(f32[16,24,128]{2,1,0:T(8,128)S(1)} %collective-permute-done.13.refs_3_) | copy-start | bytes 589828
  145.5 2.8 %copy-start.13 = (f32[16,24,128]{2,1,0:T(8,128)}, f32[16,24,128]{2,1,0:T(8,128)S(1)}, u32[]{:S(2)}) copy-start(f32[16,24,128]{2,1,0:T(8,128)S(1)} %collective-permute-done.12.refs_2_) | copy-start | bytes 589828
  148.3 0.8 copy-start
  179.7 32.2 %all-to-all-start.6 = ((f32[8,144,128]{2,1,0:T(8,128)}), f32[8,144,128]{2,1,0:T(8,128)S(1)}, u32[]{:S(2)}, u32[]{:S(2)}) async-start(f32[8,144,128]{2,1,0:T(8,128)} %shard_map.112), calls=%async_computation.6 | async-start | bytes 1179648 | tf_op jit(solution)/shard_map/all_to_all | solution.py:356
  192.9 11.0 %copy-start.16 = (f32[384,128]{1,0:T(8,128)S(1)}, f32[384,128]{1,0:T(8,128)}, u32[]{:S(2)}) copy-start(f32[384,128]{1,0:T(8,128)} %get-tuple-element.58) | copy-start | bytes 589828
  195.4 11.0 %collective-permute-start.6 = (f32[192,128]{1,0:T(8,128)}, f32[192,128]{1,0:T(8,128)S(1)}, u32[]{:S(2)}, u32[]{:S(2)}) collective-permute-start(f32[192,128]{1,0:T(8,128)} %get-tuple-element.45), channel_id=1, source_target_pairs={{0,1},{1,2},{2,3},{3,0},{4,5},{5,6},{6,7},{7,4},{8,9},{9,10},{10,1... | collective-permute-start | bytes 294920 | tf_op jit(solution)/shard_map/ppermute | solution.py:365
  197.7 8.7 %collective-permute-start.7 = (f32[192,128]{1,0:T(8,128)}, f32[192,128]{1,0:T(8,128)S(1)}, u32[]{:S(2)}, u32[]{:S(2)}) collective-permute-start(f32[192,128]{1,0:T(8,128)} %get-tuple-element.46), channel_id=1, source_target_pairs={{0,2},{1,3},{2,0},{3,1},{4,6},{5,7},{6,4},{7,5},{8,10},{9,11},{10,... | collective-permute-start | bytes 294920 | tf_op jit(solution)/shard_map/ppermute | solution.py:365
  201.4 5.9 %collective-permute-start.8 = (f32[192,128]{1,0:T(8,128)}, f32[192,128]{1,0:T(8,128)S(1)}, u32[]{:S(2)}, u32[]{:S(2)}) collective-permute-start(f32[192,128]{1,0:T(8,128)} %get-tuple-element.47), channel_id=1, source_target_pairs={{0,3},{1,0},{2,1},{3,2},{4,7},{5,4},{6,5},{7,6},{8,11},{9,8},{10,9... | collective-permute-start | bytes 294920 | tf_op jit(solution)/shard_map/ppermute | solution.py:365
  203.9 4.9 %collective-permute-start.14 = (f32[384,128]{1,0:T(8,128)S(1)}, f32[384,128]{1,0:T(8,128)S(1)}, u32[]{:S(2)}, u32[]{:S(2)}) collective-permute-start(f32[384,128]{1,0:T(8,128)S(1)} %copy-done.16), channel_id=1, source_target_pairs={{0,4},{4,0},{1,5},{5,1},{2,6},{6,2},{3,7},{7,3},{8,12},{12,8},{9,1... | collective-permute-start | bytes 589832 | tf_op jit(solution)/shard_map/ppermute | solution.py:365
  211.9 0.8 copy-start.5
  (5 other events, 3.5 us)

commit v4 on v3

--- a/solution.py
+++ b/solution.py
@@ -101,7 +101,14 @@
             mid_ref[i, MID_ROWS * j : MID_ROWS * (j + 1), :] = mid
 
 
-def query_body(count, base, q_ref, w_ref, cot_ref, far_ref, mid_ref, near_ref):
+def query_body(count, base, q_ref, w_ref, own_ref, one_ref, two_ref, three_ref, *outs):
+    far_ref, mid_ref, near_ref, cot_ref = outs
+    columns = own_ref.shape[0]
+    heads = cot_ref.shape[0] // columns
+    group = base[0] // LOCAL_HEADS
+    for k, ref in enumerate((own_ref, one_ref, two_ref, three_ref)):
+        at = pl.multiple_of(columns * ((group + heads - k) % heads), columns)
+        cot_ref[pl.ds(at, columns), :] = ref[...]
     live = iota((HEAD, TOKENS), 1) < count[0]
     grads = dot3(w_ref[...], cot_ref[...], 1, 0)
     for j in range(LOCAL_HEADS):
@@ -270,56 +277,13 @@
         )
 
 
-def mid_keys_body(both_ref, q_ref, *refs):
-    for j in range(LOCAL_HEADS):
-        wide_keys(both_ref[j], q_ref[j], refs, j)
-
-
-def keys_body(far_both, near_both, qf_ref, qn_ref, *outs):
-    for j in range(LOCAL_HEADS):
+def keys_body(far_both, mid_both, near_both, qf_ref, qm_ref, qn_ref, *outs):
+    for j in range(LOCAL_HEADS):
+        wide_keys(mid_both[j], qm_ref[j], outs[2:4], j)
         wide_keys(far_both[j], qf_ref[j], outs[:2], j)
         sums = dot3(near_both[j], split_queries(qn_ref[j]), 0, 0)
-        for i, ref in enumerate(outs[2:]):
+        for i, ref in enumerate(outs[4:]):
             ref[head_slice(j, TOKENS), :] = sums[TOKENS * i : TOKENS * (i + 1)]
-
-
-def total_of(ref):
-    total = ref[0]
-    for i in range(1, ref.shape[0]):
-        total = total + ref[i]
-    return total
-
-
-def mid_join_body(keep_ref, got_ref, weight_ref, out_ref):
-    weight = total_of(weight_ref)
-    depth = weight.shape[0] // out_ref.shape[0]
-    for i in range(out_ref.shape[0]):
-        out_ref[i, :MID_BLOCK, :] = keep_ref[i] + got_ref[i]
-        out_ref[i, MID_BLOCK:, :] = weight[depth * i : depth * (i + 1)]
-
-
-def far_join_body(mid_ref, *refs):
-    out_ref = refs[-1]
-    weight = mid_ref[0, MID_BLOCK:, :]
-    for i in range(1, mid_ref.shape[0]):
-        weight = weight + mid_ref[i, MID_BLOCK:, :]
-    for i in range(out_ref.shape[0]):
-        total = refs[0][i]
-        for ref in refs[1:-1]:
-            total = total + ref[i]
-        out_ref[i, :FAR_BLOCK, :] = total
-        out_ref[i, FAR_BLOCK:, :] = weight
-
-
-def weight_join_body(far_ref, out_ref):
-    lines = out_ref.shape[1] // (far_ref.shape[1] - FAR_BLOCK)
-    depth = out_ref.shape[1] // lines
-    for i in range(lines):
-        total = far_ref[i, FAR_BLOCK:, :]
-        for at in range(i + lines, far_ref.shape[0], lines):
-            total = total + far_ref[at, FAR_BLOCK:, :]
-        for to in range(out_ref.shape[0]):
-            out_ref[to, depth * i : depth * (i + 1), :] = total
 
 
 def finish_body(base, far_ref, mid_ref, near_ref, other_ref, dk_ref, dv_ref):
@@ -345,13 +309,6 @@
         dv_ref[HEAD * j : HEAD * (j + 1), :] = turned[HEAD:]
 
 
-def weight_order_body(in_ref, out_ref):
-    rows = out_ref.shape[0]
-    every = in_ref[...].reshape(in_ref.shape[0] * in_ref.shape[1], 128)
-    for b in range(out_ref.shape[1] // 128):
-        out_ref[:, 128 * b : 128 * b + 128] = every[rows * b : rows * (b + 1)]
-
-
 def exchange(pieces, axis):
     return lax.all_to_all(pieces, axis, 0, 0, tiled=True)
 
@@ -366,12 +323,12 @@
 
 
 def on_device(queries, keys, values, counts, out_weight, cotangent):
-    ny, nz, _, nzl = (lax.axis_size(axis) for axis in ("y", Z, "zh", "zl"))
+    ny, nz, nzh, nzl = (lax.axis_size(axis) for axis in ("y", Z, "zh", "zl"))
     heads = lax.axis_size("h")
     columns, tokens = queries.shape
     base = (lax.axis_index("h") * LOCAL_HEADS).astype(jnp.int32).reshape(1)
 
-    full_cot = to_all(cotangent, "h").reshape(heads * columns, tokens)
+    cots = [cotangent] + [shifted(cotangent, "h", k % heads) for k in range(1, 4)]
     far_out, mid_out, near_own = kernel_call(
         pack_body,
         (shaped(nz, FAR_BLOCK, 128), shaped(nzl, MID_BLOCK, 128), shaped(NEAR_BLOCK, 128)),
@@ -380,14 +337,15 @@
     )
     near_other = shifted(near_own, "c", 1)
     far_line = exchange(far_out, Z)
-    query_far, query_mid, query_near = kernel_call(
+    query_far, query_mid, query_near, full_cot = kernel_call(
         query_body,
         (
             shaped(LOCAL_HEADS, FAR_ROWS, 128),
             shaped(LOCAL_HEADS, MID_ROWS, 128),
             shaped(LOCAL_HEADS, TOKENS, 128),
+            shaped(heads * columns, tokens),
         ),
-        (counts, base, queries, out_weight, full_cot),
+        (counts, base, queries, out_weight, *cots),
         2,
     )
     near_both, near_stats = kernel_call(
@@ -440,29 +398,30 @@
     )
     planes = 2 * ny
     weight_parts = exchange(weight.reshape(planes, -1, 128), ("y", "c"))
-    mid_keep, mid_send = kernel_call(
-        mid_keys_body, (shaped(nzl, MID_BLOCK, 128),) * 2, (mid_both, query_mid), 0
+    far_keep, far_send, mid_keep, mid_send, near_keep, near_send = kernel_call(
+        keys_body,
+        (shaped(ny * nz, FAR_BLOCK, 128),) * 2
+        + (shaped(nzl, MID_BLOCK, 128),) * 2
+        + (shaped(NEAR_BLOCK, 128),) * 2,
+        (far_both, mid_both, near_both, query_far, query_mid, query_near),
+        0,
     )
     mid_got = shifted(mid_send, "c", 1)
-    depth = weight.shape[0] // (planes * nzl)
-    mid_join = kernel_call(
-        mid_join_body, shaped(nzl, MID_BLOCK + depth, 128), (mid_keep, mid_got, weight_parts), 0
-    )
-    mid_sums = exchange(mid_join, "zl")
-    far_keep, far_send, near_keep, near_send = kernel_call(
-        keys_body,
-        (shaped(ny * nz, FAR_BLOCK, 128),) * 2 + (shaped(NEAR_BLOCK, 128),) * 2,
-        (far_both, near_both, query_far, query_near),
-        0,
-    )
+    weight_line = jnp.sum(weight_parts, axis=0).reshape(nzl, -1, 128)
+    mid_sums = exchange(jnp.concatenate([mid_keep + mid_got, weight_line], axis=1), "zl")
     far_got = shifted(far_send, "c", 1)
     near_got = shifted(near_send, "c", 1)
     pieces = [far_keep[nz * k : nz * (k + 1)] + far_got[nz * k : nz * (k + 1)] for k in range(ny)]
     pieces = pieces[:1] + [shifted(pieces[k], "y", -k) for k in range(1, ny)]
-    far_join = kernel_call(
-        far_join_body, shaped(nz, FAR_BLOCK + depth, 128), (mid_sums, *pieces), 0
-    )
-    parts = exchange(far_join, Z)
+    far_total = sum(pieces[1:], pieces[0])
+    weight_own = jnp.sum(mid_sums[:, MID_BLOCK:], axis=0)
+    depth = weight_own.shape[0]
+    parts = exchange(
+        jnp.concatenate(
+            [far_total, jnp.broadcast_to(weight_own, (nz, depth, 128))], axis=1
+        ),
+        Z,
+    )
     terms = kernel_call(
         terms_body,
         (shaped(columns, tokens),) * 4 + (shaped(heads * columns, tokens),),
@@ -471,10 +430,13 @@
     )
     got = [terms[0]] + [shifted(terms[k], "h", k % heads) for k in range(1, 4)]
     output = sum(got[1:], got[0])
-    weight_rows = exchange(
-        kernel_call(weight_join_body, shaped(planes, nzl * depth, 128), (parts,), 0), ("y", "c")
-    )
-    weight_grad = kernel_call(weight_order_body, shaped(*out_weight.shape), (weight_rows,), 0)
+    weight_whole = jnp.sum(parts[:, FAR_BLOCK:].reshape(nzh, nzl, depth, 128), axis=0)
+    weight_rows = to_all(weight_whole.reshape(nzl * depth, 128), ("y", "c"))
+    weight_grad = (
+        weight_rows.reshape(out_weight.shape[1] // 128, out_weight.shape[0], 128)
+        .swapaxes(0, 1)
+        .reshape(out_weight.shape)
+    )
     key_grad, value_grad = kernel_call(
         finish_body,
         (shaped(columns, tokens), shaped(columns, tokens)),

time: 217 us -> 211 us (0.972)
  starting transfers between devices: 83.1 us -> 92.9 us
  Pallas kernels: 38.1 us -> 28.4 us
  waiting for transfers between devices: 26.4 us -> 19.7 us
    ppermute x15 -> x18, starting transfers between devices: 47.5 us -> 60.7 us  [shifted(): return lax.ppermute(x, axis, [(i, (i + apart) % size) for i in range(size)])]
    pallas_call x13 -> x8, Pallas kernels: 38.1 us -> 28.4 us  [kernel_call(): pl.pallas_call(body, out_shape=out_shape, in_specs=in_specs, out_specs=ja...]
    all_to_all x5 -> x4, waiting for transfers between devices: 9.54 us -> 0.98 us  [exchange(): return lax.all_to_all(pieces, axis, 0, 0, tiled=True)]
    all_to_all x5 -> x4, starting transfers between devices: 35.6 us -> 32.2 us  [exchange(): return lax.all_to_all(pieces, axis, 0, 0, tiled=True)]
    ppermute x15 -> x18, waiting for transfers between devices: 16.9 us -> 18.7 us  [shifted(): return lax.ppermute(x, axis, [(i, (i + apart) % size) for i in range(size)])]
    unnamed x37 -> x35, local copies, waits for them, and re-layouts: 6.28 us -> 5.14 us
  transfers between devices with their start and end apart: 20 -> 22, of which waited for: 9 -> 9; matrix products, arithmetic and copies ran while one was open for 2% -> 1% of each run, Pallas kernels for 9% -> 9%
where the time goes in v4:
time: 211 us; the launch traced here: 209 us
  starting transfers between devices  92.9 us (44%)
  blocking collectives  55.8 us (26%)
  Pallas kernels  28.4 us (13%)
  waiting for transfers between devices  19.7 us (9%)
  local copies, waits for them, and re-layouts  6.9 us (3%)
  other arithmetic  3.62 us (2%)
    ppermute x18, starting transfers between devices, shifted(): return lax.ppermute(x, axis, [(i, (i + apart) % size) for i in range(size)])  60.7 us
    all_to_all x2, blocking collectives, exchange(): return lax.all_to_all(pieces, axis, 0, 0, tiled=True)  55.8 us
    all_to_all x4, starting transfers between devices, exchange(): return lax.all_to_all(pieces, axis, 0, 0, tiled=True)  32.2 us
    pallas_call x8, Pallas kernels, kernel_call(): pl.pallas_call(body, out_shape=out_shape, in_specs=in_specs, out_specs=ja...  28.4 us
    ppermute x18, waiting for transfers between devices, shifted(): return lax.ppermute(x, axis, [(i, (i + apart) % size) for i in range(size)])  18.7 us
    unnamed x35, local copies, waits for them, and re-layouts  5.14 us
  transfers between devices with their start and end apart: 22, of which 9 were waited for; matrix products, arithmetic and copies ran while one was open for 1% of the time, Pallas kernels for 9%

profile of v4, /device:TPU:1, one launch (start us, length us, event | category | flops | bytes accessed | tf_op | source)
XLA Modules:
  0.0 209.0 jit_solution(1933070237235586204)
XLA Ops:
  1.3 2.3 %shard_map.102 = (f32[16,24,128]{2,1,0:T(8,128)}, f32[8,96,128]{2,1,0:T(8,128)}, f32[384,128]{1,0:T(8,128)}) custom-call(s32[1]{0:T(128)S(6)} %copy.18.count.refs_0_, s32[1]{0:T(128)} %bitcast.base.refs_1_, f32[192,128]{1,0:T(8,128)} %k_ref.1, f32[192,128]{1,0:T(8,128)} %v_ref.1), custom_call_target="tpu_custom_call" | custom-call | tf_op jit(solution)/shard_map/pallas_call | solution.py:73
  3.6 28.2 %all_to_all.30 = f32[16,24,128]{2,1,0:T(8,128)S(1)} all-to-all(f32[16,24,128]{2,1,0:T(8,128)} %get-tuple-element.39), channel_id=1, replica_groups=mesh['y'=4,'zh'=2,'zl'=8,'c'=2,'h'=4] {'zh','zl'}, dimensions={0} | all-to-all | bytes 393216 | tf_op jit(solution)/shard_map/all_to_all | solution.py:313
  31.9 8.8 %all-to-all-start = ((f32[8,96,128]{2,1,0:T(8,128)}), f32[8,96,128]{2,1,0:T(8,128)S(1)}, u32[]{:S(2)}, u32[]{:S(2)}) async-start(f32[8,96,128]{2,1,0:T(8,128)} %get-tuple-element.36), calls=%async_computation | async-start | bytes 786432 | tf_op jit(solution)/shard_map/all_to_all | solution.py:313
  40.6 3.2 %collective-permute-start.5 = (f32[16,24,128]{2,1,0:T(8,128)S(1)}, f32[16,24,128]{2,1,0:T(8,128)S(1)}, u32[]{:S(2)}, u32[]{:S(2)}) collective-permute-start(f32[16,24,128]{2,1,0:T(8,128)S(1)} %all_to_all.30), channel_id=1, source_target_pairs={{0,128},{128,256},{256,384},{384,0},{1,129},{129,257},{257,385},{3... | collective-permute-start | bytes 589832 | tf_op jit(solution)/shard_map/ppermute | solution.py:322
  43.8 3.4 %collective-permute-start.7 = (f32[16,24,128]{2,1,0:T(8,128)S(1)}, f32[16,24,128]{2,1,0:T(8,128)S(1)}, u32[]{:S(2)}, u32[]{:S(2)}) collective-permute-start(f32[16,24,128]{2,1,0:T(8,128)S(1)} %all_to_all.30), channel_id=1, source_target_pairs={{0,384},{128,0},{256,128},{384,256},{1,385},{129,1},{257,129},{385... | collective-permute-start | bytes 589832 | tf_op jit(solution)/shard_map/ppermute | solution.py:322
  47.2 3.5 %collective-permute-start.6 = (f32[16,24,128]{2,1,0:T(8,128)S(1)}, f32[16,24,128]{2,1,0:T(8,128)S(1)}, u32[]{:S(2)}, u32[]{:S(2)}) collective-permute-start(f32[16,24,128]{2,1,0:T(8,128)S(1)} %all_to_all.30), channel_id=1, source_target_pairs={{0,256},{128,384},{256,0},{384,128},{1,257},{129,385},{257,1},{385... | collective-permute-start | bytes 589832 | tf_op jit(solution)/shard_map/ppermute | solution.py:322
  50.8 4.8 %collective-permute-done.6 = f32[16,24,128]{2,1,0:T(8,128)S(1)} collective-permute-done((f32[16,24,128]{2,1,0:T(8,128)S(1)}, f32[16,24,128]{2,1,0:T(8,128)S(1)}, u32[]{:S(2)}, u32[]{:S(2)}) %collective-permute-start.6) | collective-permute-done | bytes 196640 | tf_op jit(solution)/shard_map/ppermute | solution.py:322
  55.7 4.3 %collective-permute-start.8 = (f32[64,24,128]{2,1,0:T(8,128)S(1)}, f32[64,24,128]{2,1,0:T(8,128)S(1)}, u32[]{:S(2)}, u32[]{:S(2)}) collective-permute-start(f32[64,24,128]{2,1,0:T(8,128)S(1)} %constant_dynamic-update-slice_fusion.far_own.refs_12_), channel_id=1, source_target_pairs={{0,4},{4,0},{1,5},{5,1},{2,6},{6,2},{3,7},{7,3},{8,12},{12,8},{9,1... | collective-permute-start | bytes 2359304 | tf_op jit(solution)/shard_map/ppermute | solution.py:322
  60.1 6.5 %collective-permute-start.4 = (f32[8,96,128]{2,1,0:T(8,128)S(1)}, f32[8,96,128]{2,1,0:T(8,128)S(1)}, u32[]{:S(2)}, u32[]{:S(2)}) collective-permute-start(f32[8,96,128]{2,1,0:T(8,128)S(1)} %all-to-all-done.refs_5_), channel_id=1, source_target_pairs={{0,4},{4,0},{1,5},{5,1},{2,6},{6,2},{3,7},{7,3},{8,12},{12,8},{9,1... | collective-permute-start | bytes 1179656 | tf_op jit(solution)/shard_map/ppermute | solution.py:322
  66.6 4.7 %collective-permute-start.1 = (f32[192,128]{1,0:T(8,128)S(1)}, f32[192,128]{1,0:T(8,128)S(1)}, u32[]{:S(2)}, u32[]{:S(2)}) collective-permute-start(f32[192,128]{1,0:T(8,128)S(1)} %copy-done.10), channel_id=1, source_target_pairs={{0,2},{1,3},{2,0},{3,1},{4,6},{5,7},{6,4},{7,5},{8,10},{9,11},{10,... | collective-permute-start | bytes 294920 | tf_op jit(solution)/shard_map/ppermute | solution.py:322
  71.3 2.2 %collective-permute-start.3 = (f32[384,128]{1,0:T(8,128)S(1)}, f32[384,128]{1,0:T(8,128)S(1)}, u32[]{:S(2)}, u32[]{:S(2)}) collective-permute-start(f32[384,128]{1,0:T(8,128)S(1)} %copy-done.5), channel_id=1, source_target_pairs={{0,4},{4,0},{1,5},{5,1},{2,6},{6,2},{3,7},{7,3},{8,12},{12,8},{9,1... | collective-permute-start | bytes 589832 | tf_op jit(solution)/shard_map/ppermute | solution.py:322
  73.5 2.2 %collective-permute-start = (f32[192,128]{1,0:T(8,128)S(1)}, f32[192,128]{1,0:T(8,128)S(1)}, u32[]{:S(2)}, u32[]{:S(2)}) collective-permute-start(f32[192,128]{1,0:T(8,128)S(1)} %copy-done.10), channel_id=1, source_target_pairs={{0,1},{1,2},{2,3},{3,0},{4,5},{5,6},{6,7},{7,4},{8,9},{9,10},{10,1... | collective-permute-start | bytes 294920 | tf_op jit(solution)/shard_map/ppermute | solution.py:322
  75.7 4.3 %collective-permute-start.2 = (f32[192,128]{1,0:T(8,128)S(1)}, f32[192,128]{1,0:T(8,128)S(1)}, u32[]{:S(2)}, u32[]{:S(2)}) collective-permute-start(f32[192,128]{1,0:T(8,128)S(1)} %copy-done.10), channel_id=1, source_target_pairs={{0,3},{1,0},{2,1},{3,2},{4,7},{5,4},{6,5},{7,6},{8,11},{9,8},{10,9... | collective-permute-start | bytes 294920 | tf_op jit(solution)/shard_map/ppermute | solution.py:322
  82.3 2.8 %shard_map.101 = (f32[3,8,128]{2,1,0:T(8,128)}, f32[3,32,128]{2,1,0:T(8,128)}, f32[3,128,128]{2,1,0:T(8,128)}, f32[768,128]{1,0:T(8,128)}) custom-call(s32[1]{0:T(128)S(6)} %copy.18.count.refs_0_, s32[1]{0:T(128)} %bitcast.base.refs_1_, f32[192,128]{1,0:T(8,128)} %q_ref.1, f32[192,768]{1,0:T(8,128)} %w_ref.3, f32[192,128]{1,0:T(8,128)} %own_ref.1, ...), custom_call_target="tpu_custom_call" | custom-call | tf_op jit(solution)/shard_map/pallas_call | solution.py:73
  85.7 2.7 %shard_map.104 = (f32[3,256,256]{2,1,0:T(8,128)}, f32[3,128,128]{2,1,0:T(8,128)}) custom-call(f32[3,128,128]{2,1,0:T(8,128)} %get-tuple-element.42.q_ref.qn_ref, f32[384,128]{1,0:T(8,128)} %get-tuple-element.35.near_own.refs_3_, f32[384,128]{1,0:T(8,128)} %copy-done.6), custom_call_target="tpu_custom_call" | custom-call | tf_op jit(solution)/shard_map/pallas_call | solution.py:73
  89.3 3.1 %shard_map.103 = (f32[3,16,1024]{2,1,0:T(8,128)}, f32[3,8,128]{2,1,0:T(8,128)}) custom-call(f32[3,8,128]{2,1,0:T(8,128)} %get-tuple-element.38.q_ref.qf_ref, f32[64,24,128]{2,1,0:T(8,128)} %copy-done, f32[64,24,128]{2,1,0:T(8,128)} %copy-done.1), custom_call_target="tpu_custom_call" | custom-call | tf_op jit(solution)/shard_map/pallas_call | solution.py:73
  93.2 8.3 %shard_map.105 = (f32[192,128]{1,0:T(8,128)}, f32[192,128]{1,0:T(8,128)}, f32[1152,128]{1,0:T(8,128)}, f32[3,16,1024]{2,1,0:T(8,128)}, f32[3,64,512]{2,1,0:T(8,128)}, /*index=5*/f32[3,256,256]{2,1,0:T(8,128)}) custom-call(s32[1]{0:T(128)S(6)} %copy.18.count.refs_0_, s32[1]{0:T(128)} %bitcast.base.refs_1_, f32[3,32,128]{2,1,0:T(8,128)} %get-tuple-element.34.refs_2_.qm_ref, ...), custom_call_target="tpu_custom_call" | custom-call | tf_op jit(solution)/shard_map/pallas_call | solution.py:73
  101.4 5.9 %all-to-all-start.2 = ((f32[8,144,128]{2,1,0:T(8,128)}), f32[8,144,128]{2,1,0:T(8,128)S(1)}, u32[]{:S(2)}, u32[]{:S(2)}) async-start(f32[8,144,128]{2,1,0:T(8,128)} %bitcast.12), calls=%async_computation.2 | async-start | bytes 1179648 | tf_op jit(solution)/shard_map/all_to_all | solution.py:313
  107.3 4.2 %shard_map.107 = (f32[64,24,128]{2,1,0:T(8,128)}, f32[64,24,128]{2,1,0:T(8,128)}, f32[8,96,128]{2,1,0:T(8,128)}, f32[8,96,128]{2,1,0:T(8,128)}, f32[384,128]{1,0:T(8,128)}, /*index=5*/f32[384,128]{1,0:T(8,128)}) custom-call(f32[3,16,1024]{2,1,0:T(8,128)} %get-tuple-element.51.far_both, f32[3,64,512]{2,1,0:T(8,128)} %get-tuple-element.52.mid_both, ...), custom_call_target="tpu_custom_call" | custom-call | tf_op jit(solution)/shard_map/pallas_call | solution.py:73
  118.2 4.3 %all-to-all-start.3 = ((f32[8,114,128]{2,1,0:T(8,128)}), f32[8,114,128]{2,1,0:T(8,128)S(1)}, u32[]{:S(2)}, u32[]{:S(2)}) async-start(f32[8,114,128]{2,1,0:T(8,128)} %pad_maximum_fusion), calls=%async_computation.3 | async-start | bytes 983040 | tf_op jit(solution)/shard_map/all_to_all | solution.py:313
  122.5 3.2 %collective-permute-start.12 = (f32[64,24,128]{2,1,0:T(8,128)S(1)}, f32[64,24,128]{2,1,0:T(8,128)S(1)}, u32[]{:S(2)}, u32[]{:S(2)}) collective-permute-start(f32[64,24,128]{2,1,0:T(8,128)S(1)} %copy-done.14), channel_id=1, source_target_pairs={{0,4},{4,0},{1,5},{5,1},{2,6},{6,2},{3,7},{7,3},{8,12},{12,8},{9,1... | collective-permute-start | bytes 2359304 | tf_op jit(solution)/shard_map/ppermute | solution.py:322
  127.6 2.9 %collective-permute-start.13 = (f32[16,24,128]{2,1,0:T(8,128)S(1)}, f32[16,24,128]{2,1,0:T(8,128)S(1)}, u32[]{:S(2)}, u32[]{:S(2)}) collective-permute-start(f32[16,24,128]{2,1,0:T(8,128)S(1)} %get-tuple-element.63), channel_id=1, source_target_pairs={{0,384},{128,0},{256,128},{384,256},{1,385},{129,1},{257,129},{385... | collective-permute-start | bytes 589832 | tf_op jit(solution)/shard_map/ppermute | solution.py:322
  130.6 2.3 %collective-permute-start.15 = (f32[16,24,128]{2,1,0:T(8,128)S(1)}, f32[16,24,128]{2,1,0:T(8,128)S(1)}, u32[]{:S(2)}, u32[]{:S(2)}) collective-permute-start(f32[16,24,128]{2,1,0:T(8,128)S(1)} %get-tuple-element.64), channel_id=1, source_target_pairs={{0,128},{128,256},{256,384},{384,0},{1,129},{129,257},{257,385},{3... | collective-permute-start | bytes 589832 | tf_op jit(solution)/shard_map/ppermute | solution.py:322
  132.9 3.2 %collective-permute-start.14 = (f32[16,24,128]{2,1,0:T(8,128)S(1)}, f32[16,24,128]{2,1,0:T(8,128)S(1)}, u32[]{:S(2)}, u32[]{:S(2)}) collective-permute-start(f32[16,24,128]{2,1,0:T(8,128)S(1)} %get-tuple-element.65), channel_id=1, source_target_pairs={{0,256},{128,384},{256,0},{384,128},{1,257},{129,385},{257,1},{385... | collective-permute-start | bytes 589832 | tf_op jit(solution)/shard_map/ppermute | solution.py:322
  136.2 3.8 %collective-permute-done.15 = f32[16,24,128]{2,1,0:T(8,128)S(1)} collective-permute-done((f32[16,24,128]{2,1,0:T(8,128)S(1)}, f32[16,24,128]{2,1,0:T(8,128)S(1)}, u32[]{:S(2)}, u32[]{:S(2)}) %collective-permute-start.15) | collective-permute-done | bytes 196640 | tf_op jit(solution)/shard_map/ppermute | solution.py:322
  139.9 3.2 %collective-permute-done.14 = f32[16,24,128]{2,1,0:T(8,128)S(1)} collective-permute-done((f32[16,24,128]{2,1,0:T(8,128)S(1)}, f32[16,24,128]{2,1,0:T(8,128)S(1)}, u32[]{:S(2)}, u32[]{:S(2)}) %collective-permute-start.14) | collective-permute-done | bytes 196640 | tf_op jit(solution)/shard_map/ppermute | solution.py:322
  144.0 27.5 %all_to_all.31.far_ref = f32[16,42,128]{2,1,0:T(8,128)S(1)} all-to-all(f32[16,42,128]{2,1,0:T(8,128)S(1)} %pad_maximum_fusion.1), channel_id=1, replica_groups=mesh['y'=4,'zh'=2,'zl'=8,'c'=2,'h'=4] {'zh','zl'}, dimensions={0} | all-to-all | bytes 688128 | tf_op jit(solution)/shard_map/all_to_all | solution.py:313
  173.2 13.3 %all-to-all-start.5 = ((f32[8,144,128]{2,1,0:T(8,128)}), f32[8,144,128]{2,1,0:T(8,128)S(1)}, u32[]{:S(2)}, u32[]{:S(2)}) async-start(f32[8,144,128]{2,1,0:T(8,128)} %broadcast_in_dim.7), calls=%async_computation.5 | async-start | bytes 1179648 | tf_op jit(solution)/shard_map/all_to_all | solution.py:313
  186.5 2.6 %shard_map.106 = (f32[192,128]{1,0:T(8,128)}, f32[192,128]{1,0:T(8,128)}, f32[192,128]{1,0:T(8,128)}, f32[192,128]{1,0:T(8,128)}, f32[768,128]{1,0:T(8,128)}) custom-call(s32[1]{0:T(128)} %bitcast.base.refs_1_, f32[192,128]{1,0:T(8,128)} %get-tuple-element.45.attended_ref, f32[192,768]{1,0:T(8,128)} %w_ref.3), custom_call_target="tpu_custom_call" | custom-call | tf_op jit(solution)/shard_map/pallas_call | solution.py:73
  191.0 6.5 %collective-permute-start.10 = (f32[192,128]{1,0:T(8,128)}, f32[192,128]{1,0:T(8,128)S(1)}, u32[]{:S(2)}, u32[]{:S(2)}) collective-permute-start(f32[192,128]{1,0:T(8,128)} %get-tuple-element.48), channel_id=1, source_target_pairs={{0,2},{1,3},{2,0},{3,1},{4,6},{5,7},{6,4},{7,5},{8,10},{9,11},{10,... | collective-permute-start | bytes 294920 | tf_op jit(solution)/shard_map/ppermute | solution.py:322
  199.5 2.5 %collective-permute-start.17 = (f32[384,128]{1,0:T(8,128)S(1)}, f32[384,128]{1,0:T(8,128)S(1)}, u32[]{:S(2)}, u32[]{:S(2)}) collective-permute-start(f32[384,128]{1,0:T(8,128)S(1)} %copy-done.15), channel_id=1, source_target_pairs={{0,4},{4,0},{1,5},{5,1},{2,6},{6,2},{3,7},{7,3},{8,12},{12,8},{9,1... | collective-permute-start | bytes 589832 | tf_op jit(solution)/shard_map/ppermute | solution.py:322
  205.7 2.5 %shard_map.108 = (f32[192,128]{1,0:T(8,128)}, f32[192,128]{1,0:T(8,128)}) custom-call(s32[1]{0:T(128)} %bitcast.base.refs_1_, f32[16,42,128]{2,1,0:T(8,128)} %copy-done.2, f32[8,114,128]{2,1,0:T(8,128)} %copy-done.3, f32[384,128]{1,0:T(8,128)} %get-tuple-element.59.near_ref, f32[384,128]{1,0:T(8,128)} %copy-done.9), custom_call_target="tpu_custom_call" | custom-call | tf_op jit(solution)/shard_map/pallas_call | solution.py:73
  (73 shorter events, 24.1 us)
Async XLA Ops:
  31.9 28.2 %all-to-all-start = ((f32[8,96,128]{2,1,0:T(8,128)}), f32[8,96,128]{2,1,0:T(8,128)S(1)}, u32[]{:S(2)}, u32[]{:S(2)}) async-start(f32[8,96,128]{2,1,0:T(8,128)} %get-tuple-element.36), calls=%async_computation | async-start | bytes 786432 | tf_op jit(solution)/shard_map/all_to_all | solution.py:313
  40.6 10.1 %collective-permute-start.5 = (f32[16,24,128]{2,1,0:T(8,128)S(1)}, f32[16,24,128]{2,1,0:T(8,128)S(1)}, u32[]{:S(2)}, u32[]{:S(2)}) collective-permute-start(f32[16,24,128]{2,1,0:T(8,128)S(1)} %all_to_all.30), channel_id=1, source_target_pairs={{0,128},{128,256},{256,384},{384,0},{1,129},{129,257},{257,385},{3... | collective-permute-start | bytes 589832 | tf_op jit(solution)/shard_map/ppermute | solution.py:322
  43.8 11.8 %collective-permute-start.7 = (f32[16,24,128]{2,1,0:T(8,128)S(1)}, f32[16,24,128]{2,1,0:T(8,128)S(1)}, u32[]{:S(2)}, u32[]{:S(2)}) collective-permute-start(f32[16,24,128]{2,1,0:T(8,128)S(1)} %all_to_all.30), channel_id=1, source_target_pairs={{0,384},{128,0},{256,128},{384,256},{1,385},{129,1},{257,129},{385... | collective-permute-start | bytes 589832 | tf_op jit(solution)/shard_map/ppermute | solution.py:322
  47.2 8.4 %collective-permute-start.6 = (f32[16,24,128]{2,1,0:T(8,128)S(1)}, f32[16,24,128]{2,1,0:T(8,128)S(1)}, u32[]{:S(2)}, u32[]{:S(2)}) collective-permute-start(f32[16,24,128]{2,1,0:T(8,128)S(1)} %all_to_all.30), channel_id=1, source_target_pairs={{0,256},{128,384},{256,0},{384,128},{1,257},{129,385},{257,1},{385... | collective-permute-start | bytes 589832 | tf_op jit(solution)/shard_map/ppermute | solution.py:322
  55.6 11.0 %copy-start.10 = (f32[192,128]{1,0:T(8,128)S(1)}, f32[192,128]{1,0:T(8,128)}, u32[]{:S(2)}) copy-start(f32[192,128]{1,0:T(8,128)} %own_ref.1) | copy-start | bytes 294916
  55.6 15.6 %copy-start.5 = (f32[384,128]{1,0:T(8,128)S(1)}, f32[384,128]{1,0:T(8,128)}, u32[]{:S(2)}) copy-start(f32[384,128]{1,0:T(8,128)} %get-tuple-element.35.near_own.refs_3_) | copy-start | bytes 589828
  55.7 32.8 %copy-start = (f32[64,24,128]{2,1,0:T(8,128)}, f32[64,24,128]{2,1,0:T(8,128)S(1)}, u32[]{:S(2)}) copy-start(f32[64,24,128]{2,1,0:T(8,128)S(1)} %constant_dynamic-update-slice_fusion.far_own.refs_12_) | copy-start | bytes 2359300
  55.7 32.7 %collective-permute-start.8 = (f32[64,24,128]{2,1,0:T(8,128)S(1)}, f32[64,24,128]{2,1,0:T(8,128)S(1)}, u32[]{:S(2)}, u32[]{:S(2)}) collective-permute-start(f32[64,24,128]{2,1,0:T(8,128)S(1)} %constant_dynamic-update-slice_fusion.far_own.refs_12_), channel_id=1, source_target_pairs={{0,4},{4,0},{1,5},{5,1},{2,6},{6,2},{3,7},{7,3},{8,12},{12,8},{9,1... | collective-permute-start | bytes 2359304 | tf_op jit(solution)/shard_map/ppermute | solution.py:322
  60.0 32.4 %copy-start.4 = (f32[8,96,128]{2,1,0:T(8,128)}, f32[8,96,128]{2,1,0:T(8,128)S(1)}, u32[]{:S(2)}) copy-start(f32[8,96,128]{2,1,0:T(8,128)S(1)} %all-to-all-done.refs_5_) | copy-start | bytes 1179652
  60.1 32.3 %collective-permute-start.4 = (f32[8,96,128]{2,1,0:T(8,128)S(1)}, f32[8,96,128]{2,1,0:T(8,128)S(1)}, u32[]{:S(2)}, u32[]{:S(2)}) collective-permute-start(f32[8,96,128]{2,1,0:T(8,128)S(1)} %all-to-all-done.refs_5_), channel_id=1, source_target_pairs={{0,4},{4,0},{1,5},{5,1},{2,6},{6,2},{3,7},{7,3},{8,12},{12,8},{9,1... | collective-permute-start | bytes 1179656 | tf_op jit(solution)/shard_map/ppermute | solution.py:322
  66.6 9.1 %collective-permute-start.1 = (f32[192,128]{1,0:T(8,128)S(1)}, f32[192,128]{1,0:T(8,128)S(1)}, u32[]{:S(2)}, u32[]{:S(2)}) collective-permute-start(f32[192,128]{1,0:T(8,128)S(1)} %copy-done.10), channel_id=1, source_target_pairs={{0,2},{1,3},{2,0},{3,1},{4,6},{5,7},{6,4},{7,5},{8,10},{9,11},{10,... | collective-permute-start | bytes 294920 | tf_op jit(solution)/shard_map/ppermute | solution.py:322
  71.3 13.8 %collective-permute-start.3 = (f32[384,128]{1,0:T(8,128)S(1)}, f32[384,128]{1,0:T(8,128)S(1)}, u32[]{:S(2)}, u32[]{:S(2)}) collective-permute-start(f32[384,128]{1,0:T(8,128)S(1)} %copy-done.5), channel_id=1, source_target_pairs={{0,4},{4,0},{1,5},{5,1},{2,6},{6,2},{3,7},{7,3},{8,12},{12,8},{9,1... | collective-permute-start | bytes 589832 | tf_op jit(solution)/shard_map/ppermute | solution.py:322
  73.5 7.2 %collective-permute-start = (f32[192,128]{1,0:T(8,128)S(1)}, f32[192,128]{1,0:T(8,128)S(1)}, u32[]{:S(2)}, u32[]{:S(2)}) collective-permute-start(f32[192,128]{1,0:T(8,128)S(1)} %copy-done.10), channel_id=1, source_target_pairs={{0,1},{1,2},{2,3},{3,0},{4,5},{5,6},{6,7},{7,4},{8,9},{9,10},{10,1... | collective-permute-start | bytes 294920 | tf_op jit(solution)/shard_map/ppermute | solution.py:322
  75.7 5.9 %copy-start.11 = (f32[192,128]{1,0:T(8,128)}, f32[192,128]{1,0:T(8,128)S(1)}, u32[]{:S(2)}) copy-start(f32[192,128]{1,0:T(8,128)S(1)} %collective-permute-done.1.two_ref) | copy-start | bytes 294916
  75.7 5.9 %collective-permute-start.2 = (f32[192,128]{1,0:T(8,128)S(1)}, f32[192,128]{1,0:T(8,128)S(1)}, u32[]{:S(2)}, u32[]{:S(2)}) collective-permute-start(f32[192,128]{1,0:T(8,128)S(1)} %copy-done.10), channel_id=1, source_target_pairs={{0,3},{1,0},{2,1},{3,2},{4,7},{5,4},{6,5},{7,6},{8,11},{9,8},{10,9... | collective-permute-start | bytes 294920 | tf_op jit(solution)/shard_map/ppermute | solution.py:322
  80.7 0.9 copy-start.12
  88.4 0.9 copy-start.1
  101.4 15.9 %all-to-all-start.2 = ((f32[8,144,128]{2,1,0:T(8,128)}), f32[8,144,128]{2,1,0:T(8,128)S(1)}, u32[]{:S(2)}, u32[]{:S(2)}) async-start(f32[8,144,128]{2,1,0:T(8,128)} %bitcast.12), calls=%async_computation.2 | async-start | bytes 1179648 | tf_op jit(solution)/shard_map/all_to_all | solution.py:313
  111.5 3.8 %collective-permute-start.16 = (f32[8,96,128]{2,1,0:T(8,128)}, f32[8,96,128]{2,1,0:T(8,128)S(1)}, u32[]{:S(2)}, u32[]{:S(2)}) collective-permute-start(f32[8,96,128]{2,1,0:T(8,128)} %get-tuple-element.57), channel_id=1, source_target_pairs={{0,4},{4,0},{1,5},{5,1},{2,6},{6,2},{3,7},{7,3},{8,12},{12,8},{9,1... | collective-permute-start | bytes 1179656 | tf_op jit(solution)/shard_map/ppermute | solution.py:322
  117.4 5.1 %copy-start.14 = (f32[64,24,128]{2,1,0:T(8,128)S(1)}, f32[64,24,128]{2,1,0:T(8,128)}, u32[]{:S(2)}) copy-start(f32[64,24,128]{2,1,0:T(8,128)} %get-tuple-element.55) | copy-start | bytes 2359300
  117.4 10.2 %copy-start.7 = (f32[64,24,128]{2,1,0:T(8,128)S(1)}, f32[64,24,128]{2,1,0:T(8,128)}, u32[]{:S(2)}) copy-start(f32[64,24,128]{2,1,0:T(8,128)} %get-tuple-element.54) | copy-start | bytes 2359300
  118.2 25.0 %all-to-all-start.3 = ((f32[8,114,128]{2,1,0:T(8,128)}), f32[8,114,128]{2,1,0:T(8,128)S(1)}, u32[]{:S(2)}, u32[]{:S(2)}) async-start(f32[8,114,128]{2,1,0:T(8,128)} %pad_maximum_fusion), calls=%async_computation.3 | async-start | bytes 983040 | tf_op jit(solution)/shard_map/all_to_all | solution.py:313
  122.5 5.1 %collective-permute-start.12 = (f32[64,24,128]{2,1,0:T(8,128)S(1)}, f32[64,24,128]{2,1,0:T(8,128)S(1)}, u32[]{:S(2)}, u32[]{:S(2)}) collective-permute-start(f32[64,24,128]{2,1,0:T(8,128)S(1)} %copy-done.14), channel_id=1, source_target_pairs={{0,4},{4,0},{1,5},{5,1},{2,6},{6,2},{3,7},{7,3},{8,12},{12,8},{9,1... | collective-permute-start | bytes 2359304 | tf_op jit(solution)/shard_map/ppermute | solution.py:322
  127.6 8.5 %collective-permute-start.13 = (f32[16,24,128]{2,1,0:T(8,128)S(1)}, f32[16,24,128]{2,1,0:T(8,128)S(1)}, u32[]{:S(2)}, u32[]{:S(2)}) collective-permute-start(f32[16,24,128]{2,1,0:T(8,128)S(1)} %get-tuple-element.63), channel_id=1, source_target_pairs={{0,384},{128,0},{256,128},{384,256},{1,385},{129,1},{257,129},{385... | collective-permute-start | bytes 589832 | tf_op jit(solution)/shard_map/ppermute | solution.py:322
  130.6 9.4 %collective-permute-start.15 = (f32[16,24,128]{2,1,0:T(8,128)S(1)}, f32[16,24,128]{2,1,0:T(8,128)S(1)}, u32[]{:S(2)}, u32[]{:S(2)}) collective-permute-start(f32[16,24,128]{2,1,0:T(8,128)S(1)} %get-tuple-element.64), channel_id=1, source_target_pairs={{0,128},{128,256},{256,384},{384,0},{1,129},{129,257},{257,385},{3... | collective-permute-start | bytes 589832 | tf_op jit(solution)/shard_map/ppermute | solution.py:322
  132.9 10.3 %collective-permute-start.14 = (f32[16,24,128]{2,1,0:T(8,128)S(1)}, f32[16,24,128]{2,1,0:T(8,128)S(1)}, u32[]{:S(2)}, u32[]{:S(2)}) collective-permute-start(f32[16,24,128]{2,1,0:T(8,128)S(1)} %get-tuple-element.65), channel_id=1, source_target_pairs={{0,256},{128,384},{256,0},{384,128},{1,257},{129,385},{257,1},{385... | collective-permute-start | bytes 589832 | tf_op jit(solution)/shard_map/ppermute | solution.py:322
  173.2 34.9 %all-to-all-start.5 = ((f32[8,144,128]{2,1,0:T(8,128)}), f32[8,144,128]{2,1,0:T(8,128)S(1)}, u32[]{:S(2)}, u32[]{:S(2)}) async-start(f32[8,144,128]{2,1,0:T(8,128)} %broadcast_in_dim.7), calls=%async_computation.5 | async-start | bytes 1179648 | tf_op jit(solution)/shard_map/all_to_all | solution.py:313
  186.5 12.9 %copy-start.15 = (f32[384,128]{1,0:T(8,128)S(1)}, f32[384,128]{1,0:T(8,128)}, u32[]{:S(2)}) copy-start(f32[384,128]{1,0:T(8,128)} %get-tuple-element.60) | copy-start | bytes 589828
  189.1 12.8 %collective-permute-start.9 = (f32[192,128]{1,0:T(8,128)}, f32[192,128]{1,0:T(8,128)S(1)}, u32[]{:S(2)}, u32[]{:S(2)}) collective-permute-start(f32[192,128]{1,0:T(8,128)} %get-tuple-element.47), channel_id=1, source_target_pairs={{0,1},{1,2},{2,3},{3,0},{4,5},{5,6},{6,7},{7,4},{8,9},{9,10},{10,1... | collective-permute-start | bytes 294920 | tf_op jit(solution)/shard_map/ppermute | solution.py:322
  191.0 10.9 %collective-permute-start.10 = (f32[192,128]{1,0:T(8,128)}, f32[192,128]{1,0:T(8,128)S(1)}, u32[]{:S(2)}, u32[]{:S(2)}) collective-permute-start(f32[192,128]{1,0:T(8,128)} %get-tuple-element.48), channel_id=1, source_target_pairs={{0,2},{1,3},{2,0},{3,1},{4,6},{5,7},{6,4},{7,5},{8,10},{9,11},{10,... | collective-permute-start | bytes 294920 | tf_op jit(solution)/shard_map/ppermute | solution.py:322
  197.5 5.9 %collective-permute-start.11 = (f32[192,128]{1,0:T(8,128)}, f32[192,128]{1,0:T(8,128)S(1)}, u32[]{:S(2)}, u32[]{:S(2)}) collective-permute-start(f32[192,128]{1,0:T(8,128)} %get-tuple-element.49), channel_id=1, source_target_pairs={{0,3},{1,0},{2,1},{3,2},{4,7},{5,4},{6,5},{7,6},{8,11},{9,8},{10,9... | collective-permute-start | bytes 294920 | tf_op jit(solution)/shard_map/ppermute | solution.py:322
  199.5 5.5 %collective-permute-start.17 = (f32[384,128]{1,0:T(8,128)S(1)}, f32[384,128]{1,0:T(8,128)S(1)}, u32[]{:S(2)}, u32[]{:S(2)}) collective-permute-start(f32[384,128]{1,0:T(8,128)S(1)} %copy-done.15), channel_id=1, source_target_pairs={{0,4},{4,0},{1,5},{5,1},{2,6},{6,2},{3,7},{7,3},{8,12},{12,8},{9,1... | collective-permute-start | bytes 589832 | tf_op jit(solution)/shard_map/ppermute | solution.py:322
  (6 other events, 4.3 us)

commit v5 on v4

--- a/solution.py
+++ b/solution.py
@@ -25,48 +25,51 @@
 Z = ("zh", "zl")
 
 
-def dot(a, b, ca, cb):
-    return lax.dot_general(
-        a,
-        b,
-        (((ca,), (cb,)), ((), ())),
-        precision=lax.Precision.HIGHEST,
-        preferred_element_type=jnp.float32,
-    )
-
-
 def halves(x):
     high = x.astype(jnp.bfloat16)
     return high, (x - high.astype(jnp.float32)).astype(jnp.bfloat16)
 
 
+def product(a, b, ca, cb):
+    return lax.dot_general(
+        a, b, (((ca,), (cb,)), ((), ())), preferred_element_type=jnp.float32
+    )
+
+
 def dot3(a, b, ca, cb):
     a_high, a_low = halves(a)
     b_high, b_low = halves(b)
-
-    def one(x, y):
-        return lax.dot_general(
-            x, y, (((ca,), (cb,)), ((), ())), preferred_element_type=jnp.float32
-        )
-
-    return one(a_low, b_high) + one(a_high, b_low) + one(a_high, b_high)
+    if ca == 1:
+        rows = a.shape[0]
+        both = product(jnp.concatenate([a_high, a_low], axis=0), b_high, ca, cb)
+        return both[rows:] + product(a_high, b_low, ca, cb) + both[:rows]
+    return product(a_low, b_high, ca, cb) + product(a_high, b_low, ca, cb) + product(a_high, b_high, ca, cb)
+
+
+def outer3(a, b):
+    a_high, a_low = halves(a)
+    b_high, b_low = halves(b)
+    return product(
+        jnp.concatenate([a_low, a_high, a_high], axis=0),
+        jnp.concatenate([b_high, b_low, b_high], axis=0),
+        0,
+        0,
+    )
 
 
 def iota(shape, dim):
     return lax.broadcasted_iota(jnp.int32, shape, dim)
 
 
-def chooser(rows, spacing, offset):
-    shape = (rows, TOKENS)
-    return (iota(shape, 1) == iota(shape, 0) * spacing + offset).astype(jnp.float32)
-
-
-def placer(rows, spacing, offset):
-    shape = (TOKENS, rows)
-    return (iota(shape, 0) == iota(shape, 1) * spacing + offset).astype(jnp.float32)
-
-
-def kernel_call(body, out_shape, operands, scalars):
+def far_rows(j, head):
+    return pl.ds(TOKENS * j + head % SPACING_WIDE, FAR_ROWS, stride=SPACING_WIDE)
+
+
+def mid_rows(j, head):
+    return pl.ds(TOKENS * j + head % SPACING_CENTRAL, MID_ROWS, stride=SPACING_CENTRAL)
+
+
+def kernel_call(body, out_shape, operands, scalars, scratch=()):
     in_specs = [pl.BlockSpec(memory_space=pltpu.SMEM)] * scalars + [
         pl.BlockSpec(memory_space=pltpu.VMEM)
     ] * (len(operands) - scalars)
@@ -75,6 +78,7 @@
         out_shape=out_shape,
         in_specs=in_specs,
         out_specs=jax.tree.map(lambda _: pl.BlockSpec(memory_space=pltpu.VMEM), out_shape),
+        scratch_shapes=[pltpu.VMEM(dims, jnp.float32) for dims in scratch],
         interpret=INTERPRET,
     )(*operands)
 
@@ -92,9 +96,10 @@
         both = jnp.where(live, both, jnp.where(feature == 0, DEAD_MARK, 0.0))
         turned = both.T
         near_ref[TOKENS * j : TOKENS * (j + 1), :] = turned
+    for j in range(LOCAL_HEADS):
         head = base[0] + j
-        far = dot(chooser(FAR_ROWS, SPACING_WIDE, head % SPACING_WIDE), turned, 1, 0)
-        mid = dot(chooser(MID_ROWS, SPACING_CENTRAL, head % SPACING_CENTRAL), turned, 1, 0)
+        far = near_ref[far_rows(j, head), :]
+        mid = near_ref[mid_rows(j, head), :]
         for i in range(far_ref.shape[0]):
             far_ref[i, FAR_ROWS * j : FAR_ROWS * (j + 1), :] = far
         for i in range(mid_ref.shape[0]):
@@ -117,12 +122,11 @@
             [q_ref[rows, :] * SCALE, jnp.where(live, grads[rows, :], 0.0)], axis=0
         )
         turned = both.T
+        near_ref[TOKENS * j : TOKENS * (j + 1), :] = turned
+    for j in range(LOCAL_HEADS):
         head = base[0] + j
-        near_ref[j] = turned
-        far_ref[j] = dot(chooser(FAR_ROWS, SPACING_WIDE, head % SPACING_WIDE), turned, 1, 0)
-        mid_ref[j] = dot(
-            chooser(MID_ROWS, SPACING_CENTRAL, head % SPACING_CENTRAL), turned, 1, 0
-        )
+        far_ref[head_slice(j, FAR_ROWS), :] = near_ref[far_rows(j, head), :]
+        mid_ref[head_slice(j, MID_ROWS), :] = near_ref[mid_rows(j, head), :]
 
 
 def split_queries(turned):
@@ -132,7 +136,7 @@
 
 def branch_scores(turned, pairs):
     rows = turned.shape[0]
-    mark = ((iota((8, 2 * HEAD), 0) == 0) & (iota((8, 2 * HEAD), 1) == 0)).astype(jnp.float32)
+    mark = ((iota((16, 2 * HEAD), 0) == 0) & (iota((16, 2 * HEAD), 1) == 0)).astype(jnp.float32)
     products = dot3(jnp.concatenate([split_queries(turned), mark], axis=0), pairs, 1, 1)
     dead = products[2 * rows : 2 * rows + 1, :] > DEAD_LEVEL
     scores = jnp.where(dead, MASKED_SCORE, products[:rows])
@@ -179,13 +183,13 @@
 def near_scores_body(q_ref, near_own, near_other, both_ref, stats_ref):
     for j in range(LOCAL_HEADS):
         pairs = near_pairs_of(near_own, near_other, j)
-        both_ref[j], stats_ref[j] = branch_scores(q_ref[j], pairs)
+        both_ref[j], stats_ref[j] = branch_scores(q_ref[head_slice(j, TOKENS), :], pairs)
 
 
 def far_scores_body(q_ref, far_own, far_other, both_ref, stats_ref):
     for j in range(LOCAL_HEADS):
         pairs = gathered((far_own, far_other), head_slice(j, FAR_ROWS))
-        both_ref[j], stats_ref[j] = branch_scores(q_ref[j], pairs)
+        both_ref[j], stats_ref[j] = branch_scores(q_ref[head_slice(j, FAR_ROWS), :], pairs)
 
 
 def attention_body(*refs):
@@ -193,65 +197,62 @@
     qm_ref, near_own, near_other, mid_own, mid_other, cot_ref = refs[2:8]
     far_in, far_stats_ref, near_in, near_stats_ref = refs[8:12]
     far_refs = refs[12:14]
-    dq_ref, attended_ref, weight_ref, far_both, mid_both, near_both = refs[14:]
+    dq_ref, attended_ref, weight_ref, far_both, mid_both, near_both = refs[14:20]
+    far_put, mid_put, back_ref, side_ref = refs[20:]
+    each = range(LOCAL_HEADS)
     lanes = iota((TOKENS, 128), 1)
-    position = iota((TOKENS, 1), 0)
-    attended = []
-    for j in range(LOCAL_HEADS):
-        head = base[0] + j
-        far_off = head % SPACING_WIDE
-        mid_off = head % SPACING_CENTRAL
-        mid_pairs = gathered((mid_own, mid_other), head_slice(j, MID_ROWS))
-        mid_start, mid_column = branch_scores(qm_ref[j], mid_pairs)
-        far_put = placer(FAR_ROWS, SPACING_WIDE, far_off)
-        mid_put = placer(MID_ROWS, SPACING_CENTRAL, mid_off)
-        far_stats = dot(far_put, far_stats_ref[j], 1, 0)
-        mid_stats = dot(mid_put, mid_column, 1, 0)
+    filler = jnp.where(lanes == 0, MASKED_SCORE, 0.0)
+    mid_pairs = [gathered((mid_own, mid_other), head_slice(j, MID_ROWS)) for j in each]
+    for j in each:
+        far_put[head_slice(j, TOKENS), :] = filler
+        mid_put[head_slice(j, TOKENS), :] = filler
+    starts = [branch_scores(qm_ref[head_slice(j, MID_ROWS), :], mid_pairs[j]) for j in each]
+    for j in each:
+        far_put[far_rows(j, base[0] + j), :] = far_stats_ref[j]
+        mid_put[mid_rows(j, base[0] + j), :] = starts[j][1]
+    factors = []
+    for j in each:
+        far_stats = far_put[head_slice(j, TOKENS), :]
+        mid_stats = mid_put[head_slice(j, TOKENS), :]
         near_stats = near_stats_ref[j]
-        in_far = position % SPACING_WIDE == far_off
-        in_mid = position % SPACING_CENTRAL == mid_off
-        far_top = jnp.where(in_far, far_stats[:, 0:1], MASKED_SCORE)
-        mid_top = jnp.where(in_mid, mid_stats[:, 0:1], MASKED_SCORE)
-        near_top = near_stats[:, 0:1]
+        far_top, mid_top, near_top = far_stats[:, 0:1], mid_stats[:, 0:1], near_stats[:, 0:1]
         top = jnp.maximum(near_top, jnp.maximum(mid_top, far_top))
         far_factor = jnp.exp(far_top - top)
         mid_factor = jnp.exp(mid_top - top)
         near_factor = jnp.exp(near_top - top)
-        total = (
-            near_factor * near_stats[:, 1:2]
-            + mid_factor * mid_stats[:, 1:2]
-            + far_factor * far_stats[:, 1:2]
+        sums = near_factor * near_stats + mid_factor * mid_stats + far_factor * far_stats
+        total = sums[:, 1:2]
+        delta = sums[:, 2:3] / total
+        near_factor = near_factor / total
+        back_ref[head_slice(j, TOKENS), :] = jnp.where(
+            lanes == 0, far_factor / total, jnp.where(lanes == 1, mid_factor / total, delta)
         )
-        far_factor = far_factor / total
-        mid_factor = mid_factor / total
-        near_factor = near_factor / total
-        delta = (
-            near_factor * near_stats[:, 2:3]
-            + mid_factor * mid_stats[:, 2:3]
-            + far_factor * far_stats[:, 2:3]
+        factors.append((near_factor, delta))
+    for j in each:
+        far_back = back_ref[far_rows(j, base[0] + j), :]
+        mid_back = back_ref[mid_rows(j, base[0] + j), :]
+        near_both[j] = branch_grads(near_in[j], *factors[j])
+        mid_both[j] = branch_grads(starts[j][0], mid_back[:, 1:2], mid_back[:, 2:3])
+        far_both[j] = branch_grads(far_in[j], far_back[:, 0:1], far_back[:, 2:3])
+    for j in each:
+        side_ref[head_slice(j, TOKENS), :] = query_side(
+            near_both[j], near_pairs_of(near_own, near_other, j)
         )
-        back = jnp.where(lanes == 0, far_factor, jnp.where(lanes == 1, mid_factor, delta))
-        far_back = dot(chooser(FAR_ROWS, SPACING_WIDE, far_off), back, 1, 0)
-        mid_back = dot(chooser(MID_ROWS, SPACING_CENTRAL, mid_off), back, 1, 0)
-        near = branch_grads(near_in[j], near_factor, delta)
-        mid = branch_grads(mid_start, mid_back[:, 1:2], mid_back[:, 2:3])
-        far = branch_grads(far_in[j], far_back[:, 0:1], far_back[:, 2:3])
-        far_both[j] = far
-        mid_both[j] = mid
-        near_both[j] = near
-        side = (
-            query_side(near, near_pairs_of(near_own, near_other, j))
-            + dot(mid_put, query_side(mid, mid_pairs), 1, 0)
-            + dot(far_put, query_side(far, gathered(far_refs, head_slice(j, FAR_ROWS))), 1, 0)
-        )
-        turned = side.T
-        dq_ref[HEAD * j : HEAD * (j + 1), :] = turned[:HEAD] * SCALE
-        attended.append(turned[HEAD:])
-    live = iota((HEAD * LOCAL_HEADS, TOKENS), 1) < count[0]
-    rows = jnp.where(live, jnp.concatenate(attended, axis=0), 0.0)
-    attended_ref[...] = rows
-    columns = rows.shape[0]
-    weight = dot3(rows, cot_ref[...], 1, 1)
+    mid_sides = [query_side(mid_both[j], mid_pairs[j]) for j in each]
+    far_sides = [query_side(far_both[j], gathered(far_refs, head_slice(j, FAR_ROWS))) for j in each]
+    for j in each:
+        at = mid_rows(j, base[0] + j)
+        side_ref[at, :] = side_ref[at, :] + mid_sides[j]
+    for j in each:
+        at = far_rows(j, base[0] + j)
+        side_ref[at, :] = side_ref[at, :] + far_sides[j]
+    live = iota((HEAD, TOKENS), 1) < count[0]
+    for j in each:
+        turned = side_ref[head_slice(j, TOKENS), :].T
+        dq_ref[head_slice(j, HEAD), :] = turned[:HEAD] * SCALE
+        attended_ref[head_slice(j, HEAD), :] = jnp.where(live, turned[HEAD:], 0.0)
+    columns = attended_ref.shape[0]
+    weight = dot3(attended_ref[...], cot_ref[...], 1, 1)
     for b in range(weight.shape[1] // 128):
         weight_ref[columns * b : columns * (b + 1), :] = weight[:, 128 * b : 128 * b + 128]
 
@@ -268,7 +269,7 @@
 
 
 def wide_keys(both, turned, refs, j):
-    sums = dot3(both, split_queries(turned), 0, 0)
+    sums = outer3(both, split_queries(turned))
     rows = turned.shape[0]
     half = sums.shape[0] // 2
     for i, ref in enumerate(refs):
@@ -279,34 +280,31 @@
 
 def keys_body(far_both, mid_both, near_both, qf_ref, qm_ref, qn_ref, *outs):
     for j in range(LOCAL_HEADS):
-        wide_keys(mid_both[j], qm_ref[j], outs[2:4], j)
-        wide_keys(far_both[j], qf_ref[j], outs[:2], j)
-        sums = dot3(near_both[j], split_queries(qn_ref[j]), 0, 0)
+        wide_keys(mid_both[j], qm_ref[head_slice(j, MID_ROWS), :], outs[2:4], j)
+        wide_keys(far_both[j], qf_ref[head_slice(j, FAR_ROWS), :], outs[:2], j)
+        sums = dot3(near_both[j], split_queries(qn_ref[head_slice(j, TOKENS), :]), 0, 0)
         for i, ref in enumerate(outs[4:]):
             ref[head_slice(j, TOKENS), :] = sums[TOKENS * i : TOKENS * (i + 1)]
 
 
-def finish_body(base, far_ref, mid_ref, near_ref, other_ref, dk_ref, dv_ref):
+def finish_body(base, far_ref, mid_ref, near_ref, other_ref, dk_ref, dv_ref, sum_ref):
     far_sum = far_ref[0, :FAR_BLOCK, :]
     for i in range(1, far_ref.shape[0]):
         far_sum = far_sum + far_ref[i, :FAR_BLOCK, :]
     mid_sum = mid_ref[0, :MID_BLOCK, :]
     for i in range(1, mid_ref.shape[0]):
         mid_sum = mid_sum + mid_ref[i, :MID_BLOCK, :]
-    for j in range(LOCAL_HEADS):
-        head = base[0] + j
-        ns = slice(TOKENS * j, TOKENS * (j + 1))
-        far_put = placer(FAR_ROWS, SPACING_WIDE, head % SPACING_WIDE)
-        mid_put = placer(MID_ROWS, SPACING_CENTRAL, head % SPACING_CENTRAL)
-        both = (
-            near_ref[ns, :]
-            + other_ref[ns, :]
-            + dot(mid_put, mid_sum[MID_ROWS * j : MID_ROWS * (j + 1)], 1, 0)
-            + dot(far_put, far_sum[FAR_ROWS * j : FAR_ROWS * (j + 1)], 1, 0)
-        )
-        turned = both.T
-        dk_ref[HEAD * j : HEAD * (j + 1), :] = turned[:HEAD]
-        dv_ref[HEAD * j : HEAD * (j + 1), :] = turned[HEAD:]
+    sum_ref[...] = near_ref[...] + other_ref[...]
+    for j in range(LOCAL_HEADS):
+        at = mid_rows(j, base[0] + j)
+        sum_ref[at, :] = sum_ref[at, :] + mid_sum[head_slice(j, MID_ROWS)]
+    for j in range(LOCAL_HEADS):
+        at = far_rows(j, base[0] + j)
+        sum_ref[at, :] = sum_ref[at, :] + far_sum[head_slice(j, FAR_ROWS)]
+    for j in range(LOCAL_HEADS):
+        turned = sum_ref[head_slice(j, TOKENS), :].T
+        dk_ref[head_slice(j, HEAD), :] = turned[:HEAD]
+        dv_ref[head_slice(j, HEAD), :] = turned[HEAD:]
 
 
 def exchange(pieces, axis):
@@ -340,9 +338,9 @@
     query_far, query_mid, query_near, full_cot = kernel_call(
         query_body,
         (
-            shaped(LOCAL_HEADS, FAR_ROWS, 128),
-            shaped(LOCAL_HEADS, MID_ROWS, 128),
-            shaped(LOCAL_HEADS, TOKENS, 128),
+            shaped(FAR_BLOCK, 128),
+            shaped(MID_BLOCK, 128),
+            shaped(NEAR_BLOCK, 128),
             shaped(heads * columns, tokens),
         ),
         (counts, base, queries, out_weight, *cots),
@@ -395,6 +393,7 @@
             far_other,
         ),
         2,
+        ((NEAR_BLOCK, 128),) * 4,
     )
     planes = 2 * ny
     weight_parts = exchange(weight.reshape(planes, -1, 128), ("y", "c"))
@@ -424,9 +423,10 @@
     )
     terms = kernel_call(
         terms_body,
-        (shaped(columns, tokens),) * 4 + (shaped(heads * columns, tokens),),
+        (shaped(columns, tokens),) * 4,
         (base, attended, out_weight),
         1,
+        ((heads * columns, tokens),),
     )
     got = [terms[0]] + [shifted(terms[k], "h", k % heads) for k in range(1, 4)]
     output = sum(got[1:], got[0])
@@ -442,6 +442,7 @@
         (shaped(columns, tokens), shaped(columns, tokens)),
         (base, parts, mid_sums, near_keep, near_got),
         1,
+        ((NEAR_BLOCK, 128),),
     )
     return output, query_grad, key_grad, value_grad, weight_grad
 

time: 211 us -> 206 us (0.976)
  Pallas kernels: 28.4 us -> 23.8 us
    pallas_call x8, Pallas kernels: 28.4 us -> 23.8 us  [kernel_call(): pl.pallas_call(body, out_shape=out_shape, in_specs=in_specs, out_specs=ja...]
  transfers between devices with their start and end apart: 22 -> 22, of which waited for: 9 -> 10; matrix products, arithmetic and copies ran while one was open for 1% -> 1% of each run, Pallas kernels for 9% -> 8%
where the time goes in v5:
time: 206 us; the launch traced here: 204 us
  starting transfers between devices  92 us (45%)
  blocking collectives  56.6 us (27%)
  Pallas kernels  23.8 us (12%)
  waiting for transfers between devices  19.4 us (9%)
  local copies, waits for them, and re-layouts  6.91 us (3%)
  other arithmetic  3.62 us (2%)
    ppermute x18, starting transfers between devices, shifted(): return lax.ppermute(x, axis, [(i, (i + apart) % size) for i in range(size)])  60.3 us
    all_to_all x2, blocking collectives, exchange(): return lax.all_to_all(pieces, axis, 0, 0, tiled=True)  56.6 us
    all_to_all x4, starting transfers between devices, exchange(): return lax.all_to_all(pieces, axis, 0, 0, tiled=True)  31.8 us
    pallas_call x8, Pallas kernels, kernel_call(): pl.pallas_call(body, out_shape=out_shape, in_specs=in_specs, out_specs=ja...  23.8 us
    ppermute x18, waiting for transfers between devices, shifted(): return lax.ppermute(x, axis, [(i, (i + apart) % size) for i in range(size)])  17.9 us
    unnamed x35, local copies, waits for them, and re-layouts  5.14 us
  transfers between devices with their start and end apart: 22, of which 10 were waited for; matrix products, arithmetic and copies ran while one was open for 1% of the time, Pallas kernels for 8%

profile of v5, /device:TPU:1, one launch (start us, length us, event | category | flops | bytes accessed | tf_op | source)
XLA Modules:
  0.0 204.1 jit_solution(615914512563458670)
XLA Ops:
  1.3 2.0 shard_map.102
  3.3 28.2 %all_to_all.30 = f32[16,24,128]{2,1,0:T(8,128)S(1)} all-to-all(f32[16,24,128]{2,1,0:T(8,128)} %get-tuple-element.39), channel_id=1, replica_groups=mesh['y'=4,'zh'=2,'zl'=8,'c'=2,'h'=4] {'zh','zl'}, dimensions={0} | all-to-all | bytes 393216 | tf_op jit(solution)/shard_map/all_to_all | solution.py:311
  31.5 8.8 %all-to-all-start = ((f32[8,96,128]{2,1,0:T(8,128)}), f32[8,96,128]{2,1,0:T(8,128)S(1)}, u32[]{:S(2)}, u32[]{:S(2)}) async-start(f32[8,96,128]{2,1,0:T(8,128)} %get-tuple-element.36), calls=%async_computation | async-start | bytes 786432 | tf_op jit(solution)/shard_map/all_to_all | solution.py:311
  40.3 3.2 %collective-permute-start.5 = (f32[16,24,128]{2,1,0:T(8,128)S(1)}, f32[16,24,128]{2,1,0:T(8,128)S(1)}, u32[]{:S(2)}, u32[]{:S(2)}) collective-permute-start(f32[16,24,128]{2,1,0:T(8,128)S(1)} %all_to_all.30), channel_id=1, source_target_pairs={{0,128},{128,256},{256,384},{384,0},{1,129},{129,257},{257,385},{3... | collective-permute-start | bytes 589832 | tf_op jit(solution)/shard_map/ppermute | solution.py:320
  43.5 3.4 %collective-permute-start.7 = (f32[16,24,128]{2,1,0:T(8,128)S(1)}, f32[16,24,128]{2,1,0:T(8,128)S(1)}, u32[]{:S(2)}, u32[]{:S(2)}) collective-permute-start(f32[16,24,128]{2,1,0:T(8,128)S(1)} %all_to_all.30), channel_id=1, source_target_pairs={{0,384},{128,0},{256,128},{384,256},{1,385},{129,1},{257,129},{385... | collective-permute-start | bytes 589832 | tf_op jit(solution)/shard_map/ppermute | solution.py:320
  46.8 3.5 %collective-permute-start.6 = (f32[16,24,128]{2,1,0:T(8,128)S(1)}, f32[16,24,128]{2,1,0:T(8,128)S(1)}, u32[]{:S(2)}, u32[]{:S(2)}) collective-permute-start(f32[16,24,128]{2,1,0:T(8,128)S(1)} %all_to_all.30), channel_id=1, source_target_pairs={{0,256},{128,384},{256,0},{384,128},{1,257},{129,385},{257,1},{385... | collective-permute-start | bytes 589832 | tf_op jit(solution)/shard_map/ppermute | solution.py:320
  50.4 4.8 %collective-permute-done.6 = f32[16,24,128]{2,1,0:T(8,128)S(1)} collective-permute-done((f32[16,24,128]{2,1,0:T(8,128)S(1)}, f32[16,24,128]{2,1,0:T(8,128)S(1)}, u32[]{:S(2)}, u32[]{:S(2)}) %collective-permute-start.6) | collective-permute-done | bytes 196640 | tf_op jit(solution)/shard_map/ppermute | solution.py:320
  55.3 4.3 %collective-permute-start.8 = (f32[64,24,128]{2,1,0:T(8,128)S(1)}, f32[64,24,128]{2,1,0:T(8,128)S(1)}, u32[]{:S(2)}, u32[]{:S(2)}) collective-permute-start(f32[64,24,128]{2,1,0:T(8,128)S(1)} %constant_dynamic-update-slice_fusion.far_own.refs_12_), channel_id=1, source_target_pairs={{0,4},{4,0},{1,5},{5,1},{2,6},{6,2},{3,7},{7,3},{8,12},{12,8},{9,1... | collective-permute-start | bytes 2359304 | tf_op jit(solution)/shard_map/ppermute | solution.py:320
  59.7 6.5 %collective-permute-start.4 = (f32[8,96,128]{2,1,0:T(8,128)S(1)}, f32[8,96,128]{2,1,0:T(8,128)S(1)}, u32[]{:S(2)}, u32[]{:S(2)}) collective-permute-start(f32[8,96,128]{2,1,0:T(8,128)S(1)} %all-to-all-done.refs_5_), channel_id=1, source_target_pairs={{0,4},{4,0},{1,5},{5,1},{2,6},{6,2},{3,7},{7,3},{8,12},{12,8},{9,1... | collective-permute-start | bytes 1179656 | tf_op jit(solution)/shard_map/ppermute | solution.py:320
  66.2 4.7 %collective-permute-start.1 = (f32[192,128]{1,0:T(8,128)S(1)}, f32[192,128]{1,0:T(8,128)S(1)}, u32[]{:S(2)}, u32[]{:S(2)}) collective-permute-start(f32[192,128]{1,0:T(8,128)S(1)} %copy-done.10), channel_id=1, source_target_pairs={{0,2},{1,3},{2,0},{3,1},{4,6},{5,7},{6,4},{7,5},{8,10},{9,11},{10,... | collective-permute-start | bytes 294920 | tf_op jit(solution)/shard_map/ppermute | solution.py:320
  70.9 2.2 %collective-permute-start.3 = (f32[384,128]{1,0:T(8,128)S(1)}, f32[384,128]{1,0:T(8,128)S(1)}, u32[]{:S(2)}, u32[]{:S(2)}) collective-permute-start(f32[384,128]{1,0:T(8,128)S(1)} %copy-done.5), channel_id=1, source_target_pairs={{0,4},{4,0},{1,5},{5,1},{2,6},{6,2},{3,7},{7,3},{8,12},{12,8},{9,1... | collective-permute-start | bytes 589832 | tf_op jit(solution)/shard_map/ppermute | solution.py:320
  73.1 2.2 %collective-permute-start = (f32[192,128]{1,0:T(8,128)S(1)}, f32[192,128]{1,0:T(8,128)S(1)}, u32[]{:S(2)}, u32[]{:S(2)}) collective-permute-start(f32[192,128]{1,0:T(8,128)S(1)} %copy-done.10), channel_id=1, source_target_pairs={{0,1},{1,2},{2,3},{3,0},{4,5},{5,6},{6,7},{7,4},{8,9},{9,10},{10,1... | collective-permute-start | bytes 294920 | tf_op jit(solution)/shard_map/ppermute | solution.py:320
  75.4 4.3 %collective-permute-start.2 = (f32[192,128]{1,0:T(8,128)S(1)}, f32[192,128]{1,0:T(8,128)S(1)}, u32[]{:S(2)}, u32[]{:S(2)}) collective-permute-start(f32[192,128]{1,0:T(8,128)S(1)} %copy-done.10), channel_id=1, source_target_pairs={{0,3},{1,0},{2,1},{3,2},{4,7},{5,4},{6,5},{7,6},{8,11},{9,8},{10,9... | collective-permute-start | bytes 294920 | tf_op jit(solution)/shard_map/ppermute | solution.py:320
  81.9 2.4 %shard_map.101 = (f32[24,128]{1,0:T(8,128)}, f32[96,128]{1,0:T(8,128)}, f32[384,128]{1,0:T(8,128)}, f32[768,128]{1,0:T(8,128)}) custom-call(s32[1]{0:T(128)S(6)} %copy.18.count.refs_0_, s32[1]{0:T(128)} %bitcast.base.refs_1_, f32[192,128]{1,0:T(8,128)} %q_ref.1, f32[192,768]{1,0:T(8,128)} %w_ref.3, f32[192,128]{1,0:T(8,128)} %own_ref.1, ...), custom_call_target="tpu_custom_call" | custom-call | tf_op jit(solution)/shard_map/pallas_call | solution.py:76
  85.1 2.7 %shard_map.104 = (f32[3,256,256]{2,1,0:T(8,128)}, f32[3,128,128]{2,1,0:T(8,128)}) custom-call(f32[384,128]{1,0:T(8,128)} %get-tuple-element.42.q_ref.qn_ref, f32[384,128]{1,0:T(8,128)} %get-tuple-element.35.near_own.refs_3_, f32[384,128]{1,0:T(8,128)} %copy-done.6), custom_call_target="tpu_custom_call" | custom-call | tf_op jit(solution)/shard_map/pallas_call | solution.py:76
  88.7 2.8 %shard_map.103 = (f32[3,16,1024]{2,1,0:T(8,128)}, f32[3,8,128]{2,1,0:T(8,128)}) custom-call(f32[24,128]{1,0:T(8,128)} %get-tuple-element.38.q_ref.qf_ref, f32[64,24,128]{2,1,0:T(8,128)} %copy-done, f32[64,24,128]{2,1,0:T(8,128)} %copy-done.1), custom_call_target="tpu_custom_call" | custom-call | tf_op jit(solution)/shard_map/pallas_call | solution.py:76
  92.2 5.6 %shard_map.105 = (f32[192,128]{1,0:T(8,128)}, f32[192,128]{1,0:T(8,128)}, f32[1152,128]{1,0:T(8,128)}, f32[3,16,1024]{2,1,0:T(8,128)}, f32[3,64,512]{2,1,0:T(8,128)}, /*index=5*/f32[3,256,256]{2,1,0:T(8,128)}) custom-call(s32[1]{0:T(128)S(6)} %copy.18.count.refs_0_, s32[1]{0:T(128)} %bitcast.base.refs_1_, f32[96,128]{1,0:T(8,128)} %get-tuple-element.34.refs_2_.qm_ref, ...), custom_call_target="tpu_custom_call" | custom-call | tf_op jit(solution)/shard_map/pallas_call | solution.py:76
  97.8 5.8 %all-to-all-start.2 = ((f32[8,144,128]{2,1,0:T(8,128)}), f32[8,144,128]{2,1,0:T(8,128)S(1)}, u32[]{:S(2)}, u32[]{:S(2)}) async-start(f32[8,144,128]{2,1,0:T(8,128)} %bitcast.12), calls=%async_computation.2 | async-start | bytes 1179648 | tf_op jit(solution)/shard_map/all_to_all | solution.py:311
  103.6 3.8 %shard_map.107 = (f32[64,24,128]{2,1,0:T(8,128)}, f32[64,24,128]{2,1,0:T(8,128)}, f32[8,96,128]{2,1,0:T(8,128)}, f32[8,96,128]{2,1,0:T(8,128)}, f32[384,128]{1,0:T(8,128)}, /*index=5*/f32[384,128]{1,0:T(8,128)}) custom-call(f32[3,16,1024]{2,1,0:T(8,128)} %get-tuple-element.51.far_both, f32[3,64,512]{2,1,0:T(8,128)} %get-tuple-element.52.mid_both, ...), custom_call_target="tpu_custom_call" | custom-call | tf_op jit(solution)/shard_map/pallas_call | solution.py:76
  114.5 4.3 %all-to-all-start.3 = ((f32[8,114,128]{2,1,0:T(8,128)}), f32[8,114,128]{2,1,0:T(8,128)S(1)}, u32[]{:S(2)}, u32[]{:S(2)}) async-start(f32[8,114,128]{2,1,0:T(8,128)} %pad_maximum_fusion), calls=%async_computation.3 | async-start | bytes 983040 | tf_op jit(solution)/shard_map/all_to_all | solution.py:311
  118.8 3.2 %collective-permute-start.12 = (f32[64,24,128]{2,1,0:T(8,128)S(1)}, f32[64,24,128]{2,1,0:T(8,128)S(1)}, u32[]{:S(2)}, u32[]{:S(2)}) collective-permute-start(f32[64,24,128]{2,1,0:T(8,128)S(1)} %copy-done.14), channel_id=1, source_target_pairs={{0,4},{4,0},{1,5},{5,1},{2,6},{6,2},{3,7},{7,3},{8,12},{12,8},{9,1... | collective-permute-start | bytes 2359304 | tf_op jit(solution)/shard_map/ppermute | solution.py:320
  123.9 2.8 %collective-permute-start.13 = (f32[16,24,128]{2,1,0:T(8,128)S(1)}, f32[16,24,128]{2,1,0:T(8,128)S(1)}, u32[]{:S(2)}, u32[]{:S(2)}) collective-permute-start(f32[16,24,128]{2,1,0:T(8,128)S(1)} %get-tuple-element.63), channel_id=1, source_target_pairs={{0,384},{128,0},{256,128},{384,256},{1,385},{129,1},{257,129},{385... | collective-permute-start | bytes 589832 | tf_op jit(solution)/shard_map/ppermute | solution.py:320
  126.7 2.5 %collective-permute-start.15 = (f32[16,24,128]{2,1,0:T(8,128)S(1)}, f32[16,24,128]{2,1,0:T(8,128)S(1)}, u32[]{:S(2)}, u32[]{:S(2)}) collective-permute-start(f32[16,24,128]{2,1,0:T(8,128)S(1)} %get-tuple-element.64), channel_id=1, source_target_pairs={{0,128},{128,256},{256,384},{384,0},{1,129},{129,257},{257,385},{3... | collective-permute-start | bytes 589832 | tf_op jit(solution)/shard_map/ppermute | solution.py:320
  129.2 2.8 %collective-permute-start.14 = (f32[16,24,128]{2,1,0:T(8,128)S(1)}, f32[16,24,128]{2,1,0:T(8,128)S(1)}, u32[]{:S(2)}, u32[]{:S(2)}) collective-permute-start(f32[16,24,128]{2,1,0:T(8,128)S(1)} %get-tuple-element.65), channel_id=1, source_target_pairs={{0,256},{128,384},{256,0},{384,128},{1,257},{129,385},{257,1},{385... | collective-permute-start | bytes 589832 | tf_op jit(solution)/shard_map/ppermute | solution.py:320
  132.1 3.8 %collective-permute-done.15 = f32[16,24,128]{2,1,0:T(8,128)S(1)} collective-permute-done((f32[16,24,128]{2,1,0:T(8,128)S(1)}, f32[16,24,128]{2,1,0:T(8,128)S(1)}, u32[]{:S(2)}, u32[]{:S(2)}) %collective-permute-start.15) | collective-permute-done | bytes 196640 | tf_op jit(solution)/shard_map/ppermute | solution.py:320
  135.9 2.8 %collective-permute-done.14 = f32[16,24,128]{2,1,0:T(8,128)S(1)} collective-permute-done((f32[16,24,128]{2,1,0:T(8,128)S(1)}, f32[16,24,128]{2,1,0:T(8,128)S(1)}, u32[]{:S(2)}, u32[]{:S(2)}) %collective-permute-start.14) | collective-permute-done | bytes 196640 | tf_op jit(solution)/shard_map/ppermute | solution.py:320
  139.6 28.3 %all_to_all.31.far_ref = f32[16,42,128]{2,1,0:T(8,128)S(1)} all-to-all(f32[16,42,128]{2,1,0:T(8,128)S(1)} %pad_maximum_fusion.1), channel_id=1, replica_groups=mesh['y'=4,'zh'=2,'zl'=8,'c'=2,'h'=4] {'zh','zl'}, dimensions={0} | all-to-all | bytes 688128 | tf_op jit(solution)/shard_map/all_to_all | solution.py:311
  169.5 12.9 %all-to-all-start.5 = ((f32[8,144,128]{2,1,0:T(8,128)}), f32[8,144,128]{2,1,0:T(8,128)S(1)}, u32[]{:S(2)}, u32[]{:S(2)}) async-start(f32[8,144,128]{2,1,0:T(8,128)} %broadcast_in_dim.7), calls=%async_computation.5 | async-start | bytes 1179648 | tf_op jit(solution)/shard_map/all_to_all | solution.py:311
  182.4 2.4 %shard_map.106 = (f32[192,128]{1,0:T(8,128)}, f32[192,128]{1,0:T(8,128)}, f32[192,128]{1,0:T(8,128)}, f32[192,128]{1,0:T(8,128)}) custom-call(s32[1]{0:T(128)} %bitcast.base.refs_1_, f32[192,128]{1,0:T(8,128)} %get-tuple-element.45.attended_ref, f32[192,768]{1,0:T(8,128)} %w_ref.3), custom_call_target="tpu_custom_call" | custom-call | tf_op jit(solution)/shard_map/pallas_call | solution.py:76
  186.8 6.5 %collective-permute-start.10 = (f32[192,128]{1,0:T(8,128)}, f32[192,128]{1,0:T(8,128)S(1)}, u32[]{:S(2)}, u32[]{:S(2)}) collective-permute-start(f32[192,128]{1,0:T(8,128)} %get-tuple-element.48), channel_id=1, source_target_pairs={{0,2},{1,3},{2,0},{3,1},{4,6},{5,7},{6,4},{7,5},{8,10},{9,11},{10,... | collective-permute-start | bytes 294920 | tf_op jit(solution)/shard_map/ppermute | solution.py:320
  195.2 2.5 %collective-permute-start.17 = (f32[384,128]{1,0:T(8,128)S(1)}, f32[384,128]{1,0:T(8,128)S(1)}, u32[]{:S(2)}, u32[]{:S(2)}) collective-permute-start(f32[384,128]{1,0:T(8,128)S(1)} %copy-done.15), channel_id=1, source_target_pairs={{0,4},{4,0},{1,5},{5,1},{2,6},{6,2},{3,7},{7,3},{8,12},{12,8},{9,1... | collective-permute-start | bytes 589832 | tf_op jit(solution)/shard_map/ppermute | solution.py:320
  201.1 2.1 %shard_map.108 = (f32[192,128]{1,0:T(8,128)}, f32[192,128]{1,0:T(8,128)}) custom-call(s32[1]{0:T(128)} %bitcast.base.refs_1_, f32[16,42,128]{2,1,0:T(8,128)} %copy-done.2, f32[8,114,128]{2,1,0:T(8,128)} %copy-done.3, f32[384,128]{1,0:T(8,128)} %get-tuple-element.59.near_ref, f32[384,128]{1,0:T(8,128)} %copy-done.9), custom_call_target="tpu_custom_call" | custom-call | tf_op jit(solution)/shard_map/pallas_call | solution.py:76
  (73 shorter events, 24.3 us)
Async XLA Ops:
  31.5 28.2 %all-to-all-start = ((f32[8,96,128]{2,1,0:T(8,128)}), f32[8,96,128]{2,1,0:T(8,128)S(1)}, u32[]{:S(2)}, u32[]{:S(2)}) async-start(f32[8,96,128]{2,1,0:T(8,128)} %get-tuple-element.36), calls=%async_computation | async-start | bytes 786432 | tf_op jit(solution)/shard_map/all_to_all | solution.py:311
  40.3 10.1 %collective-permute-start.5 = (f32[16,24,128]{2,1,0:T(8,128)S(1)}, f32[16,24,128]{2,1,0:T(8,128)S(1)}, u32[]{:S(2)}, u32[]{:S(2)}) collective-permute-start(f32[16,24,128]{2,1,0:T(8,128)S(1)} %all_to_all.30), channel_id=1, source_target_pairs={{0,128},{128,256},{256,384},{384,0},{1,129},{129,257},{257,385},{3... | collective-permute-start | bytes 589832 | tf_op jit(solution)/shard_map/ppermute | solution.py:320
  43.5 11.8 %collective-permute-start.7 = (f32[16,24,128]{2,1,0:T(8,128)S(1)}, f32[16,24,128]{2,1,0:T(8,128)S(1)}, u32[]{:S(2)}, u32[]{:S(2)}) collective-permute-start(f32[16,24,128]{2,1,0:T(8,128)S(1)} %all_to_all.30), channel_id=1, source_target_pairs={{0,384},{128,0},{256,128},{384,256},{1,385},{129,1},{257,129},{385... | collective-permute-start | bytes 589832 | tf_op jit(solution)/shard_map/ppermute | solution.py:320
  46.8 8.4 %collective-permute-start.6 = (f32[16,24,128]{2,1,0:T(8,128)S(1)}, f32[16,24,128]{2,1,0:T(8,128)S(1)}, u32[]{:S(2)}, u32[]{:S(2)}) collective-permute-start(f32[16,24,128]{2,1,0:T(8,128)S(1)} %all_to_all.30), channel_id=1, source_target_pairs={{0,256},{128,384},{256,0},{384,128},{1,257},{129,385},{257,1},{385... | collective-permute-start | bytes 589832 | tf_op jit(solution)/shard_map/ppermute | solution.py:320
  55.3 11.0 %copy-start.10 = (f32[192,128]{1,0:T(8,128)S(1)}, f32[192,128]{1,0:T(8,128)}, u32[]{:S(2)}) copy-start(f32[192,128]{1,0:T(8,128)} %own_ref.1) | copy-start | bytes 294916
  55.3 15.6 %copy-start.5 = (f32[384,128]{1,0:T(8,128)S(1)}, f32[384,128]{1,0:T(8,128)}, u32[]{:S(2)}) copy-start(f32[384,128]{1,0:T(8,128)} %get-tuple-element.35.near_own.refs_3_) | copy-start | bytes 589828
  55.3 32.4 %copy-start = (f32[64,24,128]{2,1,0:T(8,128)}, f32[64,24,128]{2,1,0:T(8,128)S(1)}, u32[]{:S(2)}) copy-start(f32[64,24,128]{2,1,0:T(8,128)S(1)} %constant_dynamic-update-slice_fusion.far_own.refs_12_) | copy-start | bytes 2359300
  55.3 32.4 %collective-permute-start.8 = (f32[64,24,128]{2,1,0:T(8,128)S(1)}, f32[64,24,128]{2,1,0:T(8,128)S(1)}, u32[]{:S(2)}, u32[]{:S(2)}) collective-permute-start(f32[64,24,128]{2,1,0:T(8,128)S(1)} %constant_dynamic-update-slice_fusion.far_own.refs_12_), channel_id=1, source_target_pairs={{0,4},{4,0},{1,5},{5,1},{2,6},{6,2},{3,7},{7,3},{8,12},{12,8},{9,1... | collective-permute-start | bytes 2359304 | tf_op jit(solution)/shard_map/ppermute | solution.py:320
  59.7 31.8 %copy-start.4 = (f32[8,96,128]{2,1,0:T(8,128)}, f32[8,96,128]{2,1,0:T(8,128)S(1)}, u32[]{:S(2)}) copy-start(f32[8,96,128]{2,1,0:T(8,128)S(1)} %all-to-all-done.refs_5_) | copy-start | bytes 1179652
  59.7 31.8 %collective-permute-start.4 = (f32[8,96,128]{2,1,0:T(8,128)S(1)}, f32[8,96,128]{2,1,0:T(8,128)S(1)}, u32[]{:S(2)}, u32[]{:S(2)}) collective-permute-start(f32[8,96,128]{2,1,0:T(8,128)S(1)} %all-to-all-done.refs_5_), channel_id=1, source_target_pairs={{0,4},{4,0},{1,5},{5,1},{2,6},{6,2},{3,7},{7,3},{8,12},{12,8},{9,1... | collective-permute-start | bytes 1179656 | tf_op jit(solution)/shard_map/ppermute | solution.py:320
  66.2 9.1 %collective-permute-start.1 = (f32[192,128]{1,0:T(8,128)S(1)}, f32[192,128]{1,0:T(8,128)S(1)}, u32[]{:S(2)}, u32[]{:S(2)}) collective-permute-start(f32[192,128]{1,0:T(8,128)S(1)} %copy-done.10), channel_id=1, source_target_pairs={{0,2},{1,3},{2,0},{3,1},{4,6},{5,7},{6,4},{7,5},{8,10},{9,11},{10,... | collective-permute-start | bytes 294920 | tf_op jit(solution)/shard_map/ppermute | solution.py:320
  70.9 13.5 %collective-permute-start.3 = (f32[384,128]{1,0:T(8,128)S(1)}, f32[384,128]{1,0:T(8,128)S(1)}, u32[]{:S(2)}, u32[]{:S(2)}) collective-permute-start(f32[384,128]{1,0:T(8,128)S(1)} %copy-done.5), channel_id=1, source_target_pairs={{0,4},{4,0},{1,5},{5,1},{2,6},{6,2},{3,7},{7,3},{8,12},{12,8},{9,1... | collective-permute-start | bytes 589832 | tf_op jit(solution)/shard_map/ppermute | solution.py:320
  73.1 7.2 %collective-permute-start = (f32[192,128]{1,0:T(8,128)S(1)}, f32[192,128]{1,0:T(8,128)S(1)}, u32[]{:S(2)}, u32[]{:S(2)}) collective-permute-start(f32[192,128]{1,0:T(8,128)S(1)} %copy-done.10), channel_id=1, source_target_pairs={{0,1},{1,2},{2,3},{3,0},{4,5},{5,6},{6,7},{7,4},{8,9},{9,10},{10,1... | collective-permute-start | bytes 294920 | tf_op jit(solution)/shard_map/ppermute | solution.py:320
  75.4 5.9 %copy-start.11 = (f32[192,128]{1,0:T(8,128)}, f32[192,128]{1,0:T(8,128)S(1)}, u32[]{:S(2)}) copy-start(f32[192,128]{1,0:T(8,128)S(1)} %collective-permute-done.1.two_ref) | copy-start | bytes 294916
  75.4 5.9 %collective-permute-start.2 = (f32[192,128]{1,0:T(8,128)S(1)}, f32[192,128]{1,0:T(8,128)S(1)}, u32[]{:S(2)}, u32[]{:S(2)}) collective-permute-start(f32[192,128]{1,0:T(8,128)S(1)} %copy-done.10), channel_id=1, source_target_pairs={{0,3},{1,0},{2,1},{3,2},{4,7},{5,4},{6,5},{7,6},{8,11},{9,8},{10,9... | collective-permute-start | bytes 294920 | tf_op jit(solution)/shard_map/ppermute | solution.py:320
  80.4 0.9 copy-start.12
  87.8 0.9 copy-start.1
  97.8 15.9 %all-to-all-start.2 = ((f32[8,144,128]{2,1,0:T(8,128)}), f32[8,144,128]{2,1,0:T(8,128)S(1)}, u32[]{:S(2)}, u32[]{:S(2)}) async-start(f32[8,144,128]{2,1,0:T(8,128)} %bitcast.12), calls=%async_computation.2 | async-start | bytes 1179648 | tf_op jit(solution)/shard_map/all_to_all | solution.py:311
  107.4 3.8 %collective-permute-start.16 = (f32[8,96,128]{2,1,0:T(8,128)}, f32[8,96,128]{2,1,0:T(8,128)S(1)}, u32[]{:S(2)}, u32[]{:S(2)}) collective-permute-start(f32[8,96,128]{2,1,0:T(8,128)} %get-tuple-element.57), channel_id=1, source_target_pairs={{0,4},{4,0},{1,5},{5,1},{2,6},{6,2},{3,7},{7,3},{8,12},{12,8},{9,1... | collective-permute-start | bytes 1179656 | tf_op jit(solution)/shard_map/ppermute | solution.py:320
  113.7 5.1 %copy-start.14 = (f32[64,24,128]{2,1,0:T(8,128)S(1)}, f32[64,24,128]{2,1,0:T(8,128)}, u32[]{:S(2)}) copy-start(f32[64,24,128]{2,1,0:T(8,128)} %get-tuple-element.55) | copy-start | bytes 2359300
  113.7 10.2 %copy-start.7 = (f32[64,24,128]{2,1,0:T(8,128)S(1)}, f32[64,24,128]{2,1,0:T(8,128)}, u32[]{:S(2)}) copy-start(f32[64,24,128]{2,1,0:T(8,128)} %get-tuple-element.54) | copy-start | bytes 2359300
  114.5 24.2 %all-to-all-start.3 = ((f32[8,114,128]{2,1,0:T(8,128)}), f32[8,114,128]{2,1,0:T(8,128)S(1)}, u32[]{:S(2)}, u32[]{:S(2)}) async-start(f32[8,114,128]{2,1,0:T(8,128)} %pad_maximum_fusion), calls=%async_computation.3 | async-start | bytes 983040 | tf_op jit(solution)/shard_map/all_to_all | solution.py:311
  118.8 5.1 %collective-permute-start.12 = (f32[64,24,128]{2,1,0:T(8,128)S(1)}, f32[64,24,128]{2,1,0:T(8,128)S(1)}, u32[]{:S(2)}, u32[]{:S(2)}) collective-permute-start(f32[64,24,128]{2,1,0:T(8,128)S(1)} %copy-done.14), channel_id=1, source_target_pairs={{0,4},{4,0},{1,5},{5,1},{2,6},{6,2},{3,7},{7,3},{8,12},{12,8},{9,1... | collective-permute-start | bytes 2359304 | tf_op jit(solution)/shard_map/ppermute | solution.py:320
  123.9 8.1 %collective-permute-start.13 = (f32[16,24,128]{2,1,0:T(8,128)S(1)}, f32[16,24,128]{2,1,0:T(8,128)S(1)}, u32[]{:S(2)}, u32[]{:S(2)}) collective-permute-start(f32[16,24,128]{2,1,0:T(8,128)S(1)} %get-tuple-element.63), channel_id=1, source_target_pairs={{0,384},{128,0},{256,128},{384,256},{1,385},{129,1},{257,129},{385... | collective-permute-start | bytes 589832 | tf_op jit(solution)/shard_map/ppermute | solution.py:320
  126.7 9.1 %collective-permute-start.15 = (f32[16,24,128]{2,1,0:T(8,128)S(1)}, f32[16,24,128]{2,1,0:T(8,128)S(1)}, u32[]{:S(2)}, u32[]{:S(2)}) collective-permute-start(f32[16,24,128]{2,1,0:T(8,128)S(1)} %get-tuple-element.64), channel_id=1, source_target_pairs={{0,128},{128,256},{256,384},{384,0},{1,129},{129,257},{257,385},{3... | collective-permute-start | bytes 589832 | tf_op jit(solution)/shard_map/ppermute | solution.py:320
  129.2 9.4 %collective-permute-start.14 = (f32[16,24,128]{2,1,0:T(8,128)S(1)}, f32[16,24,128]{2,1,0:T(8,128)S(1)}, u32[]{:S(2)}, u32[]{:S(2)}) collective-permute-start(f32[16,24,128]{2,1,0:T(8,128)S(1)} %get-tuple-element.65), channel_id=1, source_target_pairs={{0,256},{128,384},{256,0},{384,128},{1,257},{129,385},{257,1},{385... | collective-permute-start | bytes 589832 | tf_op jit(solution)/shard_map/ppermute | solution.py:320
  169.5 33.7 %all-to-all-start.5 = ((f32[8,144,128]{2,1,0:T(8,128)}), f32[8,144,128]{2,1,0:T(8,128)S(1)}, u32[]{:S(2)}, u32[]{:S(2)}) async-start(f32[8,144,128]{2,1,0:T(8,128)} %broadcast_in_dim.7), calls=%async_computation.5 | async-start | bytes 1179648 | tf_op jit(solution)/shard_map/all_to_all | solution.py:311
  182.4 12.8 %copy-start.15 = (f32[384,128]{1,0:T(8,128)S(1)}, f32[384,128]{1,0:T(8,128)}, u32[]{:S(2)}) copy-start(f32[384,128]{1,0:T(8,128)} %get-tuple-element.60) | copy-start | bytes 589828
  184.8 12.9 %collective-permute-start.9 = (f32[192,128]{1,0:T(8,128)}, f32[192,128]{1,0:T(8,128)S(1)}, u32[]{:S(2)}, u32[]{:S(2)}) collective-permute-start(f32[192,128]{1,0:T(8,128)} %get-tuple-element.47), channel_id=1, source_target_pairs={{0,1},{1,2},{2,3},{3,0},{4,5},{5,6},{6,7},{7,4},{8,9},{9,10},{10,1... | collective-permute-start | bytes 294920 | tf_op jit(solution)/shard_map/ppermute | solution.py:320
  186.8 11.0 %collective-permute-start.10 = (f32[192,128]{1,0:T(8,128)}, f32[192,128]{1,0:T(8,128)S(1)}, u32[]{:S(2)}, u32[]{:S(2)}) collective-permute-start(f32[192,128]{1,0:T(8,128)} %get-tuple-element.48), channel_id=1, source_target_pairs={{0,2},{1,3},{2,0},{3,1},{4,6},{5,7},{6,4},{7,5},{8,10},{9,11},{10,... | collective-permute-start | bytes 294920 | tf_op jit(solution)/shard_map/ppermute | solution.py:320
  193.3 5.6 %collective-permute-start.11 = (f32[192,128]{1,0:T(8,128)}, f32[192,128]{1,0:T(8,128)S(1)}, u32[]{:S(2)}, u32[]{:S(2)}) collective-permute-start(f32[192,128]{1,0:T(8,128)} %get-tuple-element.49), channel_id=1, source_target_pairs={{0,3},{1,0},{2,1},{3,2},{4,7},{5,4},{6,5},{7,6},{8,11},{9,8},{10,9... | collective-permute-start | bytes 294920 | tf_op jit(solution)/shard_map/ppermute | solution.py:320
  195.2 5.2 %collective-permute-start.17 = (f32[384,128]{1,0:T(8,128)S(1)}, f32[384,128]{1,0:T(8,128)S(1)}, u32[]{:S(2)}, u32[]{:S(2)}) collective-permute-start(f32[384,128]{1,0:T(8,128)S(1)} %copy-done.15), channel_id=1, source_target_pairs={{0,4},{4,0},{1,5},{5,1},{2,6},{6,2},{3,7},{7,3},{8,12},{12,8},{9,1... | collective-permute-start | bytes 589832 | tf_op jit(solution)/shard_map/ppermute | solution.py:320
  (6 other events, 4.3 us)

commit v6 on v5

--- a/solution.py
+++ b/solution.py
@@ -21,6 +21,7 @@
 DEAD_MARK = 1e6
 DEAD_LEVEL = 1e5
 INTERPRET = False
+TO_HBM = ("attention",)
 SEQ = ("y", "zh", "zl", "c")
 Z = ("zh", "zl")
 
@@ -69,16 +70,21 @@
     return pl.ds(TOKENS * j + head % SPACING_CENTRAL, MID_ROWS, stride=SPACING_CENTRAL)
 
 
-def kernel_call(body, out_shape, operands, scalars, scratch=()):
-    in_specs = [pl.BlockSpec(memory_space=pltpu.SMEM)] * scalars + [
-        pl.BlockSpec(memory_space=pltpu.VMEM)
-    ] * (len(operands) - scalars)
+def kernel_call(body, out_shape, operands, scalars, name, scratch=()):
+    space = pl.BlockSpec(memory_space=pltpu.VMEM)
+    in_specs = [pl.BlockSpec(memory_space=pltpu.SMEM)] * scalars + [space] * (
+        len(operands) - scalars
+    )
+    out_specs = jax.tree.map(lambda _: space, out_shape)
+    if not INTERPRET and name in TO_HBM:
+        out_shape = jax.tree.map(lambda x: pltpu.HBM(x.shape, x.dtype), out_shape)
     return pl.pallas_call(
         body,
         out_shape=out_shape,
         in_specs=in_specs,
-        out_specs=jax.tree.map(lambda _: pl.BlockSpec(memory_space=pltpu.VMEM), out_shape),
+        out_specs=out_specs,
         scratch_shapes=[pltpu.VMEM(dims, jnp.float32) for dims in scratch],
+        compiler_params=pltpu.CompilerParams(vmem_limit_bytes=16 << 20),
         interpret=INTERPRET,
     )(*operands)
 
@@ -107,7 +113,7 @@
 
 
 def query_body(count, base, q_ref, w_ref, own_ref, one_ref, two_ref, three_ref, *outs):
-    far_ref, mid_ref, near_ref, cot_ref = outs
+    out_ref, cot_ref = outs
     columns = own_ref.shape[0]
     heads = cot_ref.shape[0] // columns
     group = base[0] // LOCAL_HEADS
@@ -122,11 +128,13 @@
             [q_ref[rows, :] * SCALE, jnp.where(live, grads[rows, :], 0.0)], axis=0
         )
         turned = both.T
-        near_ref[TOKENS * j : TOKENS * (j + 1), :] = turned
+        out_ref[head_slice(j, TOKENS), :] = turned
     for j in range(LOCAL_HEADS):
         head = base[0] + j
-        far_ref[head_slice(j, FAR_ROWS), :] = near_ref[far_rows(j, head), :]
-        mid_ref[head_slice(j, MID_ROWS), :] = near_ref[mid_rows(j, head), :]
+        far, mid = out_ref[far_rows(j, head), :], out_ref[mid_rows(j, head), :]
+        out_ref[NEAR_BLOCK + MID_ROWS * j : NEAR_BLOCK + MID_ROWS * (j + 1), :] = mid
+        at = NEAR_BLOCK + MID_BLOCK + FAR_ROWS * j
+        out_ref[at : at + FAR_ROWS, :] = far
 
 
 def split_queries(turned):
@@ -180,25 +188,23 @@
     return jnp.concatenate([own[rows, :], other[rows, :]], axis=0)
 
 
-def near_scores_body(q_ref, near_own, near_other, both_ref, stats_ref):
-    for j in range(LOCAL_HEADS):
-        pairs = near_pairs_of(near_own, near_other, j)
-        both_ref[j], stats_ref[j] = branch_scores(q_ref[head_slice(j, TOKENS), :], pairs)
-
-
-def far_scores_body(q_ref, far_own, far_other, both_ref, stats_ref):
-    for j in range(LOCAL_HEADS):
-        pairs = gathered((far_own, far_other), head_slice(j, FAR_ROWS))
-        both_ref[j], stats_ref[j] = branch_scores(q_ref[head_slice(j, FAR_ROWS), :], pairs)
+def wide_keys(both, turned, refs, j):
+    sums = outer3(both, split_queries(turned))
+    rows = turned.shape[0]
+    half = sums.shape[0] // 2
+    for i, ref in enumerate(refs):
+        ref[:, head_slice(j, rows), :] = sums[half * i : half * (i + 1)].reshape(
+            half // rows, rows, 128
+        )
 
 
 def attention_body(*refs):
     count, base = refs[:2]
-    qm_ref, near_own, near_other, mid_own, mid_other, cot_ref = refs[2:8]
-    far_in, far_stats_ref, near_in, near_stats_ref = refs[8:12]
-    far_refs = refs[12:14]
-    dq_ref, attended_ref, weight_ref, far_both, mid_both, near_both = refs[14:20]
-    far_put, mid_put, back_ref, side_ref = refs[20:]
+    q_ref, near_own, near_other, mid_own, mid_other, cot_ref = refs[2:8]
+    far_refs = refs[8:10]
+    dq_ref, attended_ref, weight_ref = refs[10:13]
+    far_outs, mid_outs, near_outs = refs[13:15], refs[15:17], refs[17:19]
+    far_put, mid_put, back_ref, side_ref = refs[19:]
     each = range(LOCAL_HEADS)
     lanes = iota((TOKENS, 128), 1)
     filler = jnp.where(lanes == 0, MASKED_SCORE, 0.0)
@@ -206,15 +212,24 @@
     for j in each:
         far_put[head_slice(j, TOKENS), :] = filler
         mid_put[head_slice(j, TOKENS), :] = filler
-    starts = [branch_scores(qm_ref[head_slice(j, MID_ROWS), :], mid_pairs[j]) for j in each]
-    for j in each:
-        far_put[far_rows(j, base[0] + j), :] = far_stats_ref[j]
+    mid_at, far_at = NEAR_BLOCK, NEAR_BLOCK + MID_BLOCK
+    near_q = [q_ref[head_slice(j, TOKENS), :] for j in each]
+    mid_q = [q_ref[mid_at + MID_ROWS * j : mid_at + MID_ROWS * (j + 1), :] for j in each]
+    far_q = [q_ref[far_at + FAR_ROWS * j : far_at + FAR_ROWS * (j + 1), :] for j in each]
+    near_pairs = [near_pairs_of(near_own, near_other, j) for j in each]
+    far_pairs = [gathered(far_refs, head_slice(j, FAR_ROWS)) for j in each]
+    near_starts = [branch_scores(near_q[j], near_pairs[j]) for j in each]
+    far_starts = [branch_scores(far_q[j], far_pairs[j]) for j in each]
+    starts = [branch_scores(mid_q[j], mid_pairs[j]) for j in each]
+    for j in each:
+        far_put[far_rows(j, base[0] + j), :] = far_starts[j][1]
         mid_put[mid_rows(j, base[0] + j), :] = starts[j][1]
     factors = []
+    far_both, mid_both, near_both = [None] * 3, [None] * 3, [None] * 3
     for j in each:
         far_stats = far_put[head_slice(j, TOKENS), :]
         mid_stats = mid_put[head_slice(j, TOKENS), :]
-        near_stats = near_stats_ref[j]
+        near_stats = near_starts[j][1]
         far_top, mid_top, near_top = far_stats[:, 0:1], mid_stats[:, 0:1], near_stats[:, 0:1]
         top = jnp.maximum(near_top, jnp.maximum(mid_top, far_top))
         far_factor = jnp.exp(far_top - top)
@@ -231,15 +246,15 @@
     for j in each:
         far_back = back_ref[far_rows(j, base[0] + j), :]
         mid_back = back_ref[mid_rows(j, base[0] + j), :]
-        near_both[j] = branch_grads(near_in[j], *factors[j])
+        near_both[j] = branch_grads(near_starts[j][0], *factors[j])
         mid_both[j] = branch_grads(starts[j][0], mid_back[:, 1:2], mid_back[:, 2:3])
-        far_both[j] = branch_grads(far_in[j], far_back[:, 0:1], far_back[:, 2:3])
+        far_both[j] = branch_grads(far_starts[j][0], far_back[:, 0:1], far_back[:, 2:3])
     for j in each:
         side_ref[head_slice(j, TOKENS), :] = query_side(
-            near_both[j], near_pairs_of(near_own, near_other, j)
+            near_both[j], near_pairs[j]
         )
     mid_sides = [query_side(mid_both[j], mid_pairs[j]) for j in each]
-    far_sides = [query_side(far_both[j], gathered(far_refs, head_slice(j, FAR_ROWS))) for j in each]
+    far_sides = [query_side(far_both[j], far_pairs[j]) for j in each]
     for j in each:
         at = mid_rows(j, base[0] + j)
         side_ref[at, :] = side_ref[at, :] + mid_sides[j]
@@ -255,6 +270,12 @@
     weight = dot3(attended_ref[...], cot_ref[...], 1, 1)
     for b in range(weight.shape[1] // 128):
         weight_ref[columns * b : columns * (b + 1), :] = weight[:, 128 * b : 128 * b + 128]
+    for j in each:
+        wide_keys(mid_both[j], mid_q[j], mid_outs, j)
+        wide_keys(far_both[j], far_q[j], far_outs, j)
+        sums = dot3(near_both[j], split_queries(near_q[j]), 0, 0)
+        for i, ref in enumerate(near_outs):
+            ref[head_slice(j, TOKENS), :] = sums[TOKENS * i : TOKENS * (i + 1)]
 
 
 def terms_body(base, attended_ref, w_ref, *refs):
@@ -268,25 +289,6 @@
         ref[...] = terms_ref[pl.ds(at, columns), :]
 
 
-def wide_keys(both, turned, refs, j):
-    sums = outer3(both, split_queries(turned))
-    rows = turned.shape[0]
-    half = sums.shape[0] // 2
-    for i, ref in enumerate(refs):
-        ref[:, head_slice(j, rows), :] = sums[half * i : half * (i + 1)].reshape(
-            half // rows, rows, 128
-        )
-
-
-def keys_body(far_both, mid_both, near_both, qf_ref, qm_ref, qn_ref, *outs):
-    for j in range(LOCAL_HEADS):
-        wide_keys(mid_both[j], qm_ref[head_slice(j, MID_ROWS), :], outs[2:4], j)
-        wide_keys(far_both[j], qf_ref[head_slice(j, FAR_ROWS), :], outs[:2], j)
-        sums = dot3(near_both[j], split_queries(qn_ref[head_slice(j, TOKENS), :]), 0, 0)
-        for i, ref in enumerate(outs[4:]):
-            ref[head_slice(j, TOKENS), :] = sums[TOKENS * i : TOKENS * (i + 1)]
-
-
 def finish_body(base, far_ref, mid_ref, near_ref, other_ref, dk_ref, dv_ref, sum_ref):
     far_sum = far_ref[0, :FAR_BLOCK, :]
     for i in range(1, far_ref.shape[0]):
@@ -332,82 +334,67 @@
         (shaped(nz, FAR_BLOCK, 128), shaped(nzl, MID_BLOCK, 128), shaped(NEAR_BLOCK, 128)),
         (counts, base, keys, values),
         2,
+        "pack",
     )
     near_other = shifted(near_own, "c", 1)
     far_line = exchange(far_out, Z)
-    query_far, query_mid, query_near, full_cot = kernel_call(
+    query_rows, full_cot = kernel_call(
         query_body,
         (
-            shaped(FAR_BLOCK, 128),
-            shaped(MID_BLOCK, 128),
-            shaped(NEAR_BLOCK, 128),
+            shaped(NEAR_BLOCK + MID_BLOCK + FAR_BLOCK, 128),
             shaped(heads * columns, tokens),
         ),
         (counts, base, queries, out_weight, *cots),
         2,
-    )
-    near_both, near_stats = kernel_call(
-        near_scores_body,
-        (shaped(LOCAL_HEADS, 2 * TOKENS, 2 * TOKENS), shaped(LOCAL_HEADS, TOKENS, 128)),
-        (query_near, near_own, near_other),
-        0,
+        "query",
     )
     mid_own = exchange(mid_out, "zl")
-    far_own = jnp.concatenate(
-        [far_line] + [shifted(far_line, "y", k) for k in range(1, ny)], axis=0
-    )
+    far_lines = [far_line] + [shifted(far_line, "y", k) for k in range(1, ny)]
+    far_own = jnp.concatenate(far_lines, axis=0)
     far_other = shifted(far_own, "c", 1)
-    far_keys = 2 * ny * nz * FAR_ROWS
-    far_both, far_stats = kernel_call(
-        far_scores_body,
-        (shaped(LOCAL_HEADS, 2 * FAR_ROWS, far_keys), shaped(LOCAL_HEADS, FAR_ROWS, 128)),
-        (query_far, far_own, far_other),
-        0,
-    )
     mid_other = shifted(mid_own, "c", 1)
-    mid_keys = 2 * nzl * MID_ROWS
-    query_grad, attended, weight, far_both, mid_both, near_both = kernel_call(
+    (
+        query_grad,
+        attended,
+        weight,
+        far_keep,
+        far_send,
+        mid_keep,
+        mid_send,
+        near_keep,
+        near_send,
+    ) = kernel_call(
         attention_body,
         (
             shaped(columns, tokens),
             shaped(columns, tokens),
             shaped(out_weight.size // 128, 128),
-            shaped(LOCAL_HEADS, 2 * FAR_ROWS, far_keys),
-            shaped(LOCAL_HEADS, 2 * MID_ROWS, mid_keys),
-            shaped(LOCAL_HEADS, 2 * TOKENS, 2 * TOKENS),
-        ),
+        )
+        + (shaped(ny * nz, FAR_BLOCK, 128),) * 2
+        + (shaped(nzl, MID_BLOCK, 128),) * 2
+        + (shaped(NEAR_BLOCK, 128),) * 2,
         (
             counts,
             base,
-            query_mid,
+            query_rows,
             near_own,
             near_other,
             mid_own,
             mid_other,
             full_cot,
-            far_both,
-            far_stats,
-            near_both,
-            near_stats,
             far_own,
             far_other,
         ),
         2,
+        "attention",
         ((NEAR_BLOCK, 128),) * 4,
     )
     planes = 2 * ny
     weight_parts = exchange(weight.reshape(planes, -1, 128), ("y", "c"))
-    far_keep, far_send, mid_keep, mid_send, near_keep, near_send = kernel_call(
-        keys_body,
-        (shaped(ny * nz, FAR_BLOCK, 128),) * 2
-        + (shaped(nzl, MID_BLOCK, 128),) * 2
-        + (shaped(NEAR_BLOCK, 128),) * 2,
-        (far_both, mid_both, near_both, query_far, query_mid, query_near),
-        0,
-    )
     mid_got = shifted(mid_send, "c", 1)
     weight_line = jnp.sum(weight_parts, axis=0).reshape(nzl, -1, 128)
-    mid_sums = exchange(jnp.concatenate([mid_keep + mid_got, weight_line], axis=1), "zl")
+    mid_total = mid_keep + mid_got
+    mid_sums = exchange(jnp.concatenate([mid_total, weight_line], axis=1), "zl")
     far_got = shifted(far_send, "c", 1)
     near_got = shifted(near_send, "c", 1)
     pieces = [far_keep[nz * k : nz * (k + 1)] + far_got[nz * k : nz * (k + 1)] for k in range(ny)]
@@ -426,6 +413,7 @@
         (shaped(columns, tokens),) * 4,
         (base, attended, out_weight),
         1,
+        "terms",
         ((heads * columns, tokens),),
     )
     got = [terms[0]] + [shifted(terms[k], "h", k % heads) for k in range(1, 4)]
@@ -442,6 +430,7 @@
         (shaped(columns, tokens), shaped(columns, tokens)),
         (base, parts, mid_sums, near_keep, near_got),
         1,
+        "finish",
         ((NEAR_BLOCK, 128),),
     )
     return output, query_grad, key_grad, value_grad, weight_grad

time: 206 us -> 190 us (0.922)
  Pallas kernels: 23.8 us -> 8.18 us
  waiting for transfers between devices: 19.4 us -> 25.3 us
  local copies, waits for them, and re-layouts: 6.91 us -> 3.92 us
    pallas_call x8 -> x5, Pallas kernels: 23.8 us -> 8.18 us  [kernel_call(): pl.pallas_call(body, out_shape=out_shape, in_specs=in_specs, out_specs=ou...]
    all_to_all x4, waiting for transfers between devices: 1.5 us -> 6.39 us  [exchange(): return lax.all_to_all(pieces, axis, 0, 0, tiled=True)]
    unnamed x35 -> x27, local copies, waits for them, and re-layouts: 5.14 us -> 2.15 us
  transfers between devices with their start and end apart: 22 -> 22, of which waited for: 10 -> 9; matrix products, arithmetic and copies ran while one was open for 1% -> 0% of each run, Pallas kernels for 8% -> 1%
where the time goes in v6:
time: 190 us; the launch traced here: 188 us
  starting transfers between devices  92.1 us (48%)
  blocking collectives  55.2 us (29%)
  waiting for transfers between devices  25.3 us (13%)
  Pallas kernels  8.18 us (4%)
  local copies, waits for them, and re-layouts  3.92 us (2%)
    ppermute x18, starting transfers between devices, shifted(): return lax.ppermute(x, axis, [(i, (i + apart) % size) for i in range(size)])  60.1 us
    all_to_all x2, blocking collectives, exchange(): return lax.all_to_all(pieces, axis, 0, 0, tiled=True)  55.2 us
    all_to_all x4, starting transfers between devices, exchange(): return lax.all_to_all(pieces, axis, 0, 0, tiled=True)  32 us
    ppermute x18, waiting for transfers between devices, shifted(): return lax.ppermute(x, axis, [(i, (i + apart) % size) for i in range(size)])  18.9 us
    pallas_call x5, Pallas kernels, kernel_call(): pl.pallas_call(body, out_shape=out_shape, in_specs=in_specs, out_specs=ou...  8.18 us
    all_to_all x4, waiting for transfers between devices, exchange(): return lax.all_to_all(pieces, axis, 0, 0, tiled=True)  6.39 us
  transfers between devices with their start and end apart: 22, of which 9 were waited for; matrix products, arithmetic and copies ran while one was open for 0% of the time, Pallas kernels for 1%

profile of v6, /device:TPU:1, one launch (start us, length us, event | category | flops | bytes accessed | tf_op | source)
XLA Modules:
  0.0 188.1 jit_solution(5721442925230622734)
XLA Ops:
  3.1 0.9 shard_map.102
  4.0 28.0 %all_to_all.30 = f32[16,24,128]{2,1,0:T(8,128)S(1)} all-to-all(f32[16,24,128]{2,1,0:T(8,128)S(1)} %get-tuple-element.29), channel_id=1, replica_groups=mesh['y'=4,'zh'=2,'zl'=8,'c'=2,'h'=4] {'zh','zl'}, dimensions={0} | all-to-all | bytes 393216 | tf_op jit(solution)/shard_map/all_to_all | solution.py:313
  32.0 8.8 %all-to-all-start = ((f32[8,96,128]{2,1,0:T(8,128)}), f32[8,96,128]{2,1,0:T(8,128)S(1)}, u32[]{:S(2)}, u32[]{:S(2)}) async-start(f32[8,96,128]{2,1,0:T(8,128)} %get-tuple-element.27), calls=%async_computation | async-start | bytes 786432 | tf_op jit(solution)/shard_map/all_to_all | solution.py:313
  40.8 3.2 %collective-permute-start.5 = (f32[16,24,128]{2,1,0:T(8,128)S(1)}, f32[16,24,128]{2,1,0:T(8,128)S(1)}, u32[]{:S(2)}, u32[]{:S(2)}) collective-permute-start(f32[16,24,128]{2,1,0:T(8,128)S(1)} %all_to_all.30), channel_id=1, source_target_pairs={{0,128},{128,256},{256,384},{384,0},{1,129},{129,257},{257,385},{3... | collective-permute-start | bytes 589832 | tf_op jit(solution)/shard_map/ppermute | solution.py:322
  44.0 3.4 %collective-permute-start.7 = (f32[16,24,128]{2,1,0:T(8,128)S(1)}, f32[16,24,128]{2,1,0:T(8,128)S(1)}, u32[]{:S(2)}, u32[]{:S(2)}) collective-permute-start(f32[16,24,128]{2,1,0:T(8,128)S(1)} %all_to_all.30), channel_id=1, source_target_pairs={{0,384},{128,0},{256,128},{384,256},{1,385},{129,1},{257,129},{385... | collective-permute-start | bytes 589832 | tf_op jit(solution)/shard_map/ppermute | solution.py:322
  47.3 3.5 %collective-permute-start.6 = (f32[16,24,128]{2,1,0:T(8,128)S(1)}, f32[16,24,128]{2,1,0:T(8,128)S(1)}, u32[]{:S(2)}, u32[]{:S(2)}) collective-permute-start(f32[16,24,128]{2,1,0:T(8,128)S(1)} %all_to_all.30), channel_id=1, source_target_pairs={{0,256},{128,384},{256,0},{384,128},{1,257},{129,385},{257,1},{385... | collective-permute-start | bytes 589832 | tf_op jit(solution)/shard_map/ppermute | solution.py:322
  51.0 4.8 %collective-permute-done.6 = f32[16,24,128]{2,1,0:T(8,128)S(1)} collective-permute-done((f32[16,24,128]{2,1,0:T(8,128)S(1)}, f32[16,24,128]{2,1,0:T(8,128)S(1)}, u32[]{:S(2)}, u32[]{:S(2)}) %collective-permute-start.6) | collective-permute-done | bytes 196640 | tf_op jit(solution)/shard_map/ppermute | solution.py:322
  55.8 4.3 %collective-permute-start.8 = (f32[64,24,128]{2,1,0:T(8,128)S(1)}, f32[64,24,128]{2,1,0:T(8,128)S(1)}, u32[]{:S(2)}, u32[]{:S(2)}) collective-permute-start(f32[64,24,128]{2,1,0:T(8,128)S(1)} %constant_dynamic-update-slice_fusion.refs_8_), channel_id=1, source_target_pairs={{0,4},{4,0},{1,5},{5,1},{2,6},{6,2},{3,7},{7,3},{8,12},{12,8},{9,1... | collective-permute-start | bytes 2359304 | tf_op jit(solution)/shard_map/ppermute | solution.py:322
  60.2 6.5 %collective-permute-start.4 = (f32[8,96,128]{2,1,0:T(8,128)S(1)}, f32[8,96,128]{2,1,0:T(8,128)S(1)}, u32[]{:S(2)}, u32[]{:S(2)}) collective-permute-start(f32[8,96,128]{2,1,0:T(8,128)S(1)} %all-to-all-done.refs_5_), channel_id=1, source_target_pairs={{0,4},{4,0},{1,5},{5,1},{2,6},{6,2},{3,7},{7,3},{8,12},{12,8},{9,1... | collective-permute-start | bytes 1179656 | tf_op jit(solution)/shard_map/ppermute | solution.py:322
  66.8 4.7 %collective-permute-start.1 = (f32[192,128]{1,0:T(8,128)S(1)}, f32[192,128]{1,0:T(8,128)S(1)}, u32[]{:S(2)}, u32[]{:S(2)}) collective-permute-start(f32[192,128]{1,0:T(8,128)S(1)} %copy-done.3), channel_id=1, source_target_pairs={{0,2},{1,3},{2,0},{3,1},{4,6},{5,7},{6,4},{7,5},{8,10},{9,11},{10,... | collective-permute-start | bytes 294920 | tf_op jit(solution)/shard_map/ppermute | solution.py:322
  71.4 2.2 %collective-permute-start.3 = (f32[384,128]{1,0:T(8,128)S(1)}, f32[384,128]{1,0:T(8,128)S(1)}, u32[]{:S(2)}, u32[]{:S(2)}) collective-permute-start(f32[384,128]{1,0:T(8,128)S(1)} %get-tuple-element.26.refs_3_), channel_id=1, source_target_pairs={{0,4},{4,0},{1,5},{5,1},{2,6},{6,2},{3,7},{7,3},{8,12},{12,8},{9,1... | collective-permute-start | bytes 589832 | tf_op jit(solution)/shard_map/ppermute | solution.py:322
  73.6 2.2 %collective-permute-start = (f32[192,128]{1,0:T(8,128)S(1)}, f32[192,128]{1,0:T(8,128)S(1)}, u32[]{:S(2)}, u32[]{:S(2)}) collective-permute-start(f32[192,128]{1,0:T(8,128)S(1)} %copy-done.3), channel_id=1, source_target_pairs={{0,1},{1,2},{2,3},{3,0},{4,5},{5,6},{6,7},{7,4},{8,9},{9,10},{10,1... | collective-permute-start | bytes 294920 | tf_op jit(solution)/shard_map/ppermute | solution.py:322
  75.9 4.3 %collective-permute-start.2 = (f32[192,128]{1,0:T(8,128)S(1)}, f32[192,128]{1,0:T(8,128)S(1)}, u32[]{:S(2)}, u32[]{:S(2)}) collective-permute-start(f32[192,128]{1,0:T(8,128)S(1)} %copy-done.3), channel_id=1, source_target_pairs={{0,3},{1,0},{2,1},{3,2},{4,7},{5,4},{6,5},{7,6},{8,11},{9,8},{10,9... | collective-permute-start | bytes 294920 | tf_op jit(solution)/shard_map/ppermute | solution.py:322
  80.9 0.9 collective-permute-done.2.three_ref
  82.4 5.3 %shard_map.103 = (f32[192,128]{1,0:T(8,128)}, f32[192,128]{1,0:T(8,128)}, f32[1152,128]{1,0:T(8,128)}, f32[64,24,128]{2,1,0:T(8,128)}, f32[64,24,128]{2,1,0:T(8,...) custom-call(s32[1]{0:T(128)S(6)} %copy.18.count.refs_0_, ...), custom_call_target="tpu_custom_call" | custom-call | tf_op jit(solution)/shard_map/pallas_call | solution.py:81
  87.7 6.0 %all-to-all-start.2 = ((f32[8,144,128]{2,1,0:T(8,128)}), f32[8,144,128]{2,1,0:T(8,128)S(1)}, u32[]{:S(2)}, u32[]{:S(2)}) async-start(f32[8,144,128]{2,1,0:T(8,128)} %bitcast.12), calls=%async_computation.2 | async-start | bytes 1179648 | tf_op jit(solution)/shard_map/all_to_all | solution.py:313
  93.6 1.9 %collective-permute-start.16 = (f32[8,96,128]{2,1,0:T(8,128)S(1)}, f32[8,96,128]{2,1,0:T(8,128)S(1)}, u32[]{:S(2)}, u32[]{:S(2)}) collective-permute-start(f32[8,96,128]{2,1,0:T(8,128)S(1)} %copy-done.10), channel_id=1, source_target_pairs={{0,4},{4,0},{1,5},{5,1},{2,6},{6,2},{3,7},{7,3},{8,12},{12,8},{9,1... | collective-permute-start | bytes 1179656 | tf_op jit(solution)/shard_map/ppermute | solution.py:322
  95.6 1.7 collective-permute-done.16
  97.3 6.4 %all-to-all-done.2 = f32[8,144,128]{2,1,0:T(8,128)S(1)} async-done(((f32[8,144,128]{2,1,0:T(8,128)}), f32[8,144,128]{2,1,0:T(8,128)S(1)}, u32[]{:S(2)}, u32[]{:S(2)}) %all-to-all-start.2) | async-done | bytes 589856 | tf_op jit(solution)/shard_map/all_to_all | solution.py:313
  104.6 4.3 %all-to-all-start.3 = ((f32[8,114,128]{2,1,0:T(8,128)}), f32[8,114,128]{2,1,0:T(8,128)S(1)}, u32[]{:S(2)}, u32[]{:S(2)}) async-start(f32[8,114,128]{2,1,0:T(8,128)} %pad_maximum_fusion), calls=%async_computation.3 | async-start | bytes 983040 | tf_op jit(solution)/shard_map/all_to_all | solution.py:313
  108.8 3.2 %collective-permute-start.12 = (f32[64,24,128]{2,1,0:T(8,128)S(1)}, f32[64,24,128]{2,1,0:T(8,128)S(1)}, u32[]{:S(2)}, u32[]{:S(2)}) collective-permute-start(f32[64,24,128]{2,1,0:T(8,128)S(1)} %copy-done.9), channel_id=1, source_target_pairs={{0,4},{4,0},{1,5},{5,1},{2,6},{6,2},{3,7},{7,3},{8,12},{12,8},{9,1... | collective-permute-start | bytes 2359304 | tf_op jit(solution)/shard_map/ppermute | solution.py:322
  112.0 1.9 %collective-permute-done.12 = f32[64,24,128]{2,1,0:T(8,128)S(1)} collective-permute-done((f32[64,24,128]{2,1,0:T(8,128)S(1)}, f32[64,24,128]{2,1,0:T(8,128)S(1)}, u32[]{:S(2)}, u32[]{:S(2)}) %collective-permute-start.12) | collective-permute-done | bytes 786464 | tf_op jit(solution)/shard_map/ppermute | solution.py:322
  114.0 2.8 %collective-permute-start.13 = (f32[16,24,128]{2,1,0:T(8,128)S(1)}, f32[16,24,128]{2,1,0:T(8,128)S(1)}, u32[]{:S(2)}, u32[]{:S(2)}) collective-permute-start(f32[16,24,128]{2,1,0:T(8,128)S(1)} %get-tuple-element.45), channel_id=1, source_target_pairs={{0,384},{128,0},{256,128},{384,256},{1,385},{129,1},{257,129},{385... | collective-permute-start | bytes 589832 | tf_op jit(solution)/shard_map/ppermute | solution.py:322
  116.7 2.5 %collective-permute-start.15 = (f32[16,24,128]{2,1,0:T(8,128)S(1)}, f32[16,24,128]{2,1,0:T(8,128)S(1)}, u32[]{:S(2)}, u32[]{:S(2)}) collective-permute-start(f32[16,24,128]{2,1,0:T(8,128)S(1)} %get-tuple-element.46), channel_id=1, source_target_pairs={{0,128},{128,256},{256,384},{384,0},{1,129},{129,257},{257,385},{3... | collective-permute-start | bytes 589832 | tf_op jit(solution)/shard_map/ppermute | solution.py:322
  119.3 2.5 %collective-permute-start.14 = (f32[16,24,128]{2,1,0:T(8,128)S(1)}, f32[16,24,128]{2,1,0:T(8,128)S(1)}, u32[]{:S(2)}, u32[]{:S(2)}) collective-permute-start(f32[16,24,128]{2,1,0:T(8,128)S(1)} %get-tuple-element.47), channel_id=1, source_target_pairs={{0,256},{128,384},{256,0},{384,128},{1,257},{129,385},{257,1},{385... | collective-permute-start | bytes 589832 | tf_op jit(solution)/shard_map/ppermute | solution.py:322
  121.9 7.9 %collective-permute-done.15 = f32[16,24,128]{2,1,0:T(8,128)S(1)} collective-permute-done((f32[16,24,128]{2,1,0:T(8,128)S(1)}, f32[16,24,128]{2,1,0:T(8,128)S(1)}, u32[]{:S(2)}, u32[]{:S(2)}) %collective-permute-start.15) | collective-permute-done | bytes 196640 | tf_op jit(solution)/shard_map/ppermute | solution.py:322
  130.0 27.2 %all_to_all.31.far_ref = f32[16,42,128]{2,1,0:T(8,128)S(1)} all-to-all(f32[16,42,128]{2,1,0:T(8,128)S(1)} %pad_maximum_fusion.1), channel_id=1, replica_groups=mesh['y'=4,'zh'=2,'zl'=8,'c'=2,'h'=4] {'zh','zl'}, dimensions={0} | all-to-all | bytes 688128 | tf_op jit(solution)/shard_map/all_to_all | solution.py:313
  158.1 13.0 %all-to-all-start.5 = ((f32[8,144,128]{2,1,0:T(8,128)}), f32[8,144,128]{2,1,0:T(8,128)S(1)}, u32[]{:S(2)}, u32[]{:S(2)}) async-start(f32[8,144,128]{2,1,0:T(8,128)} %broadcast_in_dim.7), calls=%async_computation.5 | async-start | bytes 1179648 | tf_op jit(solution)/shard_map/all_to_all | solution.py:313
  171.7 1.9 %collective-permute-start.9 = (f32[192,128]{1,0:T(8,128)S(1)}, f32[192,128]{1,0:T(8,128)S(1)}, u32[]{:S(2)}, u32[]{:S(2)}) collective-permute-start(f32[192,128]{1,0:T(8,128)S(1)} %get-tuple-element.32), channel_id=1, source_target_pairs={{0,1},{1,2},{2,3},{3,0},{4,5},{5,6},{6,7},{7,4},{8,9},{9,10},{10,1... | collective-permute-start | bytes 294920 | tf_op jit(solution)/shard_map/ppermute | solution.py:322
  173.6 6.5 %collective-permute-start.10 = (f32[192,128]{1,0:T(8,128)S(1)}, f32[192,128]{1,0:T(8,128)S(1)}, u32[]{:S(2)}, u32[]{:S(2)}) collective-permute-start(f32[192,128]{1,0:T(8,128)S(1)} %get-tuple-element.33), channel_id=1, source_target_pairs={{0,2},{1,3},{2,0},{3,1},{4,6},{5,7},{6,4},{7,5},{8,10},{9,11},{10,... | collective-permute-start | bytes 294920 | tf_op jit(solution)/shard_map/ppermute | solution.py:322
  180.1 1.9 %collective-permute-start.11 = (f32[192,128]{1,0:T(8,128)S(1)}, f32[192,128]{1,0:T(8,128)S(1)}, u32[]{:S(2)}, u32[]{:S(2)}) collective-permute-start(f32[192,128]{1,0:T(8,128)S(1)} %get-tuple-element.34), channel_id=1, source_target_pairs={{0,3},{1,0},{2,1},{3,2},{4,7},{5,4},{6,5},{7,6},{8,11},{9,8},{10,9... | collective-permute-start | bytes 294920 | tf_op jit(solution)/shard_map/ppermute | solution.py:322
  182.0 2.6 %collective-permute-start.17 = (f32[384,128]{1,0:T(8,128)S(1)}, f32[384,128]{1,0:T(8,128)S(1)}, u32[]{:S(2)}, u32[]{:S(2)}) collective-permute-start(f32[384,128]{1,0:T(8,128)S(1)} %copy-done.11), channel_id=1, source_target_pairs={{0,4},{4,0},{1,5},{5,1},{2,6},{6,2},{3,7},{7,3},{8,12},{12,8},{9,1... | collective-permute-start | bytes 589832 | tf_op jit(solution)/shard_map/ppermute | solution.py:322
  (62 shorter events, 9.3 us)
Async XLA Ops:
  32.0 28.2 %all-to-all-start = ((f32[8,96,128]{2,1,0:T(8,128)}), f32[8,96,128]{2,1,0:T(8,128)S(1)}, u32[]{:S(2)}, u32[]{:S(2)}) async-start(f32[8,96,128]{2,1,0:T(8,128)} %get-tuple-element.27), calls=%async_computation | async-start | bytes 786432 | tf_op jit(solution)/shard_map/all_to_all | solution.py:313
  40.8 10.2 %collective-permute-start.5 = (f32[16,24,128]{2,1,0:T(8,128)S(1)}, f32[16,24,128]{2,1,0:T(8,128)S(1)}, u32[]{:S(2)}, u32[]{:S(2)}) collective-permute-start(f32[16,24,128]{2,1,0:T(8,128)S(1)} %all_to_all.30), channel_id=1, source_target_pairs={{0,128},{128,256},{256,384},{384,0},{1,129},{129,257},{257,385},{3... | collective-permute-start | bytes 589832 | tf_op jit(solution)/shard_map/ppermute | solution.py:322
  44.0 11.8 %collective-permute-start.7 = (f32[16,24,128]{2,1,0:T(8,128)S(1)}, f32[16,24,128]{2,1,0:T(8,128)S(1)}, u32[]{:S(2)}, u32[]{:S(2)}) collective-permute-start(f32[16,24,128]{2,1,0:T(8,128)S(1)} %all_to_all.30), channel_id=1, source_target_pairs={{0,384},{128,0},{256,128},{384,256},{1,385},{129,1},{257,129},{385... | collective-permute-start | bytes 589832 | tf_op jit(solution)/shard_map/ppermute | solution.py:322
  47.3 8.4 %collective-permute-start.6 = (f32[16,24,128]{2,1,0:T(8,128)S(1)}, f32[16,24,128]{2,1,0:T(8,128)S(1)}, u32[]{:S(2)}, u32[]{:S(2)}) collective-permute-start(f32[16,24,128]{2,1,0:T(8,128)S(1)} %all_to_all.30), channel_id=1, source_target_pairs={{0,256},{128,384},{256,0},{384,128},{1,257},{129,385},{257,1},{385... | collective-permute-start | bytes 589832 | tf_op jit(solution)/shard_map/ppermute | solution.py:322
  50.9 30.9 %copy-start = (f32[192,768]{1,0:T(8,128)S(1)}, f32[192,768]{1,0:T(8,128)}, u32[]{:S(2)}) copy-start(f32[192,768]{1,0:T(8,128)} %w_ref.3) | copy-start | bytes 1769476
  55.8 11.0 %copy-start.3 = (f32[192,128]{1,0:T(8,128)S(1)}, f32[192,128]{1,0:T(8,128)}, u32[]{:S(2)}) copy-start(f32[192,128]{1,0:T(8,128)} %own_ref.1) | copy-start | bytes 294916
  55.8 26.0 %copy-start.2 = (f32[192,128]{1,0:T(8,128)S(1)}, f32[192,128]{1,0:T(8,128)}, u32[]{:S(2)}) copy-start(f32[192,128]{1,0:T(8,128)} %q_ref.1) | copy-start | bytes 294916
  55.8 26.5 %collective-permute-start.8 = (f32[64,24,128]{2,1,0:T(8,128)S(1)}, f32[64,24,128]{2,1,0:T(8,128)S(1)}, u32[]{:S(2)}, u32[]{:S(2)}) collective-permute-start(f32[64,24,128]{2,1,0:T(8,128)S(1)} %constant_dynamic-update-slice_fusion.refs_8_), channel_id=1, source_target_pairs={{0,4},{4,0},{1,5},{5,1},{2,6},{6,2},{3,7},{7,3},{8,12},{12,8},{9,1... | collective-permute-start | bytes 2359304 | tf_op jit(solution)/shard_map/ppermute | solution.py:322
  60.2 22.2 %collective-permute-start.4 = (f32[8,96,128]{2,1,0:T(8,128)S(1)}, f32[8,96,128]{2,1,0:T(8,128)S(1)}, u32[]{:S(2)}, u32[]{:S(2)}) collective-permute-start(f32[8,96,128]{2,1,0:T(8,128)S(1)} %all-to-all-done.refs_5_), channel_id=1, source_target_pairs={{0,4},{4,0},{1,5},{5,1},{2,6},{6,2},{3,7},{7,3},{8,12},{12,8},{9,1... | collective-permute-start | bytes 1179656 | tf_op jit(solution)/shard_map/ppermute | solution.py:322
  66.8 9.1 %collective-permute-start.1 = (f32[192,128]{1,0:T(8,128)S(1)}, f32[192,128]{1,0:T(8,128)S(1)}, u32[]{:S(2)}, u32[]{:S(2)}) collective-permute-start(f32[192,128]{1,0:T(8,128)S(1)} %copy-done.3), channel_id=1, source_target_pairs={{0,2},{1,3},{2,0},{3,1},{4,6},{5,7},{6,4},{7,5},{8,10},{9,11},{10,... | collective-permute-start | bytes 294920 | tf_op jit(solution)/shard_map/ppermute | solution.py:322
  71.4 10.9 %collective-permute-start.3 = (f32[384,128]{1,0:T(8,128)S(1)}, f32[384,128]{1,0:T(8,128)S(1)}, u32[]{:S(2)}, u32[]{:S(2)}) collective-permute-start(f32[384,128]{1,0:T(8,128)S(1)} %get-tuple-element.26.refs_3_), channel_id=1, source_target_pairs={{0,4},{4,0},{1,5},{5,1},{2,6},{6,2},{3,7},{7,3},{8,12},{12,8},{9,1... | collective-permute-start | bytes 589832 | tf_op jit(solution)/shard_map/ppermute | solution.py:322
  73.6 7.2 %collective-permute-start = (f32[192,128]{1,0:T(8,128)S(1)}, f32[192,128]{1,0:T(8,128)S(1)}, u32[]{:S(2)}, u32[]{:S(2)}) collective-permute-start(f32[192,128]{1,0:T(8,128)S(1)} %copy-done.3), channel_id=1, source_target_pairs={{0,1},{1,2},{2,3},{3,0},{4,5},{5,6},{6,7},{7,4},{8,9},{9,10},{10,1... | collective-permute-start | bytes 294920 | tf_op jit(solution)/shard_map/ppermute | solution.py:322
  75.9 5.9 %collective-permute-start.2 = (f32[192,128]{1,0:T(8,128)S(1)}, f32[192,128]{1,0:T(8,128)S(1)}, u32[]{:S(2)}, u32[]{:S(2)}) collective-permute-start(f32[192,128]{1,0:T(8,128)S(1)} %copy-done.3), channel_id=1, source_target_pairs={{0,3},{1,0},{2,1},{3,2},{4,7},{5,4},{6,5},{7,6},{8,11},{9,8},{10,9... | collective-permute-start | bytes 294920 | tf_op jit(solution)/shard_map/ppermute | solution.py:322
  87.7 6.0 %copy-start.10 = (f32[8,96,128]{2,1,0:T(8,128)S(1)}, f32[8,96,128]{2,1,0:T(8,128)}, u32[]{:S(2)}) copy-start(f32[8,96,128]{2,1,0:T(8,128)} %get-tuple-element.39) | copy-start | bytes 1179652
  87.7 9.6 %copy-start.8 = (f32[8,96,128]{2,1,0:T(8,128)S(1)}, f32[8,96,128]{2,1,0:T(8,128)}, u32[]{:S(2)}) copy-start(f32[8,96,128]{2,1,0:T(8,128)} %get-tuple-element.38) | copy-start | bytes 1179652
  87.7 16.0 %all-to-all-start.2 = ((f32[8,144,128]{2,1,0:T(8,128)}), f32[8,144,128]{2,1,0:T(8,128)S(1)}, u32[]{:S(2)}, u32[]{:S(2)}) async-start(f32[8,144,128]{2,1,0:T(8,128)} %bitcast.12), calls=%async_computation.2 | async-start | bytes 1179648 | tf_op jit(solution)/shard_map/all_to_all | solution.py:313
  93.6 3.6 %collective-permute-start.16 = (f32[8,96,128]{2,1,0:T(8,128)S(1)}, f32[8,96,128]{2,1,0:T(8,128)S(1)}, u32[]{:S(2)}, u32[]{:S(2)}) collective-permute-start(f32[8,96,128]{2,1,0:T(8,128)S(1)} %copy-done.10), channel_id=1, source_target_pairs={{0,4},{4,0},{1,5},{5,1},{2,6},{6,2},{3,7},{7,3},{8,12},{12,8},{9,1... | collective-permute-start | bytes 1179656 | tf_op jit(solution)/shard_map/ppermute | solution.py:322
  103.7 5.1 %copy-start.9 = (f32[64,24,128]{2,1,0:T(8,128)S(1)}, f32[64,24,128]{2,1,0:T(8,128)}, u32[]{:S(2)}) copy-start(f32[64,24,128]{2,1,0:T(8,128)} %get-tuple-element.37) | copy-start | bytes 2359300
  103.7 10.1 %copy-start.7 = (f32[64,24,128]{2,1,0:T(8,128)S(1)}, f32[64,24,128]{2,1,0:T(8,128)}, u32[]{:S(2)}) copy-start(f32[64,24,128]{2,1,0:T(8,128)} %get-tuple-element.36) | copy-start | bytes 2359300
  104.6 25.4 %all-to-all-start.3 = ((f32[8,114,128]{2,1,0:T(8,128)}), f32[8,114,128]{2,1,0:T(8,128)S(1)}, u32[]{:S(2)}, u32[]{:S(2)}) async-start(f32[8,114,128]{2,1,0:T(8,128)} %pad_maximum_fusion), calls=%async_computation.3 | async-start | bytes 983040 | tf_op jit(solution)/shard_map/all_to_all | solution.py:313
  108.8 5.1 %collective-permute-start.12 = (f32[64,24,128]{2,1,0:T(8,128)S(1)}, f32[64,24,128]{2,1,0:T(8,128)S(1)}, u32[]{:S(2)}, u32[]{:S(2)}) collective-permute-start(f32[64,24,128]{2,1,0:T(8,128)S(1)} %copy-done.9), channel_id=1, source_target_pairs={{0,4},{4,0},{1,5},{5,1},{2,6},{6,2},{3,7},{7,3},{8,12},{12,8},{9,1... | collective-permute-start | bytes 2359304 | tf_op jit(solution)/shard_map/ppermute | solution.py:322
  114.0 8.0 %collective-permute-start.13 = (f32[16,24,128]{2,1,0:T(8,128)S(1)}, f32[16,24,128]{2,1,0:T(8,128)S(1)}, u32[]{:S(2)}, u32[]{:S(2)}) collective-permute-start(f32[16,24,128]{2,1,0:T(8,128)S(1)} %get-tuple-element.45), channel_id=1, source_target_pairs={{0,384},{128,0},{256,128},{384,256},{1,385},{129,1},{257,129},{385... | collective-permute-start | bytes 589832 | tf_op jit(solution)/shard_map/ppermute | solution.py:322
  116.7 13.1 %collective-permute-start.15 = (f32[16,24,128]{2,1,0:T(8,128)S(1)}, f32[16,24,128]{2,1,0:T(8,128)S(1)}, u32[]{:S(2)}, u32[]{:S(2)}) collective-permute-start(f32[16,24,128]{2,1,0:T(8,128)S(1)} %get-tuple-element.46), channel_id=1, source_target_pairs={{0,128},{128,256},{256,384},{384,0},{1,129},{129,257},{257,385},{3... | collective-permute-start | bytes 589832 | tf_op jit(solution)/shard_map/ppermute | solution.py:322
  119.3 10.6 %collective-permute-start.14 = (f32[16,24,128]{2,1,0:T(8,128)S(1)}, f32[16,24,128]{2,1,0:T(8,128)S(1)}, u32[]{:S(2)}, u32[]{:S(2)}) collective-permute-start(f32[16,24,128]{2,1,0:T(8,128)S(1)} %get-tuple-element.47), channel_id=1, source_target_pairs={{0,256},{128,384},{256,0},{384,128},{1,257},{129,385},{257,1},{385... | collective-permute-start | bytes 589832 | tf_op jit(solution)/shard_map/ppermute | solution.py:322
  158.1 13.0 %copy-start.4 = (f32[192,128]{1,0:T(8,128)S(1)}, f32[192,128]{1,0:T(8,128)}, u32[]{:S(2)}) copy-start(f32[192,128]{1,0:T(8,128)} %get-tuple-element.30.attended_ref) | copy-start | bytes 294916
  158.1 29.2 %all-to-all-start.5 = ((f32[8,144,128]{2,1,0:T(8,128)}), f32[8,144,128]{2,1,0:T(8,128)S(1)}, u32[]{:S(2)}, u32[]{:S(2)}) async-start(f32[8,144,128]{2,1,0:T(8,128)} %broadcast_in_dim.7), calls=%async_computation.5 | async-start | bytes 1179648 | tf_op jit(solution)/shard_map/all_to_all | solution.py:313
  171.1 10.9 %copy-start.11 = (f32[384,128]{1,0:T(8,128)S(1)}, f32[384,128]{1,0:T(8,128)}, u32[]{:S(2)}) copy-start(f32[384,128]{1,0:T(8,128)} %get-tuple-element.42) | copy-start | bytes 589828
  171.7 13.0 %collective-permute-start.9 = (f32[192,128]{1,0:T(8,128)S(1)}, f32[192,128]{1,0:T(8,128)S(1)}, u32[]{:S(2)}, u32[]{:S(2)}) collective-permute-start(f32[192,128]{1,0:T(8,128)S(1)} %get-tuple-element.32), channel_id=1, source_target_pairs={{0,1},{1,2},{2,3},{3,0},{4,5},{5,6},{6,7},{7,4},{8,9},{9,10},{10,1... | collective-permute-start | bytes 294920 | tf_op jit(solution)/shard_map/ppermute | solution.py:322
  173.6 11.1 %collective-permute-start.10 = (f32[192,128]{1,0:T(8,128)S(1)}, f32[192,128]{1,0:T(8,128)S(1)}, u32[]{:S(2)}, u32[]{:S(2)}) collective-permute-start(f32[192,128]{1,0:T(8,128)S(1)} %get-tuple-element.33), channel_id=1, source_target_pairs={{0,2},{1,3},{2,0},{3,1},{4,6},{5,7},{6,4},{7,5},{8,10},{9,11},{10,... | collective-permute-start | bytes 294920 | tf_op jit(solution)/shard_map/ppermute | solution.py:322
  180.1 5.4 %collective-permute-start.11 = (f32[192,128]{1,0:T(8,128)S(1)}, f32[192,128]{1,0:T(8,128)S(1)}, u32[]{:S(2)}, u32[]{:S(2)}) collective-permute-start(f32[192,128]{1,0:T(8,128)S(1)} %get-tuple-element.34), channel_id=1, source_target_pairs={{0,3},{1,0},{2,1},{3,2},{4,7},{5,4},{6,5},{7,6},{8,11},{9,8},{10,9... | collective-permute-start | bytes 294920 | tf_op jit(solution)/shard_map/ppermute | solution.py:322
  182.0 4.1 %collective-permute-start.17 = (f32[384,128]{1,0:T(8,128)S(1)}, f32[384,128]{1,0:T(8,128)S(1)}, u32[]{:S(2)}, u32[]{:S(2)}) collective-permute-start(f32[384,128]{1,0:T(8,128)S(1)} %copy-done.11), channel_id=1, source_target_pairs={{0,4},{4,0},{1,5},{5,1},{2,6},{6,2},{3,7},{7,3},{8,12},{12,8},{9,1... | collective-permute-start | bytes 589832 | tf_op jit(solution)/shard_map/ppermute | solution.py:322
  185.4 1.0 copy-start.1
  (2 other events, 1.8 us)

commit v7 on v6

--- a/solution.py
+++ b/solution.py
@@ -21,7 +21,7 @@
 DEAD_MARK = 1e6
 DEAD_LEVEL = 1e5
 INTERPRET = False
-TO_HBM = ("attention",)
+TO_HBM = ("attention", "keys")
 SEQ = ("y", "zh", "zl", "c")
 Z = ("zh", "zl")
 
@@ -70,12 +70,17 @@
     return pl.ds(TOKENS * j + head % SPACING_CENTRAL, MID_ROWS, stride=SPACING_CENTRAL)
 
 
-def kernel_call(body, out_shape, operands, scalars, name, scratch=()):
+def kernel_call(body, out_shape, operands, scalars, name, scratch=(), from_hbm=()):
     space = pl.BlockSpec(memory_space=pltpu.VMEM)
     in_specs = [pl.BlockSpec(memory_space=pltpu.SMEM)] * scalars + [space] * (
         len(operands) - scalars
     )
     out_specs = jax.tree.map(lambda _: space, out_shape)
+    if not INTERPRET:
+        operands = [
+            pltpu.with_memory_space_constraint(x, pltpu.HBM) if i in from_hbm else x
+            for i, x in enumerate(operands)
+        ]
     if not INTERPRET and name in TO_HBM:
         out_shape = jax.tree.map(lambda x: pltpu.HBM(x.shape, x.dtype), out_shape)
     return pl.pallas_call(
@@ -203,8 +208,8 @@
     q_ref, near_own, near_other, mid_own, mid_other, cot_ref = refs[2:8]
     far_refs = refs[8:10]
     dq_ref, attended_ref, weight_ref = refs[10:13]
-    far_outs, mid_outs, near_outs = refs[13:15], refs[15:17], refs[17:19]
-    far_put, mid_put, back_ref, side_ref = refs[19:]
+    far_out, mid_out, near_out = refs[13:16]
+    far_put, mid_put, back_ref, side_ref = refs[16:]
     each = range(LOCAL_HEADS)
     lanes = iota((TOKENS, 128), 1)
     filler = jnp.where(lanes == 0, MASKED_SCORE, 0.0)
@@ -250,6 +255,10 @@
         mid_both[j] = branch_grads(starts[j][0], mid_back[:, 1:2], mid_back[:, 2:3])
         far_both[j] = branch_grads(far_starts[j][0], far_back[:, 0:1], far_back[:, 2:3])
     for j in each:
+        far_out[j] = far_both[j]
+        mid_out[j] = mid_both[j]
+        near_out[j] = near_both[j]
+    for j in each:
         side_ref[head_slice(j, TOKENS), :] = query_side(
             near_both[j], near_pairs[j]
         )
@@ -270,11 +279,17 @@
     weight = dot3(attended_ref[...], cot_ref[...], 1, 1)
     for b in range(weight.shape[1] // 128):
         weight_ref[columns * b : columns * (b + 1), :] = weight[:, 128 * b : 128 * b + 128]
-    for j in each:
-        wide_keys(mid_both[j], mid_q[j], mid_outs, j)
-        wide_keys(far_both[j], far_q[j], far_outs, j)
-        sums = dot3(near_both[j], split_queries(near_q[j]), 0, 0)
-        for i, ref in enumerate(near_outs):
+
+
+def keys_body(far_both, mid_both, near_both, q_ref, *outs):
+    mid_at, far_at = NEAR_BLOCK, NEAR_BLOCK + MID_BLOCK
+    for j in range(LOCAL_HEADS):
+        mid_q = q_ref[mid_at + MID_ROWS * j : mid_at + MID_ROWS * (j + 1), :]
+        far_q = q_ref[far_at + FAR_ROWS * j : far_at + FAR_ROWS * (j + 1), :]
+        wide_keys(mid_both[j], mid_q, outs[2:4], j)
+        wide_keys(far_both[j], far_q, outs[:2], j)
+        sums = dot3(near_both[j], split_queries(q_ref[head_slice(j, TOKENS), :]), 0, 0)
+        for i, ref in enumerate(outs[4:]):
             ref[head_slice(j, TOKENS), :] = sums[TOKENS * i : TOKENS * (i + 1)]
 
 
@@ -335,6 +350,8 @@
         (counts, base, keys, values),
         2,
         "pack",
+        (),
+        (2, 3),
     )
     near_other = shifted(near_own, "c", 1)
     far_line = exchange(far_out, Z)
@@ -347,32 +364,25 @@
         (counts, base, queries, out_weight, *cots),
         2,
         "query",
+        (),
+        (2, 4),
     )
     mid_own = exchange(mid_out, "zl")
     far_lines = [far_line] + [shifted(far_line, "y", k) for k in range(1, ny)]
     far_own = jnp.concatenate(far_lines, axis=0)
     far_other = shifted(far_own, "c", 1)
     mid_other = shifted(mid_own, "c", 1)
-    (
-        query_grad,
-        attended,
-        weight,
-        far_keep,
-        far_send,
-        mid_keep,
-        mid_send,
-        near_keep,
-        near_send,
-    ) = kernel_call(
+    far_keys, mid_keys = 2 * ny * nz * FAR_ROWS, 2 * nzl * MID_ROWS
+    query_grad, attended, weight, far_both, mid_both, near_both = kernel_call(
         attention_body,
         (
             shaped(columns, tokens),
             shaped(columns, tokens),
             shaped(out_weight.size // 128, 128),
-        )
-        + (shaped(ny * nz, FAR_BLOCK, 128),) * 2
-        + (shaped(nzl, MID_BLOCK, 128),) * 2
-        + (shaped(NEAR_BLOCK, 128),) * 2,
+            shaped(LOCAL_HEADS, 2 * FAR_ROWS, far_keys),
+            shaped(LOCAL_HEADS, 2 * MID_ROWS, mid_keys),
+            shaped(LOCAL_HEADS, 2 * TOKENS, 2 * TOKENS),
+        ),
         (
             counts,
             base,
@@ -391,6 +401,17 @@
     )
     planes = 2 * ny
     weight_parts = exchange(weight.reshape(planes, -1, 128), ("y", "c"))
+    far_keep, far_send, mid_keep, mid_send, near_keep, near_send = kernel_call(
+        keys_body,
+        (shaped(ny * nz, FAR_BLOCK, 128),) * 2
+        + (shaped(nzl, MID_BLOCK, 128),) * 2
+        + (shaped(NEAR_BLOCK, 128),) * 2,
+        (far_both, mid_both, near_both, query_rows),
+        0,
+        "keys",
+        (),
+        (0, 1, 2),
+    )
     mid_got = shifted(mid_send, "c", 1)
     weight_line = jnp.sum(weight_parts, axis=0).reshape(nzl, -1, 128)
     mid_total = mid_keep + mid_got

time: 190 us -> 189 us (level)
  waiting for transfers between devices: 25.3 us -> 20.4 us
  Pallas kernels: 8.18 us -> 12.7 us
    all_to_all x4, waiting for transfers between devices: 6.39 us -> 1.45 us  [exchange(): return lax.all_to_all(pieces, axis, 0, 0, tiled=True)]
    pallas_call x5 -> x6, Pallas kernels: 8.18 us -> 12.7 us  [kernel_call(): pl.pallas_call(body, out_shape=out_shape, in_specs=in_specs, out_specs=ou...]
  transfers between devices with their start and end apart: 22 -> 22, of which waited for: 9 -> 8; matrix products, arithmetic and copies ran while one was open for 0% -> 1% of each run, Pallas kernels for 1% -> 4%
where the time goes in v7:
time: 189 us; the launch traced here: 187 us
  starting transfers between devices  92 us (49%)
  blocking collectives  55.2 us (29%)
  waiting for transfers between devices  20.4 us (11%)
  Pallas kernels  12.7 us (7%)
  other arithmetic  2.73 us (1%)
  local copies, waits for them, and re-layouts  2.13 us (1%)
    ppermute x18, starting transfers between devices, shifted(): return lax.ppermute(x, axis, [(i, (i + apart) % size) for i in range(size)])  60.3 us
    all_to_all x2, blocking collectives, exchange(): return lax.all_to_all(pieces, axis, 0, 0, tiled=True)  55.2 us
    all_to_all x4, starting transfers between devices, exchange(): return lax.all_to_all(pieces, axis, 0, 0, tiled=True)  31.7 us
    ppermute x18, waiting for transfers between devices, shifted(): return lax.ppermute(x, axis, [(i, (i + apart) % size) for i in range(size)])  18.9 us
    pallas_call x6, Pallas kernels, kernel_call(): pl.pallas_call(body, out_shape=out_shape, in_specs=in_specs, out_specs=ou...  12.7 us
  transfers between devices with their start and end apart: 22, of which 8 were waited for; matrix products, arithmetic and copies ran while one was open for 1% of the time, Pallas kernels for 4%

profile of v7, /device:TPU:1, one launch (start us, length us, event | category | flops | bytes accessed | tf_op | source)
XLA Modules:
  0.0 186.9 jit_solution(11459391907592975854)
XLA Ops:
  1.3 1.9 shard_map.102
  3.1 28.0 %all_to_all.30 = f32[16,24,128]{2,1,0:T(8,128)S(1)} all-to-all(f32[16,24,128]{2,1,0:T(8,128)S(1)} %get-tuple-element.32), channel_id=1, replica_groups=mesh['y'=4,'zh'=2,'zl'=8,'c'=2,'h'=4] {'zh','zl'}, dimensions={0} | all-to-all | bytes 393216 | tf_op jit(solution)/shard_map/all_to_all | solution.py:328
  31.2 8.8 %all-to-all-start = ((f32[8,96,128]{2,1,0:T(8,128)}), f32[8,96,128]{2,1,0:T(8,128)S(1)}, u32[]{:S(2)}, u32[]{:S(2)}) async-start(f32[8,96,128]{2,1,0:T(8,128)} %get-tuple-element.30), calls=%async_computation | async-start | bytes 786432 | tf_op jit(solution)/shard_map/all_to_all | solution.py:328
  39.9 3.2 %collective-permute-start.5 = (f32[16,24,128]{2,1,0:T(8,128)S(1)}, f32[16,24,128]{2,1,0:T(8,128)S(1)}, u32[]{:S(2)}, u32[]{:S(2)}) collective-permute-start(f32[16,24,128]{2,1,0:T(8,128)S(1)} %all_to_all.30), channel_id=1, source_target_pairs={{0,128},{128,256},{256,384},{384,0},{1,129},{129,257},{257,385},{3... | collective-permute-start | bytes 589832 | tf_op jit(solution)/shard_map/ppermute | solution.py:337
  43.1 3.4 %collective-permute-start.7 = (f32[16,24,128]{2,1,0:T(8,128)S(1)}, f32[16,24,128]{2,1,0:T(8,128)S(1)}, u32[]{:S(2)}, u32[]{:S(2)}) collective-permute-start(f32[16,24,128]{2,1,0:T(8,128)S(1)} %all_to_all.30), channel_id=1, source_target_pairs={{0,384},{128,0},{256,128},{384,256},{1,385},{129,1},{257,129},{385... | collective-permute-start | bytes 589832 | tf_op jit(solution)/shard_map/ppermute | solution.py:337
  46.5 3.5 %collective-permute-start.6 = (f32[16,24,128]{2,1,0:T(8,128)S(1)}, f32[16,24,128]{2,1,0:T(8,128)S(1)}, u32[]{:S(2)}, u32[]{:S(2)}) collective-permute-start(f32[16,24,128]{2,1,0:T(8,128)S(1)} %all_to_all.30), channel_id=1, source_target_pairs={{0,256},{128,384},{256,0},{384,128},{1,257},{129,385},{257,1},{385... | collective-permute-start | bytes 589832 | tf_op jit(solution)/shard_map/ppermute | solution.py:337
  50.1 4.8 %collective-permute-done.6 = f32[16,24,128]{2,1,0:T(8,128)S(1)} collective-permute-done((f32[16,24,128]{2,1,0:T(8,128)S(1)}, f32[16,24,128]{2,1,0:T(8,128)S(1)}, u32[]{:S(2)}, u32[]{:S(2)}) %collective-permute-start.6) | collective-permute-done | bytes 196640 | tf_op jit(solution)/shard_map/ppermute | solution.py:337
  55.0 4.2 %collective-permute-start.8 = (f32[64,24,128]{2,1,0:T(8,128)S(1)}, f32[64,24,128]{2,1,0:T(8,128)S(1)}, u32[]{:S(2)}, u32[]{:S(2)}) collective-permute-start(f32[64,24,128]{2,1,0:T(8,128)S(1)} %constant_dynamic-update-slice_fusion.refs_8_), channel_id=1, source_target_pairs={{0,4},{4,0},{1,5},{5,1},{2,6},{6,2},{3,7},{7,3},{8,12},{12,8},{9,1... | collective-permute-start | bytes 2359304 | tf_op jit(solution)/shard_map/ppermute | solution.py:337
  59.2 6.7 %collective-permute-start.4 = (f32[8,96,128]{2,1,0:T(8,128)S(1)}, f32[8,96,128]{2,1,0:T(8,128)S(1)}, u32[]{:S(2)}, u32[]{:S(2)}) collective-permute-start(f32[8,96,128]{2,1,0:T(8,128)S(1)} %all-to-all-done.refs_5_), channel_id=1, source_target_pairs={{0,4},{4,0},{1,5},{5,1},{2,6},{6,2},{3,7},{7,3},{8,12},{12,8},{9,1... | collective-permute-start | bytes 1179656 | tf_op jit(solution)/shard_map/ppermute | solution.py:337
  65.9 4.7 %collective-permute-start.1 = (f32[192,128]{1,0:T(8,128)S(1)}, f32[192,128]{1,0:T(8,128)S(1)}, u32[]{:S(2)}, u32[]{:S(2)}) collective-permute-start(f32[192,128]{1,0:T(8,128)S(1)} %copy-done.4), channel_id=1, source_target_pairs={{0,2},{1,3},{2,0},{3,1},{4,6},{5,7},{6,4},{7,5},{8,10},{9,11},{10,... | collective-permute-start | bytes 294920 | tf_op jit(solution)/shard_map/ppermute | solution.py:337
  70.6 2.2 %collective-permute-start.3 = (f32[384,128]{1,0:T(8,128)S(1)}, f32[384,128]{1,0:T(8,128)S(1)}, u32[]{:S(2)}, u32[]{:S(2)}) collective-permute-start(f32[384,128]{1,0:T(8,128)S(1)} %get-tuple-element.29.refs_3_), channel_id=1, source_target_pairs={{0,4},{4,0},{1,5},{5,1},{2,6},{6,2},{3,7},{7,3},{8,12},{12,8},{9,1... | collective-permute-start | bytes 589832 | tf_op jit(solution)/shard_map/ppermute | solution.py:337
  72.8 2.2 %collective-permute-start = (f32[192,128]{1,0:T(8,128)S(1)}, f32[192,128]{1,0:T(8,128)S(1)}, u32[]{:S(2)}, u32[]{:S(2)}) collective-permute-start(f32[192,128]{1,0:T(8,128)S(1)} %copy-done.4), channel_id=1, source_target_pairs={{0,1},{1,2},{2,3},{3,0},{4,5},{5,6},{6,7},{7,4},{8,9},{9,10},{10,1... | collective-permute-start | bytes 294920 | tf_op jit(solution)/shard_map/ppermute | solution.py:337
  75.0 4.3 %collective-permute-start.2 = (f32[192,128]{1,0:T(8,128)S(1)}, f32[192,128]{1,0:T(8,128)S(1)}, u32[]{:S(2)}, u32[]{:S(2)}) collective-permute-start(f32[192,128]{1,0:T(8,128)S(1)} %copy-done.4), channel_id=1, source_target_pairs={{0,3},{1,0},{2,1},{3,2},{4,7},{5,4},{6,5},{7,6},{8,11},{9,8},{10,9... | collective-permute-start | bytes 294920 | tf_op jit(solution)/shard_map/ppermute | solution.py:337
  80.9 1.5 shard_map.101
  82.4 4.2 %shard_map.103 = (f32[192,128]{1,0:T(8,128)}, f32[192,128]{1,0:T(8,128)}, f32[1152,128]{1,0:T(8,128)}, f32[3,16,1024]{2,1,0:T(8,128)}, f32[3,64,512]{2,1,0:T(8,128)}, /*index=5*/f32[3,256,256]{2,1,0:T(8,128)}) custom-call(s32[1]{0:T(128)S(6)} %copy.18.count.refs_0_, s32[1]{0:T(128)} %bitcast.base.refs_1_, f32[504,128]{1,0:T(8,128)S(1)} %get-tuple-element.28.refs_2_.q_ref, ...), custom_call_target="tpu_custom_call" | custom-call | tf_op jit(solution)/shard_map/pallas_call | solution.py:86
  86.6 5.8 %all-to-all-start.2 = ((f32[8,144,128]{2,1,0:T(8,128)}), f32[8,144,128]{2,1,0:T(8,128)S(1)}, u32[]{:S(2)}, u32[]{:S(2)}) async-start(f32[8,144,128]{2,1,0:T(8,128)} %bitcast.12), calls=%async_computation.2 | async-start | bytes 1179648 | tf_op jit(solution)/shard_map/all_to_all | solution.py:328
  92.5 3.8 %shard_map.105 = (f32[64,24,128]{2,1,0:T(8,128)}, f32[64,24,128]{2,1,0:T(8,128)}, f32[8,96,128]{2,1,0:T(8,128)}, f32[8,96,128]{2,1,0:T(8,128)}, f32[384,128]{1,0:T(8,128)}, /*index=5*/f32[384,128]{1,0:T(8,128)}) custom-call(f32[3,16,1024]{2,1,0:T(8,128)} %get-tuple-element.39.far_both, f32[3,64,512]{2,1,0:T(8,128)} %get-tuple-element.40.mid_both, ...), custom_call_target="tpu_custom_call" | custom-call | tf_op jit(solution)/shard_map/pallas_call | solution.py:86
  96.2 1.9 %collective-permute-start.16 = (f32[8,96,128]{2,1,0:T(8,128)}, f32[8,96,128]{2,1,0:T(8,128)S(1)}, u32[]{:S(2)}, u32[]{:S(2)}) collective-permute-start(f32[8,96,128]{2,1,0:T(8,128)} %get-tuple-element.45), channel_id=1, source_target_pairs={{0,4},{4,0},{1,5},{5,1},{2,6},{6,2},{3,7},{7,3},{8,12},{12,8},{9,1... | collective-permute-start | bytes 1179656 | tf_op jit(solution)/shard_map/ppermute | solution.py:337
  98.1 1.9 %collective-permute-done.16 = f32[8,96,128]{2,1,0:T(8,128)S(1)} collective-permute-done((f32[8,96,128]{2,1,0:T(8,128)}, f32[8,96,128]{2,1,0:T(8,128)S(1)}, u32[]{:S(2)}, u32[]{:S(2)}) %collective-permute-start.16) | collective-permute-done | bytes 393248 | tf_op jit(solution)/shard_map/ppermute | solution.py:337
  103.4 4.1 %all-to-all-start.3 = ((f32[8,114,128]{2,1,0:T(8,128)}), f32[8,114,128]{2,1,0:T(8,128)S(1)}, u32[]{:S(2)}, u32[]{:S(2)}) async-start(f32[8,114,128]{2,1,0:T(8,128)} %pad_maximum_fusion), calls=%async_computation.3 | async-start | bytes 983040 | tf_op jit(solution)/shard_map/all_to_all | solution.py:328
  107.5 3.2 %collective-permute-start.12 = (f32[64,24,128]{2,1,0:T(8,128)S(1)}, f32[64,24,128]{2,1,0:T(8,128)S(1)}, u32[]{:S(2)}, u32[]{:S(2)}) collective-permute-start(f32[64,24,128]{2,1,0:T(8,128)S(1)} %copy-done.5), channel_id=1, source_target_pairs={{0,4},{4,0},{1,5},{5,1},{2,6},{6,2},{3,7},{7,3},{8,12},{12,8},{9,1... | collective-permute-start | bytes 2359304 | tf_op jit(solution)/shard_map/ppermute | solution.py:337
  110.7 1.9 %collective-permute-done.12 = f32[64,24,128]{2,1,0:T(8,128)S(1)} collective-permute-done((f32[64,24,128]{2,1,0:T(8,128)S(1)}, f32[64,24,128]{2,1,0:T(8,128)S(1)}, u32[]{:S(2)}, u32[]{:S(2)}) %collective-permute-start.12) | collective-permute-done | bytes 786464 | tf_op jit(solution)/shard_map/ppermute | solution.py:337
  112.7 2.8 %collective-permute-start.13 = (f32[16,24,128]{2,1,0:T(8,128)S(1)}, f32[16,24,128]{2,1,0:T(8,128)S(1)}, u32[]{:S(2)}, u32[]{:S(2)}) collective-permute-start(f32[16,24,128]{2,1,0:T(8,128)S(1)} %get-tuple-element.51), channel_id=1, source_target_pairs={{0,384},{128,0},{256,128},{384,256},{1,385},{129,1},{257,129},{385... | collective-permute-start | bytes 589832 | tf_op jit(solution)/shard_map/ppermute | solution.py:337
  115.4 2.5 %collective-permute-start.15 = (f32[16,24,128]{2,1,0:T(8,128)S(1)}, f32[16,24,128]{2,1,0:T(8,128)S(1)}, u32[]{:S(2)}, u32[]{:S(2)}) collective-permute-start(f32[16,24,128]{2,1,0:T(8,128)S(1)} %get-tuple-element.52), channel_id=1, source_target_pairs={{0,128},{128,256},{256,384},{384,0},{1,129},{129,257},{257,385},{3... | collective-permute-start | bytes 589832 | tf_op jit(solution)/shard_map/ppermute | solution.py:337
  118.0 2.8 %collective-permute-start.14 = (f32[16,24,128]{2,1,0:T(8,128)S(1)}, f32[16,24,128]{2,1,0:T(8,128)S(1)}, u32[]{:S(2)}, u32[]{:S(2)}) collective-permute-start(f32[16,24,128]{2,1,0:T(8,128)S(1)} %get-tuple-element.53), channel_id=1, source_target_pairs={{0,256},{128,384},{256,0},{384,128},{1,257},{129,385},{257,1},{385... | collective-permute-start | bytes 589832 | tf_op jit(solution)/shard_map/ppermute | solution.py:337
  120.7 7.8 %collective-permute-done.15 = f32[16,24,128]{2,1,0:T(8,128)S(1)} collective-permute-done((f32[16,24,128]{2,1,0:T(8,128)S(1)}, f32[16,24,128]{2,1,0:T(8,128)S(1)}, u32[]{:S(2)}, u32[]{:S(2)}) %collective-permute-start.15) | collective-permute-done | bytes 196640 | tf_op jit(solution)/shard_map/ppermute | solution.py:337
  128.7 27.2 %all_to_all.31.far_ref = f32[16,42,128]{2,1,0:T(8,128)S(1)} all-to-all(f32[16,42,128]{2,1,0:T(8,128)S(1)} %pad_maximum_fusion.1), channel_id=1, replica_groups=mesh['y'=4,'zh'=2,'zl'=8,'c'=2,'h'=4] {'zh','zl'}, dimensions={0} | all-to-all | bytes 688128 | tf_op jit(solution)/shard_map/all_to_all | solution.py:328
  156.8 13.0 %all-to-all-start.5 = ((f32[8,144,128]{2,1,0:T(8,128)}), f32[8,144,128]{2,1,0:T(8,128)S(1)}, u32[]{:S(2)}, u32[]{:S(2)}) async-start(f32[8,144,128]{2,1,0:T(8,128)} %broadcast_in_dim.7), calls=%async_computation.5 | async-start | bytes 1179648 | tf_op jit(solution)/shard_map/all_to_all | solution.py:328
  170.4 1.9 %collective-permute-start.9 = (f32[192,128]{1,0:T(8,128)S(1)}, f32[192,128]{1,0:T(8,128)S(1)}, u32[]{:S(2)}, u32[]{:S(2)}) collective-permute-start(f32[192,128]{1,0:T(8,128)S(1)} %get-tuple-element.35), channel_id=1, source_target_pairs={{0,1},{1,2},{2,3},{3,0},{4,5},{5,6},{6,7},{7,4},{8,9},{9,10},{10,1... | collective-permute-start | bytes 294920 | tf_op jit(solution)/shard_map/ppermute | solution.py:337
  172.3 6.5 %collective-permute-start.10 = (f32[192,128]{1,0:T(8,128)S(1)}, f32[192,128]{1,0:T(8,128)S(1)}, u32[]{:S(2)}, u32[]{:S(2)}) collective-permute-start(f32[192,128]{1,0:T(8,128)S(1)} %get-tuple-element.36), channel_id=1, source_target_pairs={{0,2},{1,3},{2,0},{3,1},{4,6},{5,7},{6,4},{7,5},{8,10},{9,11},{10,... | collective-permute-start | bytes 294920 | tf_op jit(solution)/shard_map/ppermute | solution.py:337
  178.8 1.9 %collective-permute-start.11 = (f32[192,128]{1,0:T(8,128)S(1)}, f32[192,128]{1,0:T(8,128)S(1)}, u32[]{:S(2)}, u32[]{:S(2)}) collective-permute-start(f32[192,128]{1,0:T(8,128)S(1)} %get-tuple-element.37), channel_id=1, source_target_pairs={{0,3},{1,0},{2,1},{3,2},{4,7},{5,4},{6,5},{7,6},{8,11},{9,8},{10,9... | collective-permute-start | bytes 294920 | tf_op jit(solution)/shard_map/ppermute | solution.py:337
  180.8 2.5 %collective-permute-start.17 = (f32[384,128]{1,0:T(8,128)S(1)}, f32[384,128]{1,0:T(8,128)S(1)}, u32[]{:S(2)}, u32[]{:S(2)}) collective-permute-start(f32[384,128]{1,0:T(8,128)S(1)} %copy-done.6), channel_id=1, source_target_pairs={{0,4},{4,0},{1,5},{5,1},{2,6},{6,2},{3,7},{7,3},{8,12},{12,8},{9,1... | collective-permute-start | bytes 589832 | tf_op jit(solution)/shard_map/ppermute | solution.py:337
  (53 shorter events, 10.2 us)
Async XLA Ops:
  31.2 28.0 %all-to-all-start = ((f32[8,96,128]{2,1,0:T(8,128)}), f32[8,96,128]{2,1,0:T(8,128)S(1)}, u32[]{:S(2)}, u32[]{:S(2)}) async-start(f32[8,96,128]{2,1,0:T(8,128)} %get-tuple-element.30), calls=%async_computation | async-start | bytes 786432 | tf_op jit(solution)/shard_map/all_to_all | solution.py:328
  39.9 10.2 %collective-permute-start.5 = (f32[16,24,128]{2,1,0:T(8,128)S(1)}, f32[16,24,128]{2,1,0:T(8,128)S(1)}, u32[]{:S(2)}, u32[]{:S(2)}) collective-permute-start(f32[16,24,128]{2,1,0:T(8,128)S(1)} %all_to_all.30), channel_id=1, source_target_pairs={{0,128},{128,256},{256,384},{384,0},{1,129},{129,257},{257,385},{3... | collective-permute-start | bytes 589832 | tf_op jit(solution)/shard_map/ppermute | solution.py:337
  43.1 11.8 %collective-permute-start.7 = (f32[16,24,128]{2,1,0:T(8,128)S(1)}, f32[16,24,128]{2,1,0:T(8,128)S(1)}, u32[]{:S(2)}, u32[]{:S(2)}) collective-permute-start(f32[16,24,128]{2,1,0:T(8,128)S(1)} %all_to_all.30), channel_id=1, source_target_pairs={{0,384},{128,0},{256,128},{384,256},{1,385},{129,1},{257,129},{385... | collective-permute-start | bytes 589832 | tf_op jit(solution)/shard_map/ppermute | solution.py:337
  46.5 8.4 %collective-permute-start.6 = (f32[16,24,128]{2,1,0:T(8,128)S(1)}, f32[16,24,128]{2,1,0:T(8,128)S(1)}, u32[]{:S(2)}, u32[]{:S(2)}) collective-permute-start(f32[16,24,128]{2,1,0:T(8,128)S(1)} %all_to_all.30), channel_id=1, source_target_pairs={{0,256},{128,384},{256,0},{384,128},{1,257},{129,385},{257,1},{385... | collective-permute-start | bytes 589832 | tf_op jit(solution)/shard_map/ppermute | solution.py:337
  50.1 30.9 %copy-start = (f32[192,768]{1,0:T(8,128)S(1)}, f32[192,768]{1,0:T(8,128)}, u32[]{:S(2)}) copy-start(f32[192,768]{1,0:T(8,128)} %w_ref.3) | copy-start | bytes 1769476
  54.9 11.0 %copy-start.4 = (f32[192,128]{1,0:T(8,128)S(1)}, f32[192,128]{1,0:T(8,128)}, u32[]{:S(2)}) copy-start(f32[192,128]{1,0:T(8,128)} %own_ref.1) | copy-start | bytes 294916
  55.0 27.4 %collective-permute-start.8 = (f32[64,24,128]{2,1,0:T(8,128)S(1)}, f32[64,24,128]{2,1,0:T(8,128)S(1)}, u32[]{:S(2)}, u32[]{:S(2)}) collective-permute-start(f32[64,24,128]{2,1,0:T(8,128)S(1)} %constant_dynamic-update-slice_fusion.refs_8_), channel_id=1, source_target_pairs={{0,4},{4,0},{1,5},{5,1},{2,6},{6,2},{3,7},{7,3},{8,12},{12,8},{9,1... | collective-permute-start | bytes 2359304 | tf_op jit(solution)/shard_map/ppermute | solution.py:337
  59.2 23.2 %collective-permute-start.4 = (f32[8,96,128]{2,1,0:T(8,128)S(1)}, f32[8,96,128]{2,1,0:T(8,128)S(1)}, u32[]{:S(2)}, u32[]{:S(2)}) collective-permute-start(f32[8,96,128]{2,1,0:T(8,128)S(1)} %all-to-all-done.refs_5_), channel_id=1, source_target_pairs={{0,4},{4,0},{1,5},{5,1},{2,6},{6,2},{3,7},{7,3},{8,12},{12,8},{9,1... | collective-permute-start | bytes 1179656 | tf_op jit(solution)/shard_map/ppermute | solution.py:337
  65.9 9.1 %collective-permute-start.1 = (f32[192,128]{1,0:T(8,128)S(1)}, f32[192,128]{1,0:T(8,128)S(1)}, u32[]{:S(2)}, u32[]{:S(2)}) collective-permute-start(f32[192,128]{1,0:T(8,128)S(1)} %copy-done.4), channel_id=1, source_target_pairs={{0,2},{1,3},{2,0},{3,1},{4,6},{5,7},{6,4},{7,5},{8,10},{9,11},{10,... | collective-permute-start | bytes 294920 | tf_op jit(solution)/shard_map/ppermute | solution.py:337
  70.6 11.9 %collective-permute-start.3 = (f32[384,128]{1,0:T(8,128)S(1)}, f32[384,128]{1,0:T(8,128)S(1)}, u32[]{:S(2)}, u32[]{:S(2)}) collective-permute-start(f32[384,128]{1,0:T(8,128)S(1)} %get-tuple-element.29.refs_3_), channel_id=1, source_target_pairs={{0,4},{4,0},{1,5},{5,1},{2,6},{6,2},{3,7},{7,3},{8,12},{12,8},{9,1... | collective-permute-start | bytes 589832 | tf_op jit(solution)/shard_map/ppermute | solution.py:337
  72.8 7.2 %collective-permute-start = (f32[192,128]{1,0:T(8,128)S(1)}, f32[192,128]{1,0:T(8,128)S(1)}, u32[]{:S(2)}, u32[]{:S(2)}) collective-permute-start(f32[192,128]{1,0:T(8,128)S(1)} %copy-done.4), channel_id=1, source_target_pairs={{0,1},{1,2},{2,3},{3,0},{4,5},{5,6},{6,7},{7,4},{8,9},{9,10},{10,1... | collective-permute-start | bytes 294920 | tf_op jit(solution)/shard_map/ppermute | solution.py:337
  75.0 5.9 %collective-permute-start.2 = (f32[192,128]{1,0:T(8,128)S(1)}, f32[192,128]{1,0:T(8,128)S(1)}, u32[]{:S(2)}, u32[]{:S(2)}) collective-permute-start(f32[192,128]{1,0:T(8,128)S(1)} %copy-done.4), channel_id=1, source_target_pairs={{0,3},{1,0},{2,1},{3,2},{4,7},{5,4},{6,5},{7,6},{8,11},{9,8},{10,9... | collective-permute-start | bytes 294920 | tf_op jit(solution)/shard_map/ppermute | solution.py:337
  86.6 15.9 %all-to-all-start.2 = ((f32[8,144,128]{2,1,0:T(8,128)}), f32[8,144,128]{2,1,0:T(8,128)S(1)}, u32[]{:S(2)}, u32[]{:S(2)}) async-start(f32[8,144,128]{2,1,0:T(8,128)} %bitcast.12), calls=%async_computation.2 | async-start | bytes 1179648 | tf_op jit(solution)/shard_map/all_to_all | solution.py:328
  96.2 3.8 %collective-permute-start.16 = (f32[8,96,128]{2,1,0:T(8,128)}, f32[8,96,128]{2,1,0:T(8,128)S(1)}, u32[]{:S(2)}, u32[]{:S(2)}) collective-permute-start(f32[8,96,128]{2,1,0:T(8,128)} %get-tuple-element.45), channel_id=1, source_target_pairs={{0,4},{4,0},{1,5},{5,1},{2,6},{6,2},{3,7},{7,3},{8,12},{12,8},{9,1... | collective-permute-start | bytes 1179656 | tf_op jit(solution)/shard_map/ppermute | solution.py:337
  102.6 5.0 %copy-start.5 = (f32[64,24,128]{2,1,0:T(8,128)S(1)}, f32[64,24,128]{2,1,0:T(8,128)}, u32[]{:S(2)}) copy-start(f32[64,24,128]{2,1,0:T(8,128)} %get-tuple-element.43) | copy-start | bytes 2359300
  102.6 10.0 %copy-start.3 = (f32[64,24,128]{2,1,0:T(8,128)S(1)}, f32[64,24,128]{2,1,0:T(8,128)}, u32[]{:S(2)}) copy-start(f32[64,24,128]{2,1,0:T(8,128)} %get-tuple-element.42) | copy-start | bytes 2359300
  103.4 25.2 %all-to-all-start.3 = ((f32[8,114,128]{2,1,0:T(8,128)}), f32[8,114,128]{2,1,0:T(8,128)S(1)}, u32[]{:S(2)}, u32[]{:S(2)}) async-start(f32[8,114,128]{2,1,0:T(8,128)} %pad_maximum_fusion), calls=%async_computation.3 | async-start | bytes 983040 | tf_op jit(solution)/shard_map/all_to_all | solution.py:328
  107.5 5.1 %collective-permute-start.12 = (f32[64,24,128]{2,1,0:T(8,128)S(1)}, f32[64,24,128]{2,1,0:T(8,128)S(1)}, u32[]{:S(2)}, u32[]{:S(2)}) collective-permute-start(f32[64,24,128]{2,1,0:T(8,128)S(1)} %copy-done.5), channel_id=1, source_target_pairs={{0,4},{4,0},{1,5},{5,1},{2,6},{6,2},{3,7},{7,3},{8,12},{12,8},{9,1... | collective-permute-start | bytes 2359304 | tf_op jit(solution)/shard_map/ppermute | solution.py:337
  112.7 8.1 %collective-permute-start.13 = (f32[16,24,128]{2,1,0:T(8,128)S(1)}, f32[16,24,128]{2,1,0:T(8,128)S(1)}, u32[]{:S(2)}, u32[]{:S(2)}) collective-permute-start(f32[16,24,128]{2,1,0:T(8,128)S(1)} %get-tuple-element.51), channel_id=1, source_target_pairs={{0,384},{128,0},{256,128},{384,256},{1,385},{129,1},{257,129},{385... | collective-permute-start | bytes 589832 | tf_op jit(solution)/shard_map/ppermute | solution.py:337
  115.4 13.1 %collective-permute-start.15 = (f32[16,24,128]{2,1,0:T(8,128)S(1)}, f32[16,24,128]{2,1,0:T(8,128)S(1)}, u32[]{:S(2)}, u32[]{:S(2)}) collective-permute-start(f32[16,24,128]{2,1,0:T(8,128)S(1)} %get-tuple-element.52), channel_id=1, source_target_pairs={{0,128},{128,256},{256,384},{384,0},{1,129},{129,257},{257,385},{3... | collective-permute-start | bytes 589832 | tf_op jit(solution)/shard_map/ppermute | solution.py:337
  118.0 10.6 %collective-permute-start.14 = (f32[16,24,128]{2,1,0:T(8,128)S(1)}, f32[16,24,128]{2,1,0:T(8,128)S(1)}, u32[]{:S(2)}, u32[]{:S(2)}) collective-permute-start(f32[16,24,128]{2,1,0:T(8,128)S(1)} %get-tuple-element.53), channel_id=1, source_target_pairs={{0,256},{128,384},{256,0},{384,128},{1,257},{129,385},{257,1},{385... | collective-permute-start | bytes 589832 | tf_op jit(solution)/shard_map/ppermute | solution.py:337
  156.8 13.0 %copy-start.2 = (f32[192,128]{1,0:T(8,128)S(1)}, f32[192,128]{1,0:T(8,128)}, u32[]{:S(2)}) copy-start(f32[192,128]{1,0:T(8,128)} %get-tuple-element.33.attended_ref) | copy-start | bytes 294916
  156.8 29.2 %all-to-all-start.5 = ((f32[8,144,128]{2,1,0:T(8,128)}), f32[8,144,128]{2,1,0:T(8,128)S(1)}, u32[]{:S(2)}, u32[]{:S(2)}) async-start(f32[8,144,128]{2,1,0:T(8,128)} %broadcast_in_dim.7), calls=%async_computation.5 | async-start | bytes 1179648 | tf_op jit(solution)/shard_map/all_to_all | solution.py:328
  169.8 10.9 %copy-start.6 = (f32[384,128]{1,0:T(8,128)S(1)}, f32[384,128]{1,0:T(8,128)}, u32[]{:S(2)}) copy-start(f32[384,128]{1,0:T(8,128)} %get-tuple-element.48) | copy-start | bytes 589828
  170.4 12.9 %collective-permute-start.9 = (f32[192,128]{1,0:T(8,128)S(1)}, f32[192,128]{1,0:T(8,128)S(1)}, u32[]{:S(2)}, u32[]{:S(2)}) collective-permute-start(f32[192,128]{1,0:T(8,128)S(1)} %get-tuple-element.35), channel_id=1, source_target_pairs={{0,1},{1,2},{2,3},{3,0},{4,5},{5,6},{6,7},{7,4},{8,9},{9,10},{10,1... | collective-permute-start | bytes 294920 | tf_op jit(solution)/shard_map/ppermute | solution.py:337
  172.3 11.0 %collective-permute-start.10 = (f32[192,128]{1,0:T(8,128)S(1)}, f32[192,128]{1,0:T(8,128)S(1)}, u32[]{:S(2)}, u32[]{:S(2)}) collective-permute-start(f32[192,128]{1,0:T(8,128)S(1)} %get-tuple-element.36), channel_id=1, source_target_pairs={{0,2},{1,3},{2,0},{3,1},{4,6},{5,7},{6,4},{7,5},{8,10},{9,11},{10,... | collective-permute-start | bytes 294920 | tf_op jit(solution)/shard_map/ppermute | solution.py:337
  178.8 5.4 %collective-permute-start.11 = (f32[192,128]{1,0:T(8,128)S(1)}, f32[192,128]{1,0:T(8,128)S(1)}, u32[]{:S(2)}, u32[]{:S(2)}) collective-permute-start(f32[192,128]{1,0:T(8,128)S(1)} %get-tuple-element.37), channel_id=1, source_target_pairs={{0,3},{1,0},{2,1},{3,2},{4,7},{5,4},{6,5},{7,6},{8,11},{9,8},{10,9... | collective-permute-start | bytes 294920 | tf_op jit(solution)/shard_map/ppermute | solution.py:337
  180.8 4.1 %collective-permute-start.17 = (f32[384,128]{1,0:T(8,128)S(1)}, f32[384,128]{1,0:T(8,128)S(1)}, u32[]{:S(2)}, u32[]{:S(2)}) collective-permute-start(f32[384,128]{1,0:T(8,128)S(1)} %copy-done.6), channel_id=1, source_target_pairs={{0,4},{4,0},{1,5},{5,1},{2,6},{6,2},{3,7},{7,3},{8,12},{12,8},{9,1... | collective-permute-start | bytes 589832 | tf_op jit(solution)/shard_map/ppermute | solution.py:337
  184.2 1.0 copy-start.1

commit v8 on v7

--- a/solution.py
+++ b/solution.py
@@ -322,6 +322,17 @@
         turned = sum_ref[head_slice(j, TOKENS), :].T
         dk_ref[head_slice(j, HEAD), :] = turned[:HEAD]
         dv_ref[head_slice(j, HEAD), :] = turned[HEAD:]
+
+
+def weight_order_body(core, own_ref, other_ref, out_ref, all_ref):
+    depth = own_ref.shape[1]
+    for i in range(own_ref.shape[0]):
+        for ref, c in ((own_ref, core[0]), (other_ref, 1 - core[0])):
+            at = pl.multiple_of(depth * (2 * i + c), 8)
+            all_ref[pl.ds(at, depth), :] = ref[i]
+    rows = out_ref.shape[0]
+    for b in range(out_ref.shape[1] // 128):
+        out_ref[:, 128 * b : 128 * b + 128] = all_ref[rows * b : rows * (b + 1), :]
 
 
 def exchange(pieces, axis):
@@ -440,11 +451,16 @@
     got = [terms[0]] + [shifted(terms[k], "h", k % heads) for k in range(1, 4)]
     output = sum(got[1:], got[0])
     weight_whole = jnp.sum(parts[:, FAR_BLOCK:].reshape(nzh, nzl, depth, 128), axis=0)
-    weight_rows = to_all(weight_whole.reshape(nzl * depth, 128), ("y", "c"))
-    weight_grad = (
-        weight_rows.reshape(out_weight.shape[1] // 128, out_weight.shape[0], 128)
-        .swapaxes(0, 1)
-        .reshape(out_weight.shape)
+    own_rows = to_all(weight_whole.reshape(nzl * depth, 128), "y")
+    other_rows = shifted(own_rows, "c", 1)
+    core = lax.axis_index("c").astype(jnp.int32).reshape(1)
+    weight_grad = kernel_call(
+        weight_order_body,
+        shaped(*out_weight.shape),
+        (core, own_rows, other_rows),
+        1,
+        "weight_order",
+        (weight.shape,),
     )
     key_grad, value_grad = kernel_call(
         finish_body,

time: 189 us -> 190 us (level)
    ppermute x18 -> x19, starting transfers between devices: 60.3 us -> 71.5 us  [shifted(): return lax.ppermute(x, axis, [(i, (i + apart) % size) for i in range(size)])]
    all_to_all x4, starting transfers between devices: 31.7 us -> 22.3 us  [exchange(): return lax.all_to_all(pieces, axis, 0, 0, tiled=True)]
    pallas_call x6 -> x7, Pallas kernels: 12.7 us -> 13.6 us  [kernel_call(): pl.pallas_call(body, out_shape=out_shape, in_specs=in_specs, out_specs=ou...]
    ppermute x18 -> x19, waiting for transfers between devices: 18.9 us -> 18.8 us  [shifted(): return lax.ppermute(x, axis, [(i, (i + apart) % size) for i in range(size)])]
  transfers between devices with their start and end apart: 22 -> 23, of which waited for: 8 -> 8; matrix products, arithmetic and copies ran while one was open for 1% -> 1% of each run, Pallas kernels for 4% -> 4%
where the time goes in v8:
time: 190 us; the launch traced here: 188 us
  starting transfers between devices  93.8 us (49%)
  blocking collectives  55.2 us (29%)
  waiting for transfers between devices  20.3 us (11%)
  Pallas kernels  13.6 us (7%)
  other arithmetic  2.72 us (1%)
    ppermute x19, starting transfers between devices, shifted(): return lax.ppermute(x, axis, [(i, (i + apart) % size) for i in range(size)])  71.5 us
    all_to_all x2, blocking collectives, exchange(): return lax.all_to_all(pieces, axis, 0, 0, tiled=True)  55.2 us
    all_to_all x4, starting transfers between devices, exchange(): return lax.all_to_all(pieces, axis, 0, 0, tiled=True)  22.3 us
    ppermute x19, waiting for transfers between devices, shifted(): return lax.ppermute(x, axis, [(i, (i + apart) % size) for i in range(size)])  18.8 us
    pallas_call x7, Pallas kernels, kernel_call(): pl.pallas_call(body, out_shape=out_shape, in_specs=in_specs, out_specs=ou...  13.6 us
  transfers between devices with their start and end apart: 23, of which 8 were waited for; matrix products, arithmetic and copies ran while one was open for 1% of the time, Pallas kernels for 4%

profile of v8, /device:TPU:1, one launch (start us, length us, event | category | flops | bytes accessed | tf_op | source)
XLA Modules:
  0.0 188.2 jit_solution(2878627986676937267)
XLA Ops:
  1.3 1.9 shard_map.102
  3.1 28.0 %all_to_all.30 = f32[16,24,128]{2,1,0:T(8,128)S(1)} all-to-all(f32[16,24,128]{2,1,0:T(8,128)S(1)} %get-tuple-element.32), channel_id=1, replica_groups=mesh['y'=4,'zh'=2,'zl'=8,'c'=2,'h'=4] {'zh','zl'}, dimensions={0} | all-to-all | bytes 393216 | tf_op jit(solution)/shard_map/all_to_all | solution.py:339
  31.2 8.8 %all-to-all-start = ((f32[8,96,128]{2,1,0:T(8,128)}), f32[8,96,128]{2,1,0:T(8,128)S(1)}, u32[]{:S(2)}, u32[]{:S(2)}) async-start(f32[8,96,128]{2,1,0:T(8,128)} %get-tuple-element.30), calls=%async_computation | async-start | bytes 786432 | tf_op jit(solution)/shard_map/all_to_all | solution.py:339
  39.9 3.2 %collective-permute-start.5 = (f32[16,24,128]{2,1,0:T(8,128)S(1)}, f32[16,24,128]{2,1,0:T(8,128)S(1)}, u32[]{:S(2)}, u32[]{:S(2)}) collective-permute-start(f32[16,24,128]{2,1,0:T(8,128)S(1)} %all_to_all.30), channel_id=1, source_target_pairs={{0,128},{128,256},{256,384},{384,0},{1,129},{129,257},{257,385},{3... | collective-permute-start | bytes 589832 | tf_op jit(solution)/shard_map/ppermute | solution.py:348
  43.1 3.4 %collective-permute-start.7 = (f32[16,24,128]{2,1,0:T(8,128)S(1)}, f32[16,24,128]{2,1,0:T(8,128)S(1)}, u32[]{:S(2)}, u32[]{:S(2)}) collective-permute-start(f32[16,24,128]{2,1,0:T(8,128)S(1)} %all_to_all.30), channel_id=1, source_target_pairs={{0,384},{128,0},{256,128},{384,256},{1,385},{129,1},{257,129},{385... | collective-permute-start | bytes 589832 | tf_op jit(solution)/shard_map/ppermute | solution.py:348
  46.5 3.5 %collective-permute-start.6 = (f32[16,24,128]{2,1,0:T(8,128)S(1)}, f32[16,24,128]{2,1,0:T(8,128)S(1)}, u32[]{:S(2)}, u32[]{:S(2)}) collective-permute-start(f32[16,24,128]{2,1,0:T(8,128)S(1)} %all_to_all.30), channel_id=1, source_target_pairs={{0,256},{128,384},{256,0},{384,128},{1,257},{129,385},{257,1},{385... | collective-permute-start | bytes 589832 | tf_op jit(solution)/shard_map/ppermute | solution.py:348
  50.1 4.8 %collective-permute-done.6 = f32[16,24,128]{2,1,0:T(8,128)S(1)} collective-permute-done((f32[16,24,128]{2,1,0:T(8,128)S(1)}, f32[16,24,128]{2,1,0:T(8,128)S(1)}, u32[]{:S(2)}, u32[]{:S(2)}) %collective-permute-start.6) | collective-permute-done | bytes 196640 | tf_op jit(solution)/shard_map/ppermute | solution.py:348
  55.0 4.2 %collective-permute-start.8 = (f32[64,24,128]{2,1,0:T(8,128)S(1)}, f32[64,24,128]{2,1,0:T(8,128)S(1)}, u32[]{:S(2)}, u32[]{:S(2)}) collective-permute-start(f32[64,24,128]{2,1,0:T(8,128)S(1)} %constant_dynamic-update-slice_fusion.refs_8_), channel_id=1, source_target_pairs={{0,4},{4,0},{1,5},{5,1},{2,6},{6,2},{3,7},{7,3},{8,12},{12,8},{9,1... | collective-permute-start | bytes 2359304 | tf_op jit(solution)/shard_map/ppermute | solution.py:348
  59.2 6.7 %collective-permute-start.4 = (f32[8,96,128]{2,1,0:T(8,128)S(1)}, f32[8,96,128]{2,1,0:T(8,128)S(1)}, u32[]{:S(2)}, u32[]{:S(2)}) collective-permute-start(f32[8,96,128]{2,1,0:T(8,128)S(1)} %all-to-all-done.refs_5_), channel_id=1, source_target_pairs={{0,4},{4,0},{1,5},{5,1},{2,6},{6,2},{3,7},{7,3},{8,12},{12,8},{9,1... | collective-permute-start | bytes 1179656 | tf_op jit(solution)/shard_map/ppermute | solution.py:348
  65.9 4.7 %collective-permute-start.1 = (f32[192,128]{1,0:T(8,128)S(1)}, f32[192,128]{1,0:T(8,128)S(1)}, u32[]{:S(2)}, u32[]{:S(2)}) collective-permute-start(f32[192,128]{1,0:T(8,128)S(1)} %copy-done.4), channel_id=1, source_target_pairs={{0,2},{1,3},{2,0},{3,1},{4,6},{5,7},{6,4},{7,5},{8,10},{9,11},{10,... | collective-permute-start | bytes 294920 | tf_op jit(solution)/shard_map/ppermute | solution.py:348
  70.6 2.2 %collective-permute-start.3 = (f32[384,128]{1,0:T(8,128)S(1)}, f32[384,128]{1,0:T(8,128)S(1)}, u32[]{:S(2)}, u32[]{:S(2)}) collective-permute-start(f32[384,128]{1,0:T(8,128)S(1)} %get-tuple-element.29.refs_3_), channel_id=1, source_target_pairs={{0,4},{4,0},{1,5},{5,1},{2,6},{6,2},{3,7},{7,3},{8,12},{12,8},{9,1... | collective-permute-start | bytes 589832 | tf_op jit(solution)/shard_map/ppermute | solution.py:348
  72.8 2.2 %collective-permute-start = (f32[192,128]{1,0:T(8,128)S(1)}, f32[192,128]{1,0:T(8,128)S(1)}, u32[]{:S(2)}, u32[]{:S(2)}) collective-permute-start(f32[192,128]{1,0:T(8,128)S(1)} %copy-done.4), channel_id=1, source_target_pairs={{0,1},{1,2},{2,3},{3,0},{4,5},{5,6},{6,7},{7,4},{8,9},{9,10},{10,1... | collective-permute-start | bytes 294920 | tf_op jit(solution)/shard_map/ppermute | solution.py:348
  75.0 4.3 %collective-permute-start.2 = (f32[192,128]{1,0:T(8,128)S(1)}, f32[192,128]{1,0:T(8,128)S(1)}, u32[]{:S(2)}, u32[]{:S(2)}) collective-permute-start(f32[192,128]{1,0:T(8,128)S(1)} %copy-done.4), channel_id=1, source_target_pairs={{0,3},{1,0},{2,1},{3,2},{4,7},{5,4},{6,5},{7,6},{8,11},{9,8},{10,9... | collective-permute-start | bytes 294920 | tf_op jit(solution)/shard_map/ppermute | solution.py:348
  82.4 4.2 %shard_map.103 = (f32[192,128]{1,0:T(8,128)}, f32[192,128]{1,0:T(8,128)}, f32[1152,128]{1,0:T(8,128)}, f32[3,16,1024]{2,1,0:T(8,128)}, f32[3,64,512]{2,1,0:T(8,128)}, /*index=5*/f32[3,256,256]{2,1,0:T(8,128)}) custom-call(s32[1]{0:T(128)S(6)} %copy.14.count.refs_0_, s32[1]{0:T(128)} %bitcast.base.refs_1_, f32[504,128]{1,0:T(8,128)S(1)} %get-tuple-element.28.refs_2_.q_ref, ...), custom_call_target="tpu_custom_call" | custom-call | tf_op jit(solution)/shard_map/pallas_call | solution.py:86
  86.6 5.8 %all-to-all-start.2 = ((f32[8,144,128]{2,1,0:T(8,128)}), f32[8,144,128]{2,1,0:T(8,128)S(1)}, u32[]{:S(2)}, u32[]{:S(2)}) async-start(f32[8,144,128]{2,1,0:T(8,128)} %bitcast.5), calls=%async_computation.2 | async-start | bytes 1179648 | tf_op jit(solution)/shard_map/all_to_all | solution.py:339
  92.5 3.7 %shard_map.105 = (f32[64,24,128]{2,1,0:T(8,128)}, f32[64,24,128]{2,1,0:T(8,128)}, f32[8,96,128]{2,1,0:T(8,128)}, f32[8,96,128]{2,1,0:T(8,128)}, f32[384,128]{1,0:T(8,128)}, /*index=5*/f32[384,128]{1,0:T(8,128)}) custom-call(f32[3,16,1024]{2,1,0:T(8,128)} %get-tuple-element.39.far_both, f32[3,64,512]{2,1,0:T(8,128)} %get-tuple-element.40.mid_both, ...), custom_call_target="tpu_custom_call" | custom-call | tf_op jit(solution)/shard_map/pallas_call | solution.py:86
  96.2 1.9 %collective-permute-start.16 = (f32[8,96,128]{2,1,0:T(8,128)}, f32[8,96,128]{2,1,0:T(8,128)S(1)}, u32[]{:S(2)}, u32[]{:S(2)}) collective-permute-start(f32[8,96,128]{2,1,0:T(8,128)} %get-tuple-element.45), channel_id=1, source_target_pairs={{0,4},{4,0},{1,5},{5,1},{2,6},{6,2},{3,7},{7,3},{8,12},{12,8},{9,1... | collective-permute-start | bytes 1179656 | tf_op jit(solution)/shard_map/ppermute | solution.py:348
  98.1 1.9 %collective-permute-done.16 = f32[8,96,128]{2,1,0:T(8,128)S(1)} collective-permute-done((f32[8,96,128]{2,1,0:T(8,128)}, f32[8,96,128]{2,1,0:T(8,128)S(1)}, u32[]{:S(2)}, u32[]{:S(2)}) %collective-permute-start.16) | collective-permute-done | bytes 393248 | tf_op jit(solution)/shard_map/ppermute | solution.py:348
  103.4 4.1 %all-to-all-start.3 = ((f32[8,114,128]{2,1,0:T(8,128)}), f32[8,114,128]{2,1,0:T(8,128)S(1)}, u32[]{:S(2)}, u32[]{:S(2)}) async-start(f32[8,114,128]{2,1,0:T(8,128)} %pad_maximum_fusion), calls=%async_computation.3 | async-start | bytes 983040 | tf_op jit(solution)/shard_map/all_to_all | solution.py:339
  107.5 3.2 %collective-permute-start.12 = (f32[64,24,128]{2,1,0:T(8,128)S(1)}, f32[64,24,128]{2,1,0:T(8,128)S(1)}, u32[]{:S(2)}, u32[]{:S(2)}) collective-permute-start(f32[64,24,128]{2,1,0:T(8,128)S(1)} %copy-done.5), channel_id=1, source_target_pairs={{0,4},{4,0},{1,5},{5,1},{2,6},{6,2},{3,7},{7,3},{8,12},{12,8},{9,1... | collective-permute-start | bytes 2359304 | tf_op jit(solution)/shard_map/ppermute | solution.py:348
  110.7 1.9 %collective-permute-done.12 = f32[64,24,128]{2,1,0:T(8,128)S(1)} collective-permute-done((f32[64,24,128]{2,1,0:T(8,128)S(1)}, f32[64,24,128]{2,1,0:T(8,128)S(1)}, u32[]{:S(2)}, u32[]{:S(2)}) %collective-permute-start.12) | collective-permute-done | bytes 786464 | tf_op jit(solution)/shard_map/ppermute | solution.py:348
  112.7 2.8 %collective-permute-start.13 = (f32[16,24,128]{2,1,0:T(8,128)S(1)}, f32[16,24,128]{2,1,0:T(8,128)S(1)}, u32[]{:S(2)}, u32[]{:S(2)}) collective-permute-start(f32[16,24,128]{2,1,0:T(8,128)S(1)} %get-tuple-element.51), channel_id=1, source_target_pairs={{0,384},{128,0},{256,128},{384,256},{1,385},{129,1},{257,129},{385... | collective-permute-start | bytes 589832 | tf_op jit(solution)/shard_map/ppermute | solution.py:348
  115.4 2.5 %collective-permute-start.15 = (f32[16,24,128]{2,1,0:T(8,128)S(1)}, f32[16,24,128]{2,1,0:T(8,128)S(1)}, u32[]{:S(2)}, u32[]{:S(2)}) collective-permute-start(f32[16,24,128]{2,1,0:T(8,128)S(1)} %get-tuple-element.52), channel_id=1, source_target_pairs={{0,128},{128,256},{256,384},{384,0},{1,129},{129,257},{257,385},{3... | collective-permute-start | bytes 589832 | tf_op jit(solution)/shard_map/ppermute | solution.py:348
  118.0 2.7 %collective-permute-start.14 = (f32[16,24,128]{2,1,0:T(8,128)S(1)}, f32[16,24,128]{2,1,0:T(8,128)S(1)}, u32[]{:S(2)}, u32[]{:S(2)}) collective-permute-start(f32[16,24,128]{2,1,0:T(8,128)S(1)} %get-tuple-element.53), channel_id=1, source_target_pairs={{0,256},{128,384},{256,0},{384,128},{1,257},{129,385},{257,1},{385... | collective-permute-start | bytes 589832 | tf_op jit(solution)/shard_map/ppermute | solution.py:348
  120.7 7.9 %collective-permute-done.15 = f32[16,24,128]{2,1,0:T(8,128)S(1)} collective-permute-done((f32[16,24,128]{2,1,0:T(8,128)S(1)}, f32[16,24,128]{2,1,0:T(8,128)S(1)}, u32[]{:S(2)}, u32[]{:S(2)}) %collective-permute-start.15) | collective-permute-done | bytes 196640 | tf_op jit(solution)/shard_map/ppermute | solution.py:348
  128.7 27.2 %all_to_all.31.far_ref = f32[16,42,128]{2,1,0:T(8,128)S(1)} all-to-all(f32[16,42,128]{2,1,0:T(8,128)S(1)} %pad_maximum_fusion.1), channel_id=1, replica_groups=mesh['y'=4,'zh'=2,'zl'=8,'c'=2,'h'=4] {'zh','zl'}, dimensions={0} | all-to-all | bytes 688128 | tf_op jit(solution)/shard_map/all_to_all | solution.py:339
  156.7 3.6 %all-to-all-start.5 = ((f32[4,144,128]{2,1,0:T(8,128)}), f32[4,144,128]{2,1,0:T(8,128)S(1)}, u32[]{:S(2)}, u32[]{:S(2)}) async-start(f32[4,144,128]{2,1,0:T(8,128)} %broadcast_in_dim.7), calls=%async_computation.5 | async-start | bytes 589824 | tf_op jit(solution)/shard_map/all_to_all | solution.py:339
  160.9 1.9 %collective-permute-start.9 = (f32[192,128]{1,0:T(8,128)S(1)}, f32[192,128]{1,0:T(8,128)S(1)}, u32[]{:S(2)}, u32[]{:S(2)}) collective-permute-start(f32[192,128]{1,0:T(8,128)S(1)} %get-tuple-element.35), channel_id=1, source_target_pairs={{0,1},{1,2},{2,3},{3,0},{4,5},{5,6},{6,7},{7,4},{8,9},{9,10},{10,1... | collective-permute-start | bytes 294920 | tf_op jit(solution)/shard_map/ppermute | solution.py:348
  162.8 6.5 %collective-permute-start.10 = (f32[192,128]{1,0:T(8,128)S(1)}, f32[192,128]{1,0:T(8,128)S(1)}, u32[]{:S(2)}, u32[]{:S(2)}) collective-permute-start(f32[192,128]{1,0:T(8,128)S(1)} %get-tuple-element.36), channel_id=1, source_target_pairs={{0,2},{1,3},{2,0},{3,1},{4,6},{5,7},{6,4},{7,5},{8,10},{9,11},{10,... | collective-permute-start | bytes 294920 | tf_op jit(solution)/shard_map/ppermute | solution.py:348
  169.3 1.9 %collective-permute-start.11 = (f32[192,128]{1,0:T(8,128)S(1)}, f32[192,128]{1,0:T(8,128)S(1)}, u32[]{:S(2)}, u32[]{:S(2)}) collective-permute-start(f32[192,128]{1,0:T(8,128)S(1)} %get-tuple-element.37), channel_id=1, source_target_pairs={{0,3},{1,0},{2,1},{3,2},{4,7},{5,4},{6,5},{7,6},{8,11},{9,8},{10,9... | collective-permute-start | bytes 294920 | tf_op jit(solution)/shard_map/ppermute | solution.py:348
  171.2 11.9 %collective-permute-start.18 = (f32[4,144,128]{2,1,0:T(8,128)S(1)}, f32[4,144,128]{2,1,0:T(8,128)S(1)}, u32[]{:S(2)}, u32[]{:S(2)}) collective-permute-start(f32[4,144,128]{2,1,0:T(8,128)S(1)} %all-to-all-done.5.own_ref), channel_id=1, source_target_pairs={{0,4},{4,0},{1,5},{5,1},{2,6},{6,2},{3,7},{7,3},{8,12},{12,8},{9,1... | collective-permute-start | bytes 884744 | tf_op jit(solution)/shard_map/ppermute | solution.py:348
  183.1 1.9 %collective-permute-start.17 = (f32[384,128]{1,0:T(8,128)S(1)}, f32[384,128]{1,0:T(8,128)S(1)}, u32[]{:S(2)}, u32[]{:S(2)}) collective-permute-start(f32[384,128]{1,0:T(8,128)S(1)} %copy-done.6), channel_id=1, source_target_pairs={{0,4},{4,0},{1,5},{5,1},{2,6},{6,2},{3,7},{7,3},{8,12},{12,8},{9,1... | collective-permute-start | bytes 589832 | tf_op jit(solution)/shard_map/ppermute | solution.py:348
  (55 shorter events, 11.2 us)
Async XLA Ops:
  31.2 28.0 %all-to-all-start = ((f32[8,96,128]{2,1,0:T(8,128)}), f32[8,96,128]{2,1,0:T(8,128)S(1)}, u32[]{:S(2)}, u32[]{:S(2)}) async-start(f32[8,96,128]{2,1,0:T(8,128)} %get-tuple-element.30), calls=%async_computation | async-start | bytes 786432 | tf_op jit(solution)/shard_map/all_to_all | solution.py:339
  39.9 10.2 %collective-permute-start.5 = (f32[16,24,128]{2,1,0:T(8,128)S(1)}, f32[16,24,128]{2,1,0:T(8,128)S(1)}, u32[]{:S(2)}, u32[]{:S(2)}) collective-permute-start(f32[16,24,128]{2,1,0:T(8,128)S(1)} %all_to_all.30), channel_id=1, source_target_pairs={{0,128},{128,256},{256,384},{384,0},{1,129},{129,257},{257,385},{3... | collective-permute-start | bytes 589832 | tf_op jit(solution)/shard_map/ppermute | solution.py:348
  43.1 11.8 %collective-permute-start.7 = (f32[16,24,128]{2,1,0:T(8,128)S(1)}, f32[16,24,128]{2,1,0:T(8,128)S(1)}, u32[]{:S(2)}, u32[]{:S(2)}) collective-permute-start(f32[16,24,128]{2,1,0:T(8,128)S(1)} %all_to_all.30), channel_id=1, source_target_pairs={{0,384},{128,0},{256,128},{384,256},{1,385},{129,1},{257,129},{385... | collective-permute-start | bytes 589832 | tf_op jit(solution)/shard_map/ppermute | solution.py:348
  46.5 8.4 %collective-permute-start.6 = (f32[16,24,128]{2,1,0:T(8,128)S(1)}, f32[16,24,128]{2,1,0:T(8,128)S(1)}, u32[]{:S(2)}, u32[]{:S(2)}) collective-permute-start(f32[16,24,128]{2,1,0:T(8,128)S(1)} %all_to_all.30), channel_id=1, source_target_pairs={{0,256},{128,384},{256,0},{384,128},{1,257},{129,385},{257,1},{385... | collective-permute-start | bytes 589832 | tf_op jit(solution)/shard_map/ppermute | solution.py:348
  50.1 30.9 %copy-start = (f32[192,768]{1,0:T(8,128)S(1)}, f32[192,768]{1,0:T(8,128)}, u32[]{:S(2)}) copy-start(f32[192,768]{1,0:T(8,128)} %w_ref.3) | copy-start | bytes 1769476
  54.9 11.0 %copy-start.4 = (f32[192,128]{1,0:T(8,128)S(1)}, f32[192,128]{1,0:T(8,128)}, u32[]{:S(2)}) copy-start(f32[192,128]{1,0:T(8,128)} %own_ref.1) | copy-start | bytes 294916
  55.0 27.4 %collective-permute-start.8 = (f32[64,24,128]{2,1,0:T(8,128)S(1)}, f32[64,24,128]{2,1,0:T(8,128)S(1)}, u32[]{:S(2)}, u32[]{:S(2)}) collective-permute-start(f32[64,24,128]{2,1,0:T(8,128)S(1)} %constant_dynamic-update-slice_fusion.refs_8_), channel_id=1, source_target_pairs={{0,4},{4,0},{1,5},{5,1},{2,6},{6,2},{3,7},{7,3},{8,12},{12,8},{9,1... | collective-permute-start | bytes 2359304 | tf_op jit(solution)/shard_map/ppermute | solution.py:348
  59.2 23.2 %collective-permute-start.4 = (f32[8,96,128]{2,1,0:T(8,128)S(1)}, f32[8,96,128]{2,1,0:T(8,128)S(1)}, u32[]{:S(2)}, u32[]{:S(2)}) collective-permute-start(f32[8,96,128]{2,1,0:T(8,128)S(1)} %all-to-all-done.refs_5_), channel_id=1, source_target_pairs={{0,4},{4,0},{1,5},{5,1},{2,6},{6,2},{3,7},{7,3},{8,12},{12,8},{9,1... | collective-permute-start | bytes 1179656 | tf_op jit(solution)/shard_map/ppermute | solution.py:348
  65.9 9.1 %collective-permute-start.1 = (f32[192,128]{1,0:T(8,128)S(1)}, f32[192,128]{1,0:T(8,128)S(1)}, u32[]{:S(2)}, u32[]{:S(2)}) collective-permute-start(f32[192,128]{1,0:T(8,128)S(1)} %copy-done.4), channel_id=1, source_target_pairs={{0,2},{1,3},{2,0},{3,1},{4,6},{5,7},{6,4},{7,5},{8,10},{9,11},{10,... | collective-permute-start | bytes 294920 | tf_op jit(solution)/shard_map/ppermute | solution.py:348
  70.6 11.9 %collective-permute-start.3 = (f32[384,128]{1,0:T(8,128)S(1)}, f32[384,128]{1,0:T(8,128)S(1)}, u32[]{:S(2)}, u32[]{:S(2)}) collective-permute-start(f32[384,128]{1,0:T(8,128)S(1)} %get-tuple-element.29.refs_3_), channel_id=1, source_target_pairs={{0,4},{4,0},{1,5},{5,1},{2,6},{6,2},{3,7},{7,3},{8,12},{12,8},{9,1... | collective-permute-start | bytes 589832 | tf_op jit(solution)/shard_map/ppermute | solution.py:348
  72.8 7.2 %collective-permute-start = (f32[192,128]{1,0:T(8,128)S(1)}, f32[192,128]{1,0:T(8,128)S(1)}, u32[]{:S(2)}, u32[]{:S(2)}) collective-permute-start(f32[192,128]{1,0:T(8,128)S(1)} %copy-done.4), channel_id=1, source_target_pairs={{0,1},{1,2},{2,3},{3,0},{4,5},{5,6},{6,7},{7,4},{8,9},{9,10},{10,1... | collective-permute-start | bytes 294920 | tf_op jit(solution)/shard_map/ppermute | solution.py:348
  75.0 5.9 %collective-permute-start.2 = (f32[192,128]{1,0:T(8,128)S(1)}, f32[192,128]{1,0:T(8,128)S(1)}, u32[]{:S(2)}, u32[]{:S(2)}) collective-permute-start(f32[192,128]{1,0:T(8,128)S(1)} %copy-done.4), channel_id=1, source_target_pairs={{0,3},{1,0},{2,1},{3,2},{4,7},{5,4},{6,5},{7,6},{8,11},{9,8},{10,9... | collective-permute-start | bytes 294920 | tf_op jit(solution)/shard_map/ppermute | solution.py:348
  86.6 15.9 %all-to-all-start.2 = ((f32[8,144,128]{2,1,0:T(8,128)}), f32[8,144,128]{2,1,0:T(8,128)S(1)}, u32[]{:S(2)}, u32[]{:S(2)}) async-start(f32[8,144,128]{2,1,0:T(8,128)} %bitcast.5), calls=%async_computation.2 | async-start | bytes 1179648 | tf_op jit(solution)/shard_map/all_to_all | solution.py:339
  96.2 3.8 %collective-permute-start.16 = (f32[8,96,128]{2,1,0:T(8,128)}, f32[8,96,128]{2,1,0:T(8,128)S(1)}, u32[]{:S(2)}, u32[]{:S(2)}) collective-permute-start(f32[8,96,128]{2,1,0:T(8,128)} %get-tuple-element.45), channel_id=1, source_target_pairs={{0,4},{4,0},{1,5},{5,1},{2,6},{6,2},{3,7},{7,3},{8,12},{12,8},{9,1... | collective-permute-start | bytes 1179656 | tf_op jit(solution)/shard_map/ppermute | solution.py:348
  102.6 5.0 %copy-start.5 = (f32[64,24,128]{2,1,0:T(8,128)S(1)}, f32[64,24,128]{2,1,0:T(8,128)}, u32[]{:S(2)}) copy-start(f32[64,24,128]{2,1,0:T(8,128)} %get-tuple-element.43) | copy-start | bytes 2359300
  102.6 10.0 %copy-start.3 = (f32[64,24,128]{2,1,0:T(8,128)S(1)}, f32[64,24,128]{2,1,0:T(8,128)}, u32[]{:S(2)}) copy-start(f32[64,24,128]{2,1,0:T(8,128)} %get-tuple-element.42) | copy-start | bytes 2359300
  103.4 25.2 %all-to-all-start.3 = ((f32[8,114,128]{2,1,0:T(8,128)}), f32[8,114,128]{2,1,0:T(8,128)S(1)}, u32[]{:S(2)}, u32[]{:S(2)}) async-start(f32[8,114,128]{2,1,0:T(8,128)} %pad_maximum_fusion), calls=%async_computation.3 | async-start | bytes 983040 | tf_op jit(solution)/shard_map/all_to_all | solution.py:339
  107.5 5.1 %collective-permute-start.12 = (f32[64,24,128]{2,1,0:T(8,128)S(1)}, f32[64,24,128]{2,1,0:T(8,128)S(1)}, u32[]{:S(2)}, u32[]{:S(2)}) collective-permute-start(f32[64,24,128]{2,1,0:T(8,128)S(1)} %copy-done.5), channel_id=1, source_target_pairs={{0,4},{4,0},{1,5},{5,1},{2,6},{6,2},{3,7},{7,3},{8,12},{12,8},{9,1... | collective-permute-start | bytes 2359304 | tf_op jit(solution)/shard_map/ppermute | solution.py:348
  112.7 8.0 %collective-permute-start.13 = (f32[16,24,128]{2,1,0:T(8,128)S(1)}, f32[16,24,128]{2,1,0:T(8,128)S(1)}, u32[]{:S(2)}, u32[]{:S(2)}) collective-permute-start(f32[16,24,128]{2,1,0:T(8,128)S(1)} %get-tuple-element.51), channel_id=1, source_target_pairs={{0,384},{128,0},{256,128},{384,256},{1,385},{129,1},{257,129},{385... | collective-permute-start | bytes 589832 | tf_op jit(solution)/shard_map/ppermute | solution.py:348
  115.4 13.1 %collective-permute-start.15 = (f32[16,24,128]{2,1,0:T(8,128)S(1)}, f32[16,24,128]{2,1,0:T(8,128)S(1)}, u32[]{:S(2)}, u32[]{:S(2)}) collective-permute-start(f32[16,24,128]{2,1,0:T(8,128)S(1)} %get-tuple-element.52), channel_id=1, source_target_pairs={{0,128},{128,256},{256,384},{384,0},{1,129},{129,257},{257,385},{3... | collective-permute-start | bytes 589832 | tf_op jit(solution)/shard_map/ppermute | solution.py:348
  118.0 10.6 %collective-permute-start.14 = (f32[16,24,128]{2,1,0:T(8,128)S(1)}, f32[16,24,128]{2,1,0:T(8,128)S(1)}, u32[]{:S(2)}, u32[]{:S(2)}) collective-permute-start(f32[16,24,128]{2,1,0:T(8,128)S(1)} %get-tuple-element.53), channel_id=1, source_target_pairs={{0,256},{128,384},{256,0},{384,128},{1,257},{129,385},{257,1},{385... | collective-permute-start | bytes 589832 | tf_op jit(solution)/shard_map/ppermute | solution.py:348
  156.7 3.6 %copy-start.2 = (f32[192,128]{1,0:T(8,128)S(1)}, f32[192,128]{1,0:T(8,128)}, u32[]{:S(2)}) copy-start(f32[192,128]{1,0:T(8,128)} %get-tuple-element.33.attended_ref) | copy-start | bytes 294916
  156.7 14.5 %all-to-all-start.5 = ((f32[4,144,128]{2,1,0:T(8,128)}), f32[4,144,128]{2,1,0:T(8,128)S(1)}, u32[]{:S(2)}, u32[]{:S(2)}) async-start(f32[4,144,128]{2,1,0:T(8,128)} %broadcast_in_dim.7), calls=%async_computation.5 | async-start | bytes 589824 | tf_op jit(solution)/shard_map/all_to_all | solution.py:339
  160.3 22.8 %copy-start.6 = (f32[384,128]{1,0:T(8,128)S(1)}, f32[384,128]{1,0:T(8,128)}, u32[]{:S(2)}) copy-start(f32[384,128]{1,0:T(8,128)} %get-tuple-element.48) | copy-start | bytes 589828
  160.9 24.2 %collective-permute-start.9 = (f32[192,128]{1,0:T(8,128)S(1)}, f32[192,128]{1,0:T(8,128)S(1)}, u32[]{:S(2)}, u32[]{:S(2)}) collective-permute-start(f32[192,128]{1,0:T(8,128)S(1)} %get-tuple-element.35), channel_id=1, source_target_pairs={{0,1},{1,2},{2,3},{3,0},{4,5},{5,6},{6,7},{7,4},{8,9},{9,10},{10,1... | collective-permute-start | bytes 294920 | tf_op jit(solution)/shard_map/ppermute | solution.py:348
  162.8 22.3 %collective-permute-start.10 = (f32[192,128]{1,0:T(8,128)S(1)}, f32[192,128]{1,0:T(8,128)S(1)}, u32[]{:S(2)}, u32[]{:S(2)}) collective-permute-start(f32[192,128]{1,0:T(8,128)S(1)} %get-tuple-element.36), channel_id=1, source_target_pairs={{0,2},{1,3},{2,0},{3,1},{4,6},{5,7},{6,4},{7,5},{8,10},{9,11},{10,... | collective-permute-start | bytes 294920 | tf_op jit(solution)/shard_map/ppermute | solution.py:348
  169.3 15.8 %collective-permute-start.11 = (f32[192,128]{1,0:T(8,128)S(1)}, f32[192,128]{1,0:T(8,128)S(1)}, u32[]{:S(2)}, u32[]{:S(2)}) collective-permute-start(f32[192,128]{1,0:T(8,128)S(1)} %get-tuple-element.37), channel_id=1, source_target_pairs={{0,3},{1,0},{2,1},{3,2},{4,7},{5,4},{6,5},{7,6},{8,11},{9,8},{10,9... | collective-permute-start | bytes 294920 | tf_op jit(solution)/shard_map/ppermute | solution.py:348
  171.2 16.1 %collective-permute-start.18 = (f32[4,144,128]{2,1,0:T(8,128)S(1)}, f32[4,144,128]{2,1,0:T(8,128)S(1)}, u32[]{:S(2)}, u32[]{:S(2)}) collective-permute-start(f32[4,144,128]{2,1,0:T(8,128)S(1)} %all-to-all-done.5.own_ref), channel_id=1, source_target_pairs={{0,4},{4,0},{1,5},{5,1},{2,6},{6,2},{3,7},{7,3},{8,12},{12,8},{9,1... | collective-permute-start | bytes 884744 | tf_op jit(solution)/shard_map/ppermute | solution.py:348
  183.1 3.3 %collective-permute-start.17 = (f32[384,128]{1,0:T(8,128)S(1)}, f32[384,128]{1,0:T(8,128)S(1)}, u32[]{:S(2)}, u32[]{:S(2)}) collective-permute-start(f32[384,128]{1,0:T(8,128)S(1)} %copy-done.6), channel_id=1, source_target_pairs={{0,4},{4,0},{1,5},{5,1},{2,6},{6,2},{3,7},{7,3},{8,12},{12,8},{9,1... | collective-permute-start | bytes 589832 | tf_op jit(solution)/shard_map/ppermute | solution.py:348
  185.1 1.4 copy-start.1
